TPU v7x, 32 devices: a whole 2x2x4 slice. The times are simulated.
32 devices in a mesh: graph: 16 (over z, y, x), mp: 2 (over core).
Axes of the slice: x: 2, y: 2, z: 4, core: 2. Of those that a mesh axis runs over, the one named last changes fastest.
Arguments:
- tokens: bfloat16 [32, 256, 768], P('graph'), may hold values from -30 to 30
- token_counts: int32 [16, 2], P('graph'), may hold values from 1 to 256, 384 in all within a row
- w_qkv: bfloat16 [768, 3, 768], P(None, None, 'mp'), may hold values from -0.21875 to 0.21875
- w_out: bfloat16 [768, 768], P('mp'), may hold values from -0.21875 to 0.21875
- w_up: bfloat16 [768, 3072], P(None, 'mp'), may hold values from -0.21875 to 0.21875
- w_down: bfloat16 [3072, 768], P('mp'), may hold values from -0.109375 to 0.109375
- ln_gains: float32 [2, 768], replicated, may hold values from 0.1 to 1.9
- cache: bfloat16 [8192, 768], P('graph', 'mp'), may hold values from -6 to 6
- node_text: int32 [8192], P('graph'), may hold values from -1 to 31, as said below
- adj_tiles: int32 [64, 5], P('graph'), may hold values from -1 to 63, as said below
- adj_values: bfloat16 [64, 5, 128, 128], P('graph'), may hold values from -0.1875 to 0.1875
- w_gnn: bfloat16 [768, 768], P('mp'), may hold values from -0.21875 to 0.21875
- out_grad: bfloat16 [8192, 768], P('graph', 'mp'), may hold values from -6 to 6
Outputs:
- node_out: bfloat16 [8192, 768], P('graph', 'mp')
- w_grad: float32 [768, 768], P('mp', 'graph')
- text_grad: float32 [32, 768], P('graph', 'mp')
- node_grad: bfloat16 [8192, 768], P('graph', 'mp')
Inputs may be any that keep to these rules, and one draw needn't show every extreme that they name: `token_counts`: the counts of one row sum to 384. `node_text`: every text number below 32 is held by exactly one node; every other node holds -1. `adj_tiles`: an entry names a source tile by its global number (tile j of block q is q * 4 + j) or is -1. The entries of a row tile are distinct and include the row tile itself and one other tile of its own block. A block lists at most one tile of any other block, in one entry only; a block lists tiles of at most 12 other blocks, and some block lists tiles of 12 other blocks; a tile is listed by at most 4 other blocks.
All inputs are finite; a program needn't handle non-finite values.
Results may differ from a plain program's by a relative error of at most 0.011.
Values may be sent and summed in bfloat16 or wider, within the bound.
No kernel may reach another device: no remote copies, remote signals or barrier semaphores. Data moves between devices by JAX's collectives and lax.ppermute only.
A program may use at most 192 MiB of HBM per device.

v0:
```python
import math

import jax
import jax.numpy as jnp
from jax import lax
from jax.sharding import PartitionSpec as P

HEAD = 64


norm_eps = 1e-05
masked_score = -1e30


def layer_norm(values, scale_row):
    average = jnp.mean(values, axis=-1, keepdims=True)
    centred = values - average
    variance = jnp.mean(centred * centred, axis=-1, keepdims=True)
    return centred * lax.rsqrt(variance + norm_eps) * scale_row


def softmax_rows(scores):
    row_max = jnp.max(scores, axis=-1, keepdims=True)
    powers = jnp.exp(scores - row_max)
    return powers / jnp.sum(powers, axis=-1, keepdims=True)


def encode(tokens, token_counts, w_qkv, w_out, w_up, w_down, ln_gains):
    text_count, seq_len, model_width = tokens.shape
    half_width = w_qkv.shape[2]
    heads_here = half_width // HEAD
    counts = token_counts.reshape(text_count)
    flat_tokens = tokens.reshape(text_count * seq_len, model_width)
    projected = jnp.dot(
        flat_tokens, w_qkv.reshape(model_width, 3 * half_width), preferred_element_type=jnp.float32
    ).astype(jnp.bfloat16)
    projected = projected.reshape(text_count, seq_len, 3, heads_here, HEAD)
    scores = jnp.einsum(
        "bqhe,bkhe->bhqk",
        projected[:, :, 0],
        projected[:, :, 1],
        preferred_element_type=jnp.float32,
    ) / math.sqrt(HEAD)
    valid = jnp.arange(seq_len, dtype=jnp.int32)[None, :] < counts[:, None]
    scores = jnp.where(valid[:, None, None, :], scores, masked_score)
    attn_weights = softmax_rows(scores).astype(jnp.bfloat16)
    context = jnp.einsum(
        "bhqk,bkhe->bqhe", attn_weights, projected[:, :, 2], preferred_element_type=jnp.float32
    )
    context = context.astype(jnp.bfloat16).reshape(text_count * seq_len, half_width)
    attention_layer = lax.psum(
        jnp.dot(context, w_out, preferred_element_type=jnp.float32).astype(jnp.bfloat16), "mp"
    ).astype(jnp.float32)
    first_norm = layer_norm(flat_tokens.astype(jnp.float32) + attention_layer, ln_gains[0]).astype(
        jnp.bfloat16
    )
    inner = jax.nn.gelu(jnp.dot(first_norm, w_up, preferred_element_type=jnp.float32)).astype(
        jnp.bfloat16
    )
    mlp_out = lax.psum(
        jnp.dot(inner, w_down, preferred_element_type=jnp.float32).astype(jnp.bfloat16), "mp"
    ).astype(jnp.float32)
    second_norm = layer_norm(first_norm.astype(jnp.float32) + mlp_out, ln_gains[1])
    second_norm = second_norm.reshape(text_count, seq_len, model_width)
    pooled = jnp.sum(jnp.where(valid[:, :, None], second_norm, 0.0), axis=1) / counts[
        :, None
    ].astype(jnp.float32)
    return pooled.astype(jnp.bfloat16)


def patch_rows(base_rows, text_ids, gathered):
    picked = jnp.take(gathered, jnp.maximum(text_ids, 0), axis=0)
    return jnp.where((text_ids >= 0)[:, None], picked, base_rows)


def on_device(
    tokens,
    token_counts,
    w_qkv,
    w_out,
    w_up,
    w_down,
    ln_gains,
    cache,
    node_text,
    adj_tiles,
    adj_values,
    w_gnn,
    out_grad,
):
    shards = lax.axis_size("graph")
    self_index = lax.axis_index("graph")
    nodes_here, half_width = cache.shape
    column = lax.axis_index("mp") * half_width
    tiles_here, entries, tile_rows = (adj_values.shape[0], adj_values.shape[1], adj_values.shape[2])
    entry_count = tiles_here * entries
    flat_ids = adj_tiles.reshape(entry_count)
    is_live = flat_ids >= 0
    tile_owner = jnp.where(is_live, flat_ids // tiles_here, -1)
    is_local = tile_owner == self_index
    matches = (
        tile_owner[None, :] == jnp.arange(shards, dtype=jnp.int32)[:, None]
    ) & jnp.logical_not(is_local)[None, :]
    has_entry = jnp.any(matches, axis=1)
    entry_index = jnp.sum(
        jnp.where(matches, jnp.arange(entry_count, dtype=jnp.int32)[None, :], 0), axis=1
    )
    wanted_tile = jnp.where(has_entry, jnp.take(flat_ids, entry_index) % tiles_here, -1)
    asked = lax.all_to_all(wanted_tile, "graph", split_axis=0, concat_axis=0, tiled=True)
    sending = asked >= 0
    sent_index = jnp.maximum(asked, 0)
    pooled = encode(tokens, token_counts, w_qkv, w_out, w_up, w_down, ln_gains)
    gathered = lax.all_gather(
        lax.dynamic_slice_in_dim(pooled, column, half_width, 1), "graph", axis=0, tiled=True
    )
    features = patch_rows(cache, node_text, gathered)
    feature_tiles = features.reshape(tiles_here, tile_rows, half_width)
    cache_tiles = cache.reshape(tiles_here, tile_rows, half_width)
    id_tiles = node_text.reshape(tiles_here, tile_rows)
    out_feat = jnp.where(
        sending[:, None, None],
        jnp.take(cache_tiles, sent_index, axis=0),
        jnp.zeros((), jnp.bfloat16),
    )
    out_ids = jnp.where(sending[:, None], jnp.take(id_tiles, sent_index, axis=0), -1)
    got_feat, got_ids = (
        lax.all_to_all(out_feat, "graph", split_axis=0, concat_axis=0, tiled=True),
        lax.all_to_all(out_ids, "graph", split_axis=0, concat_axis=0, tiled=True),
    )
    remote = patch_rows(
        got_feat.reshape(shards * tile_rows, half_width),
        got_ids.reshape(shards * tile_rows),
        gathered,
    )
    remote = remote.reshape(shards, tile_rows, half_width)
    source_table = jnp.concatenate([feature_tiles, remote], axis=0)
    source_index = jnp.where(
        is_local, flat_ids - self_index * tiles_here, tiles_here + jnp.maximum(tile_owner, 0)
    )
    source_index = jnp.where(is_live, source_index, 0)
    source_nodes = jnp.take(source_table, source_index, axis=0).reshape(
        tiles_here, entries, tile_rows, half_width
    )
    weight_values = jnp.where(
        is_live.reshape(tiles_here, entries)[:, :, None, None],
        adj_values,
        jnp.zeros((), jnp.bfloat16),
    )
    neighbor_aggregate = jnp.einsum(
        "zyps,zysq->zpq", weight_values, source_nodes, preferred_element_type=jnp.float32
    )
    neighbor_aggregate = neighbor_aggregate.astype(jnp.bfloat16).reshape(nodes_here, half_width)
    partial_hidden = jnp.dot(neighbor_aggregate, w_gnn, preferred_element_type=jnp.float32)
    hidden = lax.psum_scatter(
        partial_hidden.astype(jnp.bfloat16), "mp", scatter_dimension=1, tiled=True
    ).astype(jnp.float32)
    activated, pull = jax.vjp(jax.nn.gelu, hidden)
    self_gradient = pull(out_grad.astype(jnp.float32))[0].astype(jnp.bfloat16)
    grad_hidden = lax.all_gather(self_gradient, "mp", axis=1, tiled=True)
    node_out = (features.astype(jnp.float32) + activated).astype(jnp.bfloat16)
    local_wgrad = lax.dot_general(
        neighbor_aggregate,
        grad_hidden,
        (((0,), (0,)), ((), ())),
        preferred_element_type=jnp.float32,
    )
    w_part = lax.psum_scatter(local_wgrad, "graph", scatter_dimension=1, tiled=True)
    agg_grad = lax.dot_general(
        grad_hidden, w_gnn, (((1,), (1,)), ((), ())), preferred_element_type=jnp.float32
    ).astype(jnp.bfloat16)
    gradient_tile_list = agg_grad.reshape(tiles_here, tile_rows, half_width)
    neighbor_contribution = jnp.einsum(
        "uscq,uch->usqh", weight_values, gradient_tile_list, preferred_element_type=jnp.float32
    )
    neighbor_contribution = neighbor_contribution.reshape(entry_count, tile_rows, half_width)
    outgoing = jnp.where(
        has_entry[:, None, None], jnp.take(neighbor_contribution, entry_index, axis=0), 0.0
    ).astype(jnp.bfloat16)
    incoming = lax.all_to_all(outgoing, "graph", split_axis=0, concat_axis=0, tiled=True)
    onehot_dest = (
        (sent_index[None, :] == jnp.arange(tiles_here, dtype=jnp.int32)[:, None]) & sending[None, :]
    ).astype(jnp.bfloat16)
    back_remote = jnp.dot(
        onehot_dest,
        incoming.reshape(shards, tile_rows * half_width),
        preferred_element_type=jnp.float32,
    )
    local_dest = jnp.where(is_local, flat_ids - self_index * tiles_here, tiles_here)
    back_local = (
        jnp.zeros((tiles_here + 1, tile_rows, half_width), jnp.float32)
        .at[local_dest]
        .add(neighbor_contribution)[:tiles_here]
    )
    grad_nodes = out_grad.astype(jnp.float32) + (
        back_local.reshape(tiles_here, tile_rows * half_width) + back_remote
    ).reshape(nodes_here, half_width)
    node_grad = grad_nodes.astype(jnp.bfloat16)
    texts_all = gathered.shape[0]
    text_slot = jnp.where(node_text >= 0, node_text, texts_all)
    text_term = (
        jnp.zeros((texts_all + 1, half_width), jnp.float32)
        .at[text_slot]
        .add(grad_nodes)[:texts_all]
    )
    text_part = lax.psum_scatter(text_term, "graph", scatter_dimension=0, tiled=True)
    return (node_out, w_part, text_part, node_grad)


def solution(mesh):
    placed = (
        P("graph", None, None),
        P("graph", None),
        P(None, None, "mp"),
        P("mp", None),
        P(None, "mp"),
        P("mp", None),
        P(),
        P("graph", "mp"),
        P("graph"),
        P("graph", None),
        P("graph", None, None, None),
        P("mp", None),
        P("graph", "mp"),
    )
    return jax.shard_map(
        on_device,
        mesh=mesh,
        in_specs=placed,
        out_specs=(P("graph", "mp"), P("mp", "graph"), P("graph", "mp"), P("graph", "mp")),
        check_vma=False,
    )
```

profile of v0, /device:TPU:0, one launch (start us, length us, event | category | flops | bytes accessed | tf_op | source)
XLA Modules:
  0.0 341.1 jit_solution(5058054835150567496)
XLA Ops:
  9.8 8.3 %all-to-all-start = ((s32[16,1,1]{2,1,0:T(1,128)}), s32[16,1,1]{2,1,0:T(1,128)S(1)}, u32[]{:S(2)}, u32[]{:S(2)}) async-start(s32[16,1,1]{2,1,0:T(1,128)} %copy.63), calls=%async_computation | async-start | bytes 16384 | tf_op jit(solution)/shard_map/all_to_all | solution.py:109
  18.9 3.9 %copy.56 = bf16[768,3,384]{0,2,1:T(8,128)(2,1)} copy(bf16[768,3,384]{2,0,1:T(8,128)(2,1)} %param.15) | data formatting | bytes 3538944 | tf_op args[2]
  22.8 3.7 %convolution_convert_fusion = bf16[512,1152]{1,0:T(8,128)(2,1)} fusion(bf16[512,768]{1,0:T(8,128)(2,1)S(1)} %bitcast.107, bf16[768,1152]{0,1:T(8,128)(2,1)} %bitcast.115), kind=kOutput, calls=%fused_computation.24 | convolution fusion | flops 906559488 | bytes 3735552 | tf_op jit(solution)/shard_map/dot_general | solution.py:34
  29.0 3.7 %reshape.562 = bf16[2,256,3,6,64]{1,0,4,3,2:T(2,128)(2,1)} reshape(bf16[512,1152]{0,1:T(8,128)(2,1)} %copy.57) | data formatting | bytes 2359296 | tf_op jit(solution)/shard_map/reshape | solution.py:37
  53.2 6.9 %all-to-all-start.1 = ((s32[16,1,128]{2,1,0:T(1,128)}), s32[16,1,128]{2,1,0:T(1,128)S(1)}, u32[]{:S(2)}, u32[]{:S(2)}) async-start(s32[16,1,128]{2,1,0:T(1,128)} %bitcast.124), calls=%async_computation.1 | async-start | bytes 16384 | tf_op jit(solution)/shard_map/all_to_all | solution.py:128
  60.1 2.9 select_select_fusion
  67.3 5.0 %all-to-all-start.2 = ((bf16[16,128,384]{2,1,0:T(8,128)(2,1)}), bf16[16,128,384]{2,1,0:T(8,128)(2,1)}, u32[]{:S(2)}, u32[]{:S(2)}) async-start(bf16[16,128,384]{2,1,0:T(8,128)(2,1)} %select_select_fusion), calls=%async_computation.2 | async-start | bytes 3145728 | tf_op jit(solution)/shard_map/all_to_all | solution.py:127
  72.4 5.3 %fusion.23 = bf16[512,768]{1,0:T(8,128)(2,1)} fusion(bf16[1536,768]{1,0:T(8,128)(2,1)S(1)} %copy-done, bf16[512,768]{1,0:T(8,128)(2,1)S(1)} %multiply_convert_fusion, bf16[768,1536]{1,0:T(8,128)(2,1)} %param.17), kind=kOutput, calls=%fused_computation.53 | convolution fusion | flops 2423390208 | bytes 6291456 | tf_op jit(solution)/shard_map/dot_general | solution.py:61
  81.0 17.2 %all-reduce.6.cloned.1.call-done = bf16[512,768]{1,0:T(8,128)(2,1)} async-done(((bf16[512,768]{1,0:T(8,128)(2,1)}), bf16[512,768]{1,0:T(8,128)(2,1)}) %all-reduce.6.cloned.1.call-update) | async-done | bytes 786448 | tf_op jit(solution)/shard_map/psum | solution.py:60
  100.6 41.0 %all-gather = bf16[16,2,384]{2,1,0:T(2,128)(2,1)S(1)} all-gather(bf16[1,2,384]{2,1,0:T(2,128)(2,1)S(1)} %fusion.63), channel_id=1, replica_groups=mesh['graph'=16,'mp'=2] {'graph'}, dimensions={0}, use_global_device_ids=true | all-gather | bytes 26112 | tf_op jit(solution)/shard_map/all_gather | solution.py:113
  141.7 9.1 %gather_fusion.3 = bf16[2048,384]{1,0:T(8,128)(2,1)} fusion(bf16[32,384]{1,0:T(8,128)(2,1)S(1)} %reshape.654, s32[2048]{0:T(1024)S(1)} %bitcast_clamp_fusion), kind=kCustom, calls=%fused_computation.3 | custom fusion | bytes 3153920 | tf_op jit(solution)/shard_map/jit(_take)/gather | solution.py:72
  157.3 4.0 %gather_fusion.5 = bf16[20,128,384]{2,1,0:T(8,128)(2,1)} fusion(bf16[20,128,384]{2,1,0:T(8,128)(2,1)} %pad_maximum_fusion, s32[1024]{0:T(1024)} %pad_clamp_fusion), kind=kCustom, calls=%fused_computation.5 | custom fusion | bytes 3932240 | tf_op jit(solution)/shard_map/jit(_take)/gather | solution.py:141
  167.7 4.1 %reduce-scatter.7.cloned.1.call-done = bf16[384,512]{1,0:T(8,128)(2,1)} async-done(((bf16[768,512]{1,0:T(8,128)(2,1)}), bf16[384,512]{1,0:T(8,128)(2,1)}) %reduce-scatter.7.cloned.1.call-update) | async-done | bytes 393232
  173.8 2.5 fusion.38
  176.2 2.5 all_gather.7
  179.3 2.7 fusion.47
  182.0 4.1 %gather_fusion.6 = bf16[16,128,384]{2,1,0:T(8,128)(2,1)} fusion(f32[20,128,384]{2,1,0:T(8,128)} %bitcast.104, s32[1024]{0:T(1024)} %copy-done.21), kind=kCustom, calls=%fused_computation.6 | custom fusion | bytes 3145792 | tf_op jit(solution)/shard_map/jit(_take)/gather | solution.py:177
  186.1 3.3 select_convert_fusion
  189.4 6.8 %all-to-all-start.3 = ((bf16[16,128,384]{2,1,0:T(8,128)(2,1)}), bf16[16,128,384]{2,1,0:T(8,128)(2,1)}, u32[]{:S(2)}, u32[]{:S(2)}) async-start(bf16[16,128,384]{2,1,0:T(8,128)(2,1)} %select_convert_fusion), calls=%async_computation.4 | async-start | bytes 3145728 | tf_op jit(solution)/shard_map/all_to_all | solution.py:179
  199.5 7.3 %scatter_fusion = f32[5,128,384]{2,1,0:T(8,128)S(1)} fusion(f32[5,128,384]{2,1,0:T(8,128)S(1)} %broadcast_in_dim.230, s32[20]{0:T(128)S(1)} %copy-done.26, f32[20,128,384]{2,1,0:T(8,128)} %bitcast.105), kind=kCustom, calls=%fused_computation.7 | custom fusion | flops 983040 | bytes 11796560 | tf_op jit(solution)/shard_map/scatter-add | solution.py:192
  207.4 25.1 %all-to-all-done.3 = bf16[16,128,384]{2,1,0:T(8,128)(2,1)} async-done(((bf16[16,128,384]{2,1,0:T(8,128)(2,1)}), bf16[16,128,384]{2,1,0:T(8,128)(2,1)}, u32[]{:S(2)}, u32[]{:S(2)}) %all-to-all-start.3) | async-done | bytes 1572896 | tf_op jit(solution)/shard_map/all_to_all | solution.py:179
  237.9 4.9 %scatter_custom_fusion.1 = f32[33,384]{1,0:T(8,128)} fusion(s32[512]{0:T(512)} %get-tuple-element.17, f32[512,384]{1,0:T(8,128)S(1)} %reshape.575, bf16[512,384]{1,0:T(8,128)(2,1)S(1)} %copy-done.7, f32[]{:T(128)} %constant.119.clone.1), kind=kCustom, calls=%fused_computation.80 | custom fusion | flops 589824 | bytes 1230848 | tf_op jit(solution)/shard_map/scatter-add | solution.py:203
  244.2 80.1 %all-reduce = f32[32,384]{1,0:T(8,128)} all-reduce(f32[32,384]{1,0:T(8,128)} %slice.46), channel_id=4, replica_groups=mesh['graph'=16,'mp'=2] {'graph'}, use_global_device_ids=true, to_apply=%region_15.16.clone | all-reduce | flops 12288 | bytes 98304
  326.4 8.2 %reduce-scatter.5.cloned.1.call-done = f32[384,48]{0,1:T(8,128)} async-done(((f32[384,768]{0,1:T(8,128)}), f32[384,48]{0,1:T(8,128)}) %reduce-scatter.5.cloned.1.call-update) | async-done | bytes 73744 | tf_op jit(solution)/shard_map/reduce_scatter | solution.py:167
  (159 shorter events, 63.6 us)
Async XLA Ops:
  7.2 65.2 %copy-start = (bf16[1536,768]{1,0:T(8,128)(2,1)S(1)}, bf16[1536,768]{1,0:T(8,128)(2,1)}, u32[]{:S(2)}) copy-start(bf16[1536,768]{1,0:T(8,128)(2,1)} %param.18) | copy-start | bytes 7077892
  8.2 14.6 %copy-start.27 = (pred[16]{0:T(512)(128)(4,1)}, pred[16]{0:T(512)(128)(4,1)S(1)}, u32[]{:S(2)}) copy-start(pred[16]{0:T(512)(128)(4,1)S(1)} %fusion.56) | copy-start | bytes 52
  8.4 14.5 %copy-start.33 = (s32[16]{0:T(128)}, s32[16]{0:T(128)S(1)}, u32[]{:S(2)}) copy-start(s32[16]{0:T(128)S(1)} %select_reduce_fusion.1) | copy-start | bytes 196
  8.4 14.4 %copy-start.21 = (s32[1024]{0:T(1024)}, s32[1024]{0:T(1024)S(1)}, u32[]{:S(2)}) copy-start(s32[1024]{0:T(1024)S(1)} %pad_clamp_fusion.2) | copy-start | bytes 12292
  9.8 36.6 %all-to-all-start = ((s32[16,1,1]{2,1,0:T(1,128)}), s32[16,1,1]{2,1,0:T(1,128)S(1)}, u32[]{:S(2)}, u32[]{:S(2)}) async-start(s32[16,1,1]{2,1,0:T(1,128)} %copy.63), calls=%async_computation | async-start | bytes 16384 | tf_op jit(solution)/shard_map/all_to_all | solution.py:109
  18.1 44.8 %all-reduce.4.cloned.1.call-start = ((), (), s32[]{:S(2)}) async-start(), calls=%async_computation.6 | async-start | bytes 1572864 | tf_op jit(solution)/shard_map/psum | solution.py:51
  18.9 16.5 %copy-start.31 = (pred[2,256]{1,0:T(4,128)(4,1)}, pred[2,256]{1,0:T(4,128)(4,1)S(1)}, u32[]{:S(2)}) copy-start(pred[2,256]{1,0:T(4,128)(4,1)S(1)} %iota_compare_fusion.2) | copy-start | bytes 1540
  18.9 3.9 %copy-start.2 = (bf16[2,256,768]{2,1,0:T(8,128)(2,1)S(1)}, bf16[2,256,768]{2,1,0:T(8,128)(2,1)}, u32[]{:S(2)}) copy-start(bf16[2,256,768]{2,1,0:T(8,128)(2,1)} %param.13) | copy-start | bytes 2359300
  37.4 4.6 %copy-start.13 = (s32[4,5]{1,0:T(4,128)S(1)}, s32[4,5]{1,0:T(4,128)}, u32[]{:S(2)}) copy-start(s32[4,5]{1,0:T(4,128)} %param.22) | copy-start | bytes 244
  37.4 11.3 %copy-start.1 = (bf16[512,384]{1,0:T(8,128)(2,1)S(1)}, bf16[512,384]{1,0:T(8,128)(2,1)}, u32[]{:S(2)}) copy-start(bf16[512,384]{1,0:T(8,128)(2,1)} %param.20) | copy-start | bytes 1179652
  53.2 14.1 %all-to-all-start.1 = ((s32[16,1,128]{2,1,0:T(1,128)}), s32[16,1,128]{2,1,0:T(1,128)S(1)}, u32[]{:S(2)}, u32[]{:S(2)}) async-start(s32[16,1,128]{2,1,0:T(1,128)} %bitcast.124), calls=%async_computation.1 | async-start | bytes 16384 | tf_op jit(solution)/shard_map/all_to_all | solution.py:128
  67.3 86.3 %all-to-all-start.2 = ((bf16[16,128,384]{2,1,0:T(8,128)(2,1)}), bf16[16,128,384]{2,1,0:T(8,128)(2,1)}, u32[]{:S(2)}, u32[]{:S(2)}) async-start(bf16[16,128,384]{2,1,0:T(8,128)(2,1)} %select_select_fusion), calls=%async_computation.2 | async-start | bytes 3145728 | tf_op jit(solution)/shard_map/all_to_all | solution.py:127
  72.3 5.7 %copy-start.19 = (s32[512]{0:T(512)S(1)}, s32[512]{0:T(512)}, u32[]{:S(2)}) copy-start(s32[512]{0:T(512)} %get-tuple-element.18) | copy-start | bytes 6148
  72.4 25.8 %all-reduce.6.cloned.1.call-start = ((), (), s32[]{:S(2)}) async-start(), calls=%async_computation.7 | async-start | bytes 1572864 | tf_op jit(solution)/shard_map/psum | solution.py:60
  77.8 94.1 %reduce-scatter.7.cloned.1.call-start = ((), (), s32[]{:S(2)}) async-start(), calls=%async_computation.9 | async-start | bytes 1179648
  81.0 19.1 %copy-start.14 = (f32[768]{0:T(1024)S(1)}, f32[768]{0:T(1024)}, u32[]{:S(2)}) copy-start(f32[768]{0:T(1024)} %get-tuple-element.4) | copy-start | bytes 9220
  141.7 9.1 %copy-start.16 = (s32[1024]{0:T(1024)S(1)}, s32[1024]{0:T(1024)}, u32[]{:S(2)}) copy-start(s32[1024]{0:T(1024)} %pad_clamp_fusion.3) | copy-start | bytes 12292
  157.3 4.0 %copy-start.30 = (pred[4,5]{1,0:T(4,128)(4,1)S(1)}, pred[4,5]{1,0:T(4,128)(4,1)}, u32[]{:S(2)}) copy-start(pred[4,5]{1,0:T(4,128)(4,1)} %get-tuple-element.19) | copy-start | bytes 64
  157.3 4.0 %copy-start.36 = (pred[4,5]{1,0:T(4,128)(4,1)S(1)}, pred[4,5]{1,0:T(4,128)(4,1)}, u32[]{:S(2)}) copy-start(pred[4,5]{1,0:T(4,128)(4,1)} %get-tuple-element.20) | copy-start | bytes 64
  165.3 8.5 %copy-start.6 = (bf16[512,384]{1,0:T(8,128)(2,1)S(1)}, bf16[512,384]{1,0:T(8,128)(2,1)}, u32[]{:S(2)}) copy-start(bf16[512,384]{1,0:T(8,128)(2,1)} %param.25) | copy-start | bytes 1179652
  173.8 5.0 %copy-start.12 = (bf16[384,768]{1,0:T(8,128)(2,1)S(1)}, bf16[384,768]{1,0:T(8,128)(2,1)}, u32[]{:S(2)}) copy-start(bf16[384,768]{1,0:T(8,128)(2,1)} %param.24) | copy-start | bytes 1769476
  182.0 4.1 %copy-start.28 = (pred[16]{0:T(512)(128)(4,1)S(1)}, pred[16]{0:T(512)(128)(4,1)}, u32[]{:S(2)}) copy-start(pred[16]{0:T(512)(128)(4,1)} %copy-done.27) | copy-start | bytes 52
  189.4 43.1 %all-to-all-start.3 = ((bf16[16,128,384]{2,1,0:T(8,128)(2,1)}), bf16[16,128,384]{2,1,0:T(8,128)(2,1)}, u32[]{:S(2)}, u32[]{:S(2)}) async-start(bf16[16,128,384]{2,1,0:T(8,128)(2,1)} %select_convert_fusion), calls=%async_computation.4 | async-start | bytes 3145728 | tf_op jit(solution)/shard_map/all_to_all | solution.py:179
  196.2 138.5 %reduce-scatter.5.cloned.1.call-start = ((), (), s32[]{:S(2)}) async-start(), calls=%async_computation.8 | async-start | bytes 1253376 | tf_op jit(solution)/shard_map/reduce_scatter | solution.py:167
  (22 other events, 46.1 us)
Sparse Core Ops, SparseCore 0:
  39.7 20.2 all-reduce.3
  77.9 20.1 all-reduce.5
  167.8 4.0 reduce-scatter.6
  202.0 132.5 reduce-scatter.4
where the time goes:
time: 343 us; the launch traced here: 341 us
  blocking collectives  124 us (36%)
  waiting for transfers between devices  56.7 us (17%)
  local copies, waits for them, and re-layouts  52 us (15%)
  other arithmetic  44.5 us (13%)
  starting transfers between devices  27.6 us (8%)
  matrix products  21.8 us (6%)
  between operations  15 us (4%)
    unnamed x1, blocking collectives  80.1 us
    all_gather x1, blocking collectives, on_device(): lax.all_gather(lax.dynamic_slice_in_dim(pooled, column, half_width, 1), '...  41 us
    all_to_all x1, waiting for transfers between devices, on_device(): lax.all_to_all(outgoing, 'graph', split_axis=0, concat_axis=0, tiled=True)  25.1 us
    psum x1, waiting for transfers between devices, encode(): lax.psum(jnp.dot(inner, w_down, preferred_element_type=jnp.float32).astyp...  17.2 us
    unnamed x86, local copies, waits for them, and re-layouts  13.8 us
    gather x2, local copies, waits for them, and re-layouts, patch_rows(): picked = jnp.take(gathered, jnp.maximum(text_ids, 0), axis=0)  11 us
    all_to_all x1, starting transfers between devices, on_device(): lax.all_to_all(wanted_tile, 'graph', split_axis=0, concat_axis=0, tiled=T...  8.34 us
    reduce_scatter x1, waiting for transfers between devices, on_device(): lax.psum_scatter(local_wgrad, 'graph', scatter_dimension=1, tiled=True)  8.24 us
  transfers between devices with their start and end apart: 8, of which 5 were waited for; matrix products, arithmetic and copies ran while one was open for 25% of the time, Pallas kernels for 0%

commit v1 on v0

v1 whole, which is shorter than its diff:
```python
import functools

import jax
import jax.numpy as jnp
from jax import lax
from jax.experimental import pallas as pl
from jax.experimental.pallas import tpu as pltpu
from jax.sharding import PartitionSpec as P

HEAD = 64
LANES = 128
ROWS = 16
NORM_EPS = 1e-05
MASKED = -1e30
NO_NODE = -(1 << 20)
ROOT = 0.7978845608028654
CUBE = 0.044715

VMEM = pl.BlockSpec(memory_space=pltpu.VMEM)
SMEM = pl.BlockSpec(memory_space=pltpu.SMEM)


def up_to(value, unit):
    return (value + unit - 1) // unit * unit


def call(body, outs, ins, specs, flops, scratch=(), name=None):
    moved = sum(a.size * a.dtype.itemsize for a in ins) + sum(
        o.size * o.dtype.itemsize for o in outs
    )
    many = len(outs) > 1
    return pl.pallas_call(
        body,
        out_shape=tuple(outs) if many else outs[0],
        in_specs=list(specs),
        out_specs=tuple([VMEM] * len(outs)) if many else VMEM,
        scratch_shapes=list(scratch),
        cost_estimate=pl.CostEstimate(flops=flops, bytes_accessed=moved, transcendentals=0),
        name=name,
    )(*ins)


def shape(dims, dtype=jnp.bfloat16):
    return jax.ShapeDtypeStruct(tuple(dims), dtype)


def mm(a, b, dims=(1, 0)):
    return lax.dot_general(
        a, b, (((dims[0],), (dims[1],)), ((), ())), preferred_element_type=jnp.float32
    )


def tile_of(tile_id, tiles_here):
    safe = jnp.maximum(tile_id, 0)
    owner = lax.div(safe, jnp.int32(tiles_here))
    return safe, owner, safe - owner * tiles_here


def index_body(texts_here, ids_ref, self_ref, text_ref, out_ref):
    tiles_here, entries = ids_ref.shape
    shards, lanes = out_ref.shape
    width = lanes - LANES
    texts = texts_here * shards
    me = self_ref[0]
    row = lax.broadcasted_iota(jnp.int32, (shards, LANES), 0)
    wanted = jnp.full((shards, LANES), -1, jnp.int32)
    for r in range(tiles_here):
        for k in range(entries):
            tile_id = ids_ref[r, k]
            _, owner, place = tile_of(tile_id, tiles_here)
            target = jnp.where((tile_id >= 0) & (owner != me), owner, -1)
            wanted = jnp.where(row == target, place, wanted)
    out_ref[:, width:] = wanted
    tile_rows = text_ref.shape[1]
    lane = lax.broadcasted_iota(jnp.int32, (LANES, tile_rows), 1)
    sub = lax.broadcasted_iota(jnp.int32, (LANES, LANES), 0)
    diagonal = sub == lax.broadcasted_iota(jnp.int32, (LANES, LANES), 1)
    for c in range(width // LANES):
        slot = c * LANES + lax.broadcasted_iota(jnp.int32, (LANES, 1), 0)
        part = lax.div(slot, jnp.int32(shards))
        text = jnp.where(slot < texts, (slot - part * shards) * texts_here + part, -5)
        best = jnp.full((LANES, tile_rows), NO_NODE, jnp.int32)
        for j in range(tiles_here):
            node = (me * tiles_here + j) * tile_rows + lane
            best = jnp.where(text_ref[j : j + 1, :] == text, node, best)
        column = jnp.max(best.astype(jnp.float32), axis=1, keepdims=True)
        line = jnp.max(jnp.where(diagonal, column, float(NO_NODE)), axis=0, keepdims=True)
        out_ref[:, c * LANES : (c + 1) * LANES] = jnp.broadcast_to(
            line, (shards, LANES)
        ).astype(jnp.int32)


def pack_body(asked_ref, cache_ref, out_ref):
    def one(q, carry):
        out_ref[q] = cache_ref[jnp.maximum(asked_ref[q], 0)]
        return carry

    lax.fori_loop(0, out_ref.shape[0], one, 0)


def mask_body(ids_ref, self_ref, got_ref, adj_ref, cache_ref, kept_ref, pick_ref, own_ref, base_ref):
    tiles_here, entries, tile_rows, _ = adj_ref.shape
    width = got_ref.shape[1] - LANES
    me = self_ref[0]
    table = jnp.max(got_ref[:, :width].astype(jnp.float32), axis=0, keepdims=True)
    place = lax.broadcasted_iota(jnp.int32, (tile_rows, width), 0).astype(jnp.float32)
    ones = jnp.ones((ROWS, width), jnp.bfloat16)

    def holds(tile_id):
        first = (tile_id * tile_rows).astype(jnp.float32)
        return jnp.where(table - first == place, 1.0, 0.0)

    for r in range(tiles_here):

        def one(k, total):
            tile_id = ids_ref[r, k]
            hot = holds(tile_id).astype(jnp.bfloat16)
            values = adj_ref[r, k]
            taken = mm(ones, hot, (1, 1))[0:1, :]
            keep = jnp.where(tile_id >= 0, 1.0, 0.0) * jnp.where(taken > 0.5, 0.0, 1.0)
            kept_ref[r, k] = (values.astype(jnp.float32) * keep).astype(jnp.bfloat16)
            return total + mm(values, hot)

        pick = lax.fori_loop(0, entries, one, jnp.zeros((tile_rows, width), jnp.float32))
        pick_ref[r] = pick.astype(jnp.bfloat16)
        hot = holds(me * tiles_here + r)
        own_ref[r] = hot.astype(jnp.bfloat16)
        fresh = jnp.max(hot, axis=1, keepdims=True)
        base_ref[r] = (cache_ref[r].astype(jnp.float32) * (1.0 - fresh)).astype(jnp.bfloat16)


def norm(values, gain):
    average = jnp.mean(values, axis=-1, keepdims=True)
    centred = values - average
    variance = jnp.mean(centred * centred, axis=-1, keepdims=True)
    return centred * lax.rsqrt(variance + NORM_EPS) * gain


def attend_body(seq, counts_ref, tokens_ref, w_qkv_ref, w_out_ref, out_ref, proj_ref, ctx_ref):
    half = w_out_ref.shape[0]
    texts_here = tokens_ref.shape[0] // seq
    for c in range(3):
        proj_ref[:, c * half : (c + 1) * half] = mm(
            tokens_ref[...], w_qkv_ref[:, c * half : (c + 1) * half]
        ).astype(jnp.bfloat16)
    left = lax.broadcasted_iota(jnp.int32, (seq, LANES), 1) < HEAD
    key_at = lax.broadcasted_iota(jnp.int32, (seq, seq), 1)
    for t in range(texts_here):
        rows = slice(t * seq, (t + 1) * seq)
        live = key_at < counts_ref[0, t]
        for pair in range(half // LANES):
            first = pair * LANES
            query = proj_ref[rows, first : first + LANES].astype(jnp.float32) * (HEAD**-0.5)
            key = proj_ref[rows, half + first : half + first + LANES]
            value = proj_ref[rows, 2 * half + first : 2 * half + first + LANES]
            sides = []
            for side in (left, jnp.logical_not(left)):
                scores = mm(jnp.where(side, query, 0.0).astype(jnp.bfloat16), key, (1, 1))
                scores = jnp.where(live, scores, MASKED)
                powers = jnp.exp(scores - jnp.max(scores, axis=-1, keepdims=True))
                total = jnp.sum(powers, axis=-1, keepdims=True)
                sides.append(mm((powers / total).astype(jnp.bfloat16), value))
            ctx_ref[rows, first : first + LANES] = jnp.where(left, sides[0], sides[1]).astype(
                jnp.bfloat16
            )
    out_ref[...] = mm(ctx_ref[...], w_out_ref[...]).astype(jnp.bfloat16)


def inner_body(tokens_ref, mine_ref, other_ref, up_ref, down_ref, gains_ref, first_ref, out_ref, inner_ref):
    added = mine_ref[...].astype(jnp.float32) + other_ref[...].astype(jnp.float32)
    first = norm(tokens_ref[...].astype(jnp.float32) + added, gains_ref[0:1, :])
    first_ref[...] = first.astype(jnp.bfloat16)
    hidden_units = up_ref.shape[1]
    step = hidden_units // 4
    for c in range(4):
        cols = slice(c * step, (c + 1) * step)
        value = mm(first_ref[...], up_ref[:, cols])
        gate = jnp.tanh(ROOT * (value + CUBE * (value * value * value)))
        inner_ref[:, cols] = (0.5 * value * (1.0 + gate)).astype(jnp.bfloat16)
    out_ref[...] = mm(inner_ref[...], down_ref[...]).astype(jnp.bfloat16)


def pool_body(seq, counts_ref, core_ref, first_ref, mine_ref, other_ref, gains_ref, out_ref, pooled_ref):
    shards, lanes = out_ref.shape
    texts_here = first_ref.shape[0] // seq
    half = lanes // texts_here
    for t in range(texts_here):
        rows = slice(t * seq, (t + 1) * seq)
        added = mine_ref[rows, :].astype(jnp.float32) + other_ref[rows, :].astype(jnp.float32)
        second = norm(first_ref[rows, :].astype(jnp.float32) + added, gains_ref[1:2, :])
        count = counts_ref[0, t]
        live = lax.broadcasted_iota(jnp.int32, (seq, 1), 0) < count
        total = jnp.sum(jnp.where(live, second, 0.0), axis=0, keepdims=True)
        pooled_ref[...] = jnp.broadcast_to(
            total / count.astype(jnp.float32), pooled_ref.shape
        )
        start = pl.multiple_of(core_ref[0] * half, LANES)
        own = pooled_ref[:, pl.ds(start, half)][0:1, :]
        out_ref[:, t * half : (t + 1) * half] = jnp.broadcast_to(own, (shards, half)).astype(
            jnp.bfloat16
        )


def pooled_rows(pooled_ref, half):
    parts = pooled_ref.shape[1] // half
    return jnp.concatenate([pooled_ref[:, i * half : (i + 1) * half] for i in range(parts)], axis=0)


def gather_body(ids_ref, self_ref, kept_ref, pick_ref, pooled_ref, cache_ref, remote_ref, out_ref, source_ref):
    tiles_here, entries, tile_rows, _ = kept_ref.shape
    half = cache_ref.shape[2]
    me = self_ref[0]
    pooled = pooled_rows(pooled_ref, half)
    texts = pooled.shape[0]
    for r in range(tiles_here):

        def fetch(k, carry):
            tile_id = ids_ref[r, k]
            _, owner, place = tile_of(tile_id, tiles_here)
            local = (owner == me) | (tile_id < 0)

            @pl.when(local)
            def _():
                source_ref[k] = cache_ref[place]

            @pl.when(jnp.logical_not(local))
            def _():
                source_ref[k] = remote_ref[owner]

            return carry

        lax.fori_loop(0, entries, fetch, 0)
        total = mm(pick_ref[r][:, :texts], pooled)
        for k in range(entries):
            total = total + mm(kept_ref[r, k], source_ref[k])
        out_ref[r] = total.astype(jnp.bfloat16)


def forward_body(core_ref, mine_ref, other_ref, w_own_ref, w_other_ref, grad_ref, own_ref, base_ref, pooled_ref, node_ref, slope_ref):
    rows, half = mine_ref.shape
    start = pl.multiple_of(core_ref[0] * half, LANES)
    hidden = mm(mine_ref[...], w_own_ref[:, pl.ds(start, half)]) + mm(
        other_ref[...], w_other_ref[...]
    )
    square = hidden * hidden
    gate = jnp.tanh(ROOT * hidden * (1.0 + CUBE * square))
    lifted = 0.5 * (1.0 + gate)
    slope = lifted + 0.5 * hidden * (1.0 - gate * gate) * (ROOT * (1.0 + 3.0 * CUBE * square))
    slope_ref[...] = (grad_ref[...].astype(jnp.float32) * slope).astype(jnp.bfloat16)
    pooled = pooled_rows(pooled_ref, half)
    fresh = mm(own_ref[:, : pooled.shape[0]], pooled)
    node_ref[...] = (base_ref[...].astype(jnp.float32) + fresh + hidden * lifted).astype(
        jnp.bfloat16
    )


def backward_body(
    per, texts_here, ids_ref, self_ref, core_ref, mine_ref, other_ref, agg_ref, w_own_ref, adj_ref,
    pick_ref, own_ref, grad_ref, send_ref, local_ref, down_ref, w_ref, text_ref
):
    tiles_here, entries, tile_rows, _ = adj_ref.shape
    half = agg_ref.shape[1]
    shards = send_ref.shape[0]
    me = self_ref[0]
    core = core_ref[0]
    own = pl.multiple_of(core * half, LANES)
    far = pl.multiple_of((1 - core) * half, LANES)
    down = mm(mine_ref[...], w_own_ref[:, pl.ds(own, half)], (1, 1)) + mm(
        other_ref[...], w_own_ref[:, pl.ds(far, half)], (1, 1)
    )
    down_ref[...] = down.astype(jnp.bfloat16)
    local_ref[...] = grad_ref[...].astype(jnp.float32)
    for r in range(tiles_here):
        rows = slice(r * tile_rows, (r + 1) * tile_rows)

        def one(k, carry):
            tile_id = ids_ref[r, k]
            _, owner, place = tile_of(tile_id, tiles_here)

            @pl.when((tile_id >= 0) & (owner == me))
            def _():
                local_ref[place] += mm(adj_ref[r, k], down_ref[rows, :], (0, 0))

            @pl.when((tile_id >= 0) & (owner != me))
            def _():
                send_ref[owner, :tile_rows, :] = mm(
                    adj_ref[r, k], down_ref[rows, :], (0, 0)
                ).astype(jnp.bfloat16)

            return carry

        lax.fori_loop(0, entries, one, 0)
    text_ref[...] = mm(pick_ref[...], down_ref[...], (0, 0)) + mm(
        own_ref[...], grad_ref[...].reshape(tiles_here * tile_rows, half), (0, 0)
    )
    columns = 2 * half
    w_ref[pl.ds(own, half), :] = mm(mine_ref[...], agg_ref[...], (0, 0))
    w_ref[pl.ds(far, half), :] = mm(other_ref[...], agg_ref[...], (0, 0))
    w_ref[columns:, :] = jnp.zeros((w_ref.shape[0] - columns, half), jnp.float32)
    deep = up_to(per, ROWS)
    row = lax.broadcasted_iota(jnp.int32, (ROWS, half), 0)
    for q in range(shards):
        send_ref[q, tile_rows : tile_rows + deep, :] = w_ref[q * per : q * per + deep, :].astype(
            jnp.bfloat16
        )
        block = jnp.zeros((ROWS, half), jnp.float32)
        for i in range(texts_here):
            line = text_ref[i * shards + q : i * shards + q + 1, :]
            high = line.astype(jnp.bfloat16).astype(jnp.float32)
            block = jnp.where(row == 2 * i, high, block)
            block = jnp.where(row == 2 * i + 1, line - high, block)
        send_ref[q, tile_rows + deep :, :] = block.astype(jnp.bfloat16)


def finish_body(per, texts_here, asked_ref, local_ref, got_ref, node_ref, w_ref, text_ref, sum_ref):
    tiles_here, tile_rows, half = local_ref.shape
    shards = got_ref.shape[0]
    sum_ref[...] = local_ref[...]
    deep = up_to(per, ROWS)

    def one(q, carry):
        w_sum, text_sum = carry
        asked = asked_ref[q]

        @pl.when(asked >= 0)
        def _():
            sum_ref[asked] += got_ref[q, :tile_rows, :].astype(jnp.float32)

        w_sum = w_sum + got_ref[q, tile_rows : tile_rows + deep, :].astype(jnp.float32)
        text_sum = text_sum + got_ref[q, tile_rows + deep :, :].astype(jnp.float32)
        return w_sum, text_sum

    w_sum, text_sum = lax.fori_loop(
        0,
        shards,
        one,
        (jnp.zeros((deep, half), jnp.float32), jnp.zeros((ROWS, half), jnp.float32)),
    )
    w_ref[...] = w_sum
    node_ref[...] = sum_ref[...].astype(jnp.bfloat16)
    for i in range(texts_here):
        text_ref[i : i + 1, :] = text_sum[2 * i : 2 * i + 1, :] + text_sum[2 * i + 1 : 2 * i + 2, :]


def on_device(
    tokens, token_counts, w_qkv, w_out, w_up, w_down, ln_gains, cache, node_text, adj_tiles,
    adj_values, w_gnn, out_grad
):
    shards = lax.axis_size("graph")
    cores = lax.axis_size("mp")
    me = lax.axis_index("graph").astype(jnp.int32).reshape(1)
    core_at = lax.axis_index("mp")
    core = core_at.astype(jnp.int32).reshape(1)
    texts_here, seq, width = tokens.shape
    nodes_here, half = cache.shape
    tiles_here, entries, tile_rows = adj_values.shape[:3]
    texts = texts_here * shards
    slots = up_to(texts, LANES)
    per = width // shards
    deep = up_to(per, ROWS)
    count = texts_here * seq
    inner = w_up.shape[1]

    def swap(values):
        return lax.ppermute(values, "mp", [(i, cores - 1 - i) for i in range(cores)])

    def spread(values):
        return lax.all_to_all(values, "graph", split_axis=0, concat_axis=0, tiled=True)

    index = call(
        functools.partial(index_body, texts_here),
        [shape((shards, slots + LANES), jnp.int32)],
        [adj_tiles, me, node_text.reshape(tiles_here, tile_rows)],
        [SMEM, SMEM, VMEM],
        flops=1000,
        name="index",
    )
    got = spread(index)
    asked = got[:, slots]
    cache_tiles = cache.reshape(tiles_here, tile_rows, half)
    packed = call(
        pack_body,
        [shape((shards, tile_rows, half))],
        [asked, cache_tiles],
        [SMEM, VMEM],
        flops=1000,
        name="pack",
    )
    remote = spread(packed)

    w_other = swap(lax.dynamic_slice_in_dim(w_gnn, (1 - core_at) * half, half, 1))

    flat_tokens = tokens.reshape(count, width)
    partial = call(
        functools.partial(attend_body, seq),
        [shape((count, width))],
        [token_counts, flat_tokens, w_qkv.reshape(width, 3 * half), w_out],
        [SMEM, VMEM, VMEM, VMEM],
        flops=2 * count * (width * 3 * half + half * width + 2 * seq * half * 2),
        scratch=[pltpu.VMEM((count, 3 * half), jnp.bfloat16), pltpu.VMEM((count, half), jnp.bfloat16)],
        name="attend",
    )
    first, mlp = call(
        inner_body,
        [shape((count, width)), shape((count, width))],
        [flat_tokens, partial, swap(partial), w_up, w_down, ln_gains],
        [VMEM] * 6,
        flops=4 * count * width * inner,
        scratch=[pltpu.VMEM((count, inner), jnp.bfloat16)],
        name="inner",
    )
    pooled = call(
        functools.partial(pool_body, seq),
        [shape((shards, texts_here * half))],
        [token_counts, core, first, mlp, swap(mlp), ln_gains],
        [SMEM, SMEM, VMEM, VMEM, VMEM, VMEM],
        flops=20 * count * width,
        scratch=[pltpu.VMEM((8, width), jnp.float32)],
        name="pool",
    )
    pooled = spread(pooled)

    kept, pick, own, base = call(
        mask_body,
        [
            shape(adj_values.shape),
            shape((tiles_here, tile_rows, slots)),
            shape((tiles_here, tile_rows, slots)),
            shape(cache_tiles.shape),
        ],
        [adj_tiles, me, got, adj_values, cache_tiles],
        [SMEM, SMEM, VMEM, VMEM, VMEM],
        flops=2 * adj_values.size * slots,
        name="mask",
    )
    gathered = call(
        gather_body,
        [shape((tiles_here, tile_rows, half))],
        [adj_tiles, me, kept, pick, pooled, cache_tiles, remote],
        [SMEM, SMEM] + [VMEM] * 5,
        flops=2 * adj_values.size * half,
        scratch=[pltpu.VMEM((entries, tile_rows, half), jnp.bfloat16)],
        name="gather",
    ).reshape(nodes_here, half)
    node_out, slope = call(
        forward_body,
        [shape((nodes_here, half)), shape((nodes_here, half))],
        [
            core, gathered, swap(gathered), w_gnn, w_other, out_grad, own.reshape(nodes_here, slots),
            base.reshape(nodes_here, half), pooled,
        ],
        [SMEM] + [VMEM] * 8,
        flops=4 * nodes_here * half * half,
        name="forward",
    )
    grad_tiles = out_grad.reshape(tiles_here, tile_rows, half)
    send, local = call(
        functools.partial(backward_body, per, texts_here),
        [
            shape((shards, tile_rows + deep + ROWS, half)),
            shape((tiles_here, tile_rows, half), jnp.float32),
        ],
        [
            adj_tiles, me, core, slope, swap(slope), gathered, w_gnn, adj_values,
            pick.reshape(nodes_here, slots), own.reshape(nodes_here, slots), grad_tiles,
        ],
        [SMEM, SMEM, SMEM] + [VMEM] * 8,
        flops=8 * nodes_here * half * half,
        scratch=[
            pltpu.VMEM((nodes_here, half), jnp.bfloat16),
            pltpu.VMEM((width + ROWS, half), jnp.float32),
            pltpu.VMEM((slots, half), jnp.float32),
        ],
        name="backward",
    )
    returned = spread(send)
    node_grad, w_part, text_grad = call(
        functools.partial(finish_body, per, texts_here),
        [
            shape((tiles_here, tile_rows, half)),
            shape((deep, half), jnp.float32),
            shape((texts_here, half), jnp.float32),
        ],
        [asked, local, returned],
        [SMEM, VMEM, VMEM],
        flops=1000,
        scratch=[pltpu.VMEM((tiles_here, tile_rows, half), jnp.float32)],
        name="finish",
    )
    return (node_out, w_part[:per].T, text_grad, node_grad.reshape(nodes_here, half))


def solution(mesh):
    placed = (
        P("graph", None, None),
        P("graph", None),
        P(None, None, "mp"),
        P("mp", None),
        P(None, "mp"),
        P("mp", None),
        P(),
        P("graph", "mp"),
        P("graph"),
        P("graph", None),
        P("graph", None, None, None),
        P("mp", None),
        P("graph", "mp"),
    )
    return jax.shard_map(
        on_device,
        mesh=mesh,
        in_specs=placed,
        out_specs=(P("graph", "mp"), P("mp", "graph"), P("graph", "mp"), P("graph", "mp")),
        check_vma=False,
    )
```

time: 343 us -> 186 us (0.54)
  blocking collectives: 124 us -> 64 us
  Pallas kernels: 0 us -> 46.5 us
  other arithmetic: 44.5 us -> 1.39 us
  local copies, waits for them, and re-layouts: 52 us -> 13.2 us
  matrix products: 21.8 us -> 0 us
  between operations: 15 us -> 0.72 us
  waiting for transfers between devices: 56.7 us -> 43.3 us
  starting transfers between devices: 27.6 us -> 16.9 us
    unnamed x1 -> x0, blocking collectives: 80.1 us -> none
    all_to_all x0 -> x1, blocking collectives: none -> 64 us  [spread(): lax.all_to_all(values, 'graph', split_axis=0, concat_axis=0, tiled=True)]
    pallas_call x0 -> x10, Pallas kernels: none -> 46.5 us  [call(): pl.pallas_call(body, out_shape=tuple(outs) if many else outs[0], in_specs...]
    all_gather x2 -> x0, blocking collectives: 43.5 us -> none  [the longest x1 41 us: on_device(): lax.all_gather(lax.dynamic_slice_in_dim(pooled, column, half_width, 1), '...]
    gather x7 -> x0, local copies, waits for them, and re-layouts: 22.3 us -> none  [the longest x2 11 us: patch_rows(): picked = jnp.take(gathered, jnp.maximum(text_ids, 0), axis=0)]
    dot_general x11 -> x0, matrix products: 21.8 us -> none  [the longest x1 5.33 us: encode(): jnp.dot(inner, w_down, preferred_element_type=jnp.float32)]
    psum x2 -> x0, waiting for transfers between devices: 17.2 us -> none  [the longest x1 17.2 us: encode(): lax.psum(jnp.dot(inner, w_down, preferred_element_type=jnp.float32).astyp...]
    scatter-add x2 -> x0, other arithmetic: 12.2 us -> none  [the longest x1 7.33 us: on_device(): back_local = jnp.zeros((tiles_here + 1, tile_rows, half_width), jnp.float...]
  transfers between devices with their start and end apart: 8 -> 8, of which waited for: 5 -> 6; matrix products, arithmetic and copies ran while one was open for 25% -> 1% of each run, Pallas kernels for 0% -> 5%
where the time goes in v1:
time: 186 us
  blocking collectives  64 us (34%)
  Pallas kernels  46.5 us (25%)
  waiting for transfers between devices  43.3 us (23%)
  starting transfers between devices  16.9 us (9%)
  local copies, waits for them, and re-layouts  13.2 us (7%)
    all_to_all x1, blocking collectives, spread(): lax.all_to_all(values, 'graph', split_axis=0, concat_axis=0, tiled=True)  64 us
    pallas_call x10, Pallas kernels, call(): pl.pallas_call(body, out_shape=tuple(outs) if many else outs[0], in_specs...  46.5 us
    all_to_all x3, waiting for transfers between devices, spread(): lax.all_to_all(values, 'graph', split_axis=0, concat_axis=0, tiled=True)  37.6 us
    all_to_all x3, starting transfers between devices, spread(): lax.all_to_all(values, 'graph', split_axis=0, concat_axis=0, tiled=True)  15.4 us
    unnamed x21, local copies, waits for them, and re-layouts  8.42 us
    ppermute x5, waiting for transfers between devices, swap(): lax.ppermute(values, 'mp', [(i, cores - 1 - i) for i in range(cores)])  5.67 us
  transfers between devices with their start and end apart: 8, of which 6 were waited for; matrix products, arithmetic and copies ran while one was open for 1% of the time, Pallas kernels for 5%

profile of v1, /device:TPU:0, one launch (start us, length us, event | category | flops | bytes accessed | tf_op | source)
XLA Modules:
  0.0 186.0 jit_solution(5157534464653184763)
XLA Ops:
  0.6 2.6 %copy.25 = bf16[768,3,384]{0,2,1:T(8,128)(2,1)S(1)} copy(bf16[768,3,384]{2,0,1:T(8,128)(2,1)} %param.15) | data formatting | bytes 3538944 | tf_op args[2]
  3.3 2.3 %copy.26.w_qkv_ref = bf16[768,1152]{1,0:T(8,128)(2,1)} copy(bf16[768,1152]{0,1:T(8,128)(2,1)S(1)} %bitcast.21) | data formatting | bytes 3538944 | tf_op jit(solution)/shard_map/reshape | solution.py:397
  5.5 6.1 %attend.1.mine_ref = bf16[512,768]{1,0:T(8,128)(2,1)} custom-call(s32[1,2]{1,0:T(1,128)} %counts_ref.3, bf16[512,768]{1,0:T(8,128)(2,1)} %bitcast.40, bf16[768,1152]{1,0:T(8,128)(2,1)} %copy.26.w_qkv_ref, bf16[384,768]{1,0:T(8,128)(2,1)} %w_out_ref.1), custom_call_target="tpu_custom_call" | custom-call | flops 1610612736 | bytes 3932168 | tf_op jit(solution)/shard_map/attend/pallas_call | solution.py:32
  12.1 2.1 %collective-permute-done.other_ref = bf16[512,768]{1,0:T(8,128)(2,1)S(1)} collective-permute-done((bf16[512,768]{1,0:T(8,128)(2,1)}, bf16[512,768]{1,0:T(8,128)(2,1)S(1)}, u32[]{:S(2)}, u32[]{:S(2)}) %collective-permute-start) | collective-permute-done | bytes 786464 | tf_op jit(solution)/shard_map/ppermute | solution.py:365
  15.1 7.9 %inner.1 = (bf16[512,768]{1,0:T(8,128)(2,1)}, bf16[512,768]{1,0:T(8,128)(2,1)}) custom-call(bf16[512,768]{1,0:T(8,128)(2,1)} %bitcast.41, bf16[512,768]{1,0:T(8,128)(2,1)} %attend.1.mine_ref, bf16[512,768]{1,0:T(8,128)(2,1)} %copy-done.7, bf16[768,1536]{1,0:T(8,128)(2,1)} %up_ref.1, bf16[1536,768]{1,0:T(8,128)(2,1)} %down_ref.1, f32[2,768]{1,0:T(2,128)} %gains_ref.3), custom_call_target="tpu_custom_call" | custom-call | flops 2415919104 | bytes 8656896 | tf_op jit(solution)/shard_map/inner/pallas_call | solution.py:32
  23.5 1.4 index.1
  24.9 1.3 copy.24
  26.2 8.0 %all-to-all-start = ((s32[16,1,256]{2,1,0:T(1,128)}), s32[16,1,256]{2,1,0:T(1,128)S(1)}, u32[]{:S(2)}, u32[]{:S(2)}) async-start(s32[16,1,256]{2,1,0:T(1,128)} %copy.24), calls=%async_computation | async-start | bytes 32768 | tf_op jit(solution)/shard_map/all_to_all | solution.py:368
  34.2 7.3 %all-to-all-done = s32[16,1,256]{2,1,0:T(1,128)S(1)} async-done(((s32[16,1,256]{2,1,0:T(1,128)}), s32[16,1,256]{2,1,0:T(1,128)S(1)}, u32[]{:S(2)}, u32[]{:S(2)}) %all-to-all-start) | async-done | bytes 16416 | tf_op jit(solution)/shard_map/all_to_all | solution.py:368
  42.4 3.0 %pool.1 = bf16[16,768]{1,0:T(8,128)(2,1)} custom-call(s32[1,2]{1,0:T(1,128)} %counts_ref.3, s32[1]{0:T(128)} %bitcast.core_ref, bf16[512,768]{1,0:T(8,128)(2,1)} %get-tuple-element.19.first_ref, bf16[512,768]{1,0:T(8,128)(2,1)} %get-tuple-element.20.mine_ref, bf16[512,768]{1,0:T(8,128)(2,1)} %copy-done.2, f32[2,768]{1,0:T(2,128)} %gains_ref.3), custom_call_target="tpu_custom_call" | custom-call | flops 7864320 | bytes 2390028 | tf_op jit(solution)/shard_map/pool/pallas_call | solution.py:32
  46.0 1.4 reduce.2
  48.0 3.5 %all-to-all-start.1 = ((bf16[16,2,384]{2,1,0:T(2,128)(2,1)}), bf16[16,2,384]{2,1,0:T(2,128)(2,1)S(1)}, u32[]{:S(2)}, u32[]{:S(2)}) async-start(bf16[16,2,384]{2,1,0:T(2,128)(2,1)} %reshape.62), calls=%async_computation.1 | async-start | bytes 49152 | tf_op jit(solution)/shard_map/all_to_all | solution.py:368
  52.1 2.5 %pack.1 = bf16[16,128,384]{2,1,0:T(8,128)(2,1)} custom-call(s32[16]{0:T(128)} %slice_reduce_fusion.asked_ref, bf16[4,128,384]{2,1,0:T(8,128)(2,1)} %bitcast.22), custom_call_target="tpu_custom_call" | custom-call | flops 1000 | bytes 1966144 | tf_op jit(solution)/shard_map/pack/pallas_call | solution.py:32
  54.6 4.3 %all-to-all-done.1 = bf16[16,2,384]{2,1,0:T(2,128)(2,1)S(1)} async-done(((bf16[16,2,384]{2,1,0:T(2,128)(2,1)}), bf16[16,2,384]{2,1,0:T(2,128)(2,1)S(1)}, u32[]{:S(2)}, u32[]{:S(2)}) %all-to-all-start.1) | async-done | bytes 24608 | tf_op jit(solution)/shard_map/all_to_all | solution.py:368
  58.8 3.9 %all-to-all-start.2 = ((bf16[16,128,384]{2,1,0:T(8,128)(2,1)}), bf16[16,128,384]{2,1,0:T(8,128)(2,1)S(1)}, u32[]{:S(2)}, u32[]{:S(2)}) async-start(bf16[16,128,384]{2,1,0:T(8,128)(2,1)} %pack.1), calls=%async_computation.2 | async-start | bytes 3145728 | tf_op jit(solution)/shard_map/all_to_all | solution.py:368
  62.7 5.8 %mask.1 = (bf16[4,5,128,128]{3,2,1,0:T(8,128)(2,1)}, bf16[4,128,128]{2,1,0:T(8,128)(2,1)}, bf16[4,128,128]{2,1,0:T(8,128)(2,1)}, bf16[4,128,384]{2,1,0:T(8,128)(2,1)}) custom-call(s32[4,5]{1,0:T(4,128)} %ids_ref.7, s32[1]{0:T(128)} %bitcast.1.self_ref, s32[16,256]{1,0:T(8,128)} %bitcast.36, bf16[4,5,128,128]{3,2,1,0:T(8,128)(2,1)} %adj_ref.3, ...), custom_call_target="tpu_custom_call" | custom-call | flops 83886080 | bytes 2375764 | tf_op jit(solution)/shard_map/mask/pallas_call | solution.py:32
  69.2 26.0 %all-to-all-done.2.remote_ref = bf16[16,128,384]{2,1,0:T(8,128)(2,1)S(1)} async-done(((bf16[16,128,384]{2,1,0:T(8,128)(2,1)}), bf16[16,128,384]{2,1,0:T(8,128)(2,1)S(1)}, u32[]{:S(2)}, u32[]{:S(2)}) %all-to-all-start.2) | async-done | bytes 1572896 | tf_op jit(solution)/shard_map/all_to_all | solution.py:368
  96.3 4.7 %gather.1 = bf16[4,128,384]{2,1,0:T(8,128)(2,1)} custom-call(s32[4,5]{1,0:T(4,128)} %ids_ref.7, s32[1]{0:T(128)} %bitcast.1.self_ref, bf16[4,5,128,128]{3,2,1,0:T(8,128)(2,1)} %get-tuple-element.17.kept_ref, bf16[4,128,128]{2,1,0:T(8,128)(2,1)} %get-tuple-element.18.pick_ref, bf16[16,768]{1,0:T(8,128)(2,1)} %bitcast.33, bf16[4,128,384]{2,1,0:T(8,128)(2,1)} %bitcast.24, ...), custom_call_target="tpu_custom_call" | custom-call | flops 251658240 | bytes 3170388 | tf_op jit(solution)/shard_map/gather/pallas_call | solution.py:32
  101.7 1.7 collective-permute-done.3.w_other_ref
  104.3 3.7 %forward.1 = (bf16[512,384]{1,0:T(8,128)(2,1)}, bf16[512,384]{1,0:T(8,128)(2,1)}) custom-call(s32[1]{0:T(128)} %bitcast.core_ref, bf16[512,384]{1,0:T(8,128)(2,1)} %bitcast.26, bf16[512,384]{1,0:T(8,128)(2,1)} %copy-done.4, bf16[384,768]{1,0:T(8,128)(2,1)} %w_own_ref.3, bf16[384,384]{1,0:T(8,128)(2,1)} %copy-done.5, bf16[512,384]{1,0:T(8,128)(2,1)} %grad_ref.1, ...), custom_call_target="tpu_custom_call" | custom-call | flops 301989888 | bytes 3399684 | tf_op jit(solution)/shard_map/forward/pallas_call | solution.py:32
  108.1 1.8 collective-permute-done.4.other_ref
  110.7 8.1 %backward.1 = (bf16[16,192,384]{2,1,0:T(8,128)(2,1)}, f32[4,128,384]{2,1,0:T(8,128)}) custom-call(s32[4,5]{1,0:T(4,128)} %ids_ref.7, s32[1]{0:T(128)} %bitcast.1.self_ref, s32[1]{0:T(128)} %bitcast.core_ref, bf16[512,384]{1,0:T(8,128)(2,1)} %get-tuple-element.24.mine_ref, bf16[512,384]{1,0:T(8,128)(2,1)} %copy-done.3, bf16[512,384]{1,0:T(8,128)(2,1)} %bitcast.27, ...), custom_call_target="tpu_custom_call" | custom-call | flops 603979776 | bytes 6226008 | tf_op jit(solution)/shard_map/backward/pallas_call | solution.py:32
  118.8 64.0 %all_to_all.32.got_ref = bf16[16,192,384]{2,1,0:T(8,128)(2,1)} all-to-all(bf16[16,192,384]{2,1,0:T(8,128)(2,1)} %get-tuple-element.26), channel_id=1, replica_groups=mesh['graph'=16,'mp'=2] {'graph'}, dimensions={0} | all-to-all | bytes 4718592 | tf_op jit(solution)/shard_map/all_to_all | solution.py:368
  182.7 3.2 %finish.1 = (bf16[4,128,384]{2,1,0:T(8,128)(2,1)}, f32[48,384]{1,0:T(8,128)}, f32[2,384]{1,0:T(2,128)}) custom-call(s32[16]{0:T(128)} %slice_reduce_fusion.asked_ref, f32[4,128,384]{2,1,0:T(8,128)} %get-tuple-element.25.local_ref, bf16[16,192,384]{2,1,0:T(8,128)(2,1)} %all_to_all.32.got_ref), custom_call_target="tpu_custom_call" | custom-call | flops 1000 | bytes 3615808 | tf_op jit(solution)/shard_map/finish/pallas_call | solution.py:32
  (30 shorter events, 8.5 us)
Async XLA Ops:
  11.7 2.6 %collective-permute-start = (bf16[512,768]{1,0:T(8,128)(2,1)}, bf16[512,768]{1,0:T(8,128)(2,1)S(1)}, u32[]{:S(2)}, u32[]{:S(2)}) collective-permute-start(bf16[512,768]{1,0:T(8,128)(2,1)} %attend.1.mine_ref), channel_id=1, source_target_pairs={{0,1},{1,0},{2,3},{3,2},{4,5},{5,4},{6,7},{7,6},{8,9},{9,8},{10,11... | collective-permute-start | bytes 2359304 | tf_op jit(solution)/shard_map/ppermute | solution.py:365
  14.3 0.9 copy-start.7
  23.1 18.5 %collective-permute-start.1 = (bf16[512,768]{1,0:T(8,128)(2,1)}, bf16[512,768]{1,0:T(8,128)(2,1)S(1)}, u32[]{:S(2)}, u32[]{:S(2)}) collective-permute-start(bf16[512,768]{1,0:T(8,128)(2,1)} %get-tuple-element.20.mine_ref), channel_id=1, source_target_pairs={{0,1},{1,0},{2,3},{3,2},{4,5},{5,4},{6,7},{7,6},{8,9},{9,8},{10,11... | collective-permute-start | bytes 2359304 | tf_op jit(solution)/shard_map/ppermute | solution.py:365
  26.2 15.3 %all-to-all-start = ((s32[16,1,256]{2,1,0:T(1,128)}), s32[16,1,256]{2,1,0:T(1,128)S(1)}, u32[]{:S(2)}, u32[]{:S(2)}) async-start(s32[16,1,256]{2,1,0:T(1,128)} %copy.24), calls=%async_computation | async-start | bytes 32768 | tf_op jit(solution)/shard_map/all_to_all | solution.py:368
  41.5 21.2 %copy-start.6 = (s32[16,1,256]{2,0,1:T(8,128)}, s32[16,1,256]{2,0,1:T(8,128)S(1)}, u32[]{:S(2)}) copy-start(s32[16,1,256]{2,0,1:T(8,128)S(1)} %copy.33) | copy-start | bytes 49156
  41.5 0.9 copy-start.2
  48.0 10.8 %all-to-all-start.1 = ((bf16[16,2,384]{2,1,0:T(2,128)(2,1)}), bf16[16,2,384]{2,1,0:T(2,128)(2,1)S(1)}, u32[]{:S(2)}, u32[]{:S(2)}) async-start(bf16[16,2,384]{2,1,0:T(2,128)(2,1)} %reshape.62), calls=%async_computation.1 | async-start | bytes 49152 | tf_op jit(solution)/shard_map/all_to_all | solution.py:368
  58.8 36.3 %all-to-all-start.2 = ((bf16[16,128,384]{2,1,0:T(8,128)(2,1)}), bf16[16,128,384]{2,1,0:T(8,128)(2,1)S(1)}, u32[]{:S(2)}, u32[]{:S(2)}) async-start(bf16[16,128,384]{2,1,0:T(8,128)(2,1)} %pack.1), calls=%async_computation.2 | async-start | bytes 3145728 | tf_op jit(solution)/shard_map/all_to_all | solution.py:368
  68.5 32.5 %copy-start.1 = (bf16[384,768]{1,0:T(8,128)(2,1)S(1)}, bf16[384,768]{1,0:T(8,128)(2,1)}, u32[]{:S(2)}) copy-start(bf16[384,768]{1,0:T(8,128)(2,1)} %w_own_ref.3) | copy-start | bytes 1769476
  95.2 1.2 copy-start
  101.1 2.4 %collective-permute-start.2 = (bf16[512,384]{1,0:T(8,128)(2,1)}, bf16[512,384]{1,0:T(8,128)(2,1)S(1)}, u32[]{:S(2)}, u32[]{:S(2)}) collective-permute-start(bf16[512,384]{1,0:T(8,128)(2,1)} %bitcast.25), channel_id=1, source_target_pairs={{0,1},{1,0},{2,3},{3,2},{4,5},{5,4},{6,7},{7,6},{8,9},{9,8},{10,11... | collective-permute-start | bytes 1179656 | tf_op jit(solution)/shard_map/ppermute | solution.py:365
  101.1 2.3 %collective-permute-start.3 = (bf16[384,384]{1,0:T(8,128)(2,1)S(1)}, bf16[384,384]{1,0:T(8,128)(2,1)S(1)}, u32[]{:S(2)}, u32[]{:S(2)}) collective-permute-start(bf16[384,384]{1,0:T(8,128)(2,1)S(1)} %constant_dynamic-slice_fusion), channel_id=1, source_target_pairs={{0,1},{1,0},{2,3},{3,2},{4,5},{5,4},{6,7},{7,6},{8,9},{9,8},{10,11... | collective-permute-start | bytes 884744 | tf_op jit(solution)/shard_map/ppermute | solution.py:365
  103.4 0.7 copy-start.5
  103.4 0.9 copy-start.4
  108.0 1.9 %collective-permute-start.4 = (bf16[512,384]{1,0:T(8,128)(2,1)}, bf16[512,384]{1,0:T(8,128)(2,1)S(1)}, u32[]{:S(2)}, u32[]{:S(2)}) collective-permute-start(bf16[512,384]{1,0:T(8,128)(2,1)} %get-tuple-element.24.mine_ref), channel_id=1, source_target_pairs={{0,1},{1,0},{2,3},{3,2},{4,5},{5,4},{6,7},{7,6},{8,9},{9,8},{10,11... | collective-permute-start | bytes 1179656 | tf_op jit(solution)/shard_map/ppermute | solution.py:365
  109.9 0.7 copy-start.3

commit v2 on v1

--- a/solution.py
+++ b/solution.py
@@ -1,4 +1,5 @@
 import functools
+import math
 
 import jax
 import jax.numpy as jnp
@@ -7,9 +8,11 @@
 from jax.experimental.pallas import tpu as pltpu
 from jax.sharding import PartitionSpec as P
 
+
 HEAD = 64
 LANES = 128
 ROWS = 16
+SPARE = 6 << 20
 NORM_EPS = 1e-05
 MASKED = -1e30
 NO_NODE = -(1 << 20)
@@ -24,19 +27,20 @@
     return (value + unit - 1) // unit * unit
 
 
-def call(body, outs, ins, specs, flops, scratch=(), name=None):
+def call(body, outs, ins, specs, flops, scratch=()):
     moved = sum(a.size * a.dtype.itemsize for a in ins) + sum(
         o.size * o.dtype.itemsize for o in outs
     )
     many = len(outs) > 1
+    held = sum(math.prod(s.shape) * jnp.dtype(s.dtype).itemsize for s in scratch)
     return pl.pallas_call(
         body,
         out_shape=tuple(outs) if many else outs[0],
         in_specs=list(specs),
         out_specs=tuple([VMEM] * len(outs)) if many else VMEM,
         scratch_shapes=list(scratch),
+        compiler_params=pltpu.CompilerParams(vmem_limit_bytes=moved + moved // 8 + held + SPARE),
         cost_estimate=pl.CostEstimate(flops=flops, bytes_accessed=moved, transcendentals=0),
-        name=name,
     )(*ins)
 
 
@@ -58,7 +62,7 @@
 
 def index_body(texts_here, ids_ref, self_ref, text_ref, out_ref):
     tiles_here, entries = ids_ref.shape
-    shards, lanes = out_ref.shape
+    shards, _, lanes = out_ref.shape
     width = lanes - LANES
     texts = texts_here * shards
     me = self_ref[0]
@@ -70,7 +74,7 @@
             _, owner, place = tile_of(tile_id, tiles_here)
             target = jnp.where((tile_id >= 0) & (owner != me), owner, -1)
             wanted = jnp.where(row == target, place, wanted)
-    out_ref[:, width:] = wanted
+    out_ref[:, :, width:] = wanted.reshape(shards, 1, LANES)
     tile_rows = text_ref.shape[1]
     lane = lax.broadcasted_iota(jnp.int32, (LANES, tile_rows), 1)
     sub = lax.broadcasted_iota(jnp.int32, (LANES, LANES), 0)
@@ -85,9 +89,9 @@
             best = jnp.where(text_ref[j : j + 1, :] == text, node, best)
         column = jnp.max(best.astype(jnp.float32), axis=1, keepdims=True)
         line = jnp.max(jnp.where(diagonal, column, float(NO_NODE)), axis=0, keepdims=True)
-        out_ref[:, c * LANES : (c + 1) * LANES] = jnp.broadcast_to(
-            line, (shards, LANES)
-        ).astype(jnp.int32)
+        out_ref[:, :, c * LANES : (c + 1) * LANES] = (
+            jnp.broadcast_to(line, (shards, LANES)).astype(jnp.int32).reshape(shards, 1, LANES)
+        )
 
 
 def pack_body(asked_ref, cache_ref, out_ref):
@@ -100,9 +104,12 @@
 
 def mask_body(ids_ref, self_ref, got_ref, adj_ref, cache_ref, kept_ref, pick_ref, own_ref, base_ref):
     tiles_here, entries, tile_rows, _ = adj_ref.shape
-    width = got_ref.shape[1] - LANES
+    shards, _, lanes = got_ref.shape
+    width = lanes - LANES
     me = self_ref[0]
-    table = jnp.max(got_ref[:, :width].astype(jnp.float32), axis=0, keepdims=True)
+    table = jnp.max(
+        got_ref[:, :, :width].reshape(shards, width).astype(jnp.float32), axis=0, keepdims=True
+    )
     place = lax.broadcasted_iota(jnp.int32, (tile_rows, width), 0).astype(jnp.float32)
     ones = jnp.ones((ROWS, width), jnp.bfloat16)
 
@@ -181,7 +188,7 @@
 
 
 def pool_body(seq, counts_ref, core_ref, first_ref, mine_ref, other_ref, gains_ref, out_ref, pooled_ref):
-    shards, lanes = out_ref.shape
+    _, _, lanes = out_ref.shape
     texts_here = first_ref.shape[0] // seq
     half = lanes // texts_here
     for t in range(texts_here):
@@ -196,22 +203,39 @@
         )
         start = pl.multiple_of(core_ref[0] * half, LANES)
         own = pooled_ref[:, pl.ds(start, half)][0:1, :]
-        out_ref[:, t * half : (t + 1) * half] = jnp.broadcast_to(own, (shards, half)).astype(
-            jnp.bfloat16
-        )
-
-
-def pooled_rows(pooled_ref, half):
-    parts = pooled_ref.shape[1] // half
-    return jnp.concatenate([pooled_ref[:, i * half : (i + 1) * half] for i in range(parts)], axis=0)
-
-
-def gather_body(ids_ref, self_ref, kept_ref, pick_ref, pooled_ref, cache_ref, remote_ref, out_ref, source_ref):
-    tiles_here, entries, tile_rows, _ = kept_ref.shape
-    half = cache_ref.shape[2]
+        own = own.astype(jnp.bfloat16).astype(jnp.float32)
+        out_ref[:, :, t * half : (t + 1) * half] = own.reshape(1, 1, half)
+
+
+def pooled_rows(me, near_ref, far_ref, half):
+    shards = 2 * near_ref.shape[0]
+    parts = []
+    for first in range(0, near_ref.shape[2], half):
+        for ref in (near_ref, far_ref):
+            part = ref[:, :, first : first + half].reshape(shards // 2, half)
+            parts.append(part.astype(jnp.bfloat16))
+    stacked = jnp.concatenate(parts, axis=0)
+    texts = stacked.shape[0]
+    row = lax.broadcasted_iota(jnp.int32, (texts, texts), 0)
+    column = lax.broadcasted_iota(jnp.int32, (texts, texts), 1)
+    order = jnp.where(row == (column ^ me), 1.0, 0.0).astype(jnp.bfloat16)
+    return mm(order, stacked).astype(jnp.bfloat16)
+
+
+def fresh_body(self_ref, near_ref, far_ref, pick_ref, own_ref, base_ref, start_ref, feature_ref):
+    half = base_ref.shape[2]
+    pooled = pooled_rows(self_ref[0], near_ref, far_ref, half)
+    texts = pooled.shape[0]
+    for r in range(pick_ref.shape[0]):
+        start_ref[r] = mm(pick_ref[r][:, :texts], pooled)
+        feature_ref[r] = (
+            base_ref[r].astype(jnp.float32) + mm(own_ref[r][:, :texts], pooled)
+        ).astype(jnp.bfloat16)
+
+
+def gather_body(ids_ref, self_ref, kept_ref, start_ref, cache_ref, remote_ref, out_ref, source_ref):
+    tiles_here, entries, _, _ = kept_ref.shape
     me = self_ref[0]
-    pooled = pooled_rows(pooled_ref, half)
-    texts = pooled.shape[0]
     for r in range(tiles_here):
 
         def fetch(k, carry):
@@ -230,14 +254,14 @@
             return carry
 
         lax.fori_loop(0, entries, fetch, 0)
-        total = mm(pick_ref[r][:, :texts], pooled)
+        total = start_ref[r]
         for k in range(entries):
             total = total + mm(kept_ref[r, k], source_ref[k])
         out_ref[r] = total.astype(jnp.bfloat16)
 
 
-def forward_body(core_ref, mine_ref, other_ref, w_own_ref, w_other_ref, grad_ref, own_ref, base_ref, pooled_ref, node_ref, slope_ref):
-    rows, half = mine_ref.shape
+def forward_body(core_ref, mine_ref, other_ref, w_own_ref, w_other_ref, grad_ref, feature_ref, node_ref, slope_ref):
+    _, half = mine_ref.shape
     start = pl.multiple_of(core_ref[0] * half, LANES)
     hidden = mm(mine_ref[...], w_own_ref[:, pl.ds(start, half)]) + mm(
         other_ref[...], w_other_ref[...]
@@ -247,20 +271,14 @@
     lifted = 0.5 * (1.0 + gate)
     slope = lifted + 0.5 * hidden * (1.0 - gate * gate) * (ROOT * (1.0 + 3.0 * CUBE * square))
     slope_ref[...] = (grad_ref[...].astype(jnp.float32) * slope).astype(jnp.bfloat16)
-    pooled = pooled_rows(pooled_ref, half)
-    fresh = mm(own_ref[:, : pooled.shape[0]], pooled)
-    node_ref[...] = (base_ref[...].astype(jnp.float32) + fresh + hidden * lifted).astype(
-        jnp.bfloat16
-    )
+    node_ref[...] = (feature_ref[...].astype(jnp.float32) + hidden * lifted).astype(jnp.bfloat16)
 
 
 def backward_body(
-    per, texts_here, ids_ref, self_ref, core_ref, mine_ref, other_ref, agg_ref, w_own_ref, adj_ref,
-    pick_ref, own_ref, grad_ref, send_ref, local_ref, down_ref, w_ref, text_ref
+    ids_ref, self_ref, core_ref, mine_ref, other_ref, w_own_ref, adj_ref, send_ref, down_ref
 ):
     tiles_here, entries, tile_rows, _ = adj_ref.shape
-    half = agg_ref.shape[1]
-    shards = send_ref.shape[0]
+    half = send_ref.shape[2]
     me = self_ref[0]
     core = core_ref[0]
     own = pl.multiple_of(core * half, LANES)
@@ -269,29 +287,34 @@
         other_ref[...], w_own_ref[:, pl.ds(far, half)], (1, 1)
     )
     down_ref[...] = down.astype(jnp.bfloat16)
-    local_ref[...] = grad_ref[...].astype(jnp.float32)
     for r in range(tiles_here):
         rows = slice(r * tile_rows, (r + 1) * tile_rows)
 
         def one(k, carry):
             tile_id = ids_ref[r, k]
-            _, owner, place = tile_of(tile_id, tiles_here)
-
-            @pl.when((tile_id >= 0) & (owner == me))
-            def _():
-                local_ref[place] += mm(adj_ref[r, k], down_ref[rows, :], (0, 0))
+            _, owner, _ = tile_of(tile_id, tiles_here)
 
             @pl.when((tile_id >= 0) & (owner != me))
             def _():
-                send_ref[owner, :tile_rows, :] = mm(
-                    adj_ref[r, k], down_ref[rows, :], (0, 0)
-                ).astype(jnp.bfloat16)
+                send_ref[owner] = mm(adj_ref[r, k], down_ref[rows, :], (0, 0)).astype(jnp.bfloat16)
 
             return carry
 
         lax.fori_loop(0, entries, one, 0)
+
+
+def chunk_body(
+    per, texts_here, self_ref, core_ref, mine_ref, other_ref, agg_ref, down_ref, pick_ref, own_ref,
+    grad_ref, keep_ref, give_ref, w_ref, text_ref
+):
+    kept, _, half = keep_ref.shape
+    shards = 2 * kept
+    me = self_ref[0]
+    core = core_ref[0]
+    own = pl.multiple_of(core * half, LANES)
+    far = pl.multiple_of((1 - core) * half, LANES)
     text_ref[...] = mm(pick_ref[...], down_ref[...], (0, 0)) + mm(
-        own_ref[...], grad_ref[...].reshape(tiles_here * tile_rows, half), (0, 0)
+        own_ref[...], grad_ref[...], (0, 0)
     )
     columns = 2 * half
     w_ref[pl.ds(own, half), :] = mm(mine_ref[...], agg_ref[...], (0, 0))
@@ -300,49 +323,90 @@
     deep = up_to(per, ROWS)
     row = lax.broadcasted_iota(jnp.int32, (ROWS, half), 0)
     for q in range(shards):
-        send_ref[q, tile_rows : tile_rows + deep, :] = w_ref[q * per : q * per + deep, :].astype(
-            jnp.bfloat16
-        )
+        piece = w_ref[q * per : q * per + deep, :].astype(jnp.bfloat16)
         block = jnp.zeros((ROWS, half), jnp.float32)
         for i in range(texts_here):
             line = text_ref[i * shards + q : i * shards + q + 1, :]
             high = line.astype(jnp.bfloat16).astype(jnp.float32)
-            block = jnp.where(row == 2 * i, high, block)
-            block = jnp.where(row == 2 * i + 1, line - high, block)
-        send_ref[q, tile_rows + deep :, :] = block.astype(jnp.bfloat16)
-
-
-def finish_body(per, texts_here, asked_ref, local_ref, got_ref, node_ref, w_ref, text_ref, sum_ref):
-    tiles_here, tile_rows, half = local_ref.shape
-    shards = got_ref.shape[0]
+            block = jnp.where(row == i, high, block)
+            block = jnp.where(row == ROWS // 2 + i, line - high, block)
+        block = block.astype(jnp.bfloat16)
+        step = q ^ me
+        turned = step * 0
+        reach = 1
+        while reach < shards:
+            turned = 2 * turned + ((step // reach) & 1)
+            reach *= 2
+
+        @pl.when(turned < kept)
+        def _():
+            keep_ref[turned, :deep, :] = piece
+            keep_ref[turned, deep:, :] = block
+
+        @pl.when(turned >= kept)
+        def _():
+            give_ref[turned - kept, :deep, :] = piece
+            give_ref[turned - kept, deep:, :] = block
+
+
+def fold(mine, theirs, deep):
+    total = mine.astype(jnp.float32) + theirs.astype(jnp.float32)
+    text = total[deep : deep + ROWS // 2, :] + total[deep + ROWS // 2 :, :]
+    return total[:deep, :], text
+
+
+def fold_body(deep, mine_ref, theirs_ref, keep_ref, give_ref):
+    kept = keep_ref.shape[0]
+    for s in range(2 * kept):
+        w_sum, text = fold(mine_ref[s], theirs_ref[s], deep)
+        high = text.astype(jnp.bfloat16).astype(jnp.float32)
+        out_ref = (keep_ref if s < kept else give_ref).at[s % kept]
+        out_ref[:deep, :] = w_sum.astype(jnp.bfloat16)
+        out_ref[deep:, :] = jnp.concatenate([high, text - high], axis=0).astype(jnp.bfloat16)
+
+
+def close_body(deep, mine_ref, theirs_ref, w_ref, text_ref):
+    w_sum, text = fold(mine_ref[0], theirs_ref[0], deep)
+    w_ref[...] = w_sum
+    text_ref[...] = text[: text_ref.shape[0], :]
+
+
+def local_body(ids_ref, self_ref, down_ref, adj_ref, grad_ref, local_ref):
+    tiles_here, entries, _, _ = adj_ref.shape
+    me = self_ref[0]
+    local_ref[...] = grad_ref[...].astype(jnp.float32)
+    for r in range(tiles_here):
+
+        def one(k, carry):
+            tile_id = ids_ref[r, k]
+            _, owner, place = tile_of(tile_id, tiles_here)
+
+            @pl.when((tile_id >= 0) & (owner == me))
+            def _():
+                local_ref[place] += mm(adj_ref[r, k], down_ref[r], (0, 0))
+
+            return carry
+
+        lax.fori_loop(0, entries, one, 0)
+
+
+def finish_body(asked_ref, local_ref, got_ref, node_ref, sum_ref):
     sum_ref[...] = local_ref[...]
-    deep = up_to(per, ROWS)
 
     def one(q, carry):
-        w_sum, text_sum = carry
         asked = asked_ref[q]
 
         @pl.when(asked >= 0)
         def _():
-            sum_ref[asked] += got_ref[q, :tile_rows, :].astype(jnp.float32)
-
-        w_sum = w_sum + got_ref[q, tile_rows : tile_rows + deep, :].astype(jnp.float32)
-        text_sum = text_sum + got_ref[q, tile_rows + deep :, :].astype(jnp.float32)
-        return w_sum, text_sum
-
-    w_sum, text_sum = lax.fori_loop(
-        0,
-        shards,
-        one,
-        (jnp.zeros((deep, half), jnp.float32), jnp.zeros((ROWS, half), jnp.float32)),
-    )
-    w_ref[...] = w_sum
+            sum_ref[asked] += got_ref[q].astype(jnp.float32)
+
+        return carry
+
+    lax.fori_loop(0, got_ref.shape[0], one, 0)
     node_ref[...] = sum_ref[...].astype(jnp.bfloat16)
-    for i in range(texts_here):
-        text_ref[i : i + 1, :] = text_sum[2 * i : 2 * i + 1, :] + text_sum[2 * i + 1 : 2 * i + 2, :]
-
-
-def on_device(
+
+
+def step(
     tokens, token_counts, w_qkv, w_out, w_up, w_down, ln_gains, cache, node_text, adj_tiles,
     adj_values, w_gnn, out_grad
 ):
@@ -364,19 +428,21 @@
     def swap(values):
         return lax.ppermute(values, "mp", [(i, cores - 1 - i) for i in range(cores)])
 
+    def toward(values, reach):
+        return lax.ppermute(values, "graph", [(i, i ^ reach) for i in range(shards)])
+
     def spread(values):
         return lax.all_to_all(values, "graph", split_axis=0, concat_axis=0, tiled=True)
 
     index = call(
         functools.partial(index_body, texts_here),
-        [shape((shards, slots + LANES), jnp.int32)],
+        [shape((shards, 1, slots + LANES), jnp.int32)],
         [adj_tiles, me, node_text.reshape(tiles_here, tile_rows)],
         [SMEM, SMEM, VMEM],
         flops=1000,
-        name="index",
     )
     got = spread(index)
-    asked = got[:, slots]
+    asked = got[:, 0, slots]
     cache_tiles = cache.reshape(tiles_here, tile_rows, half)
     packed = call(
         pack_body,
@@ -384,7 +450,6 @@
         [asked, cache_tiles],
         [SMEM, VMEM],
         flops=1000,
-        name="pack",
     )
     remote = spread(packed)
 
@@ -398,7 +463,6 @@
         [SMEM, VMEM, VMEM, VMEM],
         flops=2 * count * (width * 3 * half + half * width + 2 * seq * half * 2),
         scratch=[pltpu.VMEM((count, 3 * half), jnp.bfloat16), pltpu.VMEM((count, half), jnp.bfloat16)],
-        name="attend",
     )
     first, mlp = call(
         inner_body,
@@ -407,18 +471,22 @@
         [VMEM] * 6,
         flops=4 * count * width * inner,
         scratch=[pltpu.VMEM((count, inner), jnp.bfloat16)],
-        name="inner",
     )
     pooled = call(
         functools.partial(pool_body, seq),
-        [shape((shards, texts_here * half))],
+        [shape((1, 1, texts_here * half), jnp.float32)],
         [token_counts, core, first, mlp, swap(mlp), ln_gains],
         [SMEM, SMEM, VMEM, VMEM, VMEM, VMEM],
         flops=20 * count * width,
         scratch=[pltpu.VMEM((8, width), jnp.float32)],
-        name="pool",
-    )
-    pooled = spread(pooled)
+    )
+    near = pooled
+    reach = 1
+    far = toward(near, reach)
+    while 4 * reach <= shards:
+        reach *= 2
+        near = jnp.concatenate([near, far], axis=0)
+        far = toward(near, reach)
 
     kept, pick, own, base = call(
         mask_body,
@@ -431,61 +499,90 @@
         [adj_tiles, me, got, adj_values, cache_tiles],
         [SMEM, SMEM, VMEM, VMEM, VMEM],
         flops=2 * adj_values.size * slots,
-        name="mask",
+    )
+    start, features = call(
+        fresh_body,
+        [shape((tiles_here, tile_rows, half), jnp.float32), shape((tiles_here, tile_rows, half))],
+        [me, near, far, pick, own, base],
+        [SMEM] + [VMEM] * 5,
+        flops=4 * nodes_here * texts * half,
     )
     gathered = call(
         gather_body,
         [shape((tiles_here, tile_rows, half))],
-        [adj_tiles, me, kept, pick, pooled, cache_tiles, remote],
-        [SMEM, SMEM] + [VMEM] * 5,
+        [adj_tiles, me, kept, start, cache_tiles, remote],
+        [SMEM, SMEM] + [VMEM] * 4,
         flops=2 * adj_values.size * half,
         scratch=[pltpu.VMEM((entries, tile_rows, half), jnp.bfloat16)],
-        name="gather",
     ).reshape(nodes_here, half)
     node_out, slope = call(
         forward_body,
         [shape((nodes_here, half)), shape((nodes_here, half))],
         [
-            core, gathered, swap(gathered), w_gnn, w_other, out_grad, own.reshape(nodes_here, slots),
-            base.reshape(nodes_here, half), pooled,
+            core, gathered, swap(gathered), w_gnn, w_other, out_grad,
+            features.reshape(nodes_here, half),
         ],
-        [SMEM] + [VMEM] * 8,
+        [SMEM] + [VMEM] * 6,
         flops=4 * nodes_here * half * half,
-        name="forward",
     )
     grad_tiles = out_grad.reshape(tiles_here, tile_rows, half)
-    send, local = call(
-        functools.partial(backward_body, per, texts_here),
+    slope_other = swap(slope)
+    send, down = call(
+        backward_body,
+        [shape((shards, tile_rows, half)), shape((nodes_here, half))],
+        [adj_tiles, me, core, slope, slope_other, w_gnn, adj_values],
+        [SMEM, SMEM, SMEM] + [VMEM] * 4,
+        flops=4 * nodes_here * half * half + 2 * adj_values.size * half,
+    )
+    returned = spread(send)
+    keep, give = call(
+        functools.partial(chunk_body, per, texts_here),
+        [shape((shards // 2, deep + ROWS, half)), shape((shards // 2, deep + ROWS, half))],
         [
-            shape((shards, tile_rows + deep + ROWS, half)),
-            shape((tiles_here, tile_rows, half), jnp.float32),
+            me, core, slope, slope_other, gathered, down, pick.reshape(nodes_here, slots),
+            own.reshape(nodes_here, slots), out_grad,
         ],
-        [
-            adj_tiles, me, core, slope, swap(slope), gathered, w_gnn, adj_values,
-            pick.reshape(nodes_here, slots), own.reshape(nodes_here, slots), grad_tiles,
-        ],
-        [SMEM, SMEM, SMEM] + [VMEM] * 8,
-        flops=8 * nodes_here * half * half,
+        [SMEM, SMEM] + [VMEM] * 7,
+        flops=4 * nodes_here * half * (half + slots),
         scratch=[
-            pltpu.VMEM((nodes_here, half), jnp.bfloat16),
             pltpu.VMEM((width + ROWS, half), jnp.float32),
             pltpu.VMEM((slots, half), jnp.float32),
         ],
-        name="backward",
-    )
-    returned = spread(send)
-    node_grad, w_part, text_grad = call(
-        functools.partial(finish_body, per, texts_here),
-        [
-            shape((tiles_here, tile_rows, half)),
-            shape((deep, half), jnp.float32),
-            shape((texts_here, half), jnp.float32),
-        ],
+    )
+    local = call(
+        local_body,
+        [shape((tiles_here, tile_rows, half), jnp.float32)],
+        [adj_tiles, me, down.reshape(tiles_here, tile_rows, half), adj_values, grad_tiles],
+        [SMEM, SMEM] + [VMEM] * 3,
+        flops=2 * adj_values.size * half,
+    )
+    reach = 1
+    given = toward(give, reach)
+    while 2 * reach < shards:
+        part = (shards // (4 * reach), deep + ROWS, half)
+        keep, give = call(
+            functools.partial(fold_body, deep),
+            [shape(part), shape(part)],
+            [keep, given],
+            [VMEM] * 2,
+            flops=4 * math.prod(part),
+        )
+        reach *= 2
+        given = toward(give, reach)
+    w_part, text_grad = call(
+        functools.partial(close_body, deep),
+        [shape((deep, half), jnp.float32), shape((texts_here, half), jnp.float32)],
+        [keep, given],
+        [VMEM] * 2,
+        flops=1000,
+    )
+    node_grad = call(
+        finish_body,
+        [shape((tiles_here, tile_rows, half))],
         [asked, local, returned],
         [SMEM, VMEM, VMEM],
         flops=1000,
         scratch=[pltpu.VMEM((tiles_here, tile_rows, half), jnp.float32)],
-        name="finish",
     )
     return (node_out, w_part[:per].T, text_grad, node_grad.reshape(nodes_here, half))
 
@@ -507,7 +604,7 @@
         P("graph", "mp"),
     )
     return jax.shard_map(
-        on_device,
+        step,
         mesh=mesh,
         in_specs=placed,
         out_specs=(P("graph", "mp"), P("mp", "graph"), P("graph", "mp"), P("graph", "mp")),

time: 186 us -> 140 us (0.75)
  blocking collectives: 64 us -> 15.5 us
  Pallas kernels: 46.5 us -> 34.1 us
  starting transfers between devices: 16.9 us -> 28.8 us
  local copies, waits for them, and re-layouts: 13.2 us -> 21.5 us
  waiting for transfers between devices: 43.3 us -> 37.6 us
    all_to_all x1, blocking collectives: 64 us -> 15.5 us  [spread(): lax.all_to_all(values, 'graph', split_axis=0, concat_axis=0, tiled=True)]
    all_to_all x3 -> x2, waiting for transfers between devices: 37.6 us -> 0.01 us  [spread(): lax.all_to_all(values, 'graph', split_axis=0, concat_axis=0, tiled=True)]
    ppermute x0 -> x8, waiting for transfers between devices: none -> 29.7 us  [toward(): lax.ppermute(values, 'graph', [(i, i ^ reach) for i in range(shards)])]
    ppermute x0 -> x8, starting transfers between devices: none -> 19.4 us  [toward(): lax.ppermute(values, 'graph', [(i, i ^ reach) for i in range(shards)])]
    pallas_call x10 -> x17, Pallas kernels: 46.5 us -> 34.1 us  [call(): pl.pallas_call(body, out_shape=tuple(outs) if many else outs[0], in_specs...]
    unnamed x21 -> x71, local copies, waits for them, and re-layouts: 8.42 us -> 18.4 us
    all_to_all x3 -> x2, starting transfers between devices: 15.4 us -> 8.42 us  [spread(): lax.all_to_all(values, 'graph', split_axis=0, concat_axis=0, tiled=True)]
    ppermute x5, waiting for transfers between devices: 5.67 us -> 7.9 us  [swap(): lax.ppermute(values, 'mp', [(i, cores - 1 - i) for i in range(cores)])]
  transfers between devices with their start and end apart: 8 -> 15, of which waited for: 6 -> 11; matrix products, arithmetic and copies ran while one was open for 1% -> 4% of each run, Pallas kernels for 5% -> 15%
where the time goes in v2:
time: 140 us; the launch traced here: 139 us
  waiting for transfers between devices  37.6 us (27%)
  Pallas kernels  34.1 us (24%)
  starting transfers between devices  28.8 us (21%)
  local copies, waits for them, and re-layouts  21.5 us (15%)
  blocking collectives  15.5 us (11%)
    pallas_call x17, Pallas kernels, call(): pl.pallas_call(body, out_shape=tuple(outs) if many else outs[0], in_specs...  34.1 us
    ppermute x8, waiting for transfers between devices, toward(): lax.ppermute(values, 'graph', [(i, i ^ reach) for i in range(shards)])  29.7 us
    ppermute x8, starting transfers between devices, toward(): lax.ppermute(values, 'graph', [(i, i ^ reach) for i in range(shards)])  19.4 us
    unnamed x71, local copies, waits for them, and re-layouts  18.4 us
    all_to_all x1, blocking collectives, spread(): lax.all_to_all(values, 'graph', split_axis=0, concat_axis=0, tiled=True)  15.5 us
    all_to_all x2, starting transfers between devices, spread(): lax.all_to_all(values, 'graph', split_axis=0, concat_axis=0, tiled=True)  8.42 us
    ppermute x5, waiting for transfers between devices, swap(): lax.ppermute(values, 'mp', [(i, cores - 1 - i) for i in range(cores)])  7.9 us
  transfers between devices with their start and end apart: 15, of which 11 were waited for; matrix products, arithmetic and copies ran while one was open for 4% of the time, Pallas kernels for 15%

profile of v2, /device:TPU:0, one launch (start us, length us, event | category | flops | bytes accessed | tf_op | source)
XLA Modules:
  0.0 139.0 jit_solution(10396264710551155830)
XLA Ops:
  2.7 15.5 %all_to_all.15.got_ref = s32[16,1,256]{2,1,0:T(1,128)S(1)} all-to-all(s32[16,1,256]{2,1,0:T(1,128)S(1)} %shard_map.156), channel_id=1, replica_groups=mesh['graph'=16,'mp'=2] {'graph'}, dimensions={0} | all-to-all | bytes 32768 | tf_op jit(solution)/shard_map/all_to_all | solution.py:435
  20.1 2.0 %shard_map.162 = bf16[16,128,384]{2,1,0:T(8,128)(2,1)} custom-call(s32[16]{0:T(128)S(1)} %slice_reduce_fusion.asked_ref, bf16[4,128,384]{2,1,0:T(8,128)(2,1)S(1)} %bitcast.14), custom_call_target="tpu_custom_call" | custom-call | flops 1000 | bytes 1966144 | tf_op jit(solution)/shard_map/pallas_call | solution.py:36
  22.1 3.8 %all-to-all-start.1 = ((bf16[16,128,384]{2,1,0:T(8,128)(2,1)}), bf16[16,128,384]{2,1,0:T(8,128)(2,1)S(1)}, u32[]{:S(2)}, u32[]{:S(2)}) async-start(bf16[16,128,384]{2,1,0:T(8,128)(2,1)} %shard_map.162), calls=%async_computation.1 | async-start | bytes 3145728 | tf_op jit(solution)/shard_map/all_to_all | solution.py:435
  26.0 2.3 %copy.18 = bf16[768,3,384]{0,2,1:T(8,128)(2,1)} copy(bf16[768,3,384]{2,0,1:T(8,128)(2,1)S(1)} %copy-done.34) | data formatting | bytes 3538944 | tf_op args[2]
  28.2 2.7 %copy.19.w_qkv_ref = bf16[768,1152]{1,0:T(8,128)(2,1)S(1)} copy(bf16[768,1152]{0,1:T(8,128)(2,1)} %bitcast.28) | data formatting | bytes 3538944 | tf_op jit(solution)/shard_map/reshape | solution.py:462
  33.2 3.9 %shard_map.158.mine_ref = bf16[512,768]{1,0:T(8,128)(2,1)S(1)} custom-call(s32[1,2]{1,0:T(1,128)S(1)} %copy-done.28, bf16[512,768]{1,0:T(8,128)(2,1)S(1)} %bitcast.26, bf16[768,1152]{1,0:T(8,128)(2,1)S(1)} %copy.19.w_qkv_ref, bf16[384,768]{1,0:T(8,128)(2,1)S(1)} %copy-done.33), custom_call_target="tpu_custom_call" | custom-call | flops 1610612736 | bytes 3932168 | tf_op jit(solution)/shard_map/pallas_call | solution.py:36
  37.3 2.3 %collective-permute-done.other_ref = bf16[512,768]{1,0:T(8,128)(2,1)S(1)} collective-permute-done((bf16[512,768]{1,0:T(8,128)(2,1)S(1)}, bf16[512,768]{1,0:T(8,128)(2,1)S(1)}, u32[]{:S(2)}, u32[]{:S(2)}) %collective-permute-start) | collective-permute-done | bytes 786464 | tf_op jit(solution)/shard_map/ppermute | solution.py:429
  39.5 4.8 %shard_map.159 = (bf16[512,768]{1,0:T(8,128)(2,1)S(1)}, bf16[512,768]{1,0:T(8,128)(2,1)}) custom-call(bf16[512,768]{1,0:T(8,128)(2,1)S(1)} %bitcast.27, bf16[512,768]{1,0:T(8,128)(2,1)S(1)} %shard_map.158.mine_ref, bf16[512,768]{1,0:T(8,128)(2,1)S(1)} %collective-permute-done.other_ref, bf16[768,1536]{1,0:T(8,128)(2,1)S(1)} %copy-done.29, ...), custom_call_target="tpu_custom_call" | custom-call | flops 2415919104 | bytes 8656896 | tf_op jit(solution)/shard_map/pallas_call | solution.py:36
  44.5 2.5 %collective-permute-done.1.other_ref = bf16[512,768]{1,0:T(8,128)(2,1)} collective-permute-done((bf16[512,768]{1,0:T(8,128)(2,1)}, bf16[512,768]{1,0:T(8,128)(2,1)}, u32[]{:S(2)}, u32[]{:S(2)}) %collective-permute-start.1) | collective-permute-done | bytes 786464 | tf_op jit(solution)/shard_map/ppermute | solution.py:429
  47.0 2.2 %shard_map.160 = f32[1,1,768]{2,1,0:T(1,128)S(1)} custom-call(s32[1,2]{1,0:T(1,128)S(1)} %copy-done.28, s32[1]{0:T(128)} %bitcast.core_ref, bf16[512,768]{1,0:T(8,128)(2,1)S(1)} %get-tuple-element.27.first_ref, bf16[512,768]{1,0:T(8,128)(2,1)} %get-tuple-element.28.mine_ref, bf16[512,768]{1,0:T(8,128)(2,1)} %collective-permute-done.1.other_ref, ...), custom_call_target="tpu_custom_call" | custom-call | flops 7864320 | bytes 2368524 | tf_op jit(solution)/shard_map/pallas_call | solution.py:36
  54.7 2.1 %collective-permute-done.3 = f32[2,1,768]{2,1,0:T(1,128)S(1)} collective-permute-done((f32[2,1,768]{2,1,0:T(1,128)S(1)}, f32[2,1,768]{2,1,0:T(1,128)S(1)}, u32[]{:S(2)}, u32[]{:S(2)}) %collective-permute-start.3) | collective-permute-done | bytes 6176 | tf_op jit(solution)/shard_map/ppermute | solution.py:432
  58.4 2.1 %collective-permute-done.4 = f32[4,1,768]{2,1,0:T(1,128)S(1)} collective-permute-done((f32[4,1,768]{2,1,0:T(1,128)S(1)}, f32[4,1,768]{2,1,0:T(1,128)S(1)}, u32[]{:S(2)}, u32[]{:S(2)}) %collective-permute-start.4) | collective-permute-done | bytes 12320 | tf_op jit(solution)/shard_map/ppermute | solution.py:432
  61.2 2.7 %collective-permute-start.5 = (f32[8,1,768]{2,1,0:T(1,128)}, f32[8,1,768]{2,1,0:T(1,128)}, u32[]{:S(2)}, u32[]{:S(2)}) collective-permute-start(f32[8,1,768]{2,1,0:T(1,128)} %pad_maximum_fusion.near_ref), channel_id=1, source_target_pairs={{0,16},{2,18},{4,20},{6,22},{8,24},{10,26},{12,28},{14,30},{16,0},... | collective-permute-start | bytes 73736 | tf_op jit(solution)/shard_map/ppermute | solution.py:432
  64.6 4.2 %shard_map.157 = (bf16[4,5,128,128]{3,2,1,0:T(8,128)(2,1)S(1)}, bf16[4,128,128]{2,1,0:T(8,128)(2,1)S(1)}, bf16[4,128,128]{2,1,0:T(8,128)(2,1)S(1)}, bf16[4,128,384]{2,1,0:T(8,128)(2,1)S(1)}) custom-call(s32[4,5]{1,0:T(4,128)S(1)} %copy-done.21, s32[1]{0:T(128)} %bitcast.1.self_ref, s32[16,1,256]{2,1,0:T(1,128)S(1)} %all_to_all.15.got_ref, ...), custom_call_target="tpu_custom_call" | custom-call | flops 83886080 | bytes 2375764 | tf_op jit(solution)/shard_map/pallas_call | solution.py:36
  75.4 2.6 %shard_map.163 = bf16[4,128,384]{2,1,0:T(8,128)(2,1)S(1)} custom-call(s32[4,5]{1,0:T(4,128)S(1)} %copy-done.22, s32[1]{0:T(128)} %bitcast.1.self_ref, bf16[4,5,128,128]{3,2,1,0:T(8,128)(2,1)S(1)} %copy-done.11, f32[4,128,384]{2,1,0:T(8,128)S(1)} %copy-done.9, bf16[4,128,384]{2,1,0:T(8,128)(2,1)S(1)} %bitcast.16, ...), custom_call_target="tpu_custom_call" | custom-call | flops 251658240 | bytes 3801172 | tf_op jit(solution)/shard_map/pallas_call | solution.py:36
  80.3 1.9 %shard_map.164 = (bf16[512,384]{1,0:T(8,128)(2,1)}, bf16[512,384]{1,0:T(8,128)(2,1)S(1)}) custom-call(s32[1]{0:T(128)} %bitcast.core_ref, bf16[512,384]{1,0:T(8,128)(2,1)S(1)} %bitcast.18, bf16[512,384]{1,0:T(8,128)(2,1)S(1)} %collective-permute-done.6.other_ref, bf16[384,768]{1,0:T(8,128)(2,1)S(1)} %copy-done.7, ...), custom_call_target="tpu_custom_call" | custom-call | flops 301989888 | bytes 3244036 | tf_op jit(solution)/shard_map/pallas_call | solution.py:36
  83.9 4.0 %shard_map.165 = (bf16[16,128,384]{2,1,0:T(8,128)(2,1)S(1)}, bf16[512,384]{1,0:T(8,128)(2,1)S(1)}) custom-call(s32[4,5]{1,0:T(4,128)S(1)} %copy-done.23, s32[1]{0:T(128)} %bitcast.1.self_ref, s32[1]{0:T(128)} %bitcast.core_ref, bf16[512,384]{1,0:T(8,128)(2,1)S(1)} %get-tuple-element.35.mine_ref, bf16[512,384]{1,0:T(8,128)(2,1)S(1)} %collective-permute-done.8.other_ref, ...), custom_call_target="tpu_custom_call" | custom-call | flops 553648128 | bytes 3997784 | tf_op jit(solution)/shard_map/pallas_call | solution.py:36
  89.0 4.6 %all-to-all-start.2 = ((bf16[16,128,384]{2,1,0:T(8,128)(2,1)}), bf16[16,128,384]{2,1,0:T(8,128)(2,1)S(1)}, u32[]{:S(2)}, u32[]{:S(2)}) async-start(bf16[16,128,384]{2,1,0:T(8,128)(2,1)} %copy-done.4), calls=%async_computation.2 | async-start | bytes 3145728 | tf_op jit(solution)/shard_map/all_to_all | solution.py:435
  97.7 2.0 %collective-permute-start.9 = (bf16[8,64,384]{2,1,0:T(8,128)(2,1)S(1)}, bf16[8,64,384]{2,1,0:T(8,128)(2,1)S(1)}, u32[]{:S(2)}, u32[]{:S(2)}) collective-permute-start(bf16[8,64,384]{2,1,0:T(8,128)(2,1)S(1)} %get-tuple-element.38), channel_id=1, source_target_pairs={{0,2},{2,0},{4,6},{6,4},{8,10},{10,8},{12,14},{14,12},{16,18},{18,... | collective-permute-start | bytes 1179656 | tf_op jit(solution)/shard_map/ppermute | solution.py:432
  99.7 10.8 %collective-permute-done.9.theirs_ref = bf16[8,64,384]{2,1,0:T(8,128)(2,1)S(1)} collective-permute-done((bf16[8,64,384]{2,1,0:T(8,128)(2,1)S(1)}, bf16[8,64,384]{2,1,0:T(8,128)(2,1)S(1)}, u32[]{:S(2)}, u32[]{:S(2)}) %collective-permute-start.9) | collective-permute-done | bytes 393248 | tf_op jit(solution)/shard_map/ppermute | solution.py:432
  110.6 8.6 %collective-permute-start.10 = (bf16[4,64,384]{2,1,0:T(8,128)(2,1)S(1)}, bf16[4,64,384]{2,1,0:T(8,128)(2,1)S(1)}, u32[]{:S(2)}, u32[]{:S(2)}) collective-permute-start(bf16[4,64,384]{2,1,0:T(8,128)(2,1)S(1)} %get-tuple-element.40), channel_id=1, source_target_pairs={{0,4},{2,6},{4,0},{6,2},{8,12},{10,14},{12,8},{14,10},{16,20},{18,... | collective-permute-start | bytes 589832 | tf_op jit(solution)/shard_map/ppermute | solution.py:432
  119.2 7.0 %collective-permute-done.10.theirs_ref = bf16[4,64,384]{2,1,0:T(8,128)(2,1)S(1)} collective-permute-done((bf16[4,64,384]{2,1,0:T(8,128)(2,1)S(1)}, bf16[4,64,384]{2,1,0:T(8,128)(2,1)S(1)}, u32[]{:S(2)}, u32[]{:S(2)}) %collective-permute-start.10) | collective-permute-done | bytes 196640 | tf_op jit(solution)/shard_map/ppermute | solution.py:432
  126.3 4.6 %collective-permute-done.11.theirs_ref = bf16[2,64,384]{2,1,0:T(8,128)(2,1)S(1)} collective-permute-done((bf16[2,64,384]{2,1,0:T(8,128)(2,1)S(1)}, bf16[2,64,384]{2,1,0:T(8,128)(2,1)S(1)}, u32[]{:S(2)}, u32[]{:S(2)}) %collective-permute-start.11) | collective-permute-done | bytes 98336 | tf_op jit(solution)/shard_map/ppermute | solution.py:432
  132.7 2.6 %shard_map.171.local_ref = f32[4,128,384]{2,1,0:T(8,128)S(1)} custom-call(s32[4,5]{1,0:T(4,128)S(1)} %copy-done.23, s32[1]{0:T(128)} %bitcast.1.self_ref, bf16[4,128,384]{2,1,0:T(8,128)(2,1)S(1)} %bitcast.21, bf16[4,5,128,128]{3,2,1,0:T(8,128)(2,1)S(1)} %copy-done.3, bf16[4,128,384]{2,1,0:T(8,128)(2,1)S(1)} %bitcast.20), custom_call_target="tpu_custom_call" | custom-call | flops 251658240 | bytes 2228308 | tf_op jit(solution)/shard_map/pallas_call | solution.py:36
  (101 shorter events, 36.3 us)
Async XLA Ops:
  22.1 50.4 %all-to-all-start.1 = ((bf16[16,128,384]{2,1,0:T(8,128)(2,1)}), bf16[16,128,384]{2,1,0:T(8,128)(2,1)S(1)}, u32[]{:S(2)}, u32[]{:S(2)}) async-start(bf16[16,128,384]{2,1,0:T(8,128)(2,1)} %shard_map.162), calls=%async_computation.1 | async-start | bytes 3145728 | tf_op jit(solution)/shard_map/all_to_all | solution.py:435
  33.2 6.3 %copy-start.24 = (f32[2,768]{1,0:T(2,128)S(1)}, f32[2,768]{1,0:T(2,128)}, u32[]{:S(2)}) copy-start(f32[2,768]{1,0:T(2,128)} %gains_ref.3) | copy-start | bytes 18436
  33.2 6.3 %copy-start.29 = (bf16[768,1536]{1,0:T(8,128)(2,1)S(1)}, bf16[768,1536]{1,0:T(8,128)(2,1)}, u32[]{:S(2)}) copy-start(bf16[768,1536]{1,0:T(8,128)(2,1)} %up_ref.1) | copy-start | bytes 7077892
  33.2 6.3 %copy-start.30 = (bf16[1536,768]{1,0:T(8,128)(2,1)S(1)}, bf16[1536,768]{1,0:T(8,128)(2,1)}, u32[]{:S(2)}) copy-start(bf16[1536,768]{1,0:T(8,128)(2,1)} %down_ref.1) | copy-start | bytes 7077892
  33.2 6.3 %copy-start.32 = (bf16[2,256,768]{2,1,0:T(8,128)(2,1)S(1)}, bf16[2,256,768]{2,1,0:T(8,128)(2,1)}, u32[]{:S(2)}) copy-start(bf16[2,256,768]{2,1,0:T(8,128)(2,1)} %param.13) | copy-start | bytes 2359300
  37.2 2.4 %collective-permute-start = (bf16[512,768]{1,0:T(8,128)(2,1)S(1)}, bf16[512,768]{1,0:T(8,128)(2,1)S(1)}, u32[]{:S(2)}, u32[]{:S(2)}) collective-permute-start(bf16[512,768]{1,0:T(8,128)(2,1)S(1)} %shard_map.158.mine_ref), channel_id=1, source_target_pairs={{0,1},{1,0},{2,3},{3,2},{4,5},{5,4},{6,7},{7,6},{8,9},{9,8},{10,11... | collective-permute-start | bytes 2359304 | tf_op jit(solution)/shard_map/ppermute | solution.py:429
  44.4 19.5 %copy-start.1 = (bf16[512,384]{1,0:T(8,128)(2,1)S(1)}, bf16[512,384]{1,0:T(8,128)(2,1)}, u32[]{:S(2)}) copy-start(bf16[512,384]{1,0:T(8,128)(2,1)} %param.20) | copy-start | bytes 1179652
  44.4 19.5 %copy-start.3 = (bf16[4,5,128,128]{3,2,1,0:T(8,128)(2,1)S(1)}, bf16[4,5,128,128]{3,2,1,0:T(8,128)(2,1)}, u32[]{:S(2)}) copy-start(bf16[4,5,128,128]{3,2,1,0:T(8,128)(2,1)} %adj_ref.5) | copy-start | bytes 1966084
  44.4 2.6 %collective-permute-start.1 = (bf16[512,768]{1,0:T(8,128)(2,1)}, bf16[512,768]{1,0:T(8,128)(2,1)}, u32[]{:S(2)}, u32[]{:S(2)}) collective-permute-start(bf16[512,768]{1,0:T(8,128)(2,1)} %get-tuple-element.28.mine_ref), channel_id=1, source_target_pairs={{0,1},{1,0},{2,3},{3,2},{4,5},{5,4},{6,7},{7,6},{8,9},{9,8},{10,11... | collective-permute-start | bytes 2359304 | tf_op jit(solution)/shard_map/ppermute | solution.py:429
  49.2 3.7 %collective-permute-start.2 = (f32[1,1,768]{2,1,0:T(1,128)S(1)}, f32[1,1,768]{2,1,0:T(1,128)S(1)}, u32[]{:S(2)}, u32[]{:S(2)}) collective-permute-start(f32[1,1,768]{2,1,0:T(1,128)S(1)} %shard_map.160), channel_id=1, source_target_pairs={{0,2},{2,0},{4,6},{6,4},{8,10},{10,8},{12,14},{14,12},{16,18},{18,... | collective-permute-start | bytes 9224 | tf_op jit(solution)/shard_map/ppermute | solution.py:432
  52.8 4.0 %collective-permute-start.3 = (f32[2,1,768]{2,1,0:T(1,128)S(1)}, f32[2,1,768]{2,1,0:T(1,128)S(1)}, u32[]{:S(2)}, u32[]{:S(2)}) collective-permute-start(f32[2,1,768]{2,1,0:T(1,128)S(1)} %pad_maximum_fusion.2), channel_id=1, source_target_pairs={{0,4},{2,6},{4,0},{6,2},{8,12},{10,14},{12,8},{14,10},{16,20},{18,... | collective-permute-start | bytes 18440 | tf_op jit(solution)/shard_map/ppermute | solution.py:432
  56.8 3.8 %collective-permute-start.4 = (f32[4,1,768]{2,1,0:T(1,128)S(1)}, f32[4,1,768]{2,1,0:T(1,128)S(1)}, u32[]{:S(2)}, u32[]{:S(2)}) collective-permute-start(f32[4,1,768]{2,1,0:T(1,128)S(1)} %pad_maximum_fusion.1), channel_id=1, source_target_pairs={{0,8},{2,10},{4,12},{6,14},{8,0},{10,2},{12,4},{14,6},{16,24},{18,... | collective-permute-start | bytes 36872 | tf_op jit(solution)/shard_map/ppermute | solution.py:432
  61.2 7.6 %collective-permute-start.5 = (f32[8,1,768]{2,1,0:T(1,128)}, f32[8,1,768]{2,1,0:T(1,128)}, u32[]{:S(2)}, u32[]{:S(2)}) collective-permute-start(f32[8,1,768]{2,1,0:T(1,128)} %pad_maximum_fusion.near_ref), channel_id=1, source_target_pairs={{0,16},{2,18},{4,20},{6,22},{8,24},{10,26},{12,28},{14,30},{16,0},... | collective-permute-start | bytes 73736 | tf_op jit(solution)/shard_map/ppermute | solution.py:432
  78.0 5.8 %copy-start.23 = (s32[4,5]{1,0:T(4,128)S(1)}, s32[4,5]{1,0:T(4,128)}, u32[]{:S(2)}) copy-start(s32[4,5]{1,0:T(4,128)} %ids_ref.9) | copy-start | bytes 244
  78.0 2.2 %collective-permute-start.6 = (bf16[512,384]{1,0:T(8,128)(2,1)S(1)}, bf16[512,384]{1,0:T(8,128)(2,1)S(1)}, u32[]{:S(2)}, u32[]{:S(2)}) collective-permute-start(bf16[512,384]{1,0:T(8,128)(2,1)S(1)} %bitcast.17), channel_id=1, source_target_pairs={{0,1},{1,0},{2,3},{3,2},{4,5},{5,4},{6,7},{7,6},{8,9},{9,8},{10,11... | collective-permute-start | bytes 1179656 | tf_op jit(solution)/shard_map/ppermute | solution.py:429
  78.2 2.1 %collective-permute-start.7 = (bf16[384,384]{1,0:T(8,128)(2,1)S(1)}, bf16[384,384]{1,0:T(8,128)(2,1)S(1)}, u32[]{:S(2)}, u32[]{:S(2)}) collective-permute-start(bf16[384,384]{1,0:T(8,128)(2,1)S(1)} %constant_dynamic-slice_fusion), channel_id=1, source_target_pairs={{0,1},{1,0},{2,3},{3,2},{4,5},{5,4},{6,7},{7,6},{8,9},{9,8},{10,11... | collective-permute-start | bytes 884744 | tf_op jit(solution)/shard_map/ppermute | solution.py:429
  82.1 1.7 %collective-permute-start.8 = (bf16[512,384]{1,0:T(8,128)(2,1)S(1)}, bf16[512,384]{1,0:T(8,128)(2,1)S(1)}, u32[]{:S(2)}, u32[]{:S(2)}) collective-permute-start(bf16[512,384]{1,0:T(8,128)(2,1)S(1)} %get-tuple-element.35.mine_ref), channel_id=1, source_target_pairs={{0,1},{1,0},{2,3},{3,2},{4,5},{5,4},{6,7},{7,6},{8,9},{9,8},{10,11... | collective-permute-start | bytes 1179656 | tf_op jit(solution)/shard_map/ppermute | solution.py:429
  89.0 8.7 %copy-start.5 = (bf16[512,384]{1,0:T(8,128)(2,1)}, bf16[512,384]{1,0:T(8,128)(2,1)S(1)}, u32[]{:S(2)}) copy-start(bf16[512,384]{1,0:T(8,128)(2,1)S(1)} %get-tuple-element.36.down_ref) | copy-start | bytes 1179652
  89.0 48.2 %all-to-all-start.2 = ((bf16[16,128,384]{2,1,0:T(8,128)(2,1)}), bf16[16,128,384]{2,1,0:T(8,128)(2,1)S(1)}, u32[]{:S(2)}, u32[]{:S(2)}) async-start(bf16[16,128,384]{2,1,0:T(8,128)(2,1)} %copy-done.4), calls=%async_computation.2 | async-start | bytes 3145728 | tf_op jit(solution)/shard_map/all_to_all | solution.py:435
  97.7 12.8 %collective-permute-start.9 = (bf16[8,64,384]{2,1,0:T(8,128)(2,1)S(1)}, bf16[8,64,384]{2,1,0:T(8,128)(2,1)S(1)}, u32[]{:S(2)}, u32[]{:S(2)}) collective-permute-start(bf16[8,64,384]{2,1,0:T(8,128)(2,1)S(1)} %get-tuple-element.38), channel_id=1, source_target_pairs={{0,2},{2,0},{4,6},{6,4},{8,10},{10,8},{12,14},{14,12},{16,18},{18,... | collective-permute-start | bytes 1179656 | tf_op jit(solution)/shard_map/ppermute | solution.py:432
  110.5 26.7 %copy-start.26 = (s32[16]{0:T(128)S(1)}, s32[16]{0:T(128)}, u32[]{:S(2)}) copy-start(s32[16]{0:T(128)} %copy-done.25) | copy-start | bytes 196
  110.6 15.5 %collective-permute-start.10 = (bf16[4,64,384]{2,1,0:T(8,128)(2,1)S(1)}, bf16[4,64,384]{2,1,0:T(8,128)(2,1)S(1)}, u32[]{:S(2)}, u32[]{:S(2)}) collective-permute-start(bf16[4,64,384]{2,1,0:T(8,128)(2,1)S(1)} %get-tuple-element.40), channel_id=1, source_target_pairs={{0,4},{2,6},{4,0},{6,2},{8,12},{10,14},{12,8},{14,10},{16,20},{18,... | collective-permute-start | bytes 589832 | tf_op jit(solution)/shard_map/ppermute | solution.py:432
  126.3 4.7 %collective-permute-start.11 = (bf16[2,64,384]{2,1,0:T(8,128)(2,1)S(1)}, bf16[2,64,384]{2,1,0:T(8,128)(2,1)S(1)}, u32[]{:S(2)}, u32[]{:S(2)}) collective-permute-start(bf16[2,64,384]{2,1,0:T(8,128)(2,1)S(1)} %get-tuple-element.42), channel_id=1, source_target_pairs={{0,8},{2,10},{4,12},{6,14},{8,0},{10,2},{12,4},{14,6},{16,24},{18,... | collective-permute-start | bytes 294920 | tf_op jit(solution)/shard_map/ppermute | solution.py:432
  131.0 5.6 %collective-permute-start.12 = (bf16[1,64,384]{2,1,0:T(8,128)(2,1)S(1)}, bf16[1,64,384]{2,1,0:T(8,128)(2,1)S(1)}, u32[]{:S(2)}, u32[]{:S(2)}) collective-permute-start(bf16[1,64,384]{2,1,0:T(8,128)(2,1)S(1)} %get-tuple-element.44), channel_id=1, source_target_pairs={{0,16},{2,18},{4,20},{6,22},{8,24},{10,26},{12,28},{14,30},{16,0},... | collective-permute-start | bytes 147464 | tf_op jit(solution)/shard_map/ppermute | solution.py:432
  (26 other events, 48.4 us)

commit v3 on v2

--- a/solution.py
+++ b/solution.py
@@ -20,6 +20,7 @@
 CUBE = 0.044715
 
 VMEM = pl.BlockSpec(memory_space=pltpu.VMEM)
+HBM = pl.BlockSpec(memory_space=pltpu.HBM)
 SMEM = pl.BlockSpec(memory_space=pltpu.SMEM)
 
 
@@ -27,23 +28,46 @@
     return (value + unit - 1) // unit * unit
 
 
-def call(body, outs, ins, specs, flops, scratch=()):
+def call(body, outs, ins, specs, flops, scratch=(), out_specs=None):
     moved = sum(a.size * a.dtype.itemsize for a in ins) + sum(
         o.size * o.dtype.itemsize for o in outs
     )
     many = len(outs) > 1
-    held = sum(math.prod(s.shape) * jnp.dtype(s.dtype).itemsize for s in scratch)
+    ins = [
+        pltpu.with_memory_space_constraint(a, pltpu.HBM) if s is HBM else a
+        for a, s in zip(ins, specs, strict=True)
+    ]
+    held = sum(math.prod(s.shape) * jnp.dtype(s.dtype).itemsize for s in scratch if counted(s))
+    out_specs = out_specs or [VMEM] * len(outs)
+    outs = [
+        pltpu.HBM(o.shape, o.dtype) if s is HBM else o for o, s in zip(outs, out_specs, strict=True)
+    ]
     return pl.pallas_call(
         body,
         out_shape=tuple(outs) if many else outs[0],
         in_specs=list(specs),
-        out_specs=tuple([VMEM] * len(outs)) if many else VMEM,
+        out_specs=tuple(out_specs) if many else out_specs[0],
         scratch_shapes=list(scratch),
         compiler_params=pltpu.CompilerParams(vmem_limit_bytes=moved + moved // 8 + held + SPARE),
         cost_estimate=pl.CostEstimate(flops=flops, bytes_accessed=moved, transcendentals=0),
     )(*ins)
 
 
+def counted(scratch):
+    return jnp.issubdtype(scratch.dtype, jnp.number)
+
+
+def copies(pairs, sems):
+    started = [pltpu.make_async_copy(a, b, sems.at[i]) for i, (a, b) in enumerate(pairs)]
+    for copy in started:
+        copy.start()
+    return started
+
+
+def unroll(steps):
+    return steps if steps <= 8 else 1
+
+
 def shape(dims, dtype=jnp.bfloat16):
     return jax.ShapeDtypeStruct(tuple(dims), dtype)
 
@@ -60,7 +84,9 @@
     return safe, owner, safe - owner * tiles_here
 
 
-def index_body(texts_here, ids_ref, self_ref, text_ref, out_ref):
+def index_body(texts_here, ids_hbm, self_ref, text_hbm, out_ref, ids_ref, text_ref, sems):
+    for copy in copies([(ids_hbm, ids_ref), (text_hbm, text_ref)], sems):
+        copy.wait()
     tiles_here, entries = ids_ref.shape
     shards, _, lanes = out_ref.shape
     width = lanes - LANES
@@ -94,12 +120,18 @@
         )
 
 
-def pack_body(asked_ref, cache_ref, out_ref):
-    def one(q, carry):
-        out_ref[q] = cache_ref[jnp.maximum(asked_ref[q], 0)]
-        return carry
-
-    lax.fori_loop(0, out_ref.shape[0], one, 0)
+def pack_body(asked_ref, cache_hbm, out_hbm, tile_ref, in_sems, out_sems):
+    tiles_here = tile_ref.shape[0]
+    for copy in copies([(cache_hbm.at[j], tile_ref.at[j]) for j in range(tiles_here)], in_sems):
+        copy.wait()
+
+    def slot(q):
+        place = jnp.maximum(asked_ref[q], 0)
+        return pltpu.make_async_copy(tile_ref.at[place], out_hbm.at[q], out_sems.at[q])
+
+    shards = out_hbm.shape[0]
+    lax.fori_loop(0, shards, lambda q, c: (slot(q).start(), c)[1], 0)
+    lax.fori_loop(0, shards, lambda q, c: (slot(q).wait(), c)[1], 0)
 
 
 def mask_body(ids_ref, self_ref, got_ref, adj_ref, cache_ref, kept_ref, pick_ref, own_ref, base_ref):
@@ -128,7 +160,9 @@
             kept_ref[r, k] = (values.astype(jnp.float32) * keep).astype(jnp.bfloat16)
             return total + mm(values, hot)
 
-        pick = lax.fori_loop(0, entries, one, jnp.zeros((tile_rows, width), jnp.float32))
+        pick = lax.fori_loop(
+            0, entries, one, jnp.zeros((tile_rows, width), jnp.float32), unroll=unroll(entries)
+        )
         pick_ref[r] = pick.astype(jnp.bfloat16)
         hot = holds(me * tiles_here + r)
         own_ref[r] = hot.astype(jnp.bfloat16)
@@ -147,9 +181,9 @@
     half = w_out_ref.shape[0]
     texts_here = tokens_ref.shape[0] // seq
     for c in range(3):
-        proj_ref[:, c * half : (c + 1) * half] = mm(
-            tokens_ref[...], w_qkv_ref[:, c * half : (c + 1) * half]
-        ).astype(jnp.bfloat16)
+        proj_ref[:, c * half : (c + 1) * half] = mm(tokens_ref[...], w_qkv_ref[c]).astype(
+            jnp.bfloat16
+        )
     left = lax.broadcasted_iota(jnp.int32, (seq, LANES), 1) < HEAD
     key_at = lax.broadcasted_iota(jnp.int32, (seq, seq), 1)
     for t in range(texts_here):
@@ -222,45 +256,50 @@
     return mm(order, stacked).astype(jnp.bfloat16)
 
 
-def fresh_body(self_ref, near_ref, far_ref, pick_ref, own_ref, base_ref, start_ref, feature_ref):
-    half = base_ref.shape[2]
-    pooled = pooled_rows(self_ref[0], near_ref, far_ref, half)
+def gather_body(
+    ids_hbm, self_ref, kept_hbm, pick_hbm, near_hbm, far_hbm, cache_hbm, remote_ref, out_ref,
+    pooled_ref, ids_ref, kept_ref, pick_ref, near_ref, far_ref, cache_ref, source_ref, sems
+):
+    started = copies(
+        [
+            (near_hbm, near_ref), (far_hbm, far_ref), (ids_hbm, ids_ref), (cache_hbm, cache_ref),
+            (pick_hbm, pick_ref), (kept_hbm, kept_ref),
+        ],
+        sems,
+    )
+    tiles_here, entries, _, _ = kept_ref.shape
+    half = cache_ref.shape[2]
+    me = self_ref[0]
+    for copy in started:
+        copy.wait()
+    pooled = pooled_rows(me, near_ref, far_ref, half)
+    pooled_ref[...] = pooled
     texts = pooled.shape[0]
-    for r in range(pick_ref.shape[0]):
-        start_ref[r] = mm(pick_ref[r][:, :texts], pooled)
-        feature_ref[r] = (
-            base_ref[r].astype(jnp.float32) + mm(own_ref[r][:, :texts], pooled)
-        ).astype(jnp.bfloat16)
-
-
-def gather_body(ids_ref, self_ref, kept_ref, start_ref, cache_ref, remote_ref, out_ref, source_ref):
-    tiles_here, entries, _, _ = kept_ref.shape
-    me = self_ref[0]
+
+    def fetch(r, k):
+        tile_id = ids_ref[r, k]
+        _, owner, place = tile_of(tile_id, tiles_here)
+        local = (owner == me) | (tile_id < 0)
+
+        @pl.when(local)
+        def _():
+            source_ref[r % 2, k] = cache_ref[place]
+
+        @pl.when(jnp.logical_not(local))
+        def _():
+            source_ref[r % 2, k] = remote_ref[owner]
+
     for r in range(tiles_here):
-
-        def fetch(k, carry):
-            tile_id = ids_ref[r, k]
-            _, owner, place = tile_of(tile_id, tiles_here)
-            local = (owner == me) | (tile_id < 0)
-
-            @pl.when(local)
-            def _():
-                source_ref[k] = cache_ref[place]
-
-            @pl.when(jnp.logical_not(local))
-            def _():
-                source_ref[k] = remote_ref[owner]
-
-            return carry
-
-        lax.fori_loop(0, entries, fetch, 0)
-        total = start_ref[r]
+        lax.fori_loop(
+            0, entries, lambda k, c: (fetch(r, k), c)[1], 0, unroll=unroll(entries)
+        )
+        total = mm(pick_ref[r][:, :texts], pooled)
         for k in range(entries):
-            total = total + mm(kept_ref[r, k], source_ref[k])
+            total = total + mm(kept_ref[r, k], source_ref[r % 2, k])
         out_ref[r] = total.astype(jnp.bfloat16)
 
 
-def forward_body(core_ref, mine_ref, other_ref, w_own_ref, w_other_ref, grad_ref, feature_ref, node_ref, slope_ref):
+def forward_body(core_ref, mine_ref, other_ref, w_own_ref, w_other_ref, grad_ref, own_ref, base_ref, pooled_ref, node_ref, slope_ref):
     _, half = mine_ref.shape
     start = pl.multiple_of(core_ref[0] * half, LANES)
     hidden = mm(mine_ref[...], w_own_ref[:, pl.ds(start, half)]) + mm(
@@ -271,14 +310,20 @@
     lifted = 0.5 * (1.0 + gate)
     slope = lifted + 0.5 * hidden * (1.0 - gate * gate) * (ROOT * (1.0 + 3.0 * CUBE * square))
     slope_ref[...] = (grad_ref[...].astype(jnp.float32) * slope).astype(jnp.bfloat16)
-    node_ref[...] = (feature_ref[...].astype(jnp.float32) + hidden * lifted).astype(jnp.bfloat16)
+    fresh = mm(own_ref[:, : pooled_ref.shape[0]], pooled_ref[...])
+    node_ref[...] = (base_ref[...].astype(jnp.float32) + fresh + hidden * lifted).astype(
+        jnp.bfloat16
+    )
 
 
 def backward_body(
-    ids_ref, self_ref, core_ref, mine_ref, other_ref, w_own_ref, adj_ref, send_ref, down_ref
+    per, texts_here, ids_ref, self_ref, core_ref, mine_ref, other_ref, agg_ref, w_own_ref, adj_ref,
+    pick_ref, own_ref, grad_ref, send_hbm, keep_hbm, give_hbm, down_hbm,
+    down_ref, w_ref, text_ref, send_ref, rows_ref, half_ref, sems, slot_sems, row_sems
 ):
     tiles_here, entries, tile_rows, _ = adj_ref.shape
-    half = send_ref.shape[2]
+    shards, text_rows, half = rows_ref.shape
+    kept = shards // 2
     me = self_ref[0]
     core = core_ref[0]
     own = pl.multiple_of(core * half, LANES)
@@ -287,88 +332,94 @@
         other_ref[...], w_own_ref[:, pl.ds(far, half)], (1, 1)
     )
     down_ref[...] = down.astype(jnp.bfloat16)
+    down_copy = pltpu.make_async_copy(down_ref, down_hbm, sems.at[0])
+    down_copy.start()
+
+    def remote(r, k):
+        tile_id = ids_ref[r, k]
+        _, owner, _ = tile_of(tile_id, tiles_here)
+        slot = pltpu.make_async_copy(
+            send_ref.at[owner], send_hbm.at[owner, pl.ds(0, tile_rows), :], slot_sems.at[owner]
+        )
+        return (tile_id >= 0) & (owner != me), owner, slot
+
     for r in range(tiles_here):
         rows = slice(r * tile_rows, (r + 1) * tile_rows)
 
-        def one(k, carry):
-            tile_id = ids_ref[r, k]
-            _, owner, _ = tile_of(tile_id, tiles_here)
-
-            @pl.when((tile_id >= 0) & (owner != me))
+        def give_one(k, carry):
+            away, owner, slot = remote(r, k)
+
+            @pl.when(away)
             def _():
                 send_ref[owner] = mm(adj_ref[r, k], down_ref[rows, :], (0, 0)).astype(jnp.bfloat16)
+                slot.start()
 
             return carry
 
-        lax.fori_loop(0, entries, one, 0)
-
-
-def chunk_body(
-    per, texts_here, self_ref, core_ref, mine_ref, other_ref, agg_ref, down_ref, pick_ref, own_ref,
-    grad_ref, keep_ref, give_ref, w_ref, text_ref
-):
-    kept, _, half = keep_ref.shape
-    shards = 2 * kept
-    me = self_ref[0]
-    core = core_ref[0]
-    own = pl.multiple_of(core * half, LANES)
-    far = pl.multiple_of((1 - core) * half, LANES)
+        lax.fori_loop(0, entries, give_one, 0, unroll=unroll(entries))
+
     text_ref[...] = mm(pick_ref[...], down_ref[...], (0, 0)) + mm(
         own_ref[...], grad_ref[...], (0, 0)
     )
+    row = lax.broadcasted_iota(jnp.int32, (text_rows, half), 0)
+    for q in range(shards):
+        block = jnp.zeros((text_rows, half), jnp.float32)
+        for i in range(texts_here):
+            line = text_ref[i * shards + q : i * shards + q + 1, :]
+            high = line.astype(jnp.bfloat16).astype(jnp.float32)
+            block = jnp.where(row == i, high, block)
+            block = jnp.where(row == text_rows // 2 + i, line - high, block)
+        rows_ref[q] = block.astype(jnp.bfloat16)
+    row_copy = pltpu.make_async_copy(
+        rows_ref, send_hbm.at[:, pl.ds(tile_rows, text_rows), :], row_sems.at[0]
+    )
+    row_copy.start()
+
     columns = 2 * half
     w_ref[pl.ds(own, half), :] = mm(mine_ref[...], agg_ref[...], (0, 0))
     w_ref[pl.ds(far, half), :] = mm(other_ref[...], agg_ref[...], (0, 0))
     w_ref[columns:, :] = jnp.zeros((w_ref.shape[0] - columns, half), jnp.float32)
-    deep = up_to(per, ROWS)
-    row = lax.broadcasted_iota(jnp.int32, (ROWS, half), 0)
+    deep = half_ref.shape[1]
     for q in range(shards):
-        piece = w_ref[q * per : q * per + deep, :].astype(jnp.bfloat16)
-        block = jnp.zeros((ROWS, half), jnp.float32)
-        for i in range(texts_here):
-            line = text_ref[i * shards + q : i * shards + q + 1, :]
-            high = line.astype(jnp.bfloat16).astype(jnp.float32)
-            block = jnp.where(row == i, high, block)
-            block = jnp.where(row == ROWS // 2 + i, line - high, block)
-        block = block.astype(jnp.bfloat16)
         step = q ^ me
         turned = step * 0
         reach = 1
         while reach < shards:
             turned = 2 * turned + ((step // reach) & 1)
             reach *= 2
-
-        @pl.when(turned < kept)
-        def _():
-            keep_ref[turned, :deep, :] = piece
-            keep_ref[turned, deep:, :] = block
-
-        @pl.when(turned >= kept)
-        def _():
-            give_ref[turned - kept, :deep, :] = piece
-            give_ref[turned - kept, deep:, :] = block
-
-
-def fold(mine, theirs, deep):
-    total = mine.astype(jnp.float32) + theirs.astype(jnp.float32)
-    text = total[deep : deep + ROWS // 2, :] + total[deep + ROWS // 2 :, :]
-    return total[:deep, :], text
-
-
-def fold_body(deep, mine_ref, theirs_ref, keep_ref, give_ref):
+        half_ref[turned] = w_ref[q * per : q * per + deep, :].astype(jnp.bfloat16)
+    ends = copies(
+        [(half_ref.at[pl.ds(kept, kept)], give_hbm), (half_ref.at[pl.ds(0, kept)], keep_hbm)],
+        sems.at[pl.ds(1, 2)],
+    )
+
+    for r in range(tiles_here):
+
+        def wait_one(k, carry):
+            away, _, slot = remote(r, k)
+
+            @pl.when(away)
+            def _():
+                slot.wait()
+
+            return carry
+
+        lax.fori_loop(0, entries, wait_one, 0)
+    down_copy.wait()
+    row_copy.wait()
+    for copy in ends:
+        copy.wait()
+
+
+def fold_body(mine_ref, theirs_ref, keep_ref, give_ref):
     kept = keep_ref.shape[0]
     for s in range(2 * kept):
-        w_sum, text = fold(mine_ref[s], theirs_ref[s], deep)
-        high = text.astype(jnp.bfloat16).astype(jnp.float32)
-        out_ref = (keep_ref if s < kept else give_ref).at[s % kept]
-        out_ref[:deep, :] = w_sum.astype(jnp.bfloat16)
-        out_ref[deep:, :] = jnp.concatenate([high, text - high], axis=0).astype(jnp.bfloat16)
-
-
-def close_body(deep, mine_ref, theirs_ref, w_ref, text_ref):
-    w_sum, text = fold(mine_ref[0], theirs_ref[0], deep)
-    w_ref[...] = w_sum
-    text_ref[...] = text[: text_ref.shape[0], :]
+        total = mine_ref[s].astype(jnp.float32) + theirs_ref[s].astype(jnp.float32)
+        (keep_ref if s < kept else give_ref)[s % kept] = total.astype(jnp.bfloat16)
+
+
+def close_body(mine_ref, theirs_ref, w_ref):
+    w_ref[...] = mine_ref[0].astype(jnp.float32) + theirs_ref[0].astype(jnp.float32)
 
 
 def local_body(ids_ref, self_ref, down_ref, adj_ref, grad_ref, local_ref):
@@ -387,22 +438,32 @@
 
             return carry
 
-        lax.fori_loop(0, entries, one, 0)
-
-
-def finish_body(asked_ref, local_ref, got_ref, node_ref, sum_ref):
-    sum_ref[...] = local_ref[...]
+        lax.fori_loop(0, entries, one, 0, unroll=unroll(entries))
+
+
+def finish_body(asked_ref, local_hbm, got_ref, node_ref, text_ref, sum_ref, sems):
+    local = pltpu.make_async_copy(local_hbm, sum_ref, sems.at[0])
+    local.start()
+    _, tile_rows, half = sum_ref.shape
+    shards, rows, _ = got_ref.shape
+    total = jnp.zeros((rows - tile_rows, half), jnp.float32)
+    for q in range(shards):
+        total = total + got_ref[q, tile_rows:, :].astype(jnp.float32)
+    text_ref[...] = (total[: (rows - tile_rows) // 2] + total[(rows - tile_rows) // 2 :])[
+        : text_ref.shape[0]
+    ]
+    local.wait()
 
     def one(q, carry):
         asked = asked_ref[q]
 
         @pl.when(asked >= 0)
         def _():
-            sum_ref[asked] += got_ref[q].astype(jnp.float32)
+            sum_ref[asked] += got_ref[q, :tile_rows, :].astype(jnp.float32)
 
         return carry
 
-    lax.fori_loop(0, got_ref.shape[0], one, 0)
+    lax.fori_loop(0, shards, one, 0)
     node_ref[...] = sum_ref[...].astype(jnp.bfloat16)
 
 
@@ -438,8 +499,13 @@
         functools.partial(index_body, texts_here),
         [shape((shards, 1, slots + LANES), jnp.int32)],
         [adj_tiles, me, node_text.reshape(tiles_here, tile_rows)],
-        [SMEM, SMEM, VMEM],
+        [HBM, SMEM, HBM],
         flops=1000,
+        scratch=[
+            pltpu.SMEM(adj_tiles.shape, jnp.int32),
+            pltpu.VMEM((tiles_here, tile_rows), jnp.int32),
+            pltpu.SemaphoreType.DMA((2,)),
+        ],
     )
     got = spread(index)
     asked = got[:, 0, slots]
@@ -448,8 +514,14 @@
         pack_body,
         [shape((shards, tile_rows, half))],
         [asked, cache_tiles],
-        [SMEM, VMEM],
+        [SMEM, HBM],
         flops=1000,
+        scratch=[
+            pltpu.VMEM(cache_tiles.shape, jnp.bfloat16),
+            pltpu.SemaphoreType.DMA((tiles_here,)),
+            pltpu.SemaphoreType.DMA((shards,)),
+        ],
+        out_specs=[HBM],
     )
     remote = spread(packed)
 
@@ -459,7 +531,7 @@
     partial = call(
         functools.partial(attend_body, seq),
         [shape((count, width))],
-        [token_counts, flat_tokens, w_qkv.reshape(width, 3 * half), w_out],
+        [token_counts, flat_tokens, jnp.transpose(w_qkv, (1, 0, 2)), w_out],
         [SMEM, VMEM, VMEM, VMEM],
         flops=2 * count * (width * 3 * half + half * width + 2 * seq * half * 2),
         scratch=[pltpu.VMEM((count, 3 * half), jnp.bfloat16), pltpu.VMEM((count, half), jnp.bfloat16)],
@@ -500,55 +572,66 @@
         [SMEM, SMEM, VMEM, VMEM, VMEM],
         flops=2 * adj_values.size * slots,
     )
-    start, features = call(
-        fresh_body,
-        [shape((tiles_here, tile_rows, half), jnp.float32), shape((tiles_here, tile_rows, half))],
-        [me, near, far, pick, own, base],
-        [SMEM] + [VMEM] * 5,
-        flops=4 * nodes_here * texts * half,
-    )
-    gathered = call(
+    gathered, pooled = call(
         gather_body,
-        [shape((tiles_here, tile_rows, half))],
-        [adj_tiles, me, kept, start, cache_tiles, remote],
-        [SMEM, SMEM] + [VMEM] * 4,
+        [shape((tiles_here, tile_rows, half)), shape((texts, half))],
+        [adj_tiles, me, kept, pick, near, far, cache_tiles, remote],
+        [HBM, SMEM, HBM, HBM, HBM, HBM, HBM, VMEM],
         flops=2 * adj_values.size * half,
-        scratch=[pltpu.VMEM((entries, tile_rows, half), jnp.bfloat16)],
-    ).reshape(nodes_here, half)
+        scratch=[
+            pltpu.SMEM(adj_tiles.shape, jnp.int32),
+            pltpu.VMEM(kept.shape, jnp.bfloat16),
+            pltpu.VMEM(pick.shape, jnp.bfloat16),
+            pltpu.VMEM(near.shape, jnp.float32),
+            pltpu.VMEM(far.shape, jnp.float32),
+            pltpu.VMEM(cache_tiles.shape, jnp.bfloat16),
+            pltpu.VMEM((2, entries, tile_rows, half), jnp.bfloat16),
+            pltpu.SemaphoreType.DMA((6,)),
+        ],
+    )
+    gathered = gathered.reshape(nodes_here, half)
     node_out, slope = call(
         forward_body,
         [shape((nodes_here, half)), shape((nodes_here, half))],
         [
             core, gathered, swap(gathered), w_gnn, w_other, out_grad,
-            features.reshape(nodes_here, half),
-        ],
-        [SMEM] + [VMEM] * 6,
+            own.reshape(nodes_here, slots), base.reshape(nodes_here, half), pooled,
+        ],
+        [SMEM] + [VMEM] * 8,
         flops=4 * nodes_here * half * half,
     )
     grad_tiles = out_grad.reshape(tiles_here, tile_rows, half)
     slope_other = swap(slope)
-    send, down = call(
-        backward_body,
-        [shape((shards, tile_rows, half)), shape((nodes_here, half))],
-        [adj_tiles, me, core, slope, slope_other, w_gnn, adj_values],
-        [SMEM, SMEM, SMEM] + [VMEM] * 4,
-        flops=4 * nodes_here * half * half + 2 * adj_values.size * half,
-    )
-    returned = spread(send)
-    keep, give = call(
-        functools.partial(chunk_body, per, texts_here),
-        [shape((shards // 2, deep + ROWS, half)), shape((shards // 2, deep + ROWS, half))],
+    text_rows = up_to(2 * texts_here, 8)
+    halves = (shards // 2, deep, half)
+    send, keep, give, down = call(
+        functools.partial(backward_body, per, texts_here),
         [
-            me, core, slope, slope_other, gathered, down, pick.reshape(nodes_here, slots),
-            own.reshape(nodes_here, slots), out_grad,
-        ],
-        [SMEM, SMEM] + [VMEM] * 7,
-        flops=4 * nodes_here * half * (half + slots),
+            shape((shards, tile_rows + text_rows, half)),
+            shape(halves),
+            shape(halves),
+            shape((nodes_here, half)),
+        ],
+        [
+            adj_tiles, me, core, slope, slope_other, gathered, w_gnn, adj_values,
+            pick.reshape(nodes_here, slots), own.reshape(nodes_here, slots), out_grad,
+        ],
+        [SMEM, SMEM, SMEM] + [VMEM] * 8,
+        flops=8 * nodes_here * half * half + 2 * adj_values.size * half,
         scratch=[
+            pltpu.VMEM((nodes_here, half), jnp.bfloat16),
             pltpu.VMEM((width + ROWS, half), jnp.float32),
             pltpu.VMEM((slots, half), jnp.float32),
-        ],
-    )
+            pltpu.VMEM((shards, tile_rows, half), jnp.bfloat16),
+            pltpu.VMEM((shards, text_rows, half), jnp.bfloat16),
+            pltpu.VMEM((shards, deep, half), jnp.bfloat16),
+            pltpu.SemaphoreType.DMA((3,)),
+            pltpu.SemaphoreType.DMA((shards,)),
+            pltpu.SemaphoreType.DMA((1,)),
+        ],
+        out_specs=[HBM] * 4,
+    )
+    returned = spread(send)
     local = call(
         local_body,
         [shape((tiles_here, tile_rows, half), jnp.float32)],
@@ -559,9 +642,9 @@
     reach = 1
     given = toward(give, reach)
     while 2 * reach < shards:
-        part = (shards // (4 * reach), deep + ROWS, half)
+        part = (shards // (4 * reach), deep, half)
         keep, give = call(
-            functools.partial(fold_body, deep),
+            fold_body,
             [shape(part), shape(part)],
             [keep, given],
             [VMEM] * 2,
@@ -569,20 +652,19 @@
         )
         reach *= 2
         given = toward(give, reach)
-    w_part, text_grad = call(
-        functools.partial(close_body, deep),
-        [shape((deep, half), jnp.float32), shape((texts_here, half), jnp.float32)],
-        [keep, given],
-        [VMEM] * 2,
+    w_part = call(
+        close_body, [shape((deep, half), jnp.float32)], [keep, given], [VMEM] * 2, flops=1000
+    )
+    node_grad, text_grad = call(
+        finish_body,
+        [shape((tiles_here, tile_rows, half)), shape((texts_here, half), jnp.float32)],
+        [asked, local, returned],
+        [SMEM, HBM, VMEM],
         flops=1000,
-    )
-    node_grad = call(
-        finish_body,
-        [shape((tiles_here, tile_rows, half))],
-        [asked, local, returned],
-        [SMEM, VMEM, VMEM],
-        flops=1000,
-        scratch=[pltpu.VMEM((tiles_here, tile_rows, half), jnp.float32)],
+        scratch=[
+            pltpu.VMEM((tiles_here, tile_rows, half), jnp.float32),
+            pltpu.SemaphoreType.DMA((1,)),
+        ],
     )
     return (node_out, w_part[:per].T, text_grad, node_grad.reshape(nodes_here, half))
 

time: 140 us -> 127 us (0.907)
  local copies, waits for them, and re-layouts: 21.5 us -> 5.67 us
  waiting for transfers between devices: 37.6 us -> 45.8 us
  starting transfers between devices: 28.8 us -> 25.6 us
    unnamed x71 -> x48, local copies, waits for them, and re-layouts: 18.4 us -> 5.25 us
    ppermute x8, waiting for transfers between devices: 29.7 us -> 37.9 us  [toward(): lax.ppermute(values, 'graph', [(i, i ^ reach) for i in range(shards)])]
    ppermute x8, starting transfers between devices: 19.4 us -> 15.3 us  [toward(): lax.ppermute(values, 'graph', [(i, i ^ reach) for i in range(shards)])]
    reshape x1 -> x0, local copies, waits for them, and re-layouts: 2.74 us -> none  [step(): w_qkv.reshape(width, 3 * half)]
    pallas_call x17 -> x15, Pallas kernels: 34.1 us -> 33.3 us  [call(): pl.pallas_call(body, out_shape=tuple(outs) if many else outs[0], in_specs...]
  transfers between devices with their start and end apart: 15 -> 15, of which waited for: 11 -> 12; matrix products, arithmetic and copies ran while one was open for 4% -> 0% of each run, Pallas kernels for 15% -> 12%
where the time goes in v3:
time: 127 us
  waiting for transfers between devices  45.8 us (36%)
  Pallas kernels  33.3 us (26%)
  starting transfers between devices  25.6 us (20%)
  blocking collectives  15.5 us (12%)
  local copies, waits for them, and re-layouts  5.67 us (4%)
    ppermute x8, waiting for transfers between devices, toward(): lax.ppermute(values, 'graph', [(i, i ^ reach) for i in range(shards)])  37.9 us
    pallas_call x15, Pallas kernels, call(): pl.pallas_call(body, out_shape=tuple(outs) if many else outs[0], in_specs...  33.3 us
    all_to_all x1, blocking collectives, spread(): lax.all_to_all(values, 'graph', split_axis=0, concat_axis=0, tiled=True)  15.5 us
    ppermute x8, starting transfers between devices, toward(): lax.ppermute(values, 'graph', [(i, i ^ reach) for i in range(shards)])  15.3 us
    all_to_all x2, starting transfers between devices, spread(): lax.all_to_all(values, 'graph', split_axis=0, concat_axis=0, tiled=True)  9.34 us
    ppermute x5, waiting for transfers between devices, swap(): lax.ppermute(values, 'mp', [(i, cores - 1 - i) for i in range(cores)])  7.89 us
    unnamed x48, local copies, waits for them, and re-layouts  5.25 us
  transfers between devices with their start and end apart: 15, of which 12 were waited for; matrix products, arithmetic and copies ran while one was open for 0% of the time, Pallas kernels for 12%

profile of v3, /device:TPU:0, one launch (start us, length us, event | category | flops | bytes accessed | tf_op | source)
XLA Modules:
  0.0 127.0 jit_solution(16240527197512103455)
XLA Ops:
  1.5 15.5 %all_to_all.15.got_ref = s32[16,1,256]{2,1,0:T(1,128)S(1)} all-to-all(s32[16,1,256]{2,1,0:T(1,128)S(1)} %shard_map.156), channel_id=1, replica_groups=mesh['graph'=16,'mp'=2] {'graph'}, dimensions={0} | all-to-all | bytes 32768 | tf_op jit(solution)/shard_map/all_to_all | solution.py:496
  17.3 2.9 %shard_map.161 = bf16[16,128,384]{2,1,0:T(8,128)(2,1)} custom-call(s32[16]{0:T(128)S(1)} %slice_reduce_fusion.asked_ref, bf16[4,128,384]{2,1,0:T(8,128)(2,1)} %bitcast.14), custom_call_target="tpu_custom_call" | custom-call | flops 1000 | bytes 1966144 | tf_op jit(solution)/shard_map/pallas_call | solution.py:45
  20.3 3.9 %all-to-all-start.1 = ((bf16[16,128,384]{2,1,0:T(8,128)(2,1)}), bf16[16,128,384]{2,1,0:T(8,128)(2,1)S(1)}, u32[]{:S(2)}, u32[]{:S(2)}) async-start(bf16[16,128,384]{2,1,0:T(8,128)(2,1)} %shard_map.161), calls=%async_computation.1 | async-start | bytes 3145728 | tf_op jit(solution)/shard_map/all_to_all | solution.py:496
  25.7 3.9 %shard_map.158.mine_ref = bf16[512,768]{1,0:T(8,128)(2,1)S(1)} custom-call(s32[1,2]{1,0:T(1,128)S(1)} %copy-done.15, bf16[512,768]{1,0:T(8,128)(2,1)S(1)} %bitcast.27, bf16[3,768,384]{2,1,0:T(8,128)(2,1)S(1)} %bitcast.26, bf16[384,768]{1,0:T(8,128)(2,1)S(1)} %copy-done.21), custom_call_target="tpu_custom_call" | custom-call | flops 1610612736 | bytes 3932168 | tf_op jit(solution)/shard_map/pallas_call | solution.py:45
  29.7 2.3 %collective-permute-done.other_ref = bf16[512,768]{1,0:T(8,128)(2,1)S(1)} collective-permute-done((bf16[512,768]{1,0:T(8,128)(2,1)S(1)}, bf16[512,768]{1,0:T(8,128)(2,1)S(1)}, u32[]{:S(2)}, u32[]{:S(2)}) %collective-permute-start) | collective-permute-done | bytes 786464 | tf_op jit(solution)/shard_map/ppermute | solution.py:490
  32.0 4.9 %shard_map.159 = (bf16[512,768]{1,0:T(8,128)(2,1)S(1)}, bf16[512,768]{1,0:T(8,128)(2,1)}) custom-call(bf16[512,768]{1,0:T(8,128)(2,1)S(1)} %bitcast.28, bf16[512,768]{1,0:T(8,128)(2,1)S(1)} %shard_map.158.mine_ref, bf16[512,768]{1,0:T(8,128)(2,1)S(1)} %collective-permute-done.other_ref, bf16[768,1536]{1,0:T(8,128)(2,1)S(1)} %copy-done.16, ...), custom_call_target="tpu_custom_call" | custom-call | flops 2415919104 | bytes 8656896 | tf_op jit(solution)/shard_map/pallas_call | solution.py:45
  37.0 2.5 %collective-permute-done.1.other_ref = bf16[512,768]{1,0:T(8,128)(2,1)} collective-permute-done((bf16[512,768]{1,0:T(8,128)(2,1)}, bf16[512,768]{1,0:T(8,128)(2,1)}, u32[]{:S(2)}, u32[]{:S(2)}) %collective-permute-start.1) | collective-permute-done | bytes 786464 | tf_op jit(solution)/shard_map/ppermute | solution.py:490
  39.5 2.2 %shard_map.160 = f32[1,1,768]{2,1,0:T(1,128)S(1)} custom-call(s32[1,2]{1,0:T(1,128)S(1)} %copy-done.15, s32[1]{0:T(128)} %bitcast.core_ref, bf16[512,768]{1,0:T(8,128)(2,1)S(1)} %get-tuple-element.28.first_ref, bf16[512,768]{1,0:T(8,128)(2,1)} %get-tuple-element.29.mine_ref, bf16[512,768]{1,0:T(8,128)(2,1)} %collective-permute-done.1.other_ref, ...), custom_call_target="tpu_custom_call" | custom-call | flops 7864320 | bytes 2368524 | tf_op jit(solution)/shard_map/pallas_call | solution.py:45
  41.6 1.9 %collective-permute-start.2 = (f32[1,1,768]{2,1,0:T(1,128)S(1)}, f32[1,1,768]{2,1,0:T(1,128)S(1)}, u32[]{:S(2)}, u32[]{:S(2)}) collective-permute-start(f32[1,1,768]{2,1,0:T(1,128)S(1)} %shard_map.160), channel_id=1, source_target_pairs={{0,2},{2,0},{4,6},{6,4},{8,10},{10,8},{12,14},{14,12},{16,18},{18,... | collective-permute-start | bytes 9224 | tf_op jit(solution)/shard_map/ppermute | solution.py:493
  43.5 2.0 %collective-permute-done.2 = f32[1,1,768]{2,1,0:T(1,128)S(1)} collective-permute-done((f32[1,1,768]{2,1,0:T(1,128)S(1)}, f32[1,1,768]{2,1,0:T(1,128)S(1)}, u32[]{:S(2)}, u32[]{:S(2)}) %collective-permute-start.2) | collective-permute-done | bytes 3104 | tf_op jit(solution)/shard_map/ppermute | solution.py:493
  50.9 3.9 %collective-permute-done.4 = f32[4,1,768]{2,1,0:T(1,128)S(1)} collective-permute-done((f32[4,1,768]{2,1,0:T(1,128)S(1)}, f32[4,1,768]{2,1,0:T(1,128)S(1)}, u32[]{:S(2)}, u32[]{:S(2)}) %collective-permute-start.4) | collective-permute-done | bytes 12320 | tf_op jit(solution)/shard_map/ppermute | solution.py:493
  61.5 3.7 %shard_map.162 = (bf16[4,128,384]{2,1,0:T(8,128)(2,1)S(1)}, bf16[32,384]{1,0:T(8,128)(2,1)S(1)}) custom-call(s32[4,5]{1,0:T(4,128)} %ids_ref.5, s32[1]{0:T(128)} %bitcast.1.self_ref, bf16[4,5,128,128]{3,2,1,0:T(8,128)(2,1)} %copy-done.5, bf16[4,128,128]{2,1,0:T(8,128)(2,1)} %copy-done.10, f32[8,1,768]{2,1,0:T(1,128)} %copy-done.22, f32[8,1,768]{2,1,0:T(1,128)} %copy-done.23, ...), custom_call_target="tpu_custom_call" | custom-call | flops 251658240 | bytes 3219540 | tf_op jit(solution)/shard_map/pallas_call | solution.py:45
  67.5 1.9 %shard_map.163 = (bf16[512,384]{1,0:T(8,128)(2,1)}, bf16[512,384]{1,0:T(8,128)(2,1)S(1)}) custom-call(s32[1]{0:T(128)} %bitcast.core_ref, bf16[512,384]{1,0:T(8,128)(2,1)S(1)} %bitcast.20, bf16[512,384]{1,0:T(8,128)(2,1)S(1)} %collective-permute-done.6.other_ref, bf16[384,768]{1,0:T(8,128)(2,1)S(1)} %copy-done.4, ...), custom_call_target="tpu_custom_call" | custom-call | flops 301989888 | bytes 3399684 | tf_op jit(solution)/shard_map/pallas_call | solution.py:45
  71.1 5.6 %shard_map.164 = (bf16[16,136,384]{2,1,0:T(8,128)(2,1)}, bf16[8,48,384]{2,1,0:T(8,128)(2,1)}, bf16[8,48,384]{2,1,0:T(8,128)(2,1)}, bf16[512,384]{1,0:T(8,128)(2,1)}) custom-call(s32[4,5]{1,0:T(4,128)S(1)} %copy-done.13, s32[1]{0:T(128)} %bitcast.1.self_ref, s32[1]{0:T(128)} %bitcast.core_ref, bf16[512,384]{1,0:T(8,128)(2,1)S(1)} %get-tuple-element.35.mine_ref, ...), custom_call_target="tpu_custom_call" | custom-call | flops 855638016 | bytes 5734488 | tf_op jit(solution)/shard_map/pallas_call | solution.py:45
  76.8 5.5 %all-to-all-start.2 = ((bf16[16,136,384]{2,1,0:T(8,128)(2,1)}), bf16[16,136,384]{2,1,0:T(8,128)(2,1)S(1)}, u32[]{:S(2)}, u32[]{:S(2)}) async-start(bf16[16,136,384]{2,1,0:T(8,128)(2,1)} %get-tuple-element.45), calls=%async_computation.2 | async-start | bytes 3342336 | tf_op jit(solution)/shard_map/all_to_all | solution.py:496
  82.3 1.9 %collective-permute-start.9 = (bf16[8,48,384]{2,1,0:T(8,128)(2,1)}, bf16[8,48,384]{2,1,0:T(8,128)(2,1)S(1)}, u32[]{:S(2)}, u32[]{:S(2)}) collective-permute-start(bf16[8,48,384]{2,1,0:T(8,128)(2,1)} %get-tuple-element.37), channel_id=1, source_target_pairs={{0,2},{2,0},{4,6},{6,4},{8,10},{10,8},{12,14},{14,12},{16,18},{18,... | collective-permute-start | bytes 884744 | tf_op jit(solution)/shard_map/ppermute | solution.py:493
  84.2 12.1 %collective-permute-done.9.theirs_ref = bf16[8,48,384]{2,1,0:T(8,128)(2,1)S(1)} collective-permute-done((bf16[8,48,384]{2,1,0:T(8,128)(2,1)}, bf16[8,48,384]{2,1,0:T(8,128)(2,1)S(1)}, u32[]{:S(2)}, u32[]{:S(2)}) %collective-permute-start.9) | collective-permute-done | bytes 294944 | tf_op jit(solution)/shard_map/ppermute | solution.py:493
  96.4 2.4 %collective-permute-start.10 = (bf16[4,48,384]{2,1,0:T(8,128)(2,1)S(1)}, bf16[4,48,384]{2,1,0:T(8,128)(2,1)S(1)}, u32[]{:S(2)}, u32[]{:S(2)}) collective-permute-start(bf16[4,48,384]{2,1,0:T(8,128)(2,1)S(1)} %get-tuple-element.39), channel_id=1, source_target_pairs={{0,4},{2,6},{4,0},{6,2},{8,12},{10,14},{12,8},{14,10},{16,20},{18,... | collective-permute-start | bytes 442376 | tf_op jit(solution)/shard_map/ppermute | solution.py:493
  98.8 6.0 %collective-permute-done.10.theirs_ref = bf16[4,48,384]{2,1,0:T(8,128)(2,1)S(1)} collective-permute-done((bf16[4,48,384]{2,1,0:T(8,128)(2,1)S(1)}, bf16[4,48,384]{2,1,0:T(8,128)(2,1)S(1)}, u32[]{:S(2)}, u32[]{:S(2)}) %collective-permute-start.10) | collective-permute-done | bytes 147488 | tf_op jit(solution)/shard_map/ppermute | solution.py:493
  104.9 6.5 %collective-permute-done.11.theirs_ref = bf16[2,48,384]{2,1,0:T(8,128)(2,1)S(1)} collective-permute-done((bf16[2,48,384]{2,1,0:T(8,128)(2,1)S(1)}, bf16[2,48,384]{2,1,0:T(8,128)(2,1)S(1)}, u32[]{:S(2)}, u32[]{:S(2)}) %collective-permute-start.11) | collective-permute-done | bytes 73760 | tf_op jit(solution)/shard_map/ppermute | solution.py:493
  111.4 4.5 %collective-permute-start.12 = (bf16[1,48,384]{2,1,0:T(8,128)(2,1)S(1)}, bf16[1,48,384]{2,1,0:T(8,128)(2,1)S(1)}, u32[]{:S(2)}, u32[]{:S(2)}) collective-permute-start(bf16[1,48,384]{2,1,0:T(8,128)(2,1)S(1)} %get-tuple-element.43), channel_id=1, source_target_pairs={{0,16},{2,18},{4,20},{6,22},{8,24},{10,26},{12,28},{14,30},{16,0},... | collective-permute-start | bytes 110600 | tf_op jit(solution)/shard_map/ppermute | solution.py:493
  115.9 2.4 %shard_map.169.local_hbm = f32[4,128,384]{2,1,0:T(8,128)S(1)} custom-call(s32[4,5]{1,0:T(4,128)S(1)} %copy-done.13, s32[1]{0:T(128)} %bitcast.1.self_ref, bf16[4,128,384]{2,1,0:T(8,128)(2,1)S(1)} %bitcast.18, bf16[4,5,128,128]{3,2,1,0:T(8,128)(2,1)S(1)} %copy-done.2, bf16[4,128,384]{2,1,0:T(8,128)(2,1)S(1)} %bitcast.17), custom_call_target="tpu_custom_call" | custom-call | flops 251658240 | bytes 2228308 | tf_op jit(solution)/shard_map/pallas_call | solution.py:45
  119.2 4.0 %collective-permute-done.12.theirs_ref = bf16[1,48,384]{2,1,0:T(8,128)(2,1)S(1)} collective-permute-done((bf16[1,48,384]{2,1,0:T(8,128)(2,1)S(1)}, bf16[1,48,384]{2,1,0:T(8,128)(2,1)S(1)}, u32[]{:S(2)}, u32[]{:S(2)}) %collective-permute-start.12) | collective-permute-done | bytes 36896 | tf_op jit(solution)/shard_map/ppermute | solution.py:493
  123.9 2.9 %shard_map.170 = (bf16[4,128,384]{2,1,0:T(8,128)(2,1)}, f32[2,384]{1,0:T(2,128)}) custom-call(s32[16]{0:T(128)S(1)} %slice_reduce_fusion.asked_ref, f32[4,128,384]{2,1,0:T(8,128)} %copy-done.1, bf16[16,136,384]{2,1,0:T(8,128)(2,1)S(1)} %all-to-all-done.2.got_ref), custom_call_target="tpu_custom_call" | custom-call | flops 1000 | bytes 2853952 | tf_op jit(solution)/shard_map/pallas_call | solution.py:45
  (75 shorter events, 20.6 us)
Async XLA Ops:
  20.3 40.6 %all-to-all-start.1 = ((bf16[16,128,384]{2,1,0:T(8,128)(2,1)}), bf16[16,128,384]{2,1,0:T(8,128)(2,1)S(1)}, u32[]{:S(2)}, u32[]{:S(2)}) async-start(bf16[16,128,384]{2,1,0:T(8,128)(2,1)} %shard_map.161), calls=%async_computation.1 | async-start | bytes 3145728 | tf_op jit(solution)/shard_map/all_to_all | solution.py:496
  25.7 6.3 %copy-start.14 = (f32[2,768]{1,0:T(2,128)S(1)}, f32[2,768]{1,0:T(2,128)}, u32[]{:S(2)}) copy-start(f32[2,768]{1,0:T(2,128)} %gains_ref.3) | copy-start | bytes 18436
  25.7 6.3 %copy-start.16 = (bf16[768,1536]{1,0:T(8,128)(2,1)S(1)}, bf16[768,1536]{1,0:T(8,128)(2,1)}, u32[]{:S(2)}) copy-start(bf16[768,1536]{1,0:T(8,128)(2,1)} %up_ref.1) | copy-start | bytes 7077892
  25.7 6.3 %copy-start.17 = (bf16[1536,768]{1,0:T(8,128)(2,1)S(1)}, bf16[1536,768]{1,0:T(8,128)(2,1)}, u32[]{:S(2)}) copy-start(bf16[1536,768]{1,0:T(8,128)(2,1)} %down_ref.1) | copy-start | bytes 7077892
  25.7 6.3 %copy-start.20 = (bf16[2,256,768]{2,1,0:T(8,128)(2,1)S(1)}, bf16[2,256,768]{2,1,0:T(8,128)(2,1)}, u32[]{:S(2)}) copy-start(bf16[2,256,768]{2,1,0:T(8,128)(2,1)} %param.13) | copy-start | bytes 2359300
  29.6 2.4 %collective-permute-start = (bf16[512,768]{1,0:T(8,128)(2,1)S(1)}, bf16[512,768]{1,0:T(8,128)(2,1)S(1)}, u32[]{:S(2)}, u32[]{:S(2)}) collective-permute-start(bf16[512,768]{1,0:T(8,128)(2,1)S(1)} %shard_map.158.mine_ref), channel_id=1, source_target_pairs={{0,1},{1,0},{2,3},{3,2},{4,5},{5,4},{6,7},{7,6},{8,9},{9,8},{10,11... | collective-permute-start | bytes 2359304 | tf_op jit(solution)/shard_map/ppermute | solution.py:490
  36.9 19.1 %copy-start = (bf16[512,384]{1,0:T(8,128)(2,1)S(1)}, bf16[512,384]{1,0:T(8,128)(2,1)}, u32[]{:S(2)}) copy-start(bf16[512,384]{1,0:T(8,128)(2,1)} %param.20) | copy-start | bytes 1179652
  36.9 19.1 %copy-start.2 = (bf16[4,5,128,128]{3,2,1,0:T(8,128)(2,1)S(1)}, bf16[4,5,128,128]{3,2,1,0:T(8,128)(2,1)}, u32[]{:S(2)}) copy-start(bf16[4,5,128,128]{3,2,1,0:T(8,128)(2,1)} %adj_ref.5) | copy-start | bytes 1966084
  36.9 19.1 %copy-start.12 = (s32[4,5]{1,0:T(4,128)S(1)}, s32[4,5]{1,0:T(4,128)}, u32[]{:S(2)}) copy-start(s32[4,5]{1,0:T(4,128)} %ids_ref.5) | copy-start | bytes 244
  36.9 2.6 %collective-permute-start.1 = (bf16[512,768]{1,0:T(8,128)(2,1)}, bf16[512,768]{1,0:T(8,128)(2,1)}, u32[]{:S(2)}, u32[]{:S(2)}) collective-permute-start(bf16[512,768]{1,0:T(8,128)(2,1)} %get-tuple-element.29.mine_ref), channel_id=1, source_target_pairs={{0,1},{1,0},{2,3},{3,2},{4,5},{5,4},{6,7},{7,6},{8,9},{9,8},{10,11... | collective-permute-start | bytes 2359304 | tf_op jit(solution)/shard_map/ppermute | solution.py:490
  41.6 3.9 %collective-permute-start.2 = (f32[1,1,768]{2,1,0:T(1,128)S(1)}, f32[1,1,768]{2,1,0:T(1,128)S(1)}, u32[]{:S(2)}, u32[]{:S(2)}) collective-permute-start(f32[1,1,768]{2,1,0:T(1,128)S(1)} %shard_map.160), channel_id=1, source_target_pairs={{0,2},{2,0},{4,6},{6,4},{8,10},{10,8},{12,14},{14,12},{16,18},{18,... | collective-permute-start | bytes 9224 | tf_op jit(solution)/shard_map/ppermute | solution.py:493
  45.6 3.7 %collective-permute-start.3 = (f32[2,1,768]{2,1,0:T(1,128)S(1)}, f32[2,1,768]{2,1,0:T(1,128)S(1)}, u32[]{:S(2)}, u32[]{:S(2)}) collective-permute-start(f32[2,1,768]{2,1,0:T(1,128)S(1)} %pad_maximum_fusion.2), channel_id=1, source_target_pairs={{0,4},{2,6},{4,0},{6,2},{8,12},{10,14},{12,8},{14,10},{16,20},{18,... | collective-permute-start | bytes 18440 | tf_op jit(solution)/shard_map/ppermute | solution.py:493
  49.3 5.6 %collective-permute-start.4 = (f32[4,1,768]{2,1,0:T(1,128)S(1)}, f32[4,1,768]{2,1,0:T(1,128)S(1)}, u32[]{:S(2)}, u32[]{:S(2)}) collective-permute-start(f32[4,1,768]{2,1,0:T(1,128)S(1)} %pad_maximum_fusion.1), channel_id=1, source_target_pairs={{0,8},{2,10},{4,12},{6,14},{8,0},{10,2},{12,4},{14,6},{16,24},{18,... | collective-permute-start | bytes 36872 | tf_op jit(solution)/shard_map/ppermute | solution.py:493
  54.9 6.0 %collective-permute-start.5 = (f32[8,1,768]{2,1,0:T(1,128)S(1)}, f32[8,1,768]{2,1,0:T(1,128)S(1)}, u32[]{:S(2)}, u32[]{:S(2)}) collective-permute-start(f32[8,1,768]{2,1,0:T(1,128)S(1)} %pad_maximum_fusion.near_hbm), channel_id=1, source_target_pairs={{0,16},{2,18},{4,20},{6,22},{8,24},{10,26},{12,28},{14,30},{16,0},... | collective-permute-start | bytes 73736 | tf_op jit(solution)/shard_map/ppermute | solution.py:493
  65.3 2.2 %collective-permute-start.6 = (bf16[512,384]{1,0:T(8,128)(2,1)S(1)}, bf16[512,384]{1,0:T(8,128)(2,1)S(1)}, u32[]{:S(2)}, u32[]{:S(2)}) collective-permute-start(bf16[512,384]{1,0:T(8,128)(2,1)S(1)} %bitcast.19), channel_id=1, source_target_pairs={{0,1},{1,0},{2,3},{3,2},{4,5},{5,4},{6,7},{7,6},{8,9},{9,8},{10,11... | collective-permute-start | bytes 1179656 | tf_op jit(solution)/shard_map/ppermute | solution.py:490
  65.4 2.1 %collective-permute-start.7 = (bf16[384,384]{1,0:T(8,128)(2,1)S(1)}, bf16[384,384]{1,0:T(8,128)(2,1)S(1)}, u32[]{:S(2)}, u32[]{:S(2)}) collective-permute-start(bf16[384,384]{1,0:T(8,128)(2,1)S(1)} %constant_dynamic-slice_fusion), channel_id=1, source_target_pairs={{0,1},{1,0},{2,3},{3,2},{4,5},{5,4},{6,7},{7,6},{8,9},{9,8},{10,11... | collective-permute-start | bytes 884744 | tf_op jit(solution)/shard_map/ppermute | solution.py:490
  69.4 1.7 %collective-permute-start.8 = (bf16[512,384]{1,0:T(8,128)(2,1)S(1)}, bf16[512,384]{1,0:T(8,128)(2,1)S(1)}, u32[]{:S(2)}, u32[]{:S(2)}) collective-permute-start(bf16[512,384]{1,0:T(8,128)(2,1)S(1)} %get-tuple-element.35.mine_ref), channel_id=1, source_target_pairs={{0,1},{1,0},{2,3},{3,2},{4,5},{5,4},{6,7},{7,6},{8,9},{9,8},{10,11... | collective-permute-start | bytes 1179656 | tf_op jit(solution)/shard_map/ppermute | solution.py:490
  76.8 19.6 %copy-start.9 = (bf16[8,48,384]{2,1,0:T(8,128)(2,1)S(1)}, bf16[8,48,384]{2,1,0:T(8,128)(2,1)}, u32[]{:S(2)}) copy-start(bf16[8,48,384]{2,1,0:T(8,128)(2,1)} %get-tuple-element.36.mine_ref) | copy-start | bytes 884740
  76.8 39.1 %copy-start.6 = (bf16[512,384]{1,0:T(8,128)(2,1)S(1)}, bf16[512,384]{1,0:T(8,128)(2,1)}, u32[]{:S(2)}) copy-start(bf16[512,384]{1,0:T(8,128)(2,1)} %get-tuple-element.44) | copy-start | bytes 1179652
  76.8 47.1 %all-to-all-start.2 = ((bf16[16,136,384]{2,1,0:T(8,128)(2,1)}), bf16[16,136,384]{2,1,0:T(8,128)(2,1)S(1)}, u32[]{:S(2)}, u32[]{:S(2)}) async-start(bf16[16,136,384]{2,1,0:T(8,128)(2,1)} %get-tuple-element.45), calls=%async_computation.2 | async-start | bytes 3342336 | tf_op jit(solution)/shard_map/all_to_all | solution.py:496
  82.3 14.1 %collective-permute-start.9 = (bf16[8,48,384]{2,1,0:T(8,128)(2,1)}, bf16[8,48,384]{2,1,0:T(8,128)(2,1)S(1)}, u32[]{:S(2)}, u32[]{:S(2)}) collective-permute-start(bf16[8,48,384]{2,1,0:T(8,128)(2,1)} %get-tuple-element.37), channel_id=1, source_target_pairs={{0,2},{2,0},{4,6},{6,4},{8,10},{10,8},{12,14},{14,12},{16,18},{18,... | collective-permute-start | bytes 884744 | tf_op jit(solution)/shard_map/ppermute | solution.py:493
  96.4 8.4 %collective-permute-start.10 = (bf16[4,48,384]{2,1,0:T(8,128)(2,1)S(1)}, bf16[4,48,384]{2,1,0:T(8,128)(2,1)S(1)}, u32[]{:S(2)}, u32[]{:S(2)}) collective-permute-start(bf16[4,48,384]{2,1,0:T(8,128)(2,1)S(1)} %get-tuple-element.39), channel_id=1, source_target_pairs={{0,4},{2,6},{4,0},{6,2},{8,12},{10,14},{12,8},{14,10},{16,20},{18,... | collective-permute-start | bytes 442376 | tf_op jit(solution)/shard_map/ppermute | solution.py:493
  104.8 6.6 %collective-permute-start.11 = (bf16[2,48,384]{2,1,0:T(8,128)(2,1)S(1)}, bf16[2,48,384]{2,1,0:T(8,128)(2,1)S(1)}, u32[]{:S(2)}, u32[]{:S(2)}) collective-permute-start(bf16[2,48,384]{2,1,0:T(8,128)(2,1)S(1)} %get-tuple-element.41), channel_id=1, source_target_pairs={{0,8},{2,10},{4,12},{6,14},{8,0},{10,2},{12,4},{14,6},{16,24},{18,... | collective-permute-start | bytes 221192 | tf_op jit(solution)/shard_map/ppermute | solution.py:493
  111.4 11.8 %collective-permute-start.12 = (bf16[1,48,384]{2,1,0:T(8,128)(2,1)S(1)}, bf16[1,48,384]{2,1,0:T(8,128)(2,1)S(1)}, u32[]{:S(2)}, u32[]{:S(2)}) collective-permute-start(bf16[1,48,384]{2,1,0:T(8,128)(2,1)S(1)} %get-tuple-element.43), channel_id=1, source_target_pairs={{0,16},{2,18},{4,20},{6,22},{8,24},{10,26},{12,28},{14,30},{16,0},... | collective-permute-start | bytes 110600 | tf_op jit(solution)/shard_map/ppermute | solution.py:493
  (15 other events, 52.5 us)

commit v4 on v3

--- a/solution.py
+++ b/solution.py
@@ -84,23 +84,34 @@
     return safe, owner, safe - owner * tiles_here
 
 
+def side_of(owner, me, peers):
+    half = lax.div(owner, jnp.int32(peers))
+    mine = lax.div(me, jnp.int32(peers))
+    return jnp.where(half == mine, 0, 1), owner - half * peers
+
+
 def index_body(texts_here, ids_hbm, self_ref, text_hbm, out_ref, ids_ref, text_ref, sems):
     for copy in copies([(ids_hbm, ids_ref), (text_hbm, text_ref)], sems):
         copy.wait()
     tiles_here, entries = ids_ref.shape
-    shards, _, lanes = out_ref.shape
-    width = lanes - LANES
+    peers, _, lanes = out_ref.shape
+    shards = 2 * peers
+    width = lanes - 2 * LANES
     texts = texts_here * shards
     me = self_ref[0]
-    row = lax.broadcasted_iota(jnp.int32, (shards, LANES), 0)
-    wanted = jnp.full((shards, LANES), -1, jnp.int32)
+    row = lax.broadcasted_iota(jnp.int32, (peers, LANES), 0)
+    near = jnp.full((peers, LANES), -1, jnp.int32)
+    far = near
     for r in range(tiles_here):
         for k in range(entries):
             tile_id = ids_ref[r, k]
             _, owner, place = tile_of(tile_id, tiles_here)
-            target = jnp.where((tile_id >= 0) & (owner != me), owner, -1)
-            wanted = jnp.where(row == target, place, wanted)
-    out_ref[:, :, width:] = wanted.reshape(shards, 1, LANES)
+            side, spot = side_of(owner, me, peers)
+            wanted = (tile_id >= 0) & (owner != me)
+            near = jnp.where(row == jnp.where(wanted & (side == 0), spot, -1), place, near)
+            far = jnp.where(row == jnp.where(wanted & (side == 1), spot, -1), place, far)
+    out_ref[:, :, width : width + LANES] = near.reshape(peers, 1, LANES)
+    out_ref[:, :, width + LANES :] = far.reshape(peers, 1, LANES)
     tile_rows = text_ref.shape[1]
     lane = lax.broadcasted_iota(jnp.int32, (LANES, tile_rows), 1)
     sub = lax.broadcasted_iota(jnp.int32, (LANES, LANES), 0)
@@ -116,32 +127,34 @@
         column = jnp.max(best.astype(jnp.float32), axis=1, keepdims=True)
         line = jnp.max(jnp.where(diagonal, column, float(NO_NODE)), axis=0, keepdims=True)
         out_ref[:, :, c * LANES : (c + 1) * LANES] = (
-            jnp.broadcast_to(line, (shards, LANES)).astype(jnp.int32).reshape(shards, 1, LANES)
+            jnp.broadcast_to(line, (peers, LANES)).astype(jnp.int32).reshape(peers, 1, LANES)
         )
 
 
-def pack_body(asked_ref, cache_hbm, out_hbm, tile_ref, in_sems, out_sems):
-    tiles_here = tile_ref.shape[0]
-    for copy in copies([(cache_hbm.at[j], tile_ref.at[j]) for j in range(tiles_here)], in_sems):
-        copy.wait()
-
-    def slot(q):
-        place = jnp.maximum(asked_ref[q], 0)
-        return pltpu.make_async_copy(tile_ref.at[place], out_hbm.at[q], out_sems.at[q])
-
-    shards = out_hbm.shape[0]
-    lax.fori_loop(0, shards, lambda q, c: (slot(q).start(), c)[1], 0)
-    lax.fori_loop(0, shards, lambda q, c: (slot(q).wait(), c)[1], 0)
-
-
-def mask_body(ids_ref, self_ref, got_ref, adj_ref, cache_ref, kept_ref, pick_ref, own_ref, base_ref):
+def pack_body(asked_ref, cache_hbm, mate_hbm, out_hbm, tile_ref, in_sems, out_sems):
+    _, _, tile_rows, _ = tile_ref.shape
+    started = copies([(cache_hbm, tile_ref.at[0]), (mate_hbm, tile_ref.at[1])], in_sems)
+    peers = out_hbm.shape[0]
+
+    def slot(p, side):
+        place = jnp.maximum(asked_ref[p, side], 0)
+        target = out_hbm.at[p, pl.ds(side * tile_rows, tile_rows), :]
+        return pltpu.make_async_copy(tile_ref.at[side, place], target, out_sems.at[side, p])
+
+    for side in range(2):
+        started[side].wait()
+        lax.fori_loop(0, peers, lambda p, c: (slot(p, side).start(), c)[1], 0)
+    for side in range(2):
+        lax.fori_loop(0, peers, lambda p, c: (slot(p, side).wait(), c)[1], 0)
+
+
+def mask_body(ids_ref, self_ref, got_ref, mate_ref, adj_ref, cache_ref, kept_ref, pick_ref, own_ref, base_ref):
     tiles_here, entries, tile_rows, _ = adj_ref.shape
-    shards, _, lanes = got_ref.shape
-    width = lanes - LANES
+    peers, _, lanes = got_ref.shape
+    width = lanes - 2 * LANES
     me = self_ref[0]
-    table = jnp.max(
-        got_ref[:, :, :width].reshape(shards, width).astype(jnp.float32), axis=0, keepdims=True
-    )
+    both = jnp.maximum(got_ref[:, :, :width], mate_ref[:, :, :width])
+    table = jnp.max(both.reshape(peers, width).astype(jnp.float32), axis=0, keepdims=True)
     place = lax.broadcasted_iota(jnp.int32, (tile_rows, width), 0).astype(jnp.float32)
     ones = jnp.ones((ROWS, width), jnp.bfloat16)
 
@@ -267,7 +280,7 @@
         ],
         sems,
     )
-    tiles_here, entries, _, _ = kept_ref.shape
+    tiles_here, entries, tile_rows, _ = kept_ref.shape
     half = cache_ref.shape[2]
     me = self_ref[0]
     for copy in started:
@@ -287,7 +300,9 @@
 
         @pl.when(jnp.logical_not(local))
         def _():
-            source_ref[r % 2, k] = remote_ref[owner]
+            side, spot = side_of(owner, me, remote_ref.shape[0])
+            first = pl.multiple_of(side * tile_rows, tile_rows)
+            source_ref[r % 2, k] = remote_ref[spot, pl.ds(first, tile_rows), :]
 
     for r in range(tiles_here):
         lax.fori_loop(
@@ -316,14 +331,40 @@
     )
 
 
+def weight_body(
+    per, self_ref, core_ref, mine_ref, other_ref, agg_ref, keep_hbm, give_hbm, w_ref, half_ref, sems
+):
+    shards, deep, half = half_ref.shape
+    kept = shards // 2
+    me = self_ref[0]
+    own = pl.multiple_of(core_ref[0] * half, LANES)
+    far = pl.multiple_of((1 - core_ref[0]) * half, LANES)
+    columns = 2 * half
+    w_ref[pl.ds(own, half), :] = mm(mine_ref[...], agg_ref[...], (0, 0))
+    w_ref[pl.ds(far, half), :] = mm(other_ref[...], agg_ref[...], (0, 0))
+    w_ref[columns:, :] = jnp.zeros((w_ref.shape[0] - columns, half), jnp.float32)
+    for q in range(shards):
+        step = q ^ me
+        turned = step * 0
+        reach = 1
+        while reach < shards:
+            turned = 2 * turned + ((step // reach) & 1)
+            reach *= 2
+        half_ref[turned] = w_ref[q * per : q * per + deep, :].astype(jnp.bfloat16)
+    ends = copies(
+        [(half_ref.at[pl.ds(kept, kept)], give_hbm), (half_ref.at[pl.ds(0, kept)], keep_hbm)], sems
+    )
+    for copy in ends:
+        copy.wait()
+
+
 def backward_body(
-    per, texts_here, ids_ref, self_ref, core_ref, mine_ref, other_ref, agg_ref, w_own_ref, adj_ref,
-    pick_ref, own_ref, grad_ref, send_hbm, keep_hbm, give_hbm, down_hbm,
-    down_ref, w_ref, text_ref, send_ref, rows_ref, half_ref, sems, slot_sems, row_sems
+    texts_here, ids_ref, self_ref, core_ref, mine_ref, other_ref, w_own_ref, adj_ref,
+    pick_ref, own_ref, grad_ref, send_hbm, down_hbm,
+    down_ref, text_ref, send_ref, rows_ref, sems, slot_sems
 ):
     tiles_here, entries, tile_rows, _ = adj_ref.shape
     shards, text_rows, half = rows_ref.shape
-    kept = shards // 2
     me = self_ref[0]
     core = core_ref[0]
     own = pl.multiple_of(core * half, LANES)
@@ -334,30 +375,20 @@
     down_ref[...] = down.astype(jnp.bfloat16)
     down_copy = pltpu.make_async_copy(down_ref, down_hbm, sems.at[0])
     down_copy.start()
-
-    def remote(r, k):
-        tile_id = ids_ref[r, k]
-        _, owner, _ = tile_of(tile_id, tiles_here)
-        slot = pltpu.make_async_copy(
-            send_ref.at[owner], send_hbm.at[owner, pl.ds(0, tile_rows), :], slot_sems.at[owner]
-        )
-        return (tile_id >= 0) & (owner != me), owner, slot
-
     for r in range(tiles_here):
         rows = slice(r * tile_rows, (r + 1) * tile_rows)
-
-        def give_one(k, carry):
-            away, owner, slot = remote(r, k)
-
-            @pl.when(away)
-            def _():
-                send_ref[owner] = mm(adj_ref[r, k], down_ref[rows, :], (0, 0)).astype(jnp.bfloat16)
-                slot.start()
-
-            return carry
-
-        lax.fori_loop(0, entries, give_one, 0, unroll=unroll(entries))
-
+        for first in range(0, entries, 6):
+            group = range(first, min(first + 6, entries))
+            side_by_side = jnp.concatenate([adj_ref[r, k] for k in group], axis=1)
+            product = mm(side_by_side, down_ref[rows, :], (0, 0)).astype(jnp.bfloat16)
+            for k in group:
+                tile_id = ids_ref[r, k]
+                _, owner, _ = tile_of(tile_id, tiles_here)
+                slot = jnp.where((tile_id >= 0) & (owner != me), owner, shards)
+                send_ref[slot] = product[(k - first) * tile_rows : (k - first + 1) * tile_rows]
+    slots = copies(
+        [(send_ref.at[q], send_hbm.at[q, pl.ds(0, tile_rows), :]) for q in range(shards)], slot_sems
+    )
     text_ref[...] = mm(pick_ref[...], down_ref[...], (0, 0)) + mm(
         own_ref[...], grad_ref[...], (0, 0)
     )
@@ -371,44 +402,13 @@
             block = jnp.where(row == text_rows // 2 + i, line - high, block)
         rows_ref[q] = block.astype(jnp.bfloat16)
     row_copy = pltpu.make_async_copy(
-        rows_ref, send_hbm.at[:, pl.ds(tile_rows, text_rows), :], row_sems.at[0]
+        rows_ref, send_hbm.at[:, pl.ds(tile_rows, text_rows), :], sems.at[1]
     )
     row_copy.start()
-
-    columns = 2 * half
-    w_ref[pl.ds(own, half), :] = mm(mine_ref[...], agg_ref[...], (0, 0))
-    w_ref[pl.ds(far, half), :] = mm(other_ref[...], agg_ref[...], (0, 0))
-    w_ref[columns:, :] = jnp.zeros((w_ref.shape[0] - columns, half), jnp.float32)
-    deep = half_ref.shape[1]
-    for q in range(shards):
-        step = q ^ me
-        turned = step * 0
-        reach = 1
-        while reach < shards:
-            turned = 2 * turned + ((step // reach) & 1)
-            reach *= 2
-        half_ref[turned] = w_ref[q * per : q * per + deep, :].astype(jnp.bfloat16)
-    ends = copies(
-        [(half_ref.at[pl.ds(kept, kept)], give_hbm), (half_ref.at[pl.ds(0, kept)], keep_hbm)],
-        sems.at[pl.ds(1, 2)],
-    )
-
-    for r in range(tiles_here):
-
-        def wait_one(k, carry):
-            away, _, slot = remote(r, k)
-
-            @pl.when(away)
-            def _():
-                slot.wait()
-
-            return carry
-
-        lax.fori_loop(0, entries, wait_one, 0)
+    for copy in slots:
+        copy.wait()
     down_copy.wait()
     row_copy.wait()
-    for copy in ends:
-        copy.wait()
 
 
 def fold_body(mine_ref, theirs_ref, keep_ref, give_ref):
@@ -441,7 +441,9 @@
         lax.fori_loop(0, entries, one, 0, unroll=unroll(entries))
 
 
-def finish_body(asked_ref, local_hbm, got_ref, node_ref, text_ref, sum_ref, sems):
+def finish_body(
+    self_ref, asked_ref, mate_ref, local_hbm, got_ref, node_ref, text_ref, sum_ref, sems
+):
     local = pltpu.make_async_copy(local_hbm, sum_ref, sems.at[0])
     local.start()
     _, tile_rows, half = sum_ref.shape
@@ -454,8 +456,11 @@
     ]
     local.wait()
 
+    me = self_ref[0]
+
     def one(q, carry):
-        asked = asked_ref[q]
+        side, spot = side_of(q, me, shards // 2)
+        asked = jnp.where(side == 0, asked_ref[spot, 0], mate_ref[spot, 1])
 
         @pl.when(asked >= 0)
         def _():
@@ -492,12 +497,20 @@
     def toward(values, reach):
         return lax.ppermute(values, "graph", [(i, i ^ reach) for i in range(shards)])
 
-    def spread(values):
-        return lax.all_to_all(values, "graph", split_axis=0, concat_axis=0, tiled=True)
-
+    peers = shards // 2
+
+    def spread(values, groups=None):
+        return lax.all_to_all(
+            values, "graph", split_axis=0, concat_axis=0, tiled=True, axis_index_groups=groups
+        )
+
+    halves_of = [list(range(peers)), list(range(peers, shards))]
+
+    cache_tiles = cache.reshape(tiles_here, tile_rows, half)
+    mate_tiles = toward(cache_tiles, peers)
     index = call(
         functools.partial(index_body, texts_here),
-        [shape((shards, 1, slots + LANES), jnp.int32)],
+        [shape((peers, 1, slots + 2 * LANES), jnp.int32)],
         [adj_tiles, me, node_text.reshape(tiles_here, tile_rows)],
         [HBM, SMEM, HBM],
         flops=1000,
@@ -507,23 +520,27 @@
             pltpu.SemaphoreType.DMA((2,)),
         ],
     )
-    got = spread(index)
-    asked = got[:, 0, slots]
-    cache_tiles = cache.reshape(tiles_here, tile_rows, half)
+    got = spread(index, halves_of)
+    mate_got = toward(got, peers)
+
+    def places(table):
+        return table[:, 0, slots:].reshape(peers, 2, LANES)[:, :, 0]
+
+    asked = places(got)
     packed = call(
         pack_body,
-        [shape((shards, tile_rows, half))],
-        [asked, cache_tiles],
-        [SMEM, HBM],
+        [shape((peers, 2 * tile_rows, half))],
+        [asked, cache_tiles, mate_tiles],
+        [SMEM, HBM, HBM],
         flops=1000,
         scratch=[
-            pltpu.VMEM(cache_tiles.shape, jnp.bfloat16),
-            pltpu.SemaphoreType.DMA((tiles_here,)),
-            pltpu.SemaphoreType.DMA((shards,)),
+            pltpu.VMEM((2,) + cache_tiles.shape, jnp.bfloat16),
+            pltpu.SemaphoreType.DMA((2,)),
+            pltpu.SemaphoreType.DMA((2, peers)),
         ],
         out_specs=[HBM],
     )
-    remote = spread(packed)
+    remote = spread(packed, halves_of)
 
     w_other = swap(lax.dynamic_slice_in_dim(w_gnn, (1 - core_at) * half, half, 1))
 
@@ -568,8 +585,8 @@
             shape((tiles_here, tile_rows, slots)),
             shape(cache_tiles.shape),
         ],
-        [adj_tiles, me, got, adj_values, cache_tiles],
-        [SMEM, SMEM, VMEM, VMEM, VMEM],
+        [adj_tiles, me, got, mate_got, adj_values, cache_tiles],
+        [SMEM, SMEM, VMEM, VMEM, VMEM, VMEM],
         flops=2 * adj_values.size * slots,
     )
     gathered, pooled = call(
@@ -604,32 +621,38 @@
     slope_other = swap(slope)
     text_rows = up_to(2 * texts_here, 8)
     halves = (shards // 2, deep, half)
-    send, keep, give, down = call(
-        functools.partial(backward_body, per, texts_here),
+    keep, give = call(
+        functools.partial(weight_body, per),
+        [shape(halves), shape(halves)],
+        [me, core, slope, slope_other, gathered],
+        [SMEM, SMEM] + [VMEM] * 3,
+        flops=4 * nodes_here * half * half,
+        scratch=[
+            pltpu.VMEM((width + ROWS, half), jnp.float32),
+            pltpu.VMEM((shards, deep, half), jnp.bfloat16),
+            pltpu.SemaphoreType.DMA((2,)),
+        ],
+        out_specs=[HBM] * 2,
+    )
+    given = toward(give, 1)
+    send, down = call(
+        functools.partial(backward_body, texts_here),
+        [shape((shards, tile_rows + text_rows, half)), shape((nodes_here, half))],
         [
-            shape((shards, tile_rows + text_rows, half)),
-            shape(halves),
-            shape(halves),
-            shape((nodes_here, half)),
-        ],
-        [
-            adj_tiles, me, core, slope, slope_other, gathered, w_gnn, adj_values,
+            adj_tiles, me, core, slope, slope_other, w_gnn, adj_values,
             pick.reshape(nodes_here, slots), own.reshape(nodes_here, slots), out_grad,
         ],
-        [SMEM, SMEM, SMEM] + [VMEM] * 8,
-        flops=8 * nodes_here * half * half + 2 * adj_values.size * half,
+        [SMEM, SMEM, SMEM] + [VMEM] * 7,
+        flops=4 * nodes_here * half * half + 2 * adj_values.size * half,
         scratch=[
             pltpu.VMEM((nodes_here, half), jnp.bfloat16),
-            pltpu.VMEM((width + ROWS, half), jnp.float32),
             pltpu.VMEM((slots, half), jnp.float32),
-            pltpu.VMEM((shards, tile_rows, half), jnp.bfloat16),
+            pltpu.VMEM((shards + 1, tile_rows, half), jnp.bfloat16),
             pltpu.VMEM((shards, text_rows, half), jnp.bfloat16),
-            pltpu.VMEM((shards, deep, half), jnp.bfloat16),
-            pltpu.SemaphoreType.DMA((3,)),
+            pltpu.SemaphoreType.DMA((2,)),
             pltpu.SemaphoreType.DMA((shards,)),
-            pltpu.SemaphoreType.DMA((1,)),
-        ],
-        out_specs=[HBM] * 4,
+        ],
+        out_specs=[HBM] * 2,
     )
     returned = spread(send)
     local = call(
@@ -640,7 +663,6 @@
         flops=2 * adj_values.size * half,
     )
     reach = 1
-    given = toward(give, reach)
     while 2 * reach < shards:
         part = (shards // (4 * reach), deep, half)
         keep, give = call(
@@ -658,8 +680,8 @@
     node_grad, text_grad = call(
         finish_body,
         [shape((tiles_here, tile_rows, half)), shape((texts_here, half), jnp.float32)],
-        [asked, local, returned],
-        [SMEM, HBM, VMEM],
+        [me, asked, places(mate_got), local, returned],
+        [SMEM, SMEM, SMEM, HBM, VMEM],
         flops=1000,
         scratch=[
             pltpu.VMEM((tiles_here, tile_rows, half), jnp.float32),

time: 127 us -> 138 us (1.087)
  local copies, waits for them, and re-layouts: 5.67 us -> 13.4 us
  starting transfers between devices: 25.6 us -> 33.2 us
  blocking collectives: 15.5 us -> 10.1 us
    unnamed x48 -> x66, local copies, waits for them, and re-layouts: 5.25 us -> 13.2 us
    ppermute x8 -> x10, starting transfers between devices: 15.3 us -> 22.7 us  [toward(): lax.ppermute(values, 'graph', [(i, i ^ reach) for i in range(shards)])]
    all_to_all x1, blocking collectives: 15.5 us -> 10.1 us  [spread(): lax.all_to_all(values, 'graph', split_axis=0, concat_axis=0, tiled=True,...]
    ppermute x8 -> x10, waiting for transfers between devices: 37.9 us -> 38.7 us  [toward(): lax.ppermute(values, 'graph', [(i, i ^ reach) for i in range(shards)])]
    pallas_call x15 -> x16, Pallas kernels: 33.3 us -> 33.1 us  [call(): pl.pallas_call(body, out_shape=tuple(outs) if many else outs[0], in_specs...]
  transfers between devices with their start and end apart: 15 -> 17, of which waited for: 12 -> 13; matrix products, arithmetic and copies ran while one was open for 0% -> 0% of each run, Pallas kernels for 12% -> 13%
where the time goes in v4:
time: 138 us
  waiting for transfers between devices  46.6 us (34%)
  starting transfers between devices  33.2 us (24%)
  Pallas kernels  33.1 us (24%)
  local copies, waits for them, and re-layouts  13.4 us (10%)
  blocking collectives  10.1 us (7%)
    ppermute x10, waiting for transfers between devices, toward(): lax.ppermute(values, 'graph', [(i, i ^ reach) for i in range(shards)])  38.7 us
    pallas_call x16, Pallas kernels, call(): pl.pallas_call(body, out_shape=tuple(outs) if many else outs[0], in_specs...  33.1 us
    ppermute x10, starting transfers between devices, toward(): lax.ppermute(values, 'graph', [(i, i ^ reach) for i in range(shards)])  22.7 us
    unnamed x66, local copies, waits for them, and re-layouts  13.2 us
    all_to_all x1, blocking collectives, spread(): lax.all_to_all(values, 'graph', split_axis=0, concat_axis=0, tiled=True,...  10.1 us
    all_to_all x2, starting transfers between devices, spread(): lax.all_to_all(values, 'graph', split_axis=0, concat_axis=0, tiled=True,...  9.5 us
    ppermute x5, waiting for transfers between devices, swap(): lax.ppermute(values, 'mp', [(i, cores - 1 - i) for i in range(cores)])  7.9 us
  transfers between devices with their start and end apart: 17, of which 13 were waited for; matrix products, arithmetic and copies ran while one was open for 0% of the time, Pallas kernels for 13%

profile of v4, /device:TPU:0, one launch (start us, length us, event | category | flops | bytes accessed | tf_op | source)
XLA Modules:
  0.0 137.6 jit_solution(11577934289412460652)
XLA Ops:
  0.6 4.1 %collective-permute-start.7 = (bf16[4,128,384]{2,1,0:T(8,128)(2,1)}, bf16[4,128,384]{2,1,0:T(8,128)(2,1)S(1)}, u32[]{:S(2)}, u32[]{:S(2)}) collective-permute-start(bf16[4,128,384]{2,1,0:T(8,128)(2,1)} %bitcast.20), channel_id=1, source_target_pairs={{0,16},{2,18},{4,20},{6,22},{8,24},{10,26},{12,28},{14,30},{16,0},... | collective-permute-start | bytes 1179656 | tf_op jit(solution)/shard_map/ppermute | solution.py:498
  5.7 10.1 %all_to_all.15.got_ref = s32[8,1,384]{2,1,0:T(1,128)S(1)} all-to-all(s32[8,1,384]{2,1,0:T(1,128)S(1)} %shard_map.156), channel_id=1, replica_groups={{0,2,4,6,8,10,12,14},{16,18,20,22,24,26,28,30},{1,3,5,7,9,11,13,15},{17..., dimensions={0} | all-to-all | bytes 24576 | tf_op jit(solution)/shard_map/all_to_all | solution.py:503
  16.0 6.5 %collective-permute-done.7.mate_hbm = bf16[4,128,384]{2,1,0:T(8,128)(2,1)S(1)} collective-permute-done((bf16[4,128,384]{2,1,0:T(8,128)(2,1)}, bf16[4,128,384]{2,1,0:T(8,128)(2,1)S(1)}, u32[]{:S(2)}, u32[]{:S(2)}) %collective-permute-start.7) | collective-permute-done | bytes 393248 | tf_op jit(solution)/shard_map/ppermute | solution.py:498
  23.3 2.9 %shard_map.161 = bf16[8,256,384]{2,1,0:T(8,128)(2,1)} custom-call(s32[8,2]{1,0:T(8,128)S(1)} %copy.18.asked_ref, bf16[4,128,384]{2,1,0:T(8,128)(2,1)} %bitcast.21, bf16[4,128,384]{2,1,0:T(8,128)(2,1)} %copy-done.29), custom_call_target="tpu_custom_call" | custom-call | flops 1000 | bytes 2359360 | tf_op jit(solution)/shard_map/pallas_call | solution.py:45
  26.2 4.1 %all-to-all-start.1 = ((bf16[8,256,384]{2,1,0:T(8,128)(2,1)}), bf16[8,256,384]{2,1,0:T(8,128)(2,1)S(1)}, u32[]{:S(2)}, u32[]{:S(2)}) async-start(bf16[8,256,384]{2,1,0:T(8,128)(2,1)} %shard_map.161), calls=%async_computation.1 | async-start | bytes 3145728 | tf_op jit(solution)/shard_map/all_to_all | solution.py:503
  32.9 4.0 %shard_map.158.mine_ref = bf16[512,768]{1,0:T(8,128)(2,1)S(1)} custom-call(s32[1,2]{1,0:T(1,128)S(1)} %copy-done.23, bf16[512,768]{1,0:T(8,128)(2,1)S(1)} %bitcast.34, bf16[3,768,384]{2,1,0:T(8,128)(2,1)S(1)} %bitcast.33, bf16[384,768]{1,0:T(8,128)(2,1)S(1)} %copy-done.28), custom_call_target="tpu_custom_call" | custom-call | flops 1610612736 | bytes 3932168 | tf_op jit(solution)/shard_map/pallas_call | solution.py:45
  37.0 2.3 %collective-permute-done.1.other_ref = bf16[512,768]{1,0:T(8,128)(2,1)S(1)} collective-permute-done((bf16[512,768]{1,0:T(8,128)(2,1)S(1)}, bf16[512,768]{1,0:T(8,128)(2,1)S(1)}, u32[]{:S(2)}, u32[]{:S(2)}) %collective-permute-start.1) | collective-permute-done | bytes 786464 | tf_op jit(solution)/shard_map/ppermute | solution.py:495
  39.3 4.9 %shard_map.159 = (bf16[512,768]{1,0:T(8,128)(2,1)S(1)}, bf16[512,768]{1,0:T(8,128)(2,1)}) custom-call(bf16[512,768]{1,0:T(8,128)(2,1)S(1)} %bitcast.35, bf16[512,768]{1,0:T(8,128)(2,1)S(1)} %shard_map.158.mine_ref, bf16[512,768]{1,0:T(8,128)(2,1)S(1)} %collective-permute-done.1.other_ref, bf16[768,1536]{1,0:T(8,128)(2,1)S(1)} %copy-done.24, ...), custom_call_target="tpu_custom_call" | custom-call | flops 2415919104 | bytes 8656896 | tf_op jit(solution)/shard_map/pallas_call | solution.py:45
  45.1 2.5 %collective-permute-done.2.other_ref = bf16[512,768]{1,0:T(8,128)(2,1)} collective-permute-done((bf16[512,768]{1,0:T(8,128)(2,1)}, bf16[512,768]{1,0:T(8,128)(2,1)}, u32[]{:S(2)}, u32[]{:S(2)}) %collective-permute-start.2) | collective-permute-done | bytes 786464 | tf_op jit(solution)/shard_map/ppermute | solution.py:495
  48.8 2.2 %shard_map.160 = f32[1,1,768]{2,1,0:T(1,128)S(1)} custom-call(s32[1,2]{1,0:T(1,128)S(1)} %copy-done.23, s32[1]{0:T(128)} %bitcast.core_ref, bf16[512,768]{1,0:T(8,128)(2,1)S(1)} %copy-done.12, bf16[512,768]{1,0:T(8,128)(2,1)} %get-tuple-element.29.mine_ref, bf16[512,768]{1,0:T(8,128)(2,1)} %collective-permute-done.2.other_ref, f32[2,768]{1,0:T(2,128)S(1)} %copy-done.22), custom_call_target="tpu_custom_call" | custom-call | flops 7864320 | bytes 2368524 | tf_op jit(solution)/shard_map/pallas_call | solution.py:45
  58.3 2.1 %collective-permute-start.5 = (f32[4,1,768]{2,1,0:T(1,128)S(1)}, f32[4,1,768]{2,1,0:T(1,128)S(1)}, u32[]{:S(2)}, u32[]{:S(2)}) collective-permute-start(f32[4,1,768]{2,1,0:T(1,128)S(1)} %pad_maximum_fusion.1), channel_id=1, source_target_pairs={{0,8},{2,10},{4,12},{6,14},{8,0},{10,2},{12,4},{14,6},{16,24},{18,... | collective-permute-start | bytes 36872 | tf_op jit(solution)/shard_map/ppermute | solution.py:498
  62.1 3.4 %collective-permute-start.6 = (f32[8,1,768]{2,1,0:T(1,128)S(1)}, f32[8,1,768]{2,1,0:T(1,128)S(1)}, u32[]{:S(2)}, u32[]{:S(2)}) collective-permute-start(f32[8,1,768]{2,1,0:T(1,128)S(1)} %pad_maximum_fusion.near_hbm), channel_id=1, source_target_pairs={{0,16},{2,18},{4,20},{6,22},{8,24},{10,26},{12,28},{14,30},{16,0},... | collective-permute-start | bytes 73736 | tf_op jit(solution)/shard_map/ppermute | solution.py:498
  65.6 4.5 %collective-permute-done.mate_ref = s32[8,1,384]{2,1,0:T(1,128)S(1)} collective-permute-done((s32[8,1,384]{2,1,0:T(1,128)S(1)}, s32[8,1,384]{2,1,0:T(1,128)S(1)}, u32[]{:S(2)}, u32[]{:S(2)}) %collective-permute-start) | collective-permute-done | bytes 12320 | tf_op jit(solution)/shard_map/ppermute | solution.py:498
  74.2 3.8 %shard_map.162 = (bf16[4,128,384]{2,1,0:T(8,128)(2,1)S(1)}, bf16[32,384]{1,0:T(8,128)(2,1)S(1)}) custom-call(s32[4,5]{1,0:T(4,128)} %ids_ref.5, s32[1]{0:T(128)} %bitcast.1.self_ref, bf16[4,5,128,128]{3,2,1,0:T(8,128)(2,1)} %copy-done.13, bf16[4,128,128]{2,1,0:T(8,128)(2,1)} %copy-done.14, f32[8,1,768]{2,1,0:T(1,128)} %copy-done.30, ...), custom_call_target="tpu_custom_call" | custom-call | flops 251658240 | bytes 3219540 | tf_op jit(solution)/shard_map/pallas_call | solution.py:45
  83.9 3.4 %shard_map.169 = (bf16[16,136,384]{2,1,0:T(8,128)(2,1)}, bf16[512,384]{1,0:T(8,128)(2,1)}) custom-call(s32[4,5]{1,0:T(4,128)S(1)} %copy-done.21, s32[1]{0:T(128)} %bitcast.1.self_ref, s32[1]{0:T(128)} %bitcast.core_ref, bf16[512,384]{1,0:T(8,128)(2,1)S(1)} %get-tuple-element.35.mine_ref, bf16[512,384]{1,0:T(8,128)(2,1)S(1)} %collective-permute-done.10.other_ref, ...), custom_call_target="tpu_custom_call" | custom-call | flops 553648128 | bytes 4751448 | tf_op jit(solution)/shard_map/pallas_call | solution.py:45
  87.4 5.4 %all-to-all-start.2 = ((bf16[16,136,384]{2,1,0:T(8,128)(2,1)}), bf16[16,136,384]{2,1,0:T(8,128)(2,1)S(1)}, u32[]{:S(2)}, u32[]{:S(2)}) async-start(bf16[16,136,384]{2,1,0:T(8,128)(2,1)} %get-tuple-element.45), calls=%async_computation.2 | async-start | bytes 3342336 | tf_op jit(solution)/shard_map/all_to_all | solution.py:503
  98.4 8.5 %collective-permute-done.11.theirs_ref = bf16[8,48,384]{2,1,0:T(8,128)(2,1)S(1)} collective-permute-done((bf16[8,48,384]{2,1,0:T(8,128)(2,1)}, bf16[8,48,384]{2,1,0:T(8,128)(2,1)S(1)}, u32[]{:S(2)}, u32[]{:S(2)}) %collective-permute-start.11) | collective-permute-done | bytes 294944 | tf_op jit(solution)/shard_map/ppermute | solution.py:498
  107.9 2.4 %collective-permute-start.12 = (bf16[4,48,384]{2,1,0:T(8,128)(2,1)S(1)}, bf16[4,48,384]{2,1,0:T(8,128)(2,1)S(1)}, u32[]{:S(2)}, u32[]{:S(2)}) collective-permute-start(bf16[4,48,384]{2,1,0:T(8,128)(2,1)S(1)} %get-tuple-element.39), channel_id=1, source_target_pairs={{0,4},{2,6},{4,0},{6,2},{8,12},{10,14},{12,8},{14,10},{16,20},{18,... | collective-permute-start | bytes 442376 | tf_op jit(solution)/shard_map/ppermute | solution.py:498
  110.2 5.7 %collective-permute-done.12.theirs_ref = bf16[4,48,384]{2,1,0:T(8,128)(2,1)S(1)} collective-permute-done((bf16[4,48,384]{2,1,0:T(8,128)(2,1)S(1)}, bf16[4,48,384]{2,1,0:T(8,128)(2,1)S(1)}, u32[]{:S(2)}, u32[]{:S(2)}) %collective-permute-start.12) | collective-permute-done | bytes 147488 | tf_op jit(solution)/shard_map/ppermute | solution.py:498
  116.1 5.8 %collective-permute-done.13.theirs_ref = bf16[2,48,384]{2,1,0:T(8,128)(2,1)S(1)} collective-permute-done((bf16[2,48,384]{2,1,0:T(8,128)(2,1)S(1)}, bf16[2,48,384]{2,1,0:T(8,128)(2,1)S(1)}, u32[]{:S(2)}, u32[]{:S(2)}) %collective-permute-start.13) | collective-permute-done | bytes 73760 | tf_op jit(solution)/shard_map/ppermute | solution.py:498
  121.9 4.5 %collective-permute-start.14 = (bf16[1,48,384]{2,1,0:T(8,128)(2,1)S(1)}, bf16[1,48,384]{2,1,0:T(8,128)(2,1)S(1)}, u32[]{:S(2)}, u32[]{:S(2)}) collective-permute-start(bf16[1,48,384]{2,1,0:T(8,128)(2,1)S(1)} %get-tuple-element.43), channel_id=1, source_target_pairs={{0,16},{2,18},{4,20},{6,22},{8,24},{10,26},{12,28},{14,30},{16,0},... | collective-permute-start | bytes 110600 | tf_op jit(solution)/shard_map/ppermute | solution.py:498
  127.6 2.4 %shard_map.170.local_hbm = f32[4,128,384]{2,1,0:T(8,128)S(1)} custom-call(s32[4,5]{1,0:T(4,128)S(1)} %copy-done.21, s32[1]{0:T(128)} %bitcast.1.self_ref, bf16[4,128,384]{2,1,0:T(8,128)(2,1)S(1)} %bitcast.31, bf16[4,5,128,128]{3,2,1,0:T(8,128)(2,1)S(1)} %copy-done, bf16[4,128,384]{2,1,0:T(8,128)(2,1)S(1)} %bitcast.24), custom_call_target="tpu_custom_call" | custom-call | flops 251658240 | bytes 2228308 | tf_op jit(solution)/shard_map/pallas_call | solution.py:45
  130.9 2.8 %collective-permute-done.14.theirs_ref = bf16[1,48,384]{2,1,0:T(8,128)(2,1)S(1)} collective-permute-done((bf16[1,48,384]{2,1,0:T(8,128)(2,1)S(1)}, bf16[1,48,384]{2,1,0:T(8,128)(2,1)S(1)}, u32[]{:S(2)}, u32[]{:S(2)}) %collective-permute-start.14) | collective-permute-done | bytes 36896 | tf_op jit(solution)/shard_map/ppermute | solution.py:498
  134.4 3.1 %shard_map.171 = (bf16[4,128,384]{2,1,0:T(8,128)(2,1)}, f32[2,384]{1,0:T(2,128)}) custom-call(s32[1]{0:T(128)} %bitcast.1.self_ref, s32[8,2]{1,0:T(8,128)S(1)} %copy.18.asked_ref, s32[8,2]{1,0:T(8,128)S(1)} %copy.21.mate_ref, f32[4,128,384]{2,1,0:T(8,128)} %copy-done.4, bf16[16,136,384]{2,1,0:T(8,128)(2,1)S(1)} %all-to-all-done.2.got_ref), custom_call_target="tpu_custom_call" | custom-call | flops 1000 | bytes 2854020 | tf_op jit(solution)/shard_map/pallas_call | solution.py:45
  (101 shorter events, 35.2 us)
Async XLA Ops:
  0.6 21.9 %collective-permute-start.7 = (bf16[4,128,384]{2,1,0:T(8,128)(2,1)}, bf16[4,128,384]{2,1,0:T(8,128)(2,1)S(1)}, u32[]{:S(2)}, u32[]{:S(2)}) collective-permute-start(bf16[4,128,384]{2,1,0:T(8,128)(2,1)} %bitcast.20), channel_id=1, source_target_pairs={{0,16},{2,18},{4,20},{6,22},{8,24},{10,26},{12,28},{14,30},{16,0},... | collective-permute-start | bytes 1179656 | tf_op jit(solution)/shard_map/ppermute | solution.py:498
  26.2 47.4 %all-to-all-start.1 = ((bf16[8,256,384]{2,1,0:T(8,128)(2,1)}), bf16[8,256,384]{2,1,0:T(8,128)(2,1)S(1)}, u32[]{:S(2)}, u32[]{:S(2)}) async-start(bf16[8,256,384]{2,1,0:T(8,128)(2,1)} %shard_map.161), calls=%async_computation.1 | async-start | bytes 3145728 | tf_op jit(solution)/shard_map/all_to_all | solution.py:503
  32.9 6.3 %copy-start.22 = (f32[2,768]{1,0:T(2,128)S(1)}, f32[2,768]{1,0:T(2,128)}, u32[]{:S(2)}) copy-start(f32[2,768]{1,0:T(2,128)} %gains_ref.3) | copy-start | bytes 18436
  32.9 6.3 %copy-start.24 = (bf16[768,1536]{1,0:T(8,128)(2,1)S(1)}, bf16[768,1536]{1,0:T(8,128)(2,1)}, u32[]{:S(2)}) copy-start(bf16[768,1536]{1,0:T(8,128)(2,1)} %up_ref.1) | copy-start | bytes 7077892
  32.9 6.3 %copy-start.25 = (bf16[1536,768]{1,0:T(8,128)(2,1)S(1)}, bf16[1536,768]{1,0:T(8,128)(2,1)}, u32[]{:S(2)}) copy-start(bf16[1536,768]{1,0:T(8,128)(2,1)} %down_ref.1) | copy-start | bytes 7077892
  36.9 2.4 %collective-permute-start.1 = (bf16[512,768]{1,0:T(8,128)(2,1)S(1)}, bf16[512,768]{1,0:T(8,128)(2,1)S(1)}, u32[]{:S(2)}, u32[]{:S(2)}) collective-permute-start(bf16[512,768]{1,0:T(8,128)(2,1)S(1)} %shard_map.158.mine_ref), channel_id=1, source_target_pairs={{0,1},{1,0},{2,3},{3,2},{4,5},{5,4},{6,7},{7,6},{8,9},{9,8},{10,11... | collective-permute-start | bytes 2359304 | tf_op jit(solution)/shard_map/ppermute | solution.py:495
  39.3 30.8 %copy-start.20 = (s32[4,5]{1,0:T(4,128)S(1)}, s32[4,5]{1,0:T(4,128)}, u32[]{:S(2)}) copy-start(s32[4,5]{1,0:T(4,128)} %ids_ref.5) | copy-start | bytes 244
  45.0 25.1 %copy-start = (bf16[4,5,128,128]{3,2,1,0:T(8,128)(2,1)S(1)}, bf16[4,5,128,128]{3,2,1,0:T(8,128)(2,1)}, u32[]{:S(2)}) copy-start(bf16[4,5,128,128]{3,2,1,0:T(8,128)(2,1)} %adj_ref.5) | copy-start | bytes 1966084
  45.0 25.1 %copy-start.2 = (bf16[512,384]{1,0:T(8,128)(2,1)S(1)}, bf16[512,384]{1,0:T(8,128)(2,1)}, u32[]{:S(2)}) copy-start(bf16[512,384]{1,0:T(8,128)(2,1)} %param.20) | copy-start | bytes 1179652
  45.0 2.6 %collective-permute-start.2 = (bf16[512,768]{1,0:T(8,128)(2,1)}, bf16[512,768]{1,0:T(8,128)(2,1)}, u32[]{:S(2)}, u32[]{:S(2)}) collective-permute-start(bf16[512,768]{1,0:T(8,128)(2,1)} %get-tuple-element.29.mine_ref), channel_id=1, source_target_pairs={{0,1},{1,0},{2,3},{3,2},{4,5},{5,4},{6,7},{7,6},{8,9},{9,8},{10,11... | collective-permute-start | bytes 2359304 | tf_op jit(solution)/shard_map/ppermute | solution.py:495
  50.9 3.7 %collective-permute-start.3 = (f32[1,1,768]{2,1,0:T(1,128)S(1)}, f32[1,1,768]{2,1,0:T(1,128)S(1)}, u32[]{:S(2)}, u32[]{:S(2)}) collective-permute-start(f32[1,1,768]{2,1,0:T(1,128)S(1)} %shard_map.160), channel_id=1, source_target_pairs={{0,2},{2,0},{4,6},{6,4},{8,10},{10,8},{12,14},{14,12},{16,18},{18,... | collective-permute-start | bytes 9224 | tf_op jit(solution)/shard_map/ppermute | solution.py:498
  54.6 3.7 %collective-permute-start.4 = (f32[2,1,768]{2,1,0:T(1,128)S(1)}, f32[2,1,768]{2,1,0:T(1,128)S(1)}, u32[]{:S(2)}, u32[]{:S(2)}) collective-permute-start(f32[2,1,768]{2,1,0:T(1,128)S(1)} %pad_maximum_fusion.2), channel_id=1, source_target_pairs={{0,4},{2,6},{4,0},{6,2},{8,12},{10,14},{12,8},{14,10},{16,20},{18,... | collective-permute-start | bytes 18440 | tf_op jit(solution)/shard_map/ppermute | solution.py:498
  58.3 3.8 %collective-permute-start.5 = (f32[4,1,768]{2,1,0:T(1,128)S(1)}, f32[4,1,768]{2,1,0:T(1,128)S(1)}, u32[]{:S(2)}, u32[]{:S(2)}) collective-permute-start(f32[4,1,768]{2,1,0:T(1,128)S(1)} %pad_maximum_fusion.1), channel_id=1, source_target_pairs={{0,8},{2,10},{4,12},{6,14},{8,0},{10,2},{12,4},{14,6},{16,24},{18,... | collective-permute-start | bytes 36872 | tf_op jit(solution)/shard_map/ppermute | solution.py:498
  62.1 11.5 %copy-start.30 = (f32[8,1,768]{2,1,0:T(1,128)}, f32[8,1,768]{2,1,0:T(1,128)S(1)}, u32[]{:S(2)}) copy-start(f32[8,1,768]{2,1,0:T(1,128)S(1)} %pad_maximum_fusion.near_hbm) | copy-start | bytes 73732
  62.1 11.5 %collective-permute-start.6 = (f32[8,1,768]{2,1,0:T(1,128)S(1)}, f32[8,1,768]{2,1,0:T(1,128)S(1)}, u32[]{:S(2)}, u32[]{:S(2)}) collective-permute-start(f32[8,1,768]{2,1,0:T(1,128)S(1)} %pad_maximum_fusion.near_hbm), channel_id=1, source_target_pairs={{0,16},{2,18},{4,20},{6,22},{8,24},{10,26},{12,28},{14,30},{16,0},... | collective-permute-start | bytes 73736 | tf_op jit(solution)/shard_map/ppermute | solution.py:498
  65.5 4.6 %collective-permute-start = (s32[8,1,384]{2,1,0:T(1,128)S(1)}, s32[8,1,384]{2,1,0:T(1,128)S(1)}, u32[]{:S(2)}, u32[]{:S(2)}) collective-permute-start(s32[8,1,384]{2,1,0:T(1,128)S(1)} %all_to_all.15.got_ref), channel_id=1, source_target_pairs={{0,16},{2,18},{4,20},{6,22},{8,24},{10,26},{12,28},{14,30},{16,0},... | collective-permute-start | bytes 36872 | tf_op jit(solution)/shard_map/ppermute | solution.py:498
  78.0 2.2 %collective-permute-start.8 = (bf16[512,384]{1,0:T(8,128)(2,1)S(1)}, bf16[512,384]{1,0:T(8,128)(2,1)S(1)}, u32[]{:S(2)}, u32[]{:S(2)}) collective-permute-start(bf16[512,384]{1,0:T(8,128)(2,1)S(1)} %bitcast.25), channel_id=1, source_target_pairs={{0,1},{1,0},{2,3},{3,2},{4,5},{5,4},{6,7},{7,6},{8,9},{9,8},{10,11... | collective-permute-start | bytes 1179656 | tf_op jit(solution)/shard_map/ppermute | solution.py:495
  78.2 2.1 %collective-permute-start.9 = (bf16[384,384]{1,0:T(8,128)(2,1)S(1)}, bf16[384,384]{1,0:T(8,128)(2,1)S(1)}, u32[]{:S(2)}, u32[]{:S(2)}) collective-permute-start(bf16[384,384]{1,0:T(8,128)(2,1)S(1)} %constant_dynamic-slice_fusion), channel_id=1, source_target_pairs={{0,1},{1,0},{2,3},{3,2},{4,5},{5,4},{6,7},{7,6},{8,9},{9,8},{10,11... | collective-permute-start | bytes 884744 | tf_op jit(solution)/shard_map/ppermute | solution.py:495
  82.2 1.7 %collective-permute-start.10 = (bf16[512,384]{1,0:T(8,128)(2,1)S(1)}, bf16[512,384]{1,0:T(8,128)(2,1)S(1)}, u32[]{:S(2)}, u32[]{:S(2)}) collective-permute-start(bf16[512,384]{1,0:T(8,128)(2,1)S(1)} %get-tuple-element.35.mine_ref), channel_id=1, source_target_pairs={{0,1},{1,0},{2,3},{3,2},{4,5},{5,4},{6,7},{7,6},{8,9},{9,8},{10,11... | collective-permute-start | bytes 1179656 | tf_op jit(solution)/shard_map/ppermute | solution.py:495
  87.4 47.0 %all-to-all-start.2 = ((bf16[16,136,384]{2,1,0:T(8,128)(2,1)}), bf16[16,136,384]{2,1,0:T(8,128)(2,1)S(1)}, u32[]{:S(2)}, u32[]{:S(2)}) async-start(bf16[16,136,384]{2,1,0:T(8,128)(2,1)} %get-tuple-element.45), calls=%async_computation.2 | async-start | bytes 3342336 | tf_op jit(solution)/shard_map/all_to_all | solution.py:503
  96.4 10.5 %collective-permute-start.11 = (bf16[8,48,384]{2,1,0:T(8,128)(2,1)}, bf16[8,48,384]{2,1,0:T(8,128)(2,1)S(1)}, u32[]{:S(2)}, u32[]{:S(2)}) collective-permute-start(bf16[8,48,384]{2,1,0:T(8,128)(2,1)} %get-tuple-element.37), channel_id=1, source_target_pairs={{0,2},{2,0},{4,6},{6,4},{8,10},{10,8},{12,14},{14,12},{16,18},{18,... | collective-permute-start | bytes 884744 | tf_op jit(solution)/shard_map/ppermute | solution.py:498
  107.9 8.1 %collective-permute-start.12 = (bf16[4,48,384]{2,1,0:T(8,128)(2,1)S(1)}, bf16[4,48,384]{2,1,0:T(8,128)(2,1)S(1)}, u32[]{:S(2)}, u32[]{:S(2)}) collective-permute-start(bf16[4,48,384]{2,1,0:T(8,128)(2,1)S(1)} %get-tuple-element.39), channel_id=1, source_target_pairs={{0,4},{2,6},{4,0},{6,2},{8,12},{10,14},{12,8},{14,10},{16,20},{18,... | collective-permute-start | bytes 442376 | tf_op jit(solution)/shard_map/ppermute | solution.py:498
  116.0 5.8 %collective-permute-start.13 = (bf16[2,48,384]{2,1,0:T(8,128)(2,1)S(1)}, bf16[2,48,384]{2,1,0:T(8,128)(2,1)S(1)}, u32[]{:S(2)}, u32[]{:S(2)}) collective-permute-start(bf16[2,48,384]{2,1,0:T(8,128)(2,1)S(1)} %get-tuple-element.41), channel_id=1, source_target_pairs={{0,8},{2,10},{4,12},{6,14},{8,0},{10,2},{12,4},{14,6},{16,24},{18,... | collective-permute-start | bytes 221192 | tf_op jit(solution)/shard_map/ppermute | solution.py:498
  121.9 11.8 %collective-permute-start.14 = (bf16[1,48,384]{2,1,0:T(8,128)(2,1)S(1)}, bf16[1,48,384]{2,1,0:T(8,128)(2,1)S(1)}, u32[]{:S(2)}, u32[]{:S(2)}) collective-permute-start(bf16[1,48,384]{2,1,0:T(8,128)(2,1)S(1)} %get-tuple-element.43), channel_id=1, source_target_pairs={{0,16},{2,18},{4,20},{6,22},{8,24},{10,26},{12,28},{14,30},{16,0},... | collective-permute-start | bytes 110600 | tf_op jit(solution)/shard_map/ppermute | solution.py:498
  (25 other events, 65.9 us)

commit v5 on v4

--- a/solution.py
+++ b/solution.py
@@ -21,6 +21,7 @@
 
 VMEM = pl.BlockSpec(memory_space=pltpu.VMEM)
 HBM = pl.BlockSpec(memory_space=pltpu.HBM)
+PULL = pl.BlockSpec(memory_space=pltpu.HBM)
 SMEM = pl.BlockSpec(memory_space=pltpu.SMEM)
 
 
@@ -34,9 +35,14 @@
     )
     many = len(outs) > 1
     ins = [
-        pltpu.with_memory_space_constraint(a, pltpu.HBM) if s is HBM else a
+        pltpu.with_memory_space_constraint(a, pltpu.HBM) if s is HBM or s is PULL else a
         for a, s in zip(ins, specs, strict=True)
     ]
+    pulled = [i for i, s in enumerate(specs) if s is PULL]
+    if pulled:
+        body = pulling(body, pulled)
+        scratch = list(scratch) + [pltpu.VMEM(ins[i].shape, ins[i].dtype) for i in pulled]
+        scratch.append(pltpu.SemaphoreType.DMA((len(pulled),)))
     held = sum(math.prod(s.shape) * jnp.dtype(s.dtype).itemsize for s in scratch if counted(s))
     out_specs = out_specs or [VMEM] * len(outs)
     outs = [
@@ -62,6 +68,20 @@
     for copy in started:
         copy.start()
     return started
+
+
+def pulling(body, pulled):
+    def wrapped(*refs):
+        buffers, sems = refs[-len(pulled) - 1 : -1], refs[-1]
+        held = list(refs[: -len(pulled) - 1])
+        started = copies([(held[i], b) for i, b in zip(pulled, buffers)], sems)
+        for i, buffer in zip(pulled, buffers):
+            held[i] = buffer
+        for copy in started:
+            copy.wait()
+        body(*held)
+
+    return wrapped
 
 
 def unroll(steps):
@@ -148,7 +168,10 @@
         lax.fori_loop(0, peers, lambda p, c: (slot(p, side).wait(), c)[1], 0)
 
 
-def mask_body(ids_ref, self_ref, got_ref, mate_ref, adj_ref, cache_ref, kept_ref, pick_ref, own_ref, base_ref):
+def mask_body(
+    ids_ref, self_ref, got_ref, mate_ref, adj_ref, cache_ref, *refs
+):
+    outs, (kept_ref, pick_ref, own_ref, base_ref, sems) = refs[:4], refs[4:]
     tiles_here, entries, tile_rows, _ = adj_ref.shape
     peers, _, lanes = got_ref.shape
     width = lanes - 2 * LANES
@@ -157,6 +180,7 @@
     table = jnp.max(both.reshape(peers, width).astype(jnp.float32), axis=0, keepdims=True)
     place = lax.broadcasted_iota(jnp.int32, (tile_rows, width), 0).astype(jnp.float32)
     ones = jnp.ones((ROWS, width), jnp.bfloat16)
+    sent = []
 
     def holds(tile_id):
         first = (tile_id * tile_rows).astype(jnp.float32)
@@ -181,6 +205,10 @@
         own_ref[r] = hot.astype(jnp.bfloat16)
         fresh = jnp.max(hot, axis=1, keepdims=True)
         base_ref[r] = (cache_ref[r].astype(jnp.float32) * (1.0 - fresh)).astype(jnp.bfloat16)
+        row = [(ref.at[r], out.at[r]) for ref, out in zip((kept_ref, pick_ref, own_ref, base_ref), outs)]
+        sent = sent + copies(row, sems.at[r])
+    for copy in sent:
+        copy.wait()
 
 
 def norm(values, gain):
@@ -190,17 +218,30 @@
     return centred * lax.rsqrt(variance + NORM_EPS) * gain
 
 
-def attend_body(seq, counts_ref, tokens_ref, w_qkv_ref, w_out_ref, out_ref, proj_ref, ctx_ref):
+def attend_body(
+    seq, counts_ref, tokens_hbm, w_qkv_hbm, w_out_hbm, out_hbm,
+    tokens_ref, w_qkv_ref, w_out_ref, out_ref, proj_ref, ctx_ref, in_sems, out_sems
+):
     half = w_out_ref.shape[0]
     texts_here = tokens_ref.shape[0] // seq
+    started = copies(
+        [(tokens_hbm, tokens_ref)]
+        + [(w_qkv_hbm.at[c], w_qkv_ref.at[c]) for c in range(3)]
+        + [(w_out_hbm, w_out_ref)],
+        in_sems,
+    )
+    started[0].wait()
     for c in range(3):
+        started[1 + c].wait()
         proj_ref[:, c * half : (c + 1) * half] = mm(tokens_ref[...], w_qkv_ref[c]).astype(
             jnp.bfloat16
         )
+    started[4].wait()
+    sent = []
     left = lax.broadcasted_iota(jnp.int32, (seq, LANES), 1) < HEAD
     key_at = lax.broadcasted_iota(jnp.int32, (seq, seq), 1)
     for t in range(texts_here):
-        rows = slice(t * seq, (t + 1) * seq)
+        rows = pl.ds(t * seq, seq)
         live = key_at < counts_ref[0, t]
         for pair in range(half // LANES):
             first = pair * LANES
@@ -217,13 +258,30 @@
             ctx_ref[rows, first : first + LANES] = jnp.where(left, sides[0], sides[1]).astype(
                 jnp.bfloat16
             )
-    out_ref[...] = mm(ctx_ref[...], w_out_ref[...]).astype(jnp.bfloat16)
-
-
-def inner_body(tokens_ref, mine_ref, other_ref, up_ref, down_ref, gains_ref, first_ref, out_ref, inner_ref):
+        out_ref[rows, :] = mm(ctx_ref[rows, :], w_out_ref[...]).astype(jnp.bfloat16)
+        sent.append(pltpu.make_async_copy(out_ref.at[rows, :], out_hbm.at[rows, :], out_sems.at[t]))
+        sent[-1].start()
+    for copy in sent:
+        copy.wait()
+
+
+def inner_body(
+    tokens_hbm, mine_hbm, other_hbm, up_hbm, down_hbm, gains_ref, first_ref, out_ref,
+    inner_ref, tokens_ref, mine_ref, other_ref, up_ref, down_ref, sems
+):
+    started = copies(
+        [
+            (tokens_hbm, tokens_ref), (mine_hbm, mine_ref), (other_hbm, other_ref),
+            (up_hbm, up_ref), (down_hbm, down_ref),
+        ],
+        sems,
+    )
+    for copy in started[:3]:
+        copy.wait()
     added = mine_ref[...].astype(jnp.float32) + other_ref[...].astype(jnp.float32)
     first = norm(tokens_ref[...].astype(jnp.float32) + added, gains_ref[0:1, :])
     first_ref[...] = first.astype(jnp.bfloat16)
+    started[3].wait()
     hidden_units = up_ref.shape[1]
     step = hidden_units // 4
     for c in range(4):
@@ -231,6 +289,7 @@
         value = mm(first_ref[...], up_ref[:, cols])
         gate = jnp.tanh(ROOT * (value + CUBE * (value * value * value)))
         inner_ref[:, cols] = (0.5 * value * (1.0 + gate)).astype(jnp.bfloat16)
+    started[4].wait()
     out_ref[...] = mm(inner_ref[...], down_ref[...]).astype(jnp.bfloat16)
 
 
@@ -265,7 +324,15 @@
     texts = stacked.shape[0]
     row = lax.broadcasted_iota(jnp.int32, (texts, texts), 0)
     column = lax.broadcasted_iota(jnp.int32, (texts, texts), 1)
-    order = jnp.where(row == (column ^ me), 1.0, 0.0).astype(jnp.bfloat16)
+    place = column & (shards - 1)
+    offset = jnp.zeros_like(place)
+    reach = 1
+    while reach < shards:
+        offset = 2 * offset + (place & 1)
+        place = lax.shift_right_logical(place, 1)
+        reach *= 2
+    source = column - (column & (shards - 1)) + (offset ^ me)
+    order = jnp.where(row == source, 1.0, 0.0).astype(jnp.bfloat16)
     return mm(order, stacked).astype(jnp.bfloat16)
 
 
@@ -318,7 +385,7 @@
     _, half = mine_ref.shape
     start = pl.multiple_of(core_ref[0] * half, LANES)
     hidden = mm(mine_ref[...], w_own_ref[:, pl.ds(start, half)]) + mm(
-        other_ref[...], w_other_ref[...]
+        other_ref[...], w_other_ref[:, pl.ds(start, half)]
     )
     square = hidden * hidden
     gate = jnp.tanh(ROOT * hidden * (1.0 + CUBE * square))
@@ -331,40 +398,58 @@
     )
 
 
-def weight_body(
-    per, self_ref, core_ref, mine_ref, other_ref, agg_ref, keep_hbm, give_hbm, w_ref, half_ref, sems
+def chunk_body(
+    per, texts_here, self_ref, core_ref, mine_ref, other_ref, agg_ref, down_ref, pick_ref, own_ref,
+    grad_ref, keep_ref, give_ref, w_ref, text_ref
 ):
-    shards, deep, half = half_ref.shape
-    kept = shards // 2
+    kept, _, half = keep_ref.shape
+    shards = 2 * kept
+    deep = up_to(per, ROWS)
+    text_rows = keep_ref.shape[1] - deep
     me = self_ref[0]
     own = pl.multiple_of(core_ref[0] * half, LANES)
     far = pl.multiple_of((1 - core_ref[0]) * half, LANES)
     columns = 2 * half
+    text_ref[...] = mm(pick_ref[...], down_ref[...], (0, 0)) + mm(
+        own_ref[...], grad_ref[...], (0, 0)
+    )
     w_ref[pl.ds(own, half), :] = mm(mine_ref[...], agg_ref[...], (0, 0))
     w_ref[pl.ds(far, half), :] = mm(other_ref[...], agg_ref[...], (0, 0))
     w_ref[columns:, :] = jnp.zeros((w_ref.shape[0] - columns, half), jnp.float32)
+    row = lax.broadcasted_iota(jnp.int32, (text_rows, half), 0)
     for q in range(shards):
+        piece = w_ref[q * per : q * per + deep, :].astype(jnp.bfloat16)
+        block = jnp.zeros((text_rows, half), jnp.float32)
+        for i in range(texts_here):
+            line = text_ref[i * shards + q : i * shards + q + 1, :]
+            high = line.astype(jnp.bfloat16).astype(jnp.float32)
+            block = jnp.where(row == i, high, block)
+            block = jnp.where(row == text_rows // 2 + i, line - high, block)
+        block = block.astype(jnp.bfloat16)
         step = q ^ me
         turned = step * 0
         reach = 1
         while reach < shards:
             turned = 2 * turned + ((step // reach) & 1)
             reach *= 2
-        half_ref[turned] = w_ref[q * per : q * per + deep, :].astype(jnp.bfloat16)
-    ends = copies(
-        [(half_ref.at[pl.ds(kept, kept)], give_hbm), (half_ref.at[pl.ds(0, kept)], keep_hbm)], sems
-    )
-    for copy in ends:
-        copy.wait()
+
+        @pl.when(turned < kept)
+        def _():
+            keep_ref[turned, :deep, :] = piece
+            keep_ref[turned, deep:, :] = block
+
+        @pl.when(turned >= kept)
+        def _():
+            give_ref[turned - kept, :deep, :] = piece
+            give_ref[turned - kept, deep:, :] = block
 
 
 def backward_body(
-    texts_here, ids_ref, self_ref, core_ref, mine_ref, other_ref, w_own_ref, adj_ref,
-    pick_ref, own_ref, grad_ref, send_hbm, down_hbm,
-    down_ref, text_ref, send_ref, rows_ref, sems, slot_sems
+    ids_ref, self_ref, core_ref, mine_ref, other_ref, w_own_ref, adj_ref, send_hbm, down_hbm,
+    down_ref, send_ref, sems, slot_sems
 ):
     tiles_here, entries, tile_rows, _ = adj_ref.shape
-    shards, text_rows, half = rows_ref.shape
+    shards, _, half = send_hbm.shape
     me = self_ref[0]
     core = core_ref[0]
     own = pl.multiple_of(core * half, LANES)
@@ -386,40 +471,31 @@
                 _, owner, _ = tile_of(tile_id, tiles_here)
                 slot = jnp.where((tile_id >= 0) & (owner != me), owner, shards)
                 send_ref[slot] = product[(k - first) * tile_rows : (k - first + 1) * tile_rows]
-    slots = copies(
-        [(send_ref.at[q], send_hbm.at[q, pl.ds(0, tile_rows), :]) for q in range(shards)], slot_sems
-    )
-    text_ref[...] = mm(pick_ref[...], down_ref[...], (0, 0)) + mm(
-        own_ref[...], grad_ref[...], (0, 0)
-    )
-    row = lax.broadcasted_iota(jnp.int32, (text_rows, half), 0)
-    for q in range(shards):
-        block = jnp.zeros((text_rows, half), jnp.float32)
-        for i in range(texts_here):
-            line = text_ref[i * shards + q : i * shards + q + 1, :]
-            high = line.astype(jnp.bfloat16).astype(jnp.float32)
-            block = jnp.where(row == i, high, block)
-            block = jnp.where(row == text_rows // 2 + i, line - high, block)
-        rows_ref[q] = block.astype(jnp.bfloat16)
-    row_copy = pltpu.make_async_copy(
-        rows_ref, send_hbm.at[:, pl.ds(tile_rows, text_rows), :], sems.at[1]
-    )
-    row_copy.start()
-    for copy in slots:
+    for copy in copies([(send_ref.at[q], send_hbm.at[q]) for q in range(shards)], slot_sems):
         copy.wait()
     down_copy.wait()
-    row_copy.wait()
-
-
-def fold_body(mine_ref, theirs_ref, keep_ref, give_ref):
+
+
+def fold(mine, theirs, deep):
+    total = mine.astype(jnp.float32) + theirs.astype(jnp.float32)
+    lines = (total.shape[0] - deep) // 2
+    return total[:deep, :], total[deep : deep + lines, :] + total[deep + lines :, :]
+
+
+def fold_body(deep, mine_ref, theirs_ref, keep_ref, give_ref):
     kept = keep_ref.shape[0]
     for s in range(2 * kept):
-        total = mine_ref[s].astype(jnp.float32) + theirs_ref[s].astype(jnp.float32)
-        (keep_ref if s < kept else give_ref)[s % kept] = total.astype(jnp.bfloat16)
-
-
-def close_body(mine_ref, theirs_ref, w_ref):
-    w_ref[...] = mine_ref[0].astype(jnp.float32) + theirs_ref[0].astype(jnp.float32)
+        w_sum, text = fold(mine_ref[s], theirs_ref[s], deep)
+        high = text.astype(jnp.bfloat16).astype(jnp.float32)
+        out_ref = (keep_ref if s < kept else give_ref).at[s % kept]
+        out_ref[:deep, :] = w_sum.astype(jnp.bfloat16)
+        out_ref[deep:, :] = jnp.concatenate([high, text - high], axis=0).astype(jnp.bfloat16)
+
+
+def close_body(deep, mine_ref, theirs_ref, w_ref, text_ref):
+    w_sum, text = fold(mine_ref[0], theirs_ref[0], deep)
+    w_ref[...] = w_sum
+    text_ref[...] = text[: text_ref.shape[0], :]
 
 
 def local_body(ids_ref, self_ref, down_ref, adj_ref, grad_ref, local_ref):
@@ -441,22 +517,12 @@
         lax.fori_loop(0, entries, one, 0, unroll=unroll(entries))
 
 
-def finish_body(
-    self_ref, asked_ref, mate_ref, local_hbm, got_ref, node_ref, text_ref, sum_ref, sems
-):
+def finish_body(self_ref, asked_ref, mate_ref, local_hbm, got_ref, node_ref, sum_ref, sems):
     local = pltpu.make_async_copy(local_hbm, sum_ref, sems.at[0])
     local.start()
-    _, tile_rows, half = sum_ref.shape
-    shards, rows, _ = got_ref.shape
-    total = jnp.zeros((rows - tile_rows, half), jnp.float32)
-    for q in range(shards):
-        total = total + got_ref[q, tile_rows:, :].astype(jnp.float32)
-    text_ref[...] = (total[: (rows - tile_rows) // 2] + total[(rows - tile_rows) // 2 :])[
-        : text_ref.shape[0]
-    ]
+    shards = got_ref.shape[0]
+    me = self_ref[0]
     local.wait()
-
-    me = self_ref[0]
 
     def one(q, carry):
         side, spot = side_of(q, me, shards // 2)
@@ -464,7 +530,7 @@
 
         @pl.when(asked >= 0)
         def _():
-            sum_ref[asked] += got_ref[q, :tile_rows, :].astype(jnp.float32)
+            sum_ref[asked] += got_ref[q].astype(jnp.float32)
 
         return carry
 
@@ -542,24 +608,42 @@
     )
     remote = spread(packed, halves_of)
 
-    w_other = swap(lax.dynamic_slice_in_dim(w_gnn, (1 - core_at) * half, half, 1))
+    w_other = swap(w_gnn)
 
     flat_tokens = tokens.reshape(count, width)
     partial = call(
         functools.partial(attend_body, seq),
         [shape((count, width))],
         [token_counts, flat_tokens, jnp.transpose(w_qkv, (1, 0, 2)), w_out],
-        [SMEM, VMEM, VMEM, VMEM],
+        [SMEM, HBM, HBM, HBM],
         flops=2 * count * (width * 3 * half + half * width + 2 * seq * half * 2),
-        scratch=[pltpu.VMEM((count, 3 * half), jnp.bfloat16), pltpu.VMEM((count, half), jnp.bfloat16)],
+        scratch=[
+            pltpu.VMEM((count, width), jnp.bfloat16),
+            pltpu.VMEM((3, width, half), jnp.bfloat16),
+            pltpu.VMEM((half, width), jnp.bfloat16),
+            pltpu.VMEM((count, width), jnp.bfloat16),
+            pltpu.VMEM((count, 3 * half), jnp.bfloat16),
+            pltpu.VMEM((count, half), jnp.bfloat16),
+            pltpu.SemaphoreType.DMA((5,)),
+            pltpu.SemaphoreType.DMA((texts_here,)),
+        ],
+        out_specs=[HBM],
     )
     first, mlp = call(
         inner_body,
         [shape((count, width)), shape((count, width))],
         [flat_tokens, partial, swap(partial), w_up, w_down, ln_gains],
-        [VMEM] * 6,
+        [HBM] * 5 + [VMEM],
         flops=4 * count * width * inner,
-        scratch=[pltpu.VMEM((count, inner), jnp.bfloat16)],
+        scratch=[
+            pltpu.VMEM((count, inner), jnp.bfloat16),
+            pltpu.VMEM((count, width), jnp.bfloat16),
+            pltpu.VMEM((count, width), jnp.bfloat16),
+            pltpu.VMEM((count, width), jnp.bfloat16),
+            pltpu.VMEM((width, inner), jnp.bfloat16),
+            pltpu.VMEM((inner, width), jnp.bfloat16),
+            pltpu.SemaphoreType.DMA((5,)),
+        ],
     )
     pooled = call(
         functools.partial(pool_body, seq),
@@ -570,10 +654,10 @@
         scratch=[pltpu.VMEM((8, width), jnp.float32)],
     )
     near = pooled
-    reach = 1
+    reach = peers
     far = toward(near, reach)
-    while 4 * reach <= shards:
-        reach *= 2
+    while reach > 1:
+        reach = reach // 2
         near = jnp.concatenate([near, far], axis=0)
         far = toward(near, reach)
 
@@ -588,6 +672,14 @@
         [adj_tiles, me, got, mate_got, adj_values, cache_tiles],
         [SMEM, SMEM, VMEM, VMEM, VMEM, VMEM],
         flops=2 * adj_values.size * slots,
+        scratch=[
+            pltpu.VMEM(adj_values.shape, jnp.bfloat16),
+            pltpu.VMEM((tiles_here, tile_rows, slots), jnp.bfloat16),
+            pltpu.VMEM((tiles_here, tile_rows, slots), jnp.bfloat16),
+            pltpu.VMEM(cache_tiles.shape, jnp.bfloat16),
+            pltpu.SemaphoreType.DMA((tiles_here, 4)),
+        ],
+        out_specs=[HBM] * 4,
     )
     gathered, pooled = call(
         gather_body,
@@ -620,41 +712,36 @@
     grad_tiles = out_grad.reshape(tiles_here, tile_rows, half)
     slope_other = swap(slope)
     text_rows = up_to(2 * texts_here, 8)
-    halves = (shards // 2, deep, half)
-    keep, give = call(
-        functools.partial(weight_body, per),
-        [shape(halves), shape(halves)],
-        [me, core, slope, slope_other, gathered],
-        [SMEM, SMEM] + [VMEM] * 3,
-        flops=4 * nodes_here * half * half,
-        scratch=[
-            pltpu.VMEM((width + ROWS, half), jnp.float32),
-            pltpu.VMEM((shards, deep, half), jnp.bfloat16),
-            pltpu.SemaphoreType.DMA((2,)),
-        ],
-        out_specs=[HBM] * 2,
-    )
-    given = toward(give, 1)
+    halves = (shards // 2, deep + text_rows, half)
     send, down = call(
-        functools.partial(backward_body, texts_here),
-        [shape((shards, tile_rows + text_rows, half)), shape((nodes_here, half))],
-        [
-            adj_tiles, me, core, slope, slope_other, w_gnn, adj_values,
-            pick.reshape(nodes_here, slots), own.reshape(nodes_here, slots), out_grad,
-        ],
-        [SMEM, SMEM, SMEM] + [VMEM] * 7,
+        backward_body,
+        [shape((shards, tile_rows, half)), shape((nodes_here, half))],
+        [adj_tiles, me, core, slope, slope_other, w_gnn, adj_values],
+        [SMEM, SMEM, SMEM] + [VMEM] * 4,
         flops=4 * nodes_here * half * half + 2 * adj_values.size * half,
         scratch=[
             pltpu.VMEM((nodes_here, half), jnp.bfloat16),
+            pltpu.VMEM((shards + 1, tile_rows, half), jnp.bfloat16),
+            pltpu.SemaphoreType.DMA((1,)),
+            pltpu.SemaphoreType.DMA((shards,)),
+        ],
+        out_specs=[HBM] * 2,
+    )
+    returned = spread(send)
+    keep, give = call(
+        functools.partial(chunk_body, per, texts_here),
+        [shape(halves), shape(halves)],
+        [
+            me, core, slope, slope_other, gathered, down, pick.reshape(nodes_here, slots),
+            own.reshape(nodes_here, slots), out_grad,
+        ],
+        [SMEM, SMEM] + [PULL] * 7,
+        flops=4 * nodes_here * half * (half + slots),
+        scratch=[
+            pltpu.VMEM((width + ROWS, half), jnp.float32),
             pltpu.VMEM((slots, half), jnp.float32),
-            pltpu.VMEM((shards + 1, tile_rows, half), jnp.bfloat16),
-            pltpu.VMEM((shards, text_rows, half), jnp.bfloat16),
-            pltpu.SemaphoreType.DMA((2,)),
-            pltpu.SemaphoreType.DMA((shards,)),
-        ],
-        out_specs=[HBM] * 2,
-    )
-    returned = spread(send)
+        ],
+    )
     local = call(
         local_body,
         [shape((tiles_here, tile_rows, half), jnp.float32)],
@@ -663,23 +750,28 @@
         flops=2 * adj_values.size * half,
     )
     reach = 1
+    given = toward(give, reach)
     while 2 * reach < shards:
-        part = (shards // (4 * reach), deep, half)
+        part = (shards // (4 * reach), deep + text_rows, half)
         keep, give = call(
-            fold_body,
+            functools.partial(fold_body, deep),
             [shape(part), shape(part)],
             [keep, given],
             [VMEM] * 2,
             flops=4 * math.prod(part),
         )
-        reach *= 2
+        reach = 2 * reach
         given = toward(give, reach)
-    w_part = call(
-        close_body, [shape((deep, half), jnp.float32)], [keep, given], [VMEM] * 2, flops=1000
-    )
-    node_grad, text_grad = call(
+    w_part, text_grad = call(
+        functools.partial(close_body, deep),
+        [shape((deep, half), jnp.float32), shape((texts_here, half), jnp.float32)],
+        [keep, given],
+        [VMEM] * 2,
+        flops=1000,
+    )
+    node_grad = call(
         finish_body,
-        [shape((tiles_here, tile_rows, half)), shape((texts_here, half), jnp.float32)],
+        [shape((tiles_here, tile_rows, half))],
         [me, asked, places(mate_got), local, returned],
         [SMEM, SMEM, SMEM, HBM, VMEM],
         flops=1000,

time: 138 us -> 140 us (1.014)
  Pallas kernels: 33.1 us -> 42.6 us
  local copies, waits for them, and re-layouts: 13.4 us -> 4.28 us
  starting transfers between devices: 33.2 us -> 36.5 us
  waiting for transfers between devices: 46.6 us -> 44.6 us
    pallas_call x16, Pallas kernels: 33.1 us -> 42.6 us  [call(): pl.pallas_call(body, out_shape=tuple(outs) if many else outs[0], in_specs...]
    unnamed x66 -> x42, local copies, waits for them, and re-layouts: 13.2 us -> 4.11 us
    ppermute x10, starting transfers between devices: 22.7 us -> 25.8 us  [toward(): lax.ppermute(values, 'graph', [(i, i ^ reach) for i in range(shards)])]
    ppermute x10, waiting for transfers between devices: 38.7 us -> 36.3 us  [toward(): lax.ppermute(values, 'graph', [(i, i ^ reach) for i in range(shards)])]
  transfers between devices with their start and end apart: 17 -> 17, of which waited for: 13 -> 13; matrix products, arithmetic and copies ran while one was open for 0% -> 0% of each run, Pallas kernels for 13% -> 21%
where the time goes in v5:
time: 140 us; the launch traced here: 139 us
  waiting for transfers between devices  44.6 us (32%)
  Pallas kernels  42.6 us (30%)
  starting transfers between devices  36.5 us (26%)
  blocking collectives  10.1 us (7%)
  local copies, waits for them, and re-layouts  4.28 us (3%)
    pallas_call x16, Pallas kernels, call(): pl.pallas_call(body, out_shape=tuple(outs) if many else outs[0], in_specs...  42.6 us
    ppermute x10, waiting for transfers between devices, toward(): lax.ppermute(values, 'graph', [(i, i ^ reach) for i in range(shards)])  36.3 us
    ppermute x10, starting transfers between devices, toward(): lax.ppermute(values, 'graph', [(i, i ^ reach) for i in range(shards)])  25.8 us
    all_to_all x2, starting transfers between devices, spread(): lax.all_to_all(values, 'graph', split_axis=0, concat_axis=0, tiled=True,...  10.2 us
    all_to_all x1, blocking collectives, spread(): lax.all_to_all(values, 'graph', split_axis=0, concat_axis=0, tiled=True,...  10.1 us
    ppermute x5, waiting for transfers between devices, swap(): lax.ppermute(values, 'mp', [(i, cores - 1 - i) for i in range(cores)])  8.27 us
    unnamed x42, local copies, waits for them, and re-layouts  4.11 us
  transfers between devices with their start and end apart: 17, of which 13 were waited for; matrix products, arithmetic and copies ran while one was open for 0% of the time, Pallas kernels for 21%

profile of v5, /device:TPU:0, one launch (start us, length us, event | category | flops | bytes accessed | tf_op | source)
XLA Modules:
  0.0 139.3 jit_solution(2476488176073579089)
XLA Ops:
  0.6 4.1 %collective-permute-start.7 = (bf16[4,128,384]{2,1,0:T(8,128)(2,1)}, bf16[4,128,384]{2,1,0:T(8,128)(2,1)S(1)}, u32[]{:S(2)}, u32[]{:S(2)}) collective-permute-start(bf16[4,128,384]{2,1,0:T(8,128)(2,1)} %bitcast.20), channel_id=1, source_target_pairs={{0,16},{2,18},{4,20},{6,22},{8,24},{10,26},{12,28},{14,30},{16,0},... | collective-permute-start | bytes 1179656 | tf_op jit(solution)/shard_map/ppermute | solution.py:564
  5.7 10.1 %all_to_all.15.got_ref = s32[8,1,384]{2,1,0:T(1,128)S(1)} all-to-all(s32[8,1,384]{2,1,0:T(1,128)S(1)} %shard_map.156), channel_id=1, replica_groups={{0,2,4,6,8,10,12,14},{16,18,20,22,24,26,28,30},{1,3,5,7,9,11,13,15},{17..., dimensions={0} | all-to-all | bytes 24576 | tf_op jit(solution)/shard_map/all_to_all | solution.py:569
  16.0 6.5 %collective-permute-done.7.mate_hbm = bf16[4,128,384]{2,1,0:T(8,128)(2,1)S(1)} collective-permute-done((bf16[4,128,384]{2,1,0:T(8,128)(2,1)}, bf16[4,128,384]{2,1,0:T(8,128)(2,1)S(1)}, u32[]{:S(2)}, u32[]{:S(2)}) %collective-permute-start.7) | collective-permute-done | bytes 393248 | tf_op jit(solution)/shard_map/ppermute | solution.py:564
  23.3 2.9 %shard_map.161 = bf16[8,256,384]{2,1,0:T(8,128)(2,1)} custom-call(s32[8,2]{1,0:T(8,128)S(1)} %copy.18.asked_ref, bf16[4,128,384]{2,1,0:T(8,128)(2,1)} %bitcast.21, bf16[4,128,384]{2,1,0:T(8,128)(2,1)} %copy-done.16), custom_call_target="tpu_custom_call" | custom-call | flops 1000 | bytes 2359360 | tf_op jit(solution)/shard_map/pallas_call | solution.py:51
  26.2 4.0 %all-to-all-start.1 = ((bf16[8,256,384]{2,1,0:T(8,128)(2,1)}), bf16[8,256,384]{2,1,0:T(8,128)(2,1)S(1)}, u32[]{:S(2)}, u32[]{:S(2)}) async-start(bf16[8,256,384]{2,1,0:T(8,128)(2,1)} %shard_map.161), calls=%async_computation.1 | async-start | bytes 3145728 | tf_op jit(solution)/shard_map/all_to_all | solution.py:569
  30.2 7.1 %shard_map.158.mine_hbm = bf16[512,768]{1,0:T(8,128)(2,1)} custom-call(s32[1,2]{1,0:T(1,128)S(1)} %copy-done.15, bf16[512,768]{1,0:T(8,128)(2,1)} %bitcast.40, bf16[3,768,384]{2,1,0:T(8,128)(2,1)} %bitcast.39, bf16[384,768]{1,0:T(8,128)(2,1)} %w_out_hbm.1), custom_call_target="tpu_custom_call" | custom-call | flops 1610612736 | bytes 3932168 | tf_op jit(solution)/shard_map/pallas_call | solution.py:51
  37.4 2.5 %collective-permute-done.1.other_hbm = bf16[512,768]{1,0:T(8,128)(2,1)S(1)} collective-permute-done((bf16[512,768]{1,0:T(8,128)(2,1)}, bf16[512,768]{1,0:T(8,128)(2,1)S(1)}, u32[]{:S(2)}, u32[]{:S(2)}) %collective-permute-start.1) | collective-permute-done | bytes 786464 | tf_op jit(solution)/shard_map/ppermute | solution.py:561
  40.7 7.3 %shard_map.159 = (bf16[512,768]{1,0:T(8,128)(2,1)S(1)}, bf16[512,768]{1,0:T(8,128)(2,1)}) custom-call(bf16[512,768]{1,0:T(8,128)(2,1)} %bitcast.41, bf16[512,768]{1,0:T(8,128)(2,1)} %shard_map.158.mine_hbm, bf16[512,768]{1,0:T(8,128)(2,1)} %copy-done.19, bf16[768,1536]{1,0:T(8,128)(2,1)} %up_hbm.1, bf16[1536,768]{1,0:T(8,128)(2,1)} %down_hbm.1, ...), custom_call_target="tpu_custom_call" | custom-call | flops 2415919104 | bytes 8656896 | tf_op jit(solution)/shard_map/pallas_call | solution.py:51
  48.3 2.5 %collective-permute-done.2.other_ref = bf16[512,768]{1,0:T(8,128)(2,1)} collective-permute-done((bf16[512,768]{1,0:T(8,128)(2,1)}, bf16[512,768]{1,0:T(8,128)(2,1)}, u32[]{:S(2)}, u32[]{:S(2)}) %collective-permute-start.2) | collective-permute-done | bytes 786464 | tf_op jit(solution)/shard_map/ppermute | solution.py:561
  50.8 2.2 %shard_map.160 = f32[1,1,768]{2,1,0:T(1,128)S(1)} custom-call(s32[1,2]{1,0:T(1,128)S(1)} %copy-done.15, s32[1]{0:T(128)} %bitcast.core_ref.refs_1_, bf16[512,768]{1,0:T(8,128)(2,1)S(1)} %get-tuple-element.28.first_ref, bf16[512,768]{1,0:T(8,128)(2,1)} %get-tuple-element.29.mine_ref, bf16[512,768]{1,0:T(8,128)(2,1)} %collective-permute-done.2.other_ref, ...), custom_call_target="tpu_custom_call" | custom-call | flops 7864320 | bytes 2368524 | tf_op jit(solution)/shard_map/pallas_call | solution.py:51
  52.9 3.3 %collective-permute-start.3 = (f32[1,1,768]{2,1,0:T(1,128)S(1)}, f32[1,1,768]{2,1,0:T(1,128)S(1)}, u32[]{:S(2)}, u32[]{:S(2)}) collective-permute-start(f32[1,1,768]{2,1,0:T(1,128)S(1)} %shard_map.160), channel_id=1, source_target_pairs={{0,16},{2,18},{4,20},{6,22},{8,24},{10,26},{12,28},{14,30},{16,0},... | collective-permute-start | bytes 9224 | tf_op jit(solution)/shard_map/ppermute | solution.py:564
  67.5 2.9 %collective-permute-start = (s32[8,1,384]{2,1,0:T(1,128)S(1)}, s32[8,1,384]{2,1,0:T(1,128)S(1)}, u32[]{:S(2)}, u32[]{:S(2)}) collective-permute-start(s32[8,1,384]{2,1,0:T(1,128)S(1)} %all_to_all.15.got_ref), channel_id=1, source_target_pairs={{0,16},{2,18},{4,20},{6,22},{8,24},{10,26},{12,28},{14,30},{16,0},... | collective-permute-start | bytes 36872 | tf_op jit(solution)/shard_map/ppermute | solution.py:564
  74.9 3.7 %shard_map.162 = (bf16[4,128,384]{2,1,0:T(8,128)(2,1)S(1)}, bf16[32,384]{1,0:T(8,128)(2,1)S(1)}) custom-call(s32[4,5]{1,0:T(4,128)} %ids_ref.5, s32[1]{0:T(128)} %bitcast.1.self_ref.refs_0_, bf16[4,5,128,128]{3,2,1,0:T(8,128)(2,1)} %get-tuple-element.26.kept_hbm, bf16[4,128,128]{2,1,0:T(8,128)(2,1)} %get-tuple-element.27.pick_hbm, f32[8,1,768]{2,1,0:T(1,128)} %copy-done.17, ...), custom_call_target="tpu_custom_call" | custom-call | flops 251658240 | bytes 3219540 | tf_op jit(solution)/shard_map/pallas_call | solution.py:51
  80.4 3.2 %shard_map.163 = (bf16[512,384]{1,0:T(8,128)(2,1)}, bf16[512,384]{1,0:T(8,128)(2,1)S(1)}) custom-call(s32[1]{0:T(128)} %bitcast.core_ref.refs_1_, bf16[512,384]{1,0:T(8,128)(2,1)S(1)} %bitcast.26, bf16[512,384]{1,0:T(8,128)(2,1)S(1)} %collective-permute-done.8.other_ref, bf16[384,768]{1,0:T(8,128)(2,1)} %w_own_ref.3, ...), custom_call_target="tpu_custom_call" | custom-call | flops 301989888 | bytes 3694596 | tf_op jit(solution)/shard_map/pallas_call | solution.py:51
  85.3 3.9 %shard_map.164 = (bf16[16,128,384]{2,1,0:T(8,128)(2,1)}, bf16[512,384]{1,0:T(8,128)(2,1)}) custom-call(s32[4,5]{1,0:T(4,128)S(1)} %copy-done.12, s32[1]{0:T(128)} %bitcast.1.self_ref.refs_0_, s32[1]{0:T(128)} %bitcast.core_ref.refs_1_, bf16[512,384]{1,0:T(8,128)(2,1)S(1)} %get-tuple-element.35.mine_ref.refs_2_, ...), custom_call_target="tpu_custom_call" | custom-call | flops 553648128 | bytes 3997784 | tf_op jit(solution)/shard_map/pallas_call | solution.py:51
  90.0 6.2 %all-to-all-start.2 = ((bf16[16,128,384]{2,1,0:T(8,128)(2,1)}), bf16[16,128,384]{2,1,0:T(8,128)(2,1)S(1)}, u32[]{:S(2)}, u32[]{:S(2)}) async-start(bf16[16,128,384]{2,1,0:T(8,128)(2,1)} %get-tuple-element.47), calls=%async_computation.2 | async-start | bytes 3145728 | tf_op jit(solution)/shard_map/all_to_all | solution.py:569
  96.2 2.9 %shard_map.165 = (bf16[8,56,384]{2,1,0:T(8,128)(2,1)S(1)}, bf16[8,56,384]{2,1,0:T(8,128)(2,1)S(1)}) custom-call(s32[1]{0:T(128)} %bitcast.1.self_ref.refs_0_, s32[1]{0:T(128)} %bitcast.core_ref.refs_1_, bf16[512,384]{1,0:T(8,128)(2,1)} %copy-done.9, bf16[512,384]{1,0:T(8,128)(2,1)} %copy-done.10, bf16[512,384]{1,0:T(8,128)(2,1)} %bitcast.27, ...), custom_call_target="tpu_custom_call" | custom-call | flops 402653184 | bytes 2916360 | tf_op jit(solution)/shard_map/pallas_call | solution.py:51
  101.1 10.3 %collective-permute-done.11.theirs_ref = bf16[8,56,384]{2,1,0:T(8,128)(2,1)S(1)} collective-permute-done((bf16[8,56,384]{2,1,0:T(8,128)(2,1)S(1)}, bf16[8,56,384]{2,1,0:T(8,128)(2,1)S(1)}, u32[]{:S(2)}, u32[]{:S(2)}) %collective-permute-start.11) | collective-permute-done | bytes 344096 | tf_op jit(solution)/shard_map/ppermute | solution.py:564
  111.6 3.6 %collective-permute-start.12 = (bf16[4,56,384]{2,1,0:T(8,128)(2,1)S(1)}, bf16[4,56,384]{2,1,0:T(8,128)(2,1)S(1)}, u32[]{:S(2)}, u32[]{:S(2)}) collective-permute-start(bf16[4,56,384]{2,1,0:T(8,128)(2,1)S(1)} %get-tuple-element.40), channel_id=1, source_target_pairs={{0,4},{2,6},{4,0},{6,2},{8,12},{10,14},{12,8},{14,10},{16,20},{18,... | collective-permute-start | bytes 516104 | tf_op jit(solution)/shard_map/ppermute | solution.py:564
  115.2 5.7 %collective-permute-done.12.theirs_ref = bf16[4,56,384]{2,1,0:T(8,128)(2,1)S(1)} collective-permute-done((bf16[4,56,384]{2,1,0:T(8,128)(2,1)S(1)}, bf16[4,56,384]{2,1,0:T(8,128)(2,1)S(1)}, u32[]{:S(2)}, u32[]{:S(2)}) %collective-permute-start.12) | collective-permute-done | bytes 172064 | tf_op jit(solution)/shard_map/ppermute | solution.py:564
  121.0 3.5 %collective-permute-start.13 = (bf16[2,56,384]{2,1,0:T(8,128)(2,1)S(1)}, bf16[2,56,384]{2,1,0:T(8,128)(2,1)S(1)}, u32[]{:S(2)}, u32[]{:S(2)}) collective-permute-start(bf16[2,56,384]{2,1,0:T(8,128)(2,1)S(1)} %get-tuple-element.42), channel_id=1, source_target_pairs={{0,8},{2,10},{4,12},{6,14},{8,0},{10,2},{12,4},{14,6},{16,24},{18,... | collective-permute-start | bytes 258056 | tf_op jit(solution)/shard_map/ppermute | solution.py:564
  124.5 5.1 %collective-permute-done.13.theirs_ref = bf16[2,56,384]{2,1,0:T(8,128)(2,1)S(1)} collective-permute-done((bf16[2,56,384]{2,1,0:T(8,128)(2,1)S(1)}, bf16[2,56,384]{2,1,0:T(8,128)(2,1)S(1)}, u32[]{:S(2)}, u32[]{:S(2)}) %collective-permute-start.13) | collective-permute-done | bytes 86048 | tf_op jit(solution)/shard_map/ppermute | solution.py:564
  129.9 2.5 %shard_map.170.local_hbm = f32[4,128,384]{2,1,0:T(8,128)S(1)} custom-call(s32[4,5]{1,0:T(4,128)S(1)} %copy-done.13, s32[1]{0:T(128)} %bitcast.1.self_ref.refs_0_, bf16[4,128,384]{2,1,0:T(8,128)(2,1)S(1)} %bitcast.28, bf16[4,5,128,128]{3,2,1,0:T(8,128)(2,1)S(1)} %copy-done.4, bf16[4,128,384]{2,1,0:T(8,128)(2,1)S(1)} %bitcast.24), custom_call_target="tpu_custom_call" | custom-call | flops 251658240 | bytes 2228308 | tf_op jit(solution)/shard_map/pallas_call | solution.py:51
  136.0 3.1 %shard_map.171 = bf16[4,128,384]{2,1,0:T(8,128)(2,1)} custom-call(s32[1]{0:T(128)} %bitcast.1.self_ref.refs_0_, s32[8,2]{1,0:T(8,128)S(1)} %copy.18.asked_ref, s32[8,2]{1,0:T(8,128)S(1)} %copy.21.mate_ref, f32[4,128,384]{2,1,0:T(8,128)} %copy-done.3, bf16[16,128,384]{2,1,0:T(8,128)(2,1)S(1)} %all-to-all-done.2.got_ref), custom_call_target="tpu_custom_call" | custom-call | flops 1000 | bytes 2752644 | tf_op jit(solution)/shard_map/pallas_call | solution.py:51
  (76 shorter events, 28.9 us)
Async XLA Ops:
  0.6 21.9 %collective-permute-start.7 = (bf16[4,128,384]{2,1,0:T(8,128)(2,1)}, bf16[4,128,384]{2,1,0:T(8,128)(2,1)S(1)}, u32[]{:S(2)}, u32[]{:S(2)}) collective-permute-start(bf16[4,128,384]{2,1,0:T(8,128)(2,1)} %bitcast.20), channel_id=1, source_target_pairs={{0,16},{2,18},{4,20},{6,22},{8,24},{10,26},{12,28},{14,30},{16,0},... | collective-permute-start | bytes 1179656 | tf_op jit(solution)/shard_map/ppermute | solution.py:564
  26.2 48.0 %all-to-all-start.1 = ((bf16[8,256,384]{2,1,0:T(8,128)(2,1)}), bf16[8,256,384]{2,1,0:T(8,128)(2,1)S(1)}, u32[]{:S(2)}, u32[]{:S(2)}) async-start(bf16[8,256,384]{2,1,0:T(8,128)(2,1)} %shard_map.161), calls=%async_computation.1 | async-start | bytes 3145728 | tf_op jit(solution)/shard_map/all_to_all | solution.py:569
  37.3 2.6 %collective-permute-start.1 = (bf16[512,768]{1,0:T(8,128)(2,1)}, bf16[512,768]{1,0:T(8,128)(2,1)S(1)}, u32[]{:S(2)}, u32[]{:S(2)}) collective-permute-start(bf16[512,768]{1,0:T(8,128)(2,1)} %shard_map.158.mine_hbm), channel_id=1, source_target_pairs={{0,1},{1,0},{2,3},{3,2},{4,5},{5,4},{6,7},{7,6},{8,9},{9,8},{10,11... | collective-permute-start | bytes 2359304 | tf_op jit(solution)/shard_map/ppermute | solution.py:561
  48.1 24.0 %copy-start = (bf16[512,384]{1,0:T(8,128)(2,1)S(1)}, bf16[512,384]{1,0:T(8,128)(2,1)}, u32[]{:S(2)}) copy-start(bf16[512,384]{1,0:T(8,128)(2,1)} %param.20) | copy-start | bytes 1179652
  48.1 24.0 %copy-start.4 = (bf16[4,5,128,128]{3,2,1,0:T(8,128)(2,1)S(1)}, bf16[4,5,128,128]{3,2,1,0:T(8,128)(2,1)}, u32[]{:S(2)}) copy-start(bf16[4,5,128,128]{3,2,1,0:T(8,128)(2,1)} %adj_ref.5) | copy-start | bytes 1966084
  48.1 24.0 %copy-start.11 = (s32[4,5]{1,0:T(4,128)S(1)}, s32[4,5]{1,0:T(4,128)}, u32[]{:S(2)}) copy-start(s32[4,5]{1,0:T(4,128)} %ids_ref.5) | copy-start | bytes 244
  48.1 2.7 %collective-permute-start.2 = (bf16[512,768]{1,0:T(8,128)(2,1)}, bf16[512,768]{1,0:T(8,128)(2,1)}, u32[]{:S(2)}, u32[]{:S(2)}) collective-permute-start(bf16[512,768]{1,0:T(8,128)(2,1)} %get-tuple-element.29.mine_ref), channel_id=1, source_target_pairs={{0,1},{1,0},{2,3},{3,2},{4,5},{5,4},{6,7},{7,6},{8,9},{9,8},{10,11... | collective-permute-start | bytes 2359304 | tf_op jit(solution)/shard_map/ppermute | solution.py:561
  52.9 4.9 %collective-permute-start.3 = (f32[1,1,768]{2,1,0:T(1,128)S(1)}, f32[1,1,768]{2,1,0:T(1,128)S(1)}, u32[]{:S(2)}, u32[]{:S(2)}) collective-permute-start(f32[1,1,768]{2,1,0:T(1,128)S(1)} %shard_map.160), channel_id=1, source_target_pairs={{0,16},{2,18},{4,20},{6,22},{8,24},{10,26},{12,28},{14,30},{16,0},... | collective-permute-start | bytes 9224 | tf_op jit(solution)/shard_map/ppermute | solution.py:564
  57.9 3.7 %collective-permute-start.4 = (f32[2,1,768]{2,1,0:T(1,128)S(1)}, f32[2,1,768]{2,1,0:T(1,128)S(1)}, u32[]{:S(2)}, u32[]{:S(2)}) collective-permute-start(f32[2,1,768]{2,1,0:T(1,128)S(1)} %pad_maximum_fusion.2), channel_id=1, source_target_pairs={{0,8},{2,10},{4,12},{6,14},{8,0},{10,2},{12,4},{14,6},{16,24},{18,... | collective-permute-start | bytes 18440 | tf_op jit(solution)/shard_map/ppermute | solution.py:564
  59.9 18.7 %collective-permute-start.9 = (bf16[384,768]{1,0:T(8,128)(2,1)}, bf16[384,768]{1,0:T(8,128)(2,1)}, u32[]{:S(2)}, u32[]{:S(2)}) collective-permute-start(bf16[384,768]{1,0:T(8,128)(2,1)} %w_own_ref.3), channel_id=1, source_target_pairs={{0,1},{1,0},{2,3},{3,2},{4,5},{5,4},{6,7},{7,6},{8,9},{9,8},{10,11... | collective-permute-start | bytes 1769480 | tf_op jit(solution)/shard_map/ppermute | solution.py:561
  61.6 3.8 %collective-permute-start.5 = (f32[4,1,768]{2,1,0:T(1,128)S(1)}, f32[4,1,768]{2,1,0:T(1,128)S(1)}, u32[]{:S(2)}, u32[]{:S(2)}) collective-permute-start(f32[4,1,768]{2,1,0:T(1,128)S(1)} %pad_maximum_fusion.1), channel_id=1, source_target_pairs={{0,4},{2,6},{4,0},{6,2},{8,12},{10,14},{12,8},{14,10},{16,20},{18,... | collective-permute-start | bytes 36872 | tf_op jit(solution)/shard_map/ppermute | solution.py:564
  65.4 8.9 %collective-permute-start.6 = (f32[8,1,768]{2,1,0:T(1,128)S(1)}, f32[8,1,768]{2,1,0:T(1,128)S(1)}, u32[]{:S(2)}, u32[]{:S(2)}) collective-permute-start(f32[8,1,768]{2,1,0:T(1,128)S(1)} %pad_maximum_fusion.near_hbm), channel_id=1, source_target_pairs={{0,2},{2,0},{4,6},{6,4},{8,10},{10,8},{12,14},{14,12},{16,18},{18,... | collective-permute-start | bytes 73736 | tf_op jit(solution)/shard_map/ppermute | solution.py:564
  67.5 4.6 %collective-permute-start = (s32[8,1,384]{2,1,0:T(1,128)S(1)}, s32[8,1,384]{2,1,0:T(1,128)S(1)}, u32[]{:S(2)}, u32[]{:S(2)}) collective-permute-start(s32[8,1,384]{2,1,0:T(1,128)S(1)} %all_to_all.15.got_ref), channel_id=1, source_target_pairs={{0,16},{2,18},{4,20},{6,22},{8,24},{10,26},{12,28},{14,30},{16,0},... | collective-permute-start | bytes 36872 | tf_op jit(solution)/shard_map/ppermute | solution.py:564
  78.6 10.6 %copy-start.5 = (bf16[4,128,384]{2,1,0:T(8,128)(2,1)}, bf16[4,128,384]{2,1,0:T(8,128)(2,1)S(1)}, u32[]{:S(2)}) copy-start(bf16[4,128,384]{2,1,0:T(8,128)(2,1)S(1)} %get-tuple-element.30) | copy-start | bytes 1179652
  78.6 1.8 %collective-permute-start.8 = (bf16[512,384]{1,0:T(8,128)(2,1)S(1)}, bf16[512,384]{1,0:T(8,128)(2,1)S(1)}, u32[]{:S(2)}, u32[]{:S(2)}) collective-permute-start(bf16[512,384]{1,0:T(8,128)(2,1)S(1)} %bitcast.25), channel_id=1, source_target_pairs={{0,1},{1,0},{2,3},{3,2},{4,5},{5,4},{6,7},{7,6},{8,9},{9,8},{10,11... | collective-permute-start | bytes 1179656 | tf_op jit(solution)/shard_map/ppermute | solution.py:561
  83.6 1.7 %collective-permute-start.10 = (bf16[512,384]{1,0:T(8,128)(2,1)S(1)}, bf16[512,384]{1,0:T(8,128)(2,1)S(1)}, u32[]{:S(2)}, u32[]{:S(2)}) collective-permute-start(bf16[512,384]{1,0:T(8,128)(2,1)S(1)} %get-tuple-element.35.mine_ref.refs_2_), channel_id=1, source_target_pairs={{0,1},{1,0},{2,3},{3,2},{4,5},{5,4},{6,7},{7,6},{8,9},{9,8},{10,11... | collective-permute-start | bytes 1179656 | tf_op jit(solution)/shard_map/ppermute | solution.py:561
  90.0 46.0 %all-to-all-start.2 = ((bf16[16,128,384]{2,1,0:T(8,128)(2,1)}), bf16[16,128,384]{2,1,0:T(8,128)(2,1)S(1)}, u32[]{:S(2)}, u32[]{:S(2)}) async-start(bf16[16,128,384]{2,1,0:T(8,128)(2,1)} %get-tuple-element.47), calls=%async_computation.2 | async-start | bytes 3145728 | tf_op jit(solution)/shard_map/all_to_all | solution.py:569
  96.2 33.7 %copy-start.2 = (bf16[512,384]{1,0:T(8,128)(2,1)S(1)}, bf16[512,384]{1,0:T(8,128)(2,1)}, u32[]{:S(2)}) copy-start(bf16[512,384]{1,0:T(8,128)(2,1)} %refs_8_.1) | copy-start | bytes 1179652
  96.2 33.7 %copy-start.6 = (bf16[512,384]{1,0:T(8,128)(2,1)S(1)}, bf16[512,384]{1,0:T(8,128)(2,1)}, u32[]{:S(2)}) copy-start(bf16[512,384]{1,0:T(8,128)(2,1)} %get-tuple-element.36.refs_5_) | copy-start | bytes 1179652
  96.2 33.6 %copy-start.13 = (s32[4,5]{1,0:T(4,128)S(1)}, s32[4,5]{1,0:T(4,128)}, u32[]{:S(2)}) copy-start(s32[4,5]{1,0:T(4,128)} %ids_ref.5) | copy-start | bytes 244
  99.1 12.3 %collective-permute-start.11 = (bf16[8,56,384]{2,1,0:T(8,128)(2,1)S(1)}, bf16[8,56,384]{2,1,0:T(8,128)(2,1)S(1)}, u32[]{:S(2)}, u32[]{:S(2)}) collective-permute-start(bf16[8,56,384]{2,1,0:T(8,128)(2,1)S(1)} %get-tuple-element.38), channel_id=1, source_target_pairs={{0,2},{2,0},{4,6},{6,4},{8,10},{10,8},{12,14},{14,12},{16,18},{18,... | collective-permute-start | bytes 1032200 | tf_op jit(solution)/shard_map/ppermute | solution.py:564
  111.6 9.4 %collective-permute-start.12 = (bf16[4,56,384]{2,1,0:T(8,128)(2,1)S(1)}, bf16[4,56,384]{2,1,0:T(8,128)(2,1)S(1)}, u32[]{:S(2)}, u32[]{:S(2)}) collective-permute-start(bf16[4,56,384]{2,1,0:T(8,128)(2,1)S(1)} %get-tuple-element.40), channel_id=1, source_target_pairs={{0,4},{2,6},{4,0},{6,2},{8,12},{10,14},{12,8},{14,10},{16,20},{18,... | collective-permute-start | bytes 516104 | tf_op jit(solution)/shard_map/ppermute | solution.py:564
  121.0 8.6 %collective-permute-start.13 = (bf16[2,56,384]{2,1,0:T(8,128)(2,1)S(1)}, bf16[2,56,384]{2,1,0:T(8,128)(2,1)S(1)}, u32[]{:S(2)}, u32[]{:S(2)}) collective-permute-start(bf16[2,56,384]{2,1,0:T(8,128)(2,1)S(1)} %get-tuple-element.42), channel_id=1, source_target_pairs={{0,8},{2,10},{4,12},{6,14},{8,0},{10,2},{12,4},{14,6},{16,24},{18,... | collective-permute-start | bytes 258056 | tf_op jit(solution)/shard_map/ppermute | solution.py:564
  129.6 5.7 %collective-permute-start.14 = (bf16[1,56,384]{2,1,0:T(8,128)(2,1)S(1)}, bf16[1,56,384]{2,1,0:T(8,128)(2,1)S(1)}, u32[]{:S(2)}, u32[]{:S(2)}) collective-permute-start(bf16[1,56,384]{2,1,0:T(8,128)(2,1)S(1)} %get-tuple-element.44), channel_id=1, source_target_pairs={{0,16},{2,18},{4,20},{6,22},{8,24},{10,26},{12,28},{14,30},{16,0},... | collective-permute-start | bytes 129032 | tf_op jit(solution)/shard_map/ppermute | solution.py:564
  (13 other events, 57.2 us)

commit v6 on v5

--- a/solution.py
+++ b/solution.py
@@ -293,10 +293,9 @@
     out_ref[...] = mm(inner_ref[...], down_ref[...]).astype(jnp.bfloat16)
 
 
-def pool_body(seq, counts_ref, core_ref, first_ref, mine_ref, other_ref, gains_ref, out_ref, pooled_ref):
-    _, _, lanes = out_ref.shape
-    texts_here = first_ref.shape[0] // seq
-    half = lanes // texts_here
+def pool_body(seq, counts_ref, first_ref, mine_ref, other_ref, gains_ref, out_ref):
+    shards = out_ref.shape[0]
+    texts_here, width = first_ref.shape[0] // seq, first_ref.shape[1]
     for t in range(texts_here):
         rows = slice(t * seq, (t + 1) * seq)
         added = mine_ref[rows, :].astype(jnp.float32) + other_ref[rows, :].astype(jnp.float32)
@@ -304,57 +303,30 @@
         count = counts_ref[0, t]
         live = lax.broadcasted_iota(jnp.int32, (seq, 1), 0) < count
         total = jnp.sum(jnp.where(live, second, 0.0), axis=0, keepdims=True)
-        pooled_ref[...] = jnp.broadcast_to(
-            total / count.astype(jnp.float32), pooled_ref.shape
+        pooled = (total / count.astype(jnp.float32)).astype(jnp.bfloat16).astype(jnp.float32)
+        out_ref[:, :, t * width : (t + 1) * width] = jnp.broadcast_to(pooled, (shards, width)).reshape(
+            shards, 1, width
         )
-        start = pl.multiple_of(core_ref[0] * half, LANES)
-        own = pooled_ref[:, pl.ds(start, half)][0:1, :]
-        own = own.astype(jnp.bfloat16).astype(jnp.float32)
-        out_ref[:, :, t * half : (t + 1) * half] = own.reshape(1, 1, half)
-
-
-def pooled_rows(me, near_ref, far_ref, half):
-    shards = 2 * near_ref.shape[0]
-    parts = []
-    for first in range(0, near_ref.shape[2], half):
-        for ref in (near_ref, far_ref):
-            part = ref[:, :, first : first + half].reshape(shards // 2, half)
-            parts.append(part.astype(jnp.bfloat16))
-    stacked = jnp.concatenate(parts, axis=0)
-    texts = stacked.shape[0]
-    row = lax.broadcasted_iota(jnp.int32, (texts, texts), 0)
-    column = lax.broadcasted_iota(jnp.int32, (texts, texts), 1)
-    place = column & (shards - 1)
-    offset = jnp.zeros_like(place)
-    reach = 1
-    while reach < shards:
-        offset = 2 * offset + (place & 1)
-        place = lax.shift_right_logical(place, 1)
-        reach *= 2
-    source = column - (column & (shards - 1)) + (offset ^ me)
-    order = jnp.where(row == source, 1.0, 0.0).astype(jnp.bfloat16)
-    return mm(order, stacked).astype(jnp.bfloat16)
+
+
+def pooled_rows(pooled_ref, width):
+    shards, _, lanes = pooled_ref.shape
+    parts = [
+        pooled_ref[:, :, first : first + width].reshape(shards, width).astype(jnp.bfloat16)
+        for first in range(0, lanes, width)
+    ]
+    return jnp.concatenate(parts, axis=0)
 
 
 def gather_body(
-    ids_hbm, self_ref, kept_hbm, pick_hbm, near_hbm, far_hbm, cache_hbm, remote_ref, out_ref,
-    pooled_ref, ids_ref, kept_ref, pick_ref, near_ref, far_ref, cache_ref, source_ref, sems
+    ids_hbm, self_ref, kept_hbm, cache_hbm, remote_ref, out_hbm,
+    ids_ref, kept_ref, cache_ref, source_ref, out_ref, sems, out_sems
 ):
-    started = copies(
-        [
-            (near_hbm, near_ref), (far_hbm, far_ref), (ids_hbm, ids_ref), (cache_hbm, cache_ref),
-            (pick_hbm, pick_ref), (kept_hbm, kept_ref),
-        ],
-        sems,
-    )
+    started = copies([(ids_hbm, ids_ref), (cache_hbm, cache_ref), (kept_hbm, kept_ref)], sems)
     tiles_here, entries, tile_rows, _ = kept_ref.shape
-    half = cache_ref.shape[2]
     me = self_ref[0]
-    for copy in started:
-        copy.wait()
-    pooled = pooled_rows(me, near_ref, far_ref, half)
-    pooled_ref[...] = pooled
-    texts = pooled.shape[0]
+    started[0].wait()
+    started[1].wait()
 
     def fetch(r, k):
         tile_id = ids_ref[r, k]
@@ -371,36 +343,53 @@
             first = pl.multiple_of(side * tile_rows, tile_rows)
             source_ref[r % 2, k] = remote_ref[spot, pl.ds(first, tile_rows), :]
 
+    sent = []
     for r in range(tiles_here):
         lax.fori_loop(
             0, entries, lambda k, c: (fetch(r, k), c)[1], 0, unroll=unroll(entries)
         )
-        total = mm(pick_ref[r][:, :texts], pooled)
+        if r == 0:
+            started[2].wait()
+        total = jnp.zeros(out_ref.shape[1:], jnp.float32)
         for k in range(entries):
             total = total + mm(kept_ref[r, k], source_ref[r % 2, k])
         out_ref[r] = total.astype(jnp.bfloat16)
-
-
-def forward_body(core_ref, mine_ref, other_ref, w_own_ref, w_other_ref, grad_ref, own_ref, base_ref, pooled_ref, node_ref, slope_ref):
-    _, half = mine_ref.shape
+        sent.append(pltpu.make_async_copy(out_ref.at[r], out_hbm.at[r], out_sems.at[r]))
+        sent[-1].start()
+    for copy in sent:
+        copy.wait()
+
+
+def forward_body(
+    core_ref, mine_ref, other_ref, w_own_ref, w_other_ref, grad_ref, own_ref, base_ref, pick_ref,
+    pooled_ref, node_ref, slope_ref, rows_ref
+):
+    half = mine_ref.shape[1]
     start = pl.multiple_of(core_ref[0] * half, LANES)
-    hidden = mm(mine_ref[...], w_own_ref[:, pl.ds(start, half)]) + mm(
-        other_ref[...], w_other_ref[:, pl.ds(start, half)]
+    far = pl.multiple_of((1 - core_ref[0]) * half, LANES)
+    rows_ref[...] = pooled_rows(pooled_ref, rows_ref.shape[1])
+    texts = rows_ref.shape[0]
+    here = rows_ref[:, pl.ds(start, half)]
+    w_own = w_own_ref[:, pl.ds(start, half)]
+    w_other = w_other_ref[:, pl.ds(start, half)]
+    moved = (mm(here, w_own) + mm(rows_ref[:, pl.ds(far, half)], w_other)).astype(jnp.bfloat16)
+    hidden = (
+        mm(mine_ref[...], w_own) + mm(other_ref[...], w_other) + mm(pick_ref[:, :texts], moved)
     )
     square = hidden * hidden
     gate = jnp.tanh(ROOT * hidden * (1.0 + CUBE * square))
     lifted = 0.5 * (1.0 + gate)
     slope = lifted + 0.5 * hidden * (1.0 - gate * gate) * (ROOT * (1.0 + 3.0 * CUBE * square))
     slope_ref[...] = (grad_ref[...].astype(jnp.float32) * slope).astype(jnp.bfloat16)
-    fresh = mm(own_ref[:, : pooled_ref.shape[0]], pooled_ref[...])
+    fresh = mm(own_ref[:, :texts], here)
     node_ref[...] = (base_ref[...].astype(jnp.float32) + fresh + hidden * lifted).astype(
         jnp.bfloat16
     )
 
 
 def chunk_body(
-    per, texts_here, self_ref, core_ref, mine_ref, other_ref, agg_ref, down_ref, pick_ref, own_ref,
-    grad_ref, keep_ref, give_ref, w_ref, text_ref
+    per, texts_here, self_ref, core_ref, mine_ref, other_ref, part_ref, down_ref, pick_ref, own_ref,
+    grad_ref, pooled_ref, keep_ref, give_ref, w_ref, text_ref, rows_ref, agg_ref
 ):
     kept, _, half = keep_ref.shape
     shards = 2 * kept
@@ -409,6 +398,11 @@
     me = self_ref[0]
     own = pl.multiple_of(core_ref[0] * half, LANES)
     far = pl.multiple_of((1 - core_ref[0]) * half, LANES)
+    rows_ref[...] = pooled_rows(pooled_ref, rows_ref.shape[1])
+    here = rows_ref[:, pl.ds(own, half)]
+    agg_ref[...] = (
+        part_ref[...].astype(jnp.float32) + mm(pick_ref[:, : here.shape[0]], here)
+    ).astype(jnp.bfloat16)
     columns = 2 * half
     text_ref[...] = mm(pick_ref[...], down_ref[...], (0, 0)) + mm(
         own_ref[...], grad_ref[...], (0, 0)
@@ -647,19 +641,12 @@
     )
     pooled = call(
         functools.partial(pool_body, seq),
-        [shape((1, 1, texts_here * half), jnp.float32)],
-        [token_counts, core, first, mlp, swap(mlp), ln_gains],
-        [SMEM, SMEM, VMEM, VMEM, VMEM, VMEM],
+        [shape((shards, 1, texts_here * width), jnp.float32)],
+        [token_counts, first, mlp, swap(mlp), ln_gains],
+        [SMEM, VMEM, VMEM, VMEM, VMEM],
         flops=20 * count * width,
-        scratch=[pltpu.VMEM((8, width), jnp.float32)],
-    )
-    near = pooled
-    reach = peers
-    far = toward(near, reach)
-    while reach > 1:
-        reach = reach // 2
-        near = jnp.concatenate([near, far], axis=0)
-        far = toward(near, reach)
+    )
+    pooled = spread(pooled)
 
     kept, pick, own, base = call(
         mask_body,
@@ -681,33 +668,35 @@
         ],
         out_specs=[HBM] * 4,
     )
-    gathered, pooled = call(
+    gathered = call(
         gather_body,
-        [shape((tiles_here, tile_rows, half)), shape((texts, half))],
-        [adj_tiles, me, kept, pick, near, far, cache_tiles, remote],
-        [HBM, SMEM, HBM, HBM, HBM, HBM, HBM, VMEM],
+        [shape((tiles_here, tile_rows, half))],
+        [adj_tiles, me, kept, cache_tiles, remote],
+        [HBM, SMEM, HBM, HBM, VMEM],
         flops=2 * adj_values.size * half,
         scratch=[
             pltpu.SMEM(adj_tiles.shape, jnp.int32),
             pltpu.VMEM(kept.shape, jnp.bfloat16),
-            pltpu.VMEM(pick.shape, jnp.bfloat16),
-            pltpu.VMEM(near.shape, jnp.float32),
-            pltpu.VMEM(far.shape, jnp.float32),
             pltpu.VMEM(cache_tiles.shape, jnp.bfloat16),
             pltpu.VMEM((2, entries, tile_rows, half), jnp.bfloat16),
-            pltpu.SemaphoreType.DMA((6,)),
-        ],
+            pltpu.VMEM((tiles_here, tile_rows, half), jnp.bfloat16),
+            pltpu.SemaphoreType.DMA((3,)),
+            pltpu.SemaphoreType.DMA((tiles_here,)),
+        ],
+        out_specs=[HBM],
     )
     gathered = gathered.reshape(nodes_here, half)
+    picked = pick.reshape(nodes_here, slots)
     node_out, slope = call(
         forward_body,
         [shape((nodes_here, half)), shape((nodes_here, half))],
         [
             core, gathered, swap(gathered), w_gnn, w_other, out_grad,
-            own.reshape(nodes_here, slots), base.reshape(nodes_here, half), pooled,
-        ],
-        [SMEM] + [VMEM] * 8,
+            own.reshape(nodes_here, slots), base.reshape(nodes_here, half), picked, pooled,
+        ],
+        [SMEM] + [PULL] * 8 + [VMEM],
         flops=4 * nodes_here * half * half,
+        scratch=[pltpu.VMEM((texts, width), jnp.bfloat16)],
     )
     grad_tiles = out_grad.reshape(tiles_here, tile_rows, half)
     slope_other = swap(slope)
@@ -732,14 +721,16 @@
         functools.partial(chunk_body, per, texts_here),
         [shape(halves), shape(halves)],
         [
-            me, core, slope, slope_other, gathered, down, pick.reshape(nodes_here, slots),
-            own.reshape(nodes_here, slots), out_grad,
-        ],
-        [SMEM, SMEM] + [PULL] * 7,
+            me, core, slope, slope_other, gathered, down, picked,
+            own.reshape(nodes_here, slots), out_grad, pooled,
+        ],
+        [SMEM, SMEM] + [PULL] * 8,
         flops=4 * nodes_here * half * (half + slots),
         scratch=[
             pltpu.VMEM((width + ROWS, half), jnp.float32),
             pltpu.VMEM((slots, half), jnp.float32),
+            pltpu.VMEM((texts, width), jnp.bfloat16),
+            pltpu.VMEM((nodes_here, half), jnp.bfloat16),
         ],
     )
     local = call(

time: 140 us -> 136 us (0.971)
  waiting for transfers between devices: 44.6 us -> 39.7 us
    ppermute x10 -> x6, waiting for transfers between devices: 36.3 us -> 27.8 us  [toward(): lax.ppermute(values, 'graph', [(i, i ^ reach) for i in range(shards)])]
    all_to_all x2 -> x3, waiting for transfers between devices: 0.01 us -> 7.66 us  [spread(): lax.all_to_all(values, 'graph', split_axis=0, concat_axis=0, tiled=True,...]
    ppermute x10 -> x6, starting transfers between devices: 25.8 us -> 20.2 us  [toward(): lax.ppermute(values, 'graph', [(i, i ^ reach) for i in range(shards)])]
    all_to_all x2 -> x3, starting transfers between devices: 10.2 us -> 15.4 us  [spread(): lax.all_to_all(values, 'graph', split_axis=0, concat_axis=0, tiled=True,...]
    ppermute x5, waiting for transfers between devices: 8.27 us -> 4.2 us  [swap(): lax.ppermute(values, 'mp', [(i, cores - 1 - i) for i in range(cores)])]
    pallas_call x16, Pallas kernels: 42.6 us -> 44 us  [call(): pl.pallas_call(body, out_shape=tuple(outs) if many else outs[0], in_specs...]
    unnamed x42 -> x32, local copies, waits for them, and re-layouts: 4.11 us -> 4.31 us
  transfers between devices with their start and end apart: 17 -> 14, of which waited for: 13 -> 9; matrix products, arithmetic and copies ran while one was open for 0% -> 0% of each run, Pallas kernels for 21% -> 22%
where the time goes in v6:
time: 136 us
  Pallas kernels  44 us (32%)
  waiting for transfers between devices  39.7 us (29%)
  starting transfers between devices  36.4 us (27%)
  blocking collectives  10.1 us (7%)
  local copies, waits for them, and re-layouts  4.49 us (3%)
    pallas_call x16, Pallas kernels, call(): pl.pallas_call(body, out_shape=tuple(outs) if many else outs[0], in_specs...  44 us
    ppermute x6, waiting for transfers between devices, toward(): lax.ppermute(values, 'graph', [(i, i ^ reach) for i in range(shards)])  27.8 us
    ppermute x6, starting transfers between devices, toward(): lax.ppermute(values, 'graph', [(i, i ^ reach) for i in range(shards)])  20.2 us
    all_to_all x3, starting transfers between devices, spread(): lax.all_to_all(values, 'graph', split_axis=0, concat_axis=0, tiled=True,...  15.4 us
    all_to_all x1, blocking collectives, spread(): lax.all_to_all(values, 'graph', split_axis=0, concat_axis=0, tiled=True,...  10.1 us
    all_to_all x3, waiting for transfers between devices, spread(): lax.all_to_all(values, 'graph', split_axis=0, concat_axis=0, tiled=True,...  7.66 us
    unnamed x32, local copies, waits for them, and re-layouts  4.31 us
    ppermute x5, waiting for transfers between devices, swap(): lax.ppermute(values, 'mp', [(i, cores - 1 - i) for i in range(cores)])  4.2 us
  transfers between devices with their start and end apart: 14, of which 9 were waited for; matrix products, arithmetic and copies ran while one was open for 0% of the time, Pallas kernels for 22%

profile of v6, /device:TPU:0, one launch (start us, length us, event | category | flops | bytes accessed | tf_op | source)
XLA Modules:
  0.0 135.8 jit_solution(4751111793575260336)
XLA Ops:
  0.6 4.1 %collective-permute-start.1 = (bf16[4,128,384]{2,1,0:T(8,128)(2,1)}, bf16[4,128,384]{2,1,0:T(8,128)(2,1)S(1)}, u32[]{:S(2)}, u32[]{:S(2)}) collective-permute-start(bf16[4,128,384]{2,1,0:T(8,128)(2,1)} %bitcast.20), channel_id=1, source_target_pairs={{0,16},{2,18},{4,20},{6,22},{8,24},{10,26},{12,28},{14,30},{16,0},... | collective-permute-start | bytes 1179656 | tf_op jit(solution)/shard_map/ppermute | solution.py:558
  5.7 10.1 %all_to_all.20.got_ref = s32[8,1,384]{2,1,0:T(1,128)S(1)} all-to-all(s32[8,1,384]{2,1,0:T(1,128)S(1)} %shard_map.156), channel_id=1, replica_groups={{0,2,4,6,8,10,12,14},{16,18,20,22,24,26,28,30},{1,3,5,7,9,11,13,15},{17..., dimensions={0} | all-to-all | bytes 24576 | tf_op jit(solution)/shard_map/all_to_all | solution.py:563
  16.0 6.5 %collective-permute-done.1.mate_hbm = bf16[4,128,384]{2,1,0:T(8,128)(2,1)S(1)} collective-permute-done((bf16[4,128,384]{2,1,0:T(8,128)(2,1)}, bf16[4,128,384]{2,1,0:T(8,128)(2,1)S(1)}, u32[]{:S(2)}, u32[]{:S(2)}) %collective-permute-start.1) | collective-permute-done | bytes 393248 | tf_op jit(solution)/shard_map/ppermute | solution.py:558
  23.3 2.9 %shard_map.158 = bf16[8,256,384]{2,1,0:T(8,128)(2,1)} custom-call(s32[8,2]{1,0:T(8,128)S(1)} %copy.18.asked_ref, bf16[4,128,384]{2,1,0:T(8,128)(2,1)} %bitcast.21, bf16[4,128,384]{2,1,0:T(8,128)(2,1)} %copy-done.13), custom_call_target="tpu_custom_call" | custom-call | flops 1000 | bytes 2359360 | tf_op jit(solution)/shard_map/pallas_call | solution.py:51
  26.2 4.0 %all-to-all-start.1 = ((bf16[8,256,384]{2,1,0:T(8,128)(2,1)}), bf16[8,256,384]{2,1,0:T(8,128)(2,1)S(1)}, u32[]{:S(2)}, u32[]{:S(2)}) async-start(bf16[8,256,384]{2,1,0:T(8,128)(2,1)} %shard_map.158), calls=%async_computation.1 | async-start | bytes 3145728 | tf_op jit(solution)/shard_map/all_to_all | solution.py:563
  30.2 7.1 %shard_map.160.mine_hbm = bf16[512,768]{1,0:T(8,128)(2,1)} custom-call(s32[1,2]{1,0:T(1,128)S(1)} %copy-done.11, bf16[512,768]{1,0:T(8,128)(2,1)} %bitcast.41, bf16[3,768,384]{2,1,0:T(8,128)(2,1)} %bitcast.40, bf16[384,768]{1,0:T(8,128)(2,1)} %w_out_hbm.1), custom_call_target="tpu_custom_call" | custom-call | flops 1610612736 | bytes 3932168 | tf_op jit(solution)/shard_map/pallas_call | solution.py:51
  37.4 2.5 %collective-permute-done.4.other_hbm = bf16[512,768]{1,0:T(8,128)(2,1)S(1)} collective-permute-done((bf16[512,768]{1,0:T(8,128)(2,1)}, bf16[512,768]{1,0:T(8,128)(2,1)S(1)}, u32[]{:S(2)}, u32[]{:S(2)}) %collective-permute-start.4) | collective-permute-done | bytes 786464 | tf_op jit(solution)/shard_map/ppermute | solution.py:555
  40.8 7.3 %shard_map.161 = (bf16[512,768]{1,0:T(8,128)(2,1)S(1)}, bf16[512,768]{1,0:T(8,128)(2,1)}) custom-call(bf16[512,768]{1,0:T(8,128)(2,1)} %bitcast.42, bf16[512,768]{1,0:T(8,128)(2,1)} %shard_map.160.mine_hbm, bf16[512,768]{1,0:T(8,128)(2,1)} %copy-done.14, bf16[768,1536]{1,0:T(8,128)(2,1)} %up_hbm.1, bf16[1536,768]{1,0:T(8,128)(2,1)} %down_hbm.1, ...), custom_call_target="tpu_custom_call" | custom-call | flops 2415919104 | bytes 8656896 | tf_op jit(solution)/shard_map/pallas_call | solution.py:51
  48.7 3.3 %collective-permute-start = (s32[8,1,384]{2,1,0:T(1,128)S(1)}, s32[8,1,384]{2,1,0:T(1,128)S(1)}, u32[]{:S(2)}, u32[]{:S(2)}) collective-permute-start(s32[8,1,384]{2,1,0:T(1,128)S(1)} %all_to_all.20.got_ref), channel_id=1, source_target_pairs={{0,16},{2,18},{4,20},{6,22},{8,24},{10,26},{12,28},{14,30},{16,0},... | collective-permute-start | bytes 36872 | tf_op jit(solution)/shard_map/ppermute | solution.py:558
  53.6 2.1 %shard_map.157 = (bf16[4,5,128,128]{3,2,1,0:T(8,128)(2,1)}, bf16[4,128,128]{2,1,0:T(8,128)(2,1)}, bf16[4,128,128]{2,1,0:T(8,128)(2,1)}, bf16[4,128,384]{2,1,0:T(8,128)(2,1)}) custom-call(s32[4,5]{1,0:T(4,128)S(1)} %copy-done.8, s32[1]{0:T(128)} %bitcast.1.self_ref.refs_0_, s32[8,1,384]{2,1,0:T(1,128)S(1)} %all_to_all.20.got_ref, ...), custom_call_target="tpu_custom_call" | custom-call | flops 83886080 | bytes 2383956 | tf_op jit(solution)/shard_map/pallas_call | solution.py:51
  55.7 3.7 %shard_map.159 = bf16[4,128,384]{2,1,0:T(8,128)(2,1)} custom-call(s32[4,5]{1,0:T(4,128)} %ids_ref.5, s32[1]{0:T(128)} %bitcast.1.self_ref.refs_0_, bf16[4,5,128,128]{3,2,1,0:T(8,128)(2,1)} %get-tuple-element.24.kept_hbm, bf16[4,128,384]{2,1,0:T(8,128)(2,1)} %bitcast.22, bf16[8,256,384]{2,1,0:T(8,128)(2,1)S(1)} %all-to-all-done.1.remote_ref), custom_call_target="tpu_custom_call" | custom-call | flops 251658240 | bytes 3014740 | tf_op jit(solution)/shard_map/pallas_call | solution.py:51
  59.5 2.8 %shard_map.162 = f32[16,1,1536]{2,1,0:T(1,128)} custom-call(s32[1,2]{1,0:T(1,128)S(1)} %copy-done.11, bf16[512,768]{1,0:T(8,128)(2,1)S(1)} %get-tuple-element.28.first_ref, bf16[512,768]{1,0:T(8,128)(2,1)} %get-tuple-element.29.mine_ref, bf16[512,768]{1,0:T(8,128)(2,1)} %collective-permute-done.5.other_ref, f32[2,768]{1,0:T(2,128)S(1)} %copy-done.10), custom_call_target="tpu_custom_call" | custom-call | flops 7864320 | bytes 2463752 | tf_op jit(solution)/shard_map/pallas_call | solution.py:51
  62.3 7.7 %all-to-all-start.2 = ((f32[16,1,1536]{2,1,0:T(1,128)}), f32[16,1,1536]{2,1,0:T(1,128)S(1)}, u32[]{:S(2)}, u32[]{:S(2)}) async-start(f32[16,1,1536]{2,1,0:T(1,128)} %shard_map.162), calls=%async_computation.2 | async-start | bytes 196608 | tf_op jit(solution)/shard_map/all_to_all | solution.py:563
  70.1 7.7 %all-to-all-done.2.refs_9_ = f32[16,1,1536]{2,1,0:T(1,128)S(1)} async-done(((f32[16,1,1536]{2,1,0:T(1,128)}), f32[16,1,1536]{2,1,0:T(1,128)S(1)}, u32[]{:S(2)}, u32[]{:S(2)}) %all-to-all-start.2) | async-done | bytes 98336 | tf_op jit(solution)/shard_map/all_to_all | solution.py:563
  78.5 4.0 %shard_map.163 = (bf16[512,384]{1,0:T(8,128)(2,1)}, bf16[512,384]{1,0:T(8,128)(2,1)S(1)}) custom-call(s32[1]{0:T(128)} %bitcast.refs_0_.core_ref.refs_1_, bf16[512,384]{1,0:T(8,128)(2,1)} %bitcast.27, bf16[512,384]{1,0:T(8,128)(2,1)} %copy-done.12, bf16[384,768]{1,0:T(8,128)(2,1)} %w_own_ref.1, bf16[384,768]{1,0:T(8,128)(2,1)} %collective-permute-done.3.refs_4_, ...), custom_call_target="tpu_custom_call" | custom-call | flops 301989888 | bytes 3899396 | tf_op jit(solution)/shard_map/pallas_call | solution.py:51
  84.4 3.7 %shard_map.164 = (bf16[16,128,384]{2,1,0:T(8,128)(2,1)}, bf16[512,384]{1,0:T(8,128)(2,1)}) custom-call(s32[4,5]{1,0:T(4,128)S(1)} %copy-done.9, s32[1]{0:T(128)} %bitcast.1.self_ref.refs_0_, s32[1]{0:T(128)} %bitcast.refs_0_.core_ref.refs_1_, bf16[512,384]{1,0:T(8,128)(2,1)S(1)} %get-tuple-element.31.mine_ref.refs_2_, ...), custom_call_target="tpu_custom_call" | custom-call | flops 553648128 | bytes 3997784 | tf_op jit(solution)/shard_map/pallas_call | solution.py:51
  88.9 3.7 %all-to-all-start.3 = ((bf16[16,128,384]{2,1,0:T(8,128)(2,1)}), bf16[16,128,384]{2,1,0:T(8,128)(2,1)S(1)}, u32[]{:S(2)}, u32[]{:S(2)}) async-start(bf16[16,128,384]{2,1,0:T(8,128)(2,1)} %get-tuple-element.43), calls=%async_computation.3 | async-start | bytes 3145728 | tf_op jit(solution)/shard_map/all_to_all | solution.py:563
  92.6 3.0 %shard_map.165 = (bf16[8,56,384]{2,1,0:T(8,128)(2,1)S(1)}, bf16[8,56,384]{2,1,0:T(8,128)(2,1)S(1)}) custom-call(s32[1]{0:T(128)} %bitcast.1.self_ref.refs_0_, s32[1]{0:T(128)} %bitcast.refs_0_.core_ref.refs_1_, bf16[512,384]{1,0:T(8,128)(2,1)} %copy-done.6, bf16[512,384]{1,0:T(8,128)(2,1)} %copy-done.7, bf16[512,384]{1,0:T(8,128)(2,1)} %bitcast.28, ...), custom_call_target="tpu_custom_call" | custom-call | flops 402653184 | bytes 3014664 | tf_op jit(solution)/shard_map/pallas_call | solution.py:51
  97.5 10.5 %collective-permute-done.7.theirs_ref = bf16[8,56,384]{2,1,0:T(8,128)(2,1)S(1)} collective-permute-done((bf16[8,56,384]{2,1,0:T(8,128)(2,1)S(1)}, bf16[8,56,384]{2,1,0:T(8,128)(2,1)S(1)}, u32[]{:S(2)}, u32[]{:S(2)}) %collective-permute-start.7) | collective-permute-done | bytes 344096 | tf_op jit(solution)/shard_map/ppermute | solution.py:558
  108.1 9.3 %collective-permute-start.8 = (bf16[4,56,384]{2,1,0:T(8,128)(2,1)S(1)}, bf16[4,56,384]{2,1,0:T(8,128)(2,1)S(1)}, u32[]{:S(2)}, u32[]{:S(2)}) collective-permute-start(bf16[4,56,384]{2,1,0:T(8,128)(2,1)S(1)} %get-tuple-element.36), channel_id=1, source_target_pairs={{0,4},{2,6},{4,0},{6,2},{8,12},{10,14},{12,8},{14,10},{16,20},{18,... | collective-permute-start | bytes 516104 | tf_op jit(solution)/shard_map/ppermute | solution.py:558
  117.4 3.4 %collective-permute-done.8.theirs_ref = bf16[4,56,384]{2,1,0:T(8,128)(2,1)S(1)} collective-permute-done((bf16[4,56,384]{2,1,0:T(8,128)(2,1)S(1)}, bf16[4,56,384]{2,1,0:T(8,128)(2,1)S(1)}, u32[]{:S(2)}, u32[]{:S(2)}) %collective-permute-start.8) | collective-permute-done | bytes 172064 | tf_op jit(solution)/shard_map/ppermute | solution.py:558
  122.4 3.9 %collective-permute-done.9.theirs_ref = bf16[2,56,384]{2,1,0:T(8,128)(2,1)S(1)} collective-permute-done((bf16[2,56,384]{2,1,0:T(8,128)(2,1)S(1)}, bf16[2,56,384]{2,1,0:T(8,128)(2,1)S(1)}, u32[]{:S(2)}, u32[]{:S(2)}) %collective-permute-start.9) | collective-permute-done | bytes 86048 | tf_op jit(solution)/shard_map/ppermute | solution.py:558
  126.7 2.4 %shard_map.170.local_hbm = f32[4,128,384]{2,1,0:T(8,128)S(1)} custom-call(s32[4,5]{1,0:T(4,128)S(1)} %copy-done.9, s32[1]{0:T(128)} %bitcast.1.self_ref.refs_0_, bf16[4,128,384]{2,1,0:T(8,128)(2,1)S(1)} %bitcast.25, bf16[4,5,128,128]{3,2,1,0:T(8,128)(2,1)S(1)} %copy-done.3, bf16[4,128,384]{2,1,0:T(8,128)(2,1)S(1)} %bitcast.24), custom_call_target="tpu_custom_call" | custom-call | flops 251658240 | bytes 2228308 | tf_op jit(solution)/shard_map/pallas_call | solution.py:51
  132.5 3.1 %shard_map.171 = bf16[4,128,384]{2,1,0:T(8,128)(2,1)} custom-call(s32[1]{0:T(128)} %bitcast.1.self_ref.refs_0_, s32[8,2]{1,0:T(8,128)S(1)} %copy.18.asked_ref, s32[8,2]{1,0:T(8,128)S(1)} %copy.21.mate_ref, f32[4,128,384]{2,1,0:T(8,128)} %copy-done.2, bf16[16,128,384]{2,1,0:T(8,128)(2,1)S(1)} %all-to-all-done.3.got_ref), custom_call_target="tpu_custom_call" | custom-call | flops 1000 | bytes 2752644 | tf_op jit(solution)/shard_map/pallas_call | solution.py:51
  (57 shorter events, 15.8 us)
Async XLA Ops:
  0.6 21.9 %collective-permute-start.1 = (bf16[4,128,384]{2,1,0:T(8,128)(2,1)}, bf16[4,128,384]{2,1,0:T(8,128)(2,1)S(1)}, u32[]{:S(2)}, u32[]{:S(2)}) collective-permute-start(bf16[4,128,384]{2,1,0:T(8,128)(2,1)} %bitcast.20), channel_id=1, source_target_pairs={{0,16},{2,18},{4,20},{6,22},{8,24},{10,26},{12,28},{14,30},{16,0},... | collective-permute-start | bytes 1179656 | tf_op jit(solution)/shard_map/ppermute | solution.py:558
  26.2 4.0 %copy-start.11 = (s32[1,2]{1,0:T(1,128)S(1)}, s32[1,2]{1,0:T(1,128)}, u32[]{:S(2)}) copy-start(s32[1,2]{1,0:T(1,128)} %counts_ref.3) | copy-start | bytes 28
  26.2 29.5 %all-to-all-start.1 = ((bf16[8,256,384]{2,1,0:T(8,128)(2,1)}), bf16[8,256,384]{2,1,0:T(8,128)(2,1)S(1)}, u32[]{:S(2)}, u32[]{:S(2)}) async-start(bf16[8,256,384]{2,1,0:T(8,128)(2,1)} %shard_map.158), calls=%async_computation.1 | async-start | bytes 3145728 | tf_op jit(solution)/shard_map/all_to_all | solution.py:563
  30.2 10.6 %copy-start.10 = (f32[2,768]{1,0:T(2,128)S(1)}, f32[2,768]{1,0:T(2,128)}, u32[]{:S(2)}) copy-start(f32[2,768]{1,0:T(2,128)} %gains_ref.3) | copy-start | bytes 18436
  37.3 16.3 %copy-start = (bf16[512,384]{1,0:T(8,128)(2,1)S(1)}, bf16[512,384]{1,0:T(8,128)(2,1)}, u32[]{:S(2)}) copy-start(bf16[512,384]{1,0:T(8,128)(2,1)} %param.20) | copy-start | bytes 1179652
  37.3 16.3 %copy-start.3 = (bf16[4,5,128,128]{3,2,1,0:T(8,128)(2,1)S(1)}, bf16[4,5,128,128]{3,2,1,0:T(8,128)(2,1)}, u32[]{:S(2)}) copy-start(bf16[4,5,128,128]{3,2,1,0:T(8,128)(2,1)} %adj_ref.5) | copy-start | bytes 1966084
  37.3 16.3 %copy-start.8 = (s32[4,5]{1,0:T(4,128)S(1)}, s32[4,5]{1,0:T(4,128)}, u32[]{:S(2)}) copy-start(s32[4,5]{1,0:T(4,128)} %ids_ref.5) | copy-start | bytes 244
  37.3 2.6 %collective-permute-start.4 = (bf16[512,768]{1,0:T(8,128)(2,1)}, bf16[512,768]{1,0:T(8,128)(2,1)S(1)}, u32[]{:S(2)}, u32[]{:S(2)}) collective-permute-start(bf16[512,768]{1,0:T(8,128)(2,1)} %shard_map.160.mine_hbm), channel_id=1, source_target_pairs={{0,1},{1,0},{2,3},{3,2},{4,5},{5,4},{6,7},{7,6},{8,9},{9,8},{10,11... | collective-permute-start | bytes 2359304 | tf_op jit(solution)/shard_map/ppermute | solution.py:555
  48.1 11.4 %collective-permute-start.5 = (bf16[512,768]{1,0:T(8,128)(2,1)}, bf16[512,768]{1,0:T(8,128)(2,1)}, u32[]{:S(2)}, u32[]{:S(2)}) collective-permute-start(bf16[512,768]{1,0:T(8,128)(2,1)} %get-tuple-element.29.mine_ref), channel_id=1, source_target_pairs={{0,1},{1,0},{2,3},{3,2},{4,5},{5,4},{6,7},{7,6},{8,9},{9,8},{10,11... | collective-permute-start | bytes 2359304 | tf_op jit(solution)/shard_map/ppermute | solution.py:555
  48.3 21.8 %collective-permute-start.3 = (bf16[384,768]{1,0:T(8,128)(2,1)}, bf16[384,768]{1,0:T(8,128)(2,1)}, u32[]{:S(2)}, u32[]{:S(2)}) collective-permute-start(bf16[384,768]{1,0:T(8,128)(2,1)} %w_own_ref.1), channel_id=1, source_target_pairs={{0,1},{1,0},{2,3},{3,2},{4,5},{5,4},{6,7},{7,6},{8,9},{9,8},{10,11... | collective-permute-start | bytes 1769480 | tf_op jit(solution)/shard_map/ppermute | solution.py:555
  48.7 4.9 %collective-permute-start = (s32[8,1,384]{2,1,0:T(1,128)S(1)}, s32[8,1,384]{2,1,0:T(1,128)S(1)}, u32[]{:S(2)}, u32[]{:S(2)}) collective-permute-start(s32[8,1,384]{2,1,0:T(1,128)S(1)} %all_to_all.20.got_ref), channel_id=1, source_target_pairs={{0,16},{2,18},{4,20},{6,22},{8,24},{10,26},{12,28},{14,30},{16,0},... | collective-permute-start | bytes 36872 | tf_op jit(solution)/shard_map/ppermute | solution.py:558
  59.4 18.3 %collective-permute-start.2 = (bf16[512,384]{1,0:T(8,128)(2,1)}, bf16[512,384]{1,0:T(8,128)(2,1)S(1)}, u32[]{:S(2)}, u32[]{:S(2)}) collective-permute-start(bf16[512,384]{1,0:T(8,128)(2,1)} %bitcast.26), channel_id=1, source_target_pairs={{0,1},{1,0},{2,3},{3,2},{4,5},{5,4},{6,7},{7,6},{8,9},{9,8},{10,11... | collective-permute-start | bytes 1179656 | tf_op jit(solution)/shard_map/ppermute | solution.py:555
  62.3 15.4 %all-to-all-start.2 = ((f32[16,1,1536]{2,1,0:T(1,128)}), f32[16,1,1536]{2,1,0:T(1,128)S(1)}, u32[]{:S(2)}, u32[]{:S(2)}) async-start(f32[16,1,1536]{2,1,0:T(1,128)} %shard_map.162), calls=%async_computation.2 | async-start | bytes 196608 | tf_op jit(solution)/shard_map/all_to_all | solution.py:563
  70.0 14.3 %copy-start.9 = (s32[4,5]{1,0:T(4,128)S(1)}, s32[4,5]{1,0:T(4,128)}, u32[]{:S(2)}) copy-start(s32[4,5]{1,0:T(4,128)} %ids_ref.5) | copy-start | bytes 244
  77.7 10.4 %copy-start.5 = (f32[16,1,1536]{2,1,0:T(1,128)}, f32[16,1,1536]{2,1,0:T(1,128)S(1)}, u32[]{:S(2)}) copy-start(f32[16,1,1536]{2,1,0:T(1,128)S(1)} %all-to-all-done.2.refs_9_) | copy-start | bytes 294916
  82.6 6.3 %copy-start.6 = (bf16[512,384]{1,0:T(8,128)(2,1)}, bf16[512,384]{1,0:T(8,128)(2,1)S(1)}, u32[]{:S(2)}) copy-start(bf16[512,384]{1,0:T(8,128)(2,1)S(1)} %get-tuple-element.31.mine_ref.refs_2_) | copy-start | bytes 1179652
  82.6 1.8 %collective-permute-start.6 = (bf16[512,384]{1,0:T(8,128)(2,1)S(1)}, bf16[512,384]{1,0:T(8,128)(2,1)S(1)}, u32[]{:S(2)}, u32[]{:S(2)}) collective-permute-start(bf16[512,384]{1,0:T(8,128)(2,1)S(1)} %get-tuple-element.31.mine_ref.refs_2_), channel_id=1, source_target_pairs={{0,1},{1,0},{2,3},{3,2},{4,5},{5,4},{6,7},{7,6},{8,9},{9,8},{10,11... | collective-permute-start | bytes 1179656 | tf_op jit(solution)/shard_map/ppermute | solution.py:555
  88.9 43.7 %all-to-all-start.3 = ((bf16[16,128,384]{2,1,0:T(8,128)(2,1)}), bf16[16,128,384]{2,1,0:T(8,128)(2,1)S(1)}, u32[]{:S(2)}, u32[]{:S(2)}) async-start(bf16[16,128,384]{2,1,0:T(8,128)(2,1)} %get-tuple-element.43), calls=%async_computation.3 | async-start | bytes 3145728 | tf_op jit(solution)/shard_map/all_to_all | solution.py:563
  92.6 34.1 %copy-start.1 = (bf16[512,384]{1,0:T(8,128)(2,1)S(1)}, bf16[512,384]{1,0:T(8,128)(2,1)}, u32[]{:S(2)}) copy-start(bf16[512,384]{1,0:T(8,128)(2,1)} %refs_8_.1) | copy-start | bytes 1179652
  92.6 34.1 %copy-start.4 = (bf16[512,384]{1,0:T(8,128)(2,1)S(1)}, bf16[512,384]{1,0:T(8,128)(2,1)}, u32[]{:S(2)}) copy-start(bf16[512,384]{1,0:T(8,128)(2,1)} %get-tuple-element.32.refs_5_) | copy-start | bytes 1179652
  95.6 12.3 %collective-permute-start.7 = (bf16[8,56,384]{2,1,0:T(8,128)(2,1)S(1)}, bf16[8,56,384]{2,1,0:T(8,128)(2,1)S(1)}, u32[]{:S(2)}, u32[]{:S(2)}) collective-permute-start(bf16[8,56,384]{2,1,0:T(8,128)(2,1)S(1)} %get-tuple-element.34), channel_id=1, source_target_pairs={{0,2},{2,0},{4,6},{6,4},{8,10},{10,8},{12,14},{14,12},{16,18},{18,... | collective-permute-start | bytes 1032200 | tf_op jit(solution)/shard_map/ppermute | solution.py:558
  108.1 12.7 %collective-permute-start.8 = (bf16[4,56,384]{2,1,0:T(8,128)(2,1)S(1)}, bf16[4,56,384]{2,1,0:T(8,128)(2,1)S(1)}, u32[]{:S(2)}, u32[]{:S(2)}) collective-permute-start(bf16[4,56,384]{2,1,0:T(8,128)(2,1)S(1)} %get-tuple-element.36), channel_id=1, source_target_pairs={{0,4},{2,6},{4,0},{6,2},{8,12},{10,14},{12,8},{14,10},{16,20},{18,... | collective-permute-start | bytes 516104 | tf_op jit(solution)/shard_map/ppermute | solution.py:558
  120.9 5.5 %collective-permute-start.9 = (bf16[2,56,384]{2,1,0:T(8,128)(2,1)S(1)}, bf16[2,56,384]{2,1,0:T(8,128)(2,1)S(1)}, u32[]{:S(2)}, u32[]{:S(2)}) collective-permute-start(bf16[2,56,384]{2,1,0:T(8,128)(2,1)S(1)} %get-tuple-element.38), channel_id=1, source_target_pairs={{0,8},{2,10},{4,12},{6,14},{8,0},{10,2},{12,4},{14,6},{16,24},{18,... | collective-permute-start | bytes 258056 | tf_op jit(solution)/shard_map/ppermute | solution.py:558
  126.4 5.5 %collective-permute-start.10 = (bf16[1,56,384]{2,1,0:T(8,128)(2,1)S(1)}, bf16[1,56,384]{2,1,0:T(8,128)(2,1)S(1)}, u32[]{:S(2)}, u32[]{:S(2)}) collective-permute-start(bf16[1,56,384]{2,1,0:T(8,128)(2,1)S(1)} %get-tuple-element.40), channel_id=1, source_target_pairs={{0,16},{2,18},{4,20},{6,22},{8,24},{10,26},{12,28},{14,30},{16,0},... | collective-permute-start | bytes 129032 | tf_op jit(solution)/shard_map/ppermute | solution.py:558
  (5 other events, 4.1 us)

commit v7 on v6

--- a/solution.py
+++ b/solution.py
@@ -21,6 +21,7 @@
 
 VMEM = pl.BlockSpec(memory_space=pltpu.VMEM)
 HBM = pl.BlockSpec(memory_space=pltpu.HBM)
+HELD = pl.BlockSpec(memory_space=pltpu.VMEM)
 PULL = pl.BlockSpec(memory_space=pltpu.HBM)
 SMEM = pl.BlockSpec(memory_space=pltpu.SMEM)
 
@@ -29,13 +30,17 @@
     return (value + unit - 1) // unit * unit
 
 
-def call(body, outs, ins, specs, flops, scratch=(), out_specs=None):
+def call(body, outs, ins, specs, flops, scratch=(), out_specs=None, aliases=None):
     moved = sum(a.size * a.dtype.itemsize for a in ins) + sum(
         o.size * o.dtype.itemsize for o in outs
     )
     many = len(outs) > 1
     ins = [
         pltpu.with_memory_space_constraint(a, pltpu.HBM) if s is HBM or s is PULL else a
+        for a, s in zip(ins, specs, strict=True)
+    ]
+    ins = [
+        pltpu.with_memory_space_constraint(a, pltpu.VMEM) if s is HELD else a
         for a, s in zip(ins, specs, strict=True)
     ]
     pulled = [i for i, s in enumerate(specs) if s is PULL]
@@ -54,6 +59,7 @@
         in_specs=list(specs),
         out_specs=tuple(out_specs) if many else out_specs[0],
         scratch_shapes=list(scratch),
+        input_output_aliases=aliases or {},
         compiler_params=pltpu.CompilerParams(vmem_limit_bytes=moved + moved // 8 + held + SPARE),
         cost_estimate=pl.CostEstimate(flops=flops, bytes_accessed=moved, transcendentals=0),
     )(*ins)
@@ -151,21 +157,28 @@
         )
 
 
-def pack_body(asked_ref, cache_hbm, mate_hbm, out_hbm, tile_ref, in_sems, out_sems):
-    _, _, tile_rows, _ = tile_ref.shape
-    started = copies([(cache_hbm, tile_ref.at[0]), (mate_hbm, tile_ref.at[1])], in_sems)
+def pack_near_body(asked_ref, cache_hbm, out_hbm, tile_ref, in_sems, out_sems):
+    copy = pltpu.make_async_copy(cache_hbm, tile_ref, in_sems.at[0])
+    copy.start()
+    copy.wait()
+    place_tiles(0, asked_ref, tile_ref, out_hbm, out_sems)
+
+
+def pack_far_body(asked_ref, mate_ref, near_hbm, out_hbm, out_sems):
+    place_tiles(1, asked_ref, mate_ref, out_hbm, out_sems)
+
+
+def place_tiles(side, asked_ref, tile_ref, out_hbm, out_sems):
+    tile_rows = tile_ref.shape[1]
     peers = out_hbm.shape[0]
 
-    def slot(p, side):
+    def slot(p):
         place = jnp.maximum(asked_ref[p, side], 0)
         target = out_hbm.at[p, pl.ds(side * tile_rows, tile_rows), :]
-        return pltpu.make_async_copy(tile_ref.at[side, place], target, out_sems.at[side, p])
-
-    for side in range(2):
-        started[side].wait()
-        lax.fori_loop(0, peers, lambda p, c: (slot(p, side).start(), c)[1], 0)
-    for side in range(2):
-        lax.fori_loop(0, peers, lambda p, c: (slot(p, side).wait(), c)[1], 0)
+        return pltpu.make_async_copy(tile_ref.at[place], target, out_sems.at[p])
+
+    lax.fori_loop(0, peers, lambda p, c: (slot(p).start(), c)[1], 0)
+    lax.fori_loop(0, peers, lambda p, c: (slot(p).wait(), c)[1], 0)
 
 
 def mask_body(
@@ -294,7 +307,6 @@
 
 
 def pool_body(seq, counts_ref, first_ref, mine_ref, other_ref, gains_ref, out_ref):
-    shards = out_ref.shape[0]
     texts_here, width = first_ref.shape[0] // seq, first_ref.shape[1]
     for t in range(texts_here):
         rows = slice(t * seq, (t + 1) * seq)
@@ -304,23 +316,35 @@
         live = lax.broadcasted_iota(jnp.int32, (seq, 1), 0) < count
         total = jnp.sum(jnp.where(live, second, 0.0), axis=0, keepdims=True)
         pooled = (total / count.astype(jnp.float32)).astype(jnp.bfloat16).astype(jnp.float32)
-        out_ref[:, :, t * width : (t + 1) * width] = jnp.broadcast_to(pooled, (shards, width)).reshape(
-            shards, 1, width
-        )
-
-
-def pooled_rows(pooled_ref, width):
-    shards, _, lanes = pooled_ref.shape
-    parts = [
-        pooled_ref[:, :, first : first + width].reshape(shards, width).astype(jnp.bfloat16)
-        for first in range(0, lanes, width)
-    ]
-    return jnp.concatenate(parts, axis=0)
+        out_ref[:, :, t * width : (t + 1) * width] = pooled.reshape(1, 1, width)
+
+
+def pooled_rows(me, near_ref, far_ref, width):
+    shards = 2 * near_ref.shape[0]
+    parts = []
+    for first in range(0, near_ref.shape[2], width):
+        for ref in (near_ref, far_ref):
+            part = ref[:, :, first : first + width].reshape(shards // 2, width)
+            parts.append(part.astype(jnp.bfloat16))
+    stacked = jnp.concatenate(parts, axis=0)
+    texts = stacked.shape[0]
+    row = lax.broadcasted_iota(jnp.int32, (texts, texts), 0)
+    column = lax.broadcasted_iota(jnp.int32, (texts, texts), 1)
+    place = column & (shards - 1)
+    offset = jnp.zeros_like(place)
+    reach = 1
+    while reach < shards:
+        offset = 2 * offset + (place & 1)
+        place = lax.shift_right_logical(place, 1)
+        reach *= 2
+    source = column - (column & (shards - 1)) + (offset ^ me)
+    order = jnp.where(row == source, 1.0, 0.0).astype(jnp.bfloat16)
+    return mm(order, stacked).astype(jnp.bfloat16)
 
 
 def gather_body(
-    ids_hbm, self_ref, kept_hbm, cache_hbm, remote_ref, out_hbm,
-    ids_ref, kept_ref, cache_ref, source_ref, out_ref, sems, out_sems
+    ids_hbm, self_ref, kept_hbm, cache_hbm, remote_ref, out_ref,
+    ids_ref, kept_ref, cache_ref, source_ref, sems
 ):
     started = copies([(ids_hbm, ids_ref), (cache_hbm, cache_ref), (kept_hbm, kept_ref)], sems)
     tiles_here, entries, tile_rows, _ = kept_ref.shape
@@ -343,7 +367,6 @@
             first = pl.multiple_of(side * tile_rows, tile_rows)
             source_ref[r % 2, k] = remote_ref[spot, pl.ds(first, tile_rows), :]
 
-    sent = []
     for r in range(tiles_here):
         lax.fori_loop(
             0, entries, lambda k, c: (fetch(r, k), c)[1], 0, unroll=unroll(entries)
@@ -354,42 +377,49 @@
         for k in range(entries):
             total = total + mm(kept_ref[r, k], source_ref[r % 2, k])
         out_ref[r] = total.astype(jnp.bfloat16)
-        sent.append(pltpu.make_async_copy(out_ref.at[r], out_hbm.at[r], out_sems.at[r]))
-        sent[-1].start()
-    for copy in sent:
-        copy.wait()
 
 
 def forward_body(
-    core_ref, mine_ref, other_ref, w_own_ref, w_other_ref, grad_ref, own_ref, base_ref, pick_ref,
-    pooled_ref, node_ref, slope_ref, rows_ref
+    self_ref, core_ref, mine_ref, other_ref, w_own_ref, w_other_ref, grad_ref, own_ref, base_ref,
+    pick_ref, near_ref, far_ref, node_hbm, slope_ref, agg_hbm, slope_hbm,
+    rows_ref, node_ref, agg_ref, node_sems, agg_sems, slope_sems
 ):
     half = mine_ref.shape[1]
     start = pl.multiple_of(core_ref[0] * half, LANES)
     far = pl.multiple_of((1 - core_ref[0]) * half, LANES)
-    rows_ref[...] = pooled_rows(pooled_ref, rows_ref.shape[1])
+    rows_ref[...] = pooled_rows(self_ref[0], near_ref, far_ref, rows_ref.shape[1])
     texts = rows_ref.shape[0]
     here = rows_ref[:, pl.ds(start, half)]
     w_own = w_own_ref[:, pl.ds(start, half)]
     w_other = w_other_ref[:, pl.ds(start, half)]
     moved = (mm(here, w_own) + mm(rows_ref[:, pl.ds(far, half)], w_other)).astype(jnp.bfloat16)
-    hidden = (
-        mm(mine_ref[...], w_own) + mm(other_ref[...], w_other) + mm(pick_ref[:, :texts], moved)
-    )
-    square = hidden * hidden
-    gate = jnp.tanh(ROOT * hidden * (1.0 + CUBE * square))
-    lifted = 0.5 * (1.0 + gate)
-    slope = lifted + 0.5 * hidden * (1.0 - gate * gate) * (ROOT * (1.0 + 3.0 * CUBE * square))
-    slope_ref[...] = (grad_ref[...].astype(jnp.float32) * slope).astype(jnp.bfloat16)
-    fresh = mm(own_ref[:, :texts], here)
-    node_ref[...] = (base_ref[...].astype(jnp.float32) + fresh + hidden * lifted).astype(
-        jnp.bfloat16
-    )
+    blocks = node_sems.shape[0]
+    step = mine_ref.shape[0] // blocks
+    sent = []
+    for block in range(blocks):
+        at = pl.ds(block * step, step)
+        pick = pick_ref[at, :][:, :texts]
+        hidden = mm(mine_ref[at, :], w_own) + mm(other_ref[at, :], w_other) + mm(pick, moved)
+        square = hidden * hidden
+        gate = jnp.tanh(ROOT * hidden * (1.0 + CUBE * square))
+        lifted = 0.5 * (1.0 + gate)
+        slope = lifted + 0.5 * hidden * (1.0 - gate * gate) * (ROOT * (1.0 + 3.0 * CUBE * square))
+        slope_ref[at, :] = (grad_ref[at, :].astype(jnp.float32) * slope).astype(jnp.bfloat16)
+        fresh = mm(own_ref[at, :][:, :texts], here)
+        node_ref[at, :] = (base_ref[at, :].astype(jnp.float32) + fresh + hidden * lifted).astype(
+            jnp.bfloat16
+        )
+        agg_ref[at, :] = (mine_ref[at, :].astype(jnp.float32) + mm(pick, here)).astype(jnp.bfloat16)
+        sent += copies([(node_ref.at[at, :], node_hbm.at[at, :])], node_sems.at[pl.ds(block, 1)])
+        sent += copies([(agg_ref.at[at, :], agg_hbm.at[at, :])], agg_sems.at[pl.ds(block, 1)])
+        sent += copies([(slope_ref.at[at, :], slope_hbm.at[at, :])], slope_sems.at[pl.ds(block, 1)])
+    for copy in sent:
+        copy.wait()
 
 
 def chunk_body(
-    per, texts_here, self_ref, core_ref, mine_ref, other_ref, part_ref, down_ref, pick_ref, own_ref,
-    grad_ref, pooled_ref, keep_ref, give_ref, w_ref, text_ref, rows_ref, agg_ref
+    per, texts_here, self_ref, core_ref, mine_ref, other_ref, agg_ref, down_ref, pick_ref, own_ref,
+    grad_ref, keep_ref, give_ref, w_ref, text_ref
 ):
     kept, _, half = keep_ref.shape
     shards = 2 * kept
@@ -398,11 +428,6 @@
     me = self_ref[0]
     own = pl.multiple_of(core_ref[0] * half, LANES)
     far = pl.multiple_of((1 - core_ref[0]) * half, LANES)
-    rows_ref[...] = pooled_rows(pooled_ref, rows_ref.shape[1])
-    here = rows_ref[:, pl.ds(own, half)]
-    agg_ref[...] = (
-        part_ref[...].astype(jnp.float32) + mm(pick_ref[:, : here.shape[0]], here)
-    ).astype(jnp.bfloat16)
     columns = 2 * half
     text_ref[...] = mm(pick_ref[...], down_ref[...], (0, 0)) + mm(
         own_ref[...], grad_ref[...], (0, 0)
@@ -588,17 +613,27 @@
 
     asked = places(got)
     packed = call(
-        pack_body,
+        pack_near_body,
         [shape((peers, 2 * tile_rows, half))],
-        [asked, cache_tiles, mate_tiles],
-        [SMEM, HBM, HBM],
+        [asked, cache_tiles],
+        [SMEM, HBM],
         flops=1000,
         scratch=[
-            pltpu.VMEM((2,) + cache_tiles.shape, jnp.bfloat16),
-            pltpu.SemaphoreType.DMA((2,)),
-            pltpu.SemaphoreType.DMA((2, peers)),
+            pltpu.VMEM(cache_tiles.shape, jnp.bfloat16),
+            pltpu.SemaphoreType.DMA((1,)),
+            pltpu.SemaphoreType.DMA((peers,)),
         ],
         out_specs=[HBM],
+    )
+    packed = call(
+        pack_far_body,
+        [shape((peers, 2 * tile_rows, half))],
+        [asked, mate_tiles, packed],
+        [SMEM, VMEM, HBM],
+        flops=1000,
+        scratch=[pltpu.SemaphoreType.DMA((peers,))],
+        out_specs=[HBM],
+        aliases={2: 0},
     )
     remote = spread(packed, halves_of)
 
@@ -641,12 +676,18 @@
     )
     pooled = call(
         functools.partial(pool_body, seq),
-        [shape((shards, 1, texts_here * width), jnp.float32)],
+        [shape((1, 1, texts_here * width), jnp.float32)],
         [token_counts, first, mlp, swap(mlp), ln_gains],
         [SMEM, VMEM, VMEM, VMEM, VMEM],
         flops=20 * count * width,
     )
-    pooled = spread(pooled)
+    near = pooled
+    reach = peers
+    far = toward(near, reach)
+    while reach > 1:
+        reach = reach // 2
+        near = jnp.concatenate([near, far], axis=0)
+        far = toward(near, reach)
 
     kept, pick, own, base = call(
         mask_body,
@@ -679,24 +720,29 @@
             pltpu.VMEM(kept.shape, jnp.bfloat16),
             pltpu.VMEM(cache_tiles.shape, jnp.bfloat16),
             pltpu.VMEM((2, entries, tile_rows, half), jnp.bfloat16),
-            pltpu.VMEM((tiles_here, tile_rows, half), jnp.bfloat16),
             pltpu.SemaphoreType.DMA((3,)),
-            pltpu.SemaphoreType.DMA((tiles_here,)),
-        ],
-        out_specs=[HBM],
+        ],
     )
     gathered = gathered.reshape(nodes_here, half)
     picked = pick.reshape(nodes_here, slots)
-    node_out, slope = call(
+    node_out, slope, aggregate, slope_kept = call(
         forward_body,
-        [shape((nodes_here, half)), shape((nodes_here, half))],
+        [shape((nodes_here, half))] * 4,
         [
-            core, gathered, swap(gathered), w_gnn, w_other, out_grad,
-            own.reshape(nodes_here, slots), base.reshape(nodes_here, half), picked, pooled,
-        ],
-        [SMEM] + [PULL] * 8 + [VMEM],
+            me, core, gathered, swap(gathered), w_gnn, w_other, out_grad,
+            own.reshape(nodes_here, slots), base.reshape(nodes_here, half), picked, near, far,
+        ],
+        [SMEM, SMEM, HELD, HELD] + [VMEM] * 8,
         flops=4 * nodes_here * half * half,
-        scratch=[pltpu.VMEM((texts, width), jnp.bfloat16)],
+        scratch=[
+            pltpu.VMEM((texts, width), jnp.bfloat16),
+            pltpu.VMEM((nodes_here, half), jnp.bfloat16),
+            pltpu.VMEM((nodes_here, half), jnp.bfloat16),
+            pltpu.SemaphoreType.DMA((tiles_here,)),
+            pltpu.SemaphoreType.DMA((tiles_here,)),
+            pltpu.SemaphoreType.DMA((tiles_here,)),
+        ],
+        out_specs=[HBM, VMEM, HBM, HBM],
     )
     grad_tiles = out_grad.reshape(tiles_here, tile_rows, half)
     slope_other = swap(slope)
@@ -721,16 +767,14 @@
         functools.partial(chunk_body, per, texts_here),
         [shape(halves), shape(halves)],
         [
-            me, core, slope, slope_other, gathered, down, picked,
-            own.reshape(nodes_here, slots), out_grad, pooled,
-        ],
-        [SMEM, SMEM] + [PULL] * 8,
+            me, core, slope_kept, slope_other, aggregate, down, picked,
+            own.reshape(nodes_here, slots), out_grad,
+        ],
+        [SMEM, SMEM] + [PULL] * 7,
         flops=4 * nodes_here * half * (half + slots),
         scratch=[
             pltpu.VMEM((width + ROWS, half), jnp.float32),
             pltpu.VMEM((slots, half), jnp.float32),
-            pltpu.VMEM((texts, width), jnp.bfloat16),
-            pltpu.VMEM((nodes_here, half), jnp.bfloat16),
         ],
     )
     local = call(

time: 136 us -> 127 us (0.934)
  waiting for transfers between devices: 39.7 us -> 36.8 us
  starting transfers between devices: 36.4 us -> 33.6 us
  Pallas kernels: 44 us -> 42 us
    all_to_all x3 -> x2, waiting for transfers between devices: 7.66 us -> 0.01 us  [spread(): lax.all_to_all(values, 'graph', split_axis=0, concat_axis=0, tiled=True,...]
    all_to_all x3 -> x2, starting transfers between devices: 15.4 us -> 9.28 us  [spread(): lax.all_to_all(values, 'graph', split_axis=0, concat_axis=0, tiled=True,...]
    ppermute x6 -> x10, waiting for transfers between devices: 27.8 us -> 32.5 us  [toward(): lax.ppermute(values, 'graph', [(i, i ^ reach) for i in range(shards)])]
    ppermute x6 -> x10, starting transfers between devices: 20.2 us -> 23.8 us  [toward(): lax.ppermute(values, 'graph', [(i, i ^ reach) for i in range(shards)])]
    pallas_call x16 -> x17, Pallas kernels: 44 us -> 42 us  [call(): pl.pallas_call(body, out_shape=tuple(outs) if many else outs[0], in_specs...]
  transfers between devices with their start and end apart: 14 -> 17, of which waited for: 9 -> 10; matrix products, arithmetic and copies ran while one was open for 0% -> 0% of each run, Pallas kernels for 22% -> 24%
where the time goes in v7:
time: 127 us
  Pallas kernels  42 us (33%)
  waiting for transfers between devices  36.8 us (29%)
  starting transfers between devices  33.6 us (26%)
  blocking collectives  10.1 us (8%)
  local copies, waits for them, and re-layouts  3.18 us (3%)
    pallas_call x17, Pallas kernels, call(): pl.pallas_call(body, out_shape=tuple(outs) if many else outs[0], in_specs...  42 us
    ppermute x10, waiting for transfers between devices, toward(): lax.ppermute(values, 'graph', [(i, i ^ reach) for i in range(shards)])  32.5 us
    ppermute x10, starting transfers between devices, toward(): lax.ppermute(values, 'graph', [(i, i ^ reach) for i in range(shards)])  23.8 us
    all_to_all x1, blocking collectives, spread(): lax.all_to_all(values, 'graph', split_axis=0, concat_axis=0, tiled=True,...  10.1 us
    all_to_all x2, starting transfers between devices, spread(): lax.all_to_all(values, 'graph', split_axis=0, concat_axis=0, tiled=True,...  9.28 us
    ppermute x5, waiting for transfers between devices, swap(): lax.ppermute(values, 'mp', [(i, cores - 1 - i) for i in range(cores)])  4.2 us
    unnamed x32, local copies, waits for them, and re-layouts  3.01 us
  transfers between devices with their start and end apart: 17, of which 10 were waited for; matrix products, arithmetic and copies ran while one was open for 0% of the time, Pallas kernels for 24%

profile of v7, /device:TPU:0, one launch (start us, length us, event | category | flops | bytes accessed | tf_op | source)
XLA Modules:
  0.0 126.9 jit_solution(16304613333280674641)
XLA Ops:
  0.6 4.1 %collective-permute-start.1 = (bf16[4,128,384]{2,1,0:T(8,128)(2,1)}, bf16[4,128,384]{2,1,0:T(8,128)(2,1)S(1)}, u32[]{:S(2)}, u32[]{:S(2)}) collective-permute-start(bf16[4,128,384]{2,1,0:T(8,128)(2,1)} %bitcast.20), channel_id=1, source_target_pairs={{0,16},{2,18},{4,20},{6,22},{8,24},{10,26},{12,28},{14,30},{16,0},... | collective-permute-start | bytes 1179656 | tf_op jit(solution)/shard_map/ppermute | solution.py:583
  5.7 10.1 %all_to_all.15.got_ref = s32[8,1,384]{2,1,0:T(1,128)S(1)} all-to-all(s32[8,1,384]{2,1,0:T(1,128)S(1)} %shard_map.156), channel_id=1, replica_groups={{0,2,4,6,8,10,12,14},{16,18,20,22,24,26,28,30},{1,3,5,7,9,11,13,15},{17..., dimensions={0} | all-to-all | bytes 24576 | tf_op jit(solution)/shard_map/all_to_all | solution.py:588
  16.0 2.6 %shard_map.158.near_hbm = bf16[8,256,384]{2,1,0:T(8,128)(2,1)} custom-call(s32[8,2]{1,0:T(8,128)S(1)} %copy.20.asked_ref, bf16[4,128,384]{2,1,0:T(8,128)(2,1)} %bitcast.21), custom_call_target="tpu_custom_call" | custom-call | flops 1000 | bytes 1966144 | tf_op jit(solution)/shard_map/pallas_call | solution.py:56
  18.6 3.9 %collective-permute-done.1.mate_ref = bf16[4,128,384]{2,1,0:T(8,128)(2,1)S(1)} collective-permute-done((bf16[4,128,384]{2,1,0:T(8,128)(2,1)}, bf16[4,128,384]{2,1,0:T(8,128)(2,1)S(1)}, u32[]{:S(2)}, u32[]{:S(2)}) %collective-permute-start.1) | collective-permute-done | bytes 393248 | tf_op jit(solution)/shard_map/ppermute | solution.py:583
  24.2 4.0 %all-to-all-start.1 = ((bf16[8,256,384]{2,1,0:T(8,128)(2,1)}), bf16[8,256,384]{2,1,0:T(8,128)(2,1)S(1)}, u32[]{:S(2)}, u32[]{:S(2)}) async-start(bf16[8,256,384]{2,1,0:T(8,128)(2,1)} %shard_map.159), calls=%async_computation.1 | async-start | bytes 3145728 | tf_op jit(solution)/shard_map/all_to_all | solution.py:588
  28.2 7.1 %shard_map.161.mine_hbm = bf16[512,768]{1,0:T(8,128)(2,1)} custom-call(s32[1,2]{1,0:T(1,128)S(1)} %copy-done.13, bf16[512,768]{1,0:T(8,128)(2,1)} %bitcast.40, bf16[3,768,384]{2,1,0:T(8,128)(2,1)} %bitcast.39, bf16[384,768]{1,0:T(8,128)(2,1)} %w_out_hbm.1), custom_call_target="tpu_custom_call" | custom-call | flops 1610612736 | bytes 3932168 | tf_op jit(solution)/shard_map/pallas_call | solution.py:56
  35.3 2.5 %collective-permute-done.4.other_hbm = bf16[512,768]{1,0:T(8,128)(2,1)S(1)} collective-permute-done((bf16[512,768]{1,0:T(8,128)(2,1)}, bf16[512,768]{1,0:T(8,128)(2,1)S(1)}, u32[]{:S(2)}, u32[]{:S(2)}) %collective-permute-start.4) | collective-permute-done | bytes 786464 | tf_op jit(solution)/shard_map/ppermute | solution.py:580
  38.7 6.4 %shard_map.162 = (bf16[512,768]{1,0:T(8,128)(2,1)S(1)}, bf16[512,768]{1,0:T(8,128)(2,1)S(1)}) custom-call(bf16[512,768]{1,0:T(8,128)(2,1)} %bitcast.41, bf16[512,768]{1,0:T(8,128)(2,1)} %shard_map.161.mine_hbm, bf16[512,768]{1,0:T(8,128)(2,1)} %copy-done.14, bf16[768,1536]{1,0:T(8,128)(2,1)} %up_hbm.1, bf16[1536,768]{1,0:T(8,128)(2,1)} %down_hbm.1, ...), custom_call_target="tpu_custom_call" | custom-call | flops 2415919104 | bytes 8656896 | tf_op jit(solution)/shard_map/pallas_call | solution.py:56
  45.4 3.3 %collective-permute-start = (s32[8,1,384]{2,1,0:T(1,128)S(1)}, s32[8,1,384]{2,1,0:T(1,128)S(1)}, u32[]{:S(2)}, u32[]{:S(2)}) collective-permute-start(s32[8,1,384]{2,1,0:T(1,128)S(1)} %all_to_all.15.got_ref), channel_id=1, source_target_pairs={{0,16},{2,18},{4,20},{6,22},{8,24},{10,26},{12,28},{14,30},{16,0},... | collective-permute-start | bytes 36872 | tf_op jit(solution)/shard_map/ppermute | solution.py:583
  56.8 3.3 %shard_map.160 = bf16[4,128,384]{2,1,0:T(8,128)(2,1)S(1)} custom-call(s32[4,5]{1,0:T(4,128)} %ids_ref.5, s32[1]{0:T(128)} %bitcast.self_ref.refs_0_, bf16[4,5,128,128]{3,2,1,0:T(8,128)(2,1)} %get-tuple-element.26.kept_hbm, bf16[4,128,384]{2,1,0:T(8,128)(2,1)} %bitcast.22, bf16[8,256,384]{2,1,0:T(8,128)(2,1)S(1)} %all-to-all-done.1.remote_ref), custom_call_target="tpu_custom_call" | custom-call | flops 251658240 | bytes 3014740 | tf_op jit(solution)/shard_map/pallas_call | solution.py:56
  61.7 2.4 %collective-permute-done.8 = f32[4,1,1536]{2,1,0:T(1,128)S(1)} collective-permute-done((f32[4,1,1536]{2,1,0:T(1,128)S(1)}, f32[4,1,1536]{2,1,0:T(1,128)S(1)}, u32[]{:S(2)}, u32[]{:S(2)}) %collective-permute-start.8) | collective-permute-done | bytes 24608 | tf_op jit(solution)/shard_map/ppermute | solution.py:583
  65.6 2.6 %collective-permute-done.9.far_ref = f32[8,1,1536]{2,1,0:T(1,128)S(1)} collective-permute-done((f32[8,1,1536]{2,1,0:T(1,128)S(1)}, f32[8,1,1536]{2,1,0:T(1,128)S(1)}, u32[]{:S(2)}, u32[]{:S(2)}) %collective-permute-start.9) | collective-permute-done | bytes 49184 | tf_op jit(solution)/shard_map/ppermute | solution.py:583
  69.3 3.5 %shard_map.164 = (bf16[512,384]{1,0:T(8,128)(2,1)}, bf16[512,384]{1,0:T(8,128)(2,1)S(1)}, bf16[512,384]{1,0:T(8,128)(2,1)}, bf16[512,384]{1,0:T(8,128)(2,1)}) custom-call(s32[1]{0:T(128)} %bitcast.self_ref.refs_0_, s32[1]{0:T(128)} %bitcast.1.core_ref.refs_1_, bf16[512,384]{1,0:T(8,128)(2,1)S(1)} %bitcast.27, ...), custom_call_target="tpu_custom_call" | custom-call | flops 301989888 | bytes 4685832 | tf_op jit(solution)/shard_map/pallas_call | solution.py:56
  74.6 3.9 %shard_map.165 = (bf16[16,128,384]{2,1,0:T(8,128)(2,1)}, bf16[512,384]{1,0:T(8,128)(2,1)}) custom-call(s32[4,5]{1,0:T(4,128)S(1)} %copy-done.11, s32[1]{0:T(128)} %bitcast.self_ref.refs_0_, s32[1]{0:T(128)} %bitcast.1.core_ref.refs_1_, bf16[512,384]{1,0:T(8,128)(2,1)S(1)} %get-tuple-element.34.mine_ref, ...), custom_call_target="tpu_custom_call" | custom-call | flops 553648128 | bytes 3997784 | tf_op jit(solution)/shard_map/pallas_call | solution.py:56
  78.6 5.3 %all-to-all-start.2 = ((bf16[16,128,384]{2,1,0:T(8,128)(2,1)}), bf16[16,128,384]{2,1,0:T(8,128)(2,1)S(1)}, u32[]{:S(2)}, u32[]{:S(2)}) async-start(bf16[16,128,384]{2,1,0:T(8,128)(2,1)} %get-tuple-element.47), calls=%async_computation.2 | async-start | bytes 3145728 | tf_op jit(solution)/shard_map/all_to_all | solution.py:588
  83.9 2.9 %shard_map.166 = (bf16[8,56,384]{2,1,0:T(8,128)(2,1)S(1)}, bf16[8,56,384]{2,1,0:T(8,128)(2,1)S(1)}) custom-call(s32[1]{0:T(128)} %bitcast.self_ref.refs_0_, s32[1]{0:T(128)} %bitcast.1.core_ref.refs_1_, bf16[512,384]{1,0:T(8,128)(2,1)} %get-tuple-element.33.refs_2_, bf16[512,384]{1,0:T(8,128)(2,1)} %copy-done.9, bf16[512,384]{1,0:T(8,128)(2,1)} %get-tuple-element.35.refs_4_, ...), custom_call_target="tpu_custom_call" | custom-call | flops 402653184 | bytes 2916360 | tf_op jit(solution)/shard_map/pallas_call | solution.py:56
  88.7 10.4 %collective-permute-done.11.theirs_ref = bf16[8,56,384]{2,1,0:T(8,128)(2,1)S(1)} collective-permute-done((bf16[8,56,384]{2,1,0:T(8,128)(2,1)S(1)}, bf16[8,56,384]{2,1,0:T(8,128)(2,1)S(1)}, u32[]{:S(2)}, u32[]{:S(2)}) %collective-permute-start.11) | collective-permute-done | bytes 344096 | tf_op jit(solution)/shard_map/ppermute | solution.py:583
  99.2 3.6 %collective-permute-start.12 = (bf16[4,56,384]{2,1,0:T(8,128)(2,1)S(1)}, bf16[4,56,384]{2,1,0:T(8,128)(2,1)S(1)}, u32[]{:S(2)}, u32[]{:S(2)}) collective-permute-start(bf16[4,56,384]{2,1,0:T(8,128)(2,1)S(1)} %get-tuple-element.40), channel_id=1, source_target_pairs={{0,4},{2,6},{4,0},{6,2},{8,12},{10,14},{12,8},{14,10},{16,20},{18,... | collective-permute-start | bytes 516104 | tf_op jit(solution)/shard_map/ppermute | solution.py:583
  102.8 5.8 %collective-permute-done.12.theirs_ref = bf16[4,56,384]{2,1,0:T(8,128)(2,1)S(1)} collective-permute-done((bf16[4,56,384]{2,1,0:T(8,128)(2,1)S(1)}, bf16[4,56,384]{2,1,0:T(8,128)(2,1)S(1)}, u32[]{:S(2)}, u32[]{:S(2)}) %collective-permute-start.12) | collective-permute-done | bytes 172064 | tf_op jit(solution)/shard_map/ppermute | solution.py:583
  108.6 3.5 %collective-permute-start.13 = (bf16[2,56,384]{2,1,0:T(8,128)(2,1)S(1)}, bf16[2,56,384]{2,1,0:T(8,128)(2,1)S(1)}, u32[]{:S(2)}, u32[]{:S(2)}) collective-permute-start(bf16[2,56,384]{2,1,0:T(8,128)(2,1)S(1)} %get-tuple-element.42), channel_id=1, source_target_pairs={{0,8},{2,10},{4,12},{6,14},{8,0},{10,2},{12,4},{14,6},{16,24},{18,... | collective-permute-start | bytes 258056 | tf_op jit(solution)/shard_map/ppermute | solution.py:583
  112.1 5.1 %collective-permute-done.13.theirs_ref = bf16[2,56,384]{2,1,0:T(8,128)(2,1)S(1)} collective-permute-done((bf16[2,56,384]{2,1,0:T(8,128)(2,1)S(1)}, bf16[2,56,384]{2,1,0:T(8,128)(2,1)S(1)}, u32[]{:S(2)}, u32[]{:S(2)}) %collective-permute-start.13) | collective-permute-done | bytes 86048 | tf_op jit(solution)/shard_map/ppermute | solution.py:583
  117.5 2.4 %shard_map.171.local_hbm = f32[4,128,384]{2,1,0:T(8,128)S(1)} custom-call(s32[4,5]{1,0:T(4,128)S(1)} %copy-done.11, s32[1]{0:T(128)} %bitcast.self_ref.refs_0_, bf16[4,128,384]{2,1,0:T(8,128)(2,1)S(1)} %bitcast.25, bf16[4,5,128,128]{3,2,1,0:T(8,128)(2,1)S(1)} %copy-done.4, bf16[4,128,384]{2,1,0:T(8,128)(2,1)S(1)} %bitcast.24), custom_call_target="tpu_custom_call" | custom-call | flops 251658240 | bytes 2228308 | tf_op jit(solution)/shard_map/pallas_call | solution.py:56
  120.8 2.1 %collective-permute-done.14.theirs_ref = bf16[1,56,384]{2,1,0:T(8,128)(2,1)S(1)} collective-permute-done((bf16[1,56,384]{2,1,0:T(8,128)(2,1)S(1)}, bf16[1,56,384]{2,1,0:T(8,128)(2,1)S(1)}, u32[]{:S(2)}, u32[]{:S(2)}) %collective-permute-start.14) | collective-permute-done | bytes 43040 | tf_op jit(solution)/shard_map/ppermute | solution.py:583
  123.6 3.1 %shard_map.172 = bf16[4,128,384]{2,1,0:T(8,128)(2,1)} custom-call(s32[1]{0:T(128)} %bitcast.self_ref.refs_0_, s32[8,2]{1,0:T(8,128)S(1)} %copy.20.asked_ref, s32[8,2]{1,0:T(8,128)S(1)} %copy.23.mate_ref, f32[4,128,384]{2,1,0:T(8,128)} %copy-done.3, bf16[16,128,384]{2,1,0:T(8,128)(2,1)S(1)} %all-to-all-done.2.got_ref), custom_call_target="tpu_custom_call" | custom-call | flops 1000 | bytes 2752644 | tf_op jit(solution)/shard_map/pallas_call | solution.py:56
  (67 shorter events, 22.0 us)
Async XLA Ops:
  0.6 21.9 %collective-permute-start.1 = (bf16[4,128,384]{2,1,0:T(8,128)(2,1)}, bf16[4,128,384]{2,1,0:T(8,128)(2,1)S(1)}, u32[]{:S(2)}, u32[]{:S(2)}) collective-permute-start(bf16[4,128,384]{2,1,0:T(8,128)(2,1)} %bitcast.20), channel_id=1, source_target_pairs={{0,16},{2,18},{4,20},{6,22},{8,24},{10,26},{12,28},{14,30},{16,0},... | collective-permute-start | bytes 1179656 | tf_op jit(solution)/shard_map/ppermute | solution.py:583
  24.2 32.6 %all-to-all-start.1 = ((bf16[8,256,384]{2,1,0:T(8,128)(2,1)}), bf16[8,256,384]{2,1,0:T(8,128)(2,1)S(1)}, u32[]{:S(2)}, u32[]{:S(2)}) async-start(bf16[8,256,384]{2,1,0:T(8,128)(2,1)} %shard_map.159), calls=%async_computation.1 | async-start | bytes 3145728 | tf_op jit(solution)/shard_map/all_to_all | solution.py:588
  28.2 10.5 %copy-start.12 = (f32[2,768]{1,0:T(2,128)S(1)}, f32[2,768]{1,0:T(2,128)}, u32[]{:S(2)}) copy-start(f32[2,768]{1,0:T(2,128)} %gains_ref.3) | copy-start | bytes 18436
  35.2 2.6 %collective-permute-start.4 = (bf16[512,768]{1,0:T(8,128)(2,1)}, bf16[512,768]{1,0:T(8,128)(2,1)S(1)}, u32[]{:S(2)}, u32[]{:S(2)}) collective-permute-start(bf16[512,768]{1,0:T(8,128)(2,1)} %shard_map.161.mine_hbm), channel_id=1, source_target_pairs={{0,1},{1,0},{2,3},{3,2},{4,5},{5,4},{6,7},{7,6},{8,9},{9,8},{10,11... | collective-permute-start | bytes 2359304 | tf_op jit(solution)/shard_map/ppermute | solution.py:580
  45.2 3.6 %collective-permute-start.5 = (bf16[512,768]{1,0:T(8,128)(2,1)S(1)}, bf16[512,768]{1,0:T(8,128)(2,1)S(1)}, u32[]{:S(2)}, u32[]{:S(2)}) collective-permute-start(bf16[512,768]{1,0:T(8,128)(2,1)S(1)} %get-tuple-element.31.mine_ref), channel_id=1, source_target_pairs={{0,1},{1,0},{2,3},{3,2},{4,5},{5,4},{6,7},{7,6},{8,9},{9,8},{10,11... | collective-permute-start | bytes 2359304 | tf_op jit(solution)/shard_map/ppermute | solution.py:580
  45.4 6.8 %collective-permute-start = (s32[8,1,384]{2,1,0:T(1,128)S(1)}, s32[8,1,384]{2,1,0:T(1,128)S(1)}, u32[]{:S(2)}, u32[]{:S(2)}) collective-permute-start(s32[8,1,384]{2,1,0:T(1,128)S(1)} %all_to_all.15.got_ref), channel_id=1, source_target_pairs={{0,16},{2,18},{4,20},{6,22},{8,24},{10,26},{12,28},{14,30},{16,0},... | collective-permute-start | bytes 36872 | tf_op jit(solution)/shard_map/ppermute | solution.py:583
  48.6 17.0 %collective-permute-start.3 = (bf16[384,768]{1,0:T(8,128)(2,1)}, bf16[384,768]{1,0:T(8,128)(2,1)}, u32[]{:S(2)}, u32[]{:S(2)}) collective-permute-start(bf16[384,768]{1,0:T(8,128)(2,1)} %w_own_ref.3), channel_id=1, source_target_pairs={{0,1},{1,0},{2,3},{3,2},{4,5},{5,4},{6,7},{7,6},{8,9},{9,8},{10,11... | collective-permute-start | bytes 1769480 | tf_op jit(solution)/shard_map/ppermute | solution.py:580
  50.1 4.6 %collective-permute-start.6 = (f32[1,1,1536]{2,1,0:T(1,128)S(1)}, f32[1,1,1536]{2,1,0:T(1,128)S(1)}, u32[]{:S(2)}, u32[]{:S(2)}) collective-permute-start(f32[1,1,1536]{2,1,0:T(1,128)S(1)} %shard_map.163), channel_id=1, source_target_pairs={{0,16},{2,18},{4,20},{6,22},{8,24},{10,26},{12,28},{14,30},{16,0},... | collective-permute-start | bytes 18440 | tf_op jit(solution)/shard_map/ppermute | solution.py:583
  54.7 5.4 %collective-permute-start.7 = (f32[2,1,1536]{2,1,0:T(1,128)S(1)}, f32[2,1,1536]{2,1,0:T(1,128)S(1)}, u32[]{:S(2)}, u32[]{:S(2)}) collective-permute-start(f32[2,1,1536]{2,1,0:T(1,128)S(1)} %pad_maximum_fusion.2), channel_id=1, source_target_pairs={{0,8},{2,10},{4,12},{6,14},{8,0},{10,2},{12,4},{14,6},{16,24},{18,... | collective-permute-start | bytes 36872 | tf_op jit(solution)/shard_map/ppermute | solution.py:583
  56.8 11.5 %copy-start.1 = (bf16[512,384]{1,0:T(8,128)(2,1)S(1)}, bf16[512,384]{1,0:T(8,128)(2,1)}, u32[]{:S(2)}) copy-start(bf16[512,384]{1,0:T(8,128)(2,1)} %refs_8_.1) | copy-start | bytes 1179652
  56.8 11.5 %copy-start.6 = (bf16[4,128,128]{2,1,0:T(8,128)(2,1)S(1)}, bf16[4,128,128]{2,1,0:T(8,128)(2,1)}, u32[]{:S(2)}) copy-start(bf16[4,128,128]{2,1,0:T(8,128)(2,1)} %get-tuple-element.29) | copy-start | bytes 393220
  56.8 11.5 %copy-start.7 = (bf16[4,128,128]{2,1,0:T(8,128)(2,1)S(1)}, bf16[4,128,128]{2,1,0:T(8,128)(2,1)}, u32[]{:S(2)}) copy-start(bf16[4,128,128]{2,1,0:T(8,128)(2,1)} %get-tuple-element.27) | copy-start | bytes 393220
  60.0 8.2 %collective-permute-start.2 = (bf16[512,384]{1,0:T(8,128)(2,1)S(1)}, bf16[512,384]{1,0:T(8,128)(2,1)S(1)}, u32[]{:S(2)}, u32[]{:S(2)}) collective-permute-start(bf16[512,384]{1,0:T(8,128)(2,1)S(1)} %bitcast.26), channel_id=1, source_target_pairs={{0,1},{1,0},{2,3},{3,2},{4,5},{5,4},{6,7},{7,6},{8,9},{9,8},{10,11... | collective-permute-start | bytes 1179656 | tf_op jit(solution)/shard_map/ppermute | solution.py:580
  60.2 3.9 %collective-permute-start.8 = (f32[4,1,1536]{2,1,0:T(1,128)S(1)}, f32[4,1,1536]{2,1,0:T(1,128)S(1)}, u32[]{:S(2)}, u32[]{:S(2)}) collective-permute-start(f32[4,1,1536]{2,1,0:T(1,128)S(1)} %pad_maximum_fusion.1), channel_id=1, source_target_pairs={{0,4},{2,6},{4,0},{6,2},{8,12},{10,14},{12,8},{14,10},{16,20},{18,... | collective-permute-start | bytes 73736 | tf_op jit(solution)/shard_map/ppermute | solution.py:583
  64.1 10.5 %copy-start.11 = (s32[4,5]{1,0:T(4,128)S(1)}, s32[4,5]{1,0:T(4,128)}, u32[]{:S(2)}) copy-start(s32[4,5]{1,0:T(4,128)} %ids_ref.5) | copy-start | bytes 244
  64.1 4.2 %collective-permute-start.9 = (f32[8,1,1536]{2,1,0:T(1,128)S(1)}, f32[8,1,1536]{2,1,0:T(1,128)S(1)}, u32[]{:S(2)}, u32[]{:S(2)}) collective-permute-start(f32[8,1,1536]{2,1,0:T(1,128)S(1)} %pad_maximum_fusion.near_ref), channel_id=1, source_target_pairs={{0,2},{2,0},{4,6},{6,4},{8,10},{10,8},{12,14},{14,12},{16,18},{18,... | collective-permute-start | bytes 147464 | tf_op jit(solution)/shard_map/ppermute | solution.py:583
  72.8 1.8 %collective-permute-start.10 = (bf16[512,384]{1,0:T(8,128)(2,1)S(1)}, bf16[512,384]{1,0:T(8,128)(2,1)S(1)}, u32[]{:S(2)}, u32[]{:S(2)}) collective-permute-start(bf16[512,384]{1,0:T(8,128)(2,1)S(1)} %get-tuple-element.34.mine_ref), channel_id=1, source_target_pairs={{0,1},{1,0},{2,3},{3,2},{4,5},{5,4},{6,7},{7,6},{8,9},{9,8},{10,11... | collective-permute-start | bytes 1179656 | tf_op jit(solution)/shard_map/ppermute | solution.py:580
  78.6 45.1 %all-to-all-start.2 = ((bf16[16,128,384]{2,1,0:T(8,128)(2,1)}), bf16[16,128,384]{2,1,0:T(8,128)(2,1)S(1)}, u32[]{:S(2)}, u32[]{:S(2)}) async-start(bf16[16,128,384]{2,1,0:T(8,128)(2,1)} %get-tuple-element.47), calls=%async_computation.2 | async-start | bytes 3145728 | tf_op jit(solution)/shard_map/all_to_all | solution.py:588
  83.8 33.7 %copy-start.2 = (bf16[512,384]{1,0:T(8,128)(2,1)S(1)}, bf16[512,384]{1,0:T(8,128)(2,1)}, u32[]{:S(2)}) copy-start(bf16[512,384]{1,0:T(8,128)(2,1)} %refs_8_.1) | copy-start | bytes 1179652
  83.9 33.6 %copy-start.5 = (bf16[512,384]{1,0:T(8,128)(2,1)S(1)}, bf16[512,384]{1,0:T(8,128)(2,1)}, u32[]{:S(2)}) copy-start(bf16[512,384]{1,0:T(8,128)(2,1)} %get-tuple-element.36.refs_5_) | copy-start | bytes 1179652
  86.7 12.3 %collective-permute-start.11 = (bf16[8,56,384]{2,1,0:T(8,128)(2,1)S(1)}, bf16[8,56,384]{2,1,0:T(8,128)(2,1)S(1)}, u32[]{:S(2)}, u32[]{:S(2)}) collective-permute-start(bf16[8,56,384]{2,1,0:T(8,128)(2,1)S(1)} %get-tuple-element.38), channel_id=1, source_target_pairs={{0,2},{2,0},{4,6},{6,4},{8,10},{10,8},{12,14},{14,12},{16,18},{18,... | collective-permute-start | bytes 1032200 | tf_op jit(solution)/shard_map/ppermute | solution.py:583
  99.2 9.4 %collective-permute-start.12 = (bf16[4,56,384]{2,1,0:T(8,128)(2,1)S(1)}, bf16[4,56,384]{2,1,0:T(8,128)(2,1)S(1)}, u32[]{:S(2)}, u32[]{:S(2)}) collective-permute-start(bf16[4,56,384]{2,1,0:T(8,128)(2,1)S(1)} %get-tuple-element.40), channel_id=1, source_target_pairs={{0,4},{2,6},{4,0},{6,2},{8,12},{10,14},{12,8},{14,10},{16,20},{18,... | collective-permute-start | bytes 516104 | tf_op jit(solution)/shard_map/ppermute | solution.py:583
  108.6 8.6 %collective-permute-start.13 = (bf16[2,56,384]{2,1,0:T(8,128)(2,1)S(1)}, bf16[2,56,384]{2,1,0:T(8,128)(2,1)S(1)}, u32[]{:S(2)}, u32[]{:S(2)}) collective-permute-start(bf16[2,56,384]{2,1,0:T(8,128)(2,1)S(1)} %get-tuple-element.42), channel_id=1, source_target_pairs={{0,8},{2,10},{4,12},{6,14},{8,0},{10,2},{12,4},{14,6},{16,24},{18,... | collective-permute-start | bytes 258056 | tf_op jit(solution)/shard_map/ppermute | solution.py:583
  117.2 5.7 %collective-permute-start.14 = (bf16[1,56,384]{2,1,0:T(8,128)(2,1)S(1)}, bf16[1,56,384]{2,1,0:T(8,128)(2,1)S(1)}, u32[]{:S(2)}, u32[]{:S(2)}) collective-permute-start(bf16[1,56,384]{2,1,0:T(8,128)(2,1)S(1)} %get-tuple-element.44), channel_id=1, source_target_pairs={{0,16},{2,18},{4,20},{6,22},{8,24},{10,26},{12,28},{14,30},{16,0},... | collective-permute-start | bytes 129032 | tf_op jit(solution)/shard_map/ppermute | solution.py:583
  (8 other events, 31.9 us)

commit v8 on v7

--- a/solution.py
+++ b/solution.py
@@ -279,22 +279,15 @@
 
 
 def inner_body(
-    tokens_hbm, mine_hbm, other_hbm, up_hbm, down_hbm, gains_ref, first_ref, out_ref,
-    inner_ref, tokens_ref, mine_ref, other_ref, up_ref, down_ref, sems
+    tokens_ref, mine_hbm, other_ref, up_hbm, down_hbm, gains_ref, first_ref, out_ref,
+    inner_ref, mine_ref, up_ref, down_ref, sems
 ):
-    started = copies(
-        [
-            (tokens_hbm, tokens_ref), (mine_hbm, mine_ref), (other_hbm, other_ref),
-            (up_hbm, up_ref), (down_hbm, down_ref),
-        ],
-        sems,
-    )
-    for copy in started[:3]:
-        copy.wait()
+    started = copies([(mine_hbm, mine_ref), (up_hbm, up_ref), (down_hbm, down_ref)], sems)
+    started[0].wait()
     added = mine_ref[...].astype(jnp.float32) + other_ref[...].astype(jnp.float32)
     first = norm(tokens_ref[...].astype(jnp.float32) + added, gains_ref[0:1, :])
     first_ref[...] = first.astype(jnp.bfloat16)
-    started[3].wait()
+    started[1].wait()
     hidden_units = up_ref.shape[1]
     step = hidden_units // 4
     for c in range(4):
@@ -302,7 +295,7 @@
         value = mm(first_ref[...], up_ref[:, cols])
         gate = jnp.tanh(ROOT * (value + CUBE * (value * value * value)))
         inner_ref[:, cols] = (0.5 * value * (1.0 + gate)).astype(jnp.bfloat16)
-    started[4].wait()
+    started[2].wait()
     out_ref[...] = mm(inner_ref[...], down_ref[...]).astype(jnp.bfloat16)
 
 
@@ -343,31 +336,35 @@
 
 
 def gather_body(
-    ids_hbm, self_ref, kept_hbm, cache_hbm, remote_ref, out_ref,
+    row_from, ids_hbm, self_ref, kept_hbm, cache_hbm, remote_ref, out_ref,
     ids_ref, kept_ref, cache_ref, source_ref, sems
 ):
-    started = copies([(ids_hbm, ids_ref), (cache_hbm, cache_ref), (kept_hbm, kept_ref)], sems)
-    tiles_here, entries, tile_rows, _ = kept_ref.shape
+    rows, entries, tile_rows, _ = kept_ref.shape
+    started = copies(
+        [(ids_hbm, ids_ref), (cache_hbm, cache_ref), (kept_hbm.at[pl.ds(row_from, rows)], kept_ref)],
+        sems,
+    )
+    tiles_here = cache_ref.shape[0]
     me = self_ref[0]
     started[0].wait()
     started[1].wait()
 
     def fetch(r, k):
-        tile_id = ids_ref[r, k]
+        tile_id = ids_ref[row_from + r, k]
         _, owner, place = tile_of(tile_id, tiles_here)
         local = (owner == me) | (tile_id < 0)
 
         @pl.when(local)
         def _():
-            source_ref[r % 2, k] = cache_ref[place]
+            source_ref[r, k] = cache_ref[place]
 
         @pl.when(jnp.logical_not(local))
         def _():
             side, spot = side_of(owner, me, remote_ref.shape[0])
             first = pl.multiple_of(side * tile_rows, tile_rows)
-            source_ref[r % 2, k] = remote_ref[spot, pl.ds(first, tile_rows), :]
-
-    for r in range(tiles_here):
+            source_ref[r, k] = remote_ref[spot, pl.ds(first, tile_rows), :]
+
+    for r in range(rows):
         lax.fori_loop(
             0, entries, lambda k, c: (fetch(r, k), c)[1], 0, unroll=unroll(entries)
         )
@@ -375,16 +372,17 @@
             started[2].wait()
         total = jnp.zeros(out_ref.shape[1:], jnp.float32)
         for k in range(entries):
-            total = total + mm(kept_ref[r, k], source_ref[r % 2, k])
+            total = total + mm(kept_ref[r, k], source_ref[r, k])
         out_ref[r] = total.astype(jnp.bfloat16)
 
 
 def forward_body(
-    self_ref, core_ref, mine_ref, other_ref, w_own_ref, w_other_ref, grad_ref, own_ref, base_ref,
-    pick_ref, near_ref, far_ref, node_hbm, slope_ref, agg_hbm, slope_hbm,
-    rows_ref, node_ref, agg_ref, node_sems, agg_sems, slope_sems
+    self_ref, core_ref, top_ref, bottom_ref, far_top_ref, far_bottom_ref, w_own_ref, w_other_ref,
+    grad_ref, own_ref, base_hbm, pick_ref, near_ref, far_ref, node_hbm, slope_ref, agg_hbm, slope_hbm,
+    rows_ref, node_ref, agg_ref, base_ref, node_sems, agg_sems, slope_sems, base_sems
 ):
-    half = mine_ref.shape[1]
+    based = copies([(base_hbm, base_ref)], base_sems)
+    half = top_ref.shape[1]
     start = pl.multiple_of(core_ref[0] * half, LANES)
     far = pl.multiple_of((1 - core_ref[0]) * half, LANES)
     rows_ref[...] = pooled_rows(self_ref[0], near_ref, far_ref, rows_ref.shape[1])
@@ -394,22 +392,31 @@
     w_other = w_other_ref[:, pl.ds(start, half)]
     moved = (mm(here, w_own) + mm(rows_ref[:, pl.ds(far, half)], w_other)).astype(jnp.bfloat16)
     blocks = node_sems.shape[0]
-    step = mine_ref.shape[0] // blocks
+    step = grad_ref.shape[0] // blocks
     sent = []
     for block in range(blocks):
         at = pl.ds(block * step, step)
+        mine_ref, other_ref = (
+            (top_ref, far_top_ref) if 2 * block < blocks else (bottom_ref, far_bottom_ref)
+        )
+        within = pl.ds((2 * block % blocks) * step // 2, step)
         pick = pick_ref[at, :][:, :texts]
-        hidden = mm(mine_ref[at, :], w_own) + mm(other_ref[at, :], w_other) + mm(pick, moved)
+        hidden = (
+            mm(mine_ref[within, :], w_own) + mm(other_ref[within, :], w_other) + mm(pick, moved)
+        )
         square = hidden * hidden
         gate = jnp.tanh(ROOT * hidden * (1.0 + CUBE * square))
         lifted = 0.5 * (1.0 + gate)
         slope = lifted + 0.5 * hidden * (1.0 - gate * gate) * (ROOT * (1.0 + 3.0 * CUBE * square))
         slope_ref[at, :] = (grad_ref[at, :].astype(jnp.float32) * slope).astype(jnp.bfloat16)
         fresh = mm(own_ref[at, :][:, :texts], here)
+        for copy in based:
+            copy.wait()
+        based = []
         node_ref[at, :] = (base_ref[at, :].astype(jnp.float32) + fresh + hidden * lifted).astype(
             jnp.bfloat16
         )
-        agg_ref[at, :] = (mine_ref[at, :].astype(jnp.float32) + mm(pick, here)).astype(jnp.bfloat16)
+        agg_ref[at, :] = (mine_ref[within, :].astype(jnp.float32) + mm(pick, here)).astype(jnp.bfloat16)
         sent += copies([(node_ref.at[at, :], node_hbm.at[at, :])], node_sems.at[pl.ds(block, 1)])
         sent += copies([(agg_ref.at[at, :], agg_hbm.at[at, :])], agg_sems.at[pl.ds(block, 1)])
         sent += copies([(slope_ref.at[at, :], slope_hbm.at[at, :])], slope_sems.at[pl.ds(block, 1)])
@@ -479,6 +486,28 @@
     down_ref[...] = down.astype(jnp.bfloat16)
     down_copy = pltpu.make_async_copy(down_ref, down_hbm, sems.at[0])
     down_copy.start()
+
+    def slot_of(r, k):
+        tile_id = ids_ref[r, k]
+        _, owner, _ = tile_of(tile_id, tiles_here)
+        away = (tile_id >= 0) & (owner != me)
+        return away, jnp.where(away, owner, shards)
+
+    def slot_copy(slot):
+        return pltpu.make_async_copy(send_ref.at[slot], send_hbm.at[slot], slot_sems.at[slot])
+
+    def each_away(r, act):
+        def one(k, carry):
+            away, slot = slot_of(r, k)
+
+            @pl.when(away)
+            def _():
+                act(slot_copy(slot))
+
+            return carry
+
+        lax.fori_loop(0, entries, one, 0)
+
     for r in range(tiles_here):
         rows = slice(r * tile_rows, (r + 1) * tile_rows)
         for first in range(0, entries, 6):
@@ -486,12 +515,11 @@
             side_by_side = jnp.concatenate([adj_ref[r, k] for k in group], axis=1)
             product = mm(side_by_side, down_ref[rows, :], (0, 0)).astype(jnp.bfloat16)
             for k in group:
-                tile_id = ids_ref[r, k]
-                _, owner, _ = tile_of(tile_id, tiles_here)
-                slot = jnp.where((tile_id >= 0) & (owner != me), owner, shards)
+                _, slot = slot_of(r, k)
                 send_ref[slot] = product[(k - first) * tile_rows : (k - first + 1) * tile_rows]
-    for copy in copies([(send_ref.at[q], send_hbm.at[q]) for q in range(shards)], slot_sems):
-        copy.wait()
+        each_away(r, lambda copy: copy.start())
+    for r in range(tiles_here):
+        each_away(r, lambda copy: copy.wait())
     down_copy.wait()
 
 
@@ -536,12 +564,14 @@
         lax.fori_loop(0, entries, one, 0, unroll=unroll(entries))
 
 
-def finish_body(self_ref, asked_ref, mate_ref, local_hbm, got_ref, node_ref, sum_ref, sems):
-    local = pltpu.make_async_copy(local_hbm, sum_ref, sems.at[0])
-    local.start()
+def finish_body(
+    self_ref, asked_ref, mate_ref, local_hbm, got_ref, node_hbm, sum_ref, local_ref, node_ref, sems, out_sems
+):
+    tiles_here = sum_ref.shape[0]
+    started = copies([(local_hbm.at[j], local_ref.at[j]) for j in range(tiles_here)], sems)
     shards = got_ref.shape[0]
     me = self_ref[0]
-    local.wait()
+    sum_ref[...] = jnp.zeros_like(sum_ref)
 
     def one(q, carry):
         side, spot = side_of(q, me, shards // 2)
@@ -554,7 +584,13 @@
         return carry
 
     lax.fori_loop(0, shards, one, 0)
-    node_ref[...] = sum_ref[...].astype(jnp.bfloat16)
+    sent = []
+    for j in range(tiles_here):
+        started[j].wait()
+        node_ref[j] = (sum_ref[j] + local_ref[j]).astype(jnp.bfloat16)
+        sent += copies([(node_ref.at[j], node_hbm.at[j])], out_sems.at[pl.ds(j, 1)])
+    for copy in sent:
+        copy.wait()
 
 
 def step(
@@ -662,16 +698,14 @@
         inner_body,
         [shape((count, width)), shape((count, width))],
         [flat_tokens, partial, swap(partial), w_up, w_down, ln_gains],
-        [HBM] * 5 + [VMEM],
+        [VMEM, HBM, VMEM, HBM, HBM, VMEM],
         flops=4 * count * width * inner,
         scratch=[
             pltpu.VMEM((count, inner), jnp.bfloat16),
             pltpu.VMEM((count, width), jnp.bfloat16),
-            pltpu.VMEM((count, width), jnp.bfloat16),
-            pltpu.VMEM((count, width), jnp.bfloat16),
             pltpu.VMEM((width, inner), jnp.bfloat16),
             pltpu.VMEM((inner, width), jnp.bfloat16),
-            pltpu.SemaphoreType.DMA((5,)),
+            pltpu.SemaphoreType.DMA((3,)),
         ],
     )
     pooled = call(
@@ -709,38 +743,46 @@
         ],
         out_specs=[HBM] * 4,
     )
-    gathered = call(
-        gather_body,
-        [shape((tiles_here, tile_rows, half))],
-        [adj_tiles, me, kept, cache_tiles, remote],
-        [HBM, SMEM, HBM, HBM, VMEM],
-        flops=2 * adj_values.size * half,
-        scratch=[
-            pltpu.SMEM(adj_tiles.shape, jnp.int32),
-            pltpu.VMEM(kept.shape, jnp.bfloat16),
-            pltpu.VMEM(cache_tiles.shape, jnp.bfloat16),
-            pltpu.VMEM((2, entries, tile_rows, half), jnp.bfloat16),
-            pltpu.SemaphoreType.DMA((3,)),
-        ],
-    )
-    gathered = gathered.reshape(nodes_here, half)
+    rows = tiles_here // 2
+
+    def gather(row_from):
+        part = call(
+            functools.partial(gather_body, row_from),
+            [shape((rows, tile_rows, half))],
+            [adj_tiles, me, kept, cache_tiles, remote],
+            [HBM, SMEM, HBM, HBM, VMEM],
+            flops=adj_values.size * half,
+            scratch=[
+                pltpu.SMEM(adj_tiles.shape, jnp.int32),
+                pltpu.VMEM((rows,) + kept.shape[1:], jnp.bfloat16),
+                pltpu.VMEM(cache_tiles.shape, jnp.bfloat16),
+                pltpu.VMEM((rows, entries, tile_rows, half), jnp.bfloat16),
+                pltpu.SemaphoreType.DMA((3,)),
+            ],
+        )
+        return part.reshape(rows * tile_rows, half)
+
+    top, bottom = gather(0), gather(rows)
     picked = pick.reshape(nodes_here, slots)
     node_out, slope, aggregate, slope_kept = call(
         forward_body,
         [shape((nodes_here, half))] * 4,
         [
-            me, core, gathered, swap(gathered), w_gnn, w_other, out_grad,
+            me, core, top, bottom, swap(top), swap(bottom), w_gnn, w_other,
+            out_grad,
             own.reshape(nodes_here, slots), base.reshape(nodes_here, half), picked, near, far,
         ],
-        [SMEM, SMEM, HELD, HELD] + [VMEM] * 8,
+        [SMEM, SMEM] + [HELD] * 4 + [VMEM] * 4 + [HBM] + [VMEM] * 3,
         flops=4 * nodes_here * half * half,
         scratch=[
             pltpu.VMEM((texts, width), jnp.bfloat16),
             pltpu.VMEM((nodes_here, half), jnp.bfloat16),
             pltpu.VMEM((nodes_here, half), jnp.bfloat16),
+            pltpu.VMEM((nodes_here, half), jnp.bfloat16),
             pltpu.SemaphoreType.DMA((tiles_here,)),
             pltpu.SemaphoreType.DMA((tiles_here,)),
             pltpu.SemaphoreType.DMA((tiles_here,)),
+            pltpu.SemaphoreType.DMA((1,)),
         ],
         out_specs=[HBM, VMEM, HBM, HBM],
     )
@@ -812,8 +854,12 @@
         flops=1000,
         scratch=[
             pltpu.VMEM((tiles_here, tile_rows, half), jnp.float32),
-            pltpu.SemaphoreType.DMA((1,)),
-        ],
+            pltpu.VMEM((tiles_here, tile_rows, half), jnp.float32),
+            pltpu.VMEM((tiles_here, tile_rows, half), jnp.bfloat16),
+            pltpu.SemaphoreType.DMA((tiles_here,)),
+            pltpu.SemaphoreType.DMA((tiles_here,)),
+        ],
+        out_specs=[HBM],
     )
     return (node_out, w_part[:per].T, text_grad, node_grad.reshape(nodes_here, half))
 

time: 127 us -> 131 us (1.031)
  starting transfers between devices: 33.6 us -> 35.8 us
  local copies, waits for them, and re-layouts: 3.18 us -> 1.31 us
    ppermute x5 -> x6, waiting for transfers between devices: 4.2 us -> 6.35 us  [swap(): lax.ppermute(values, 'mp', [(i, cores - 1 - i) for i in range(cores)])]
    unnamed x32 -> x30, local copies, waits for them, and re-layouts: 3.01 us -> 1.14 us
    pallas_call x17 -> x18, Pallas kernels: 42 us -> 42.9 us  [call(): pl.pallas_call(body, out_shape=tuple(outs) if many else outs[0], in_specs...]
  transfers between devices with their start and end apart: 17 -> 18, of which waited for: 10 -> 11; matrix products, arithmetic and copies ran while one was open for 0% -> 1% of each run, Pallas kernels for 24% -> 23%
where the time goes in v8:
time: 131 us; the launch traced here: 130 us
  Pallas kernels  42.9 us (33%)
  waiting for transfers between devices  37.8 us (29%)
  starting transfers between devices  35.8 us (27%)
  blocking collectives  10.1 us (8%)
  local copies, waits for them, and re-layouts  1.31 us (1%)
    pallas_call x18, Pallas kernels, call(): pl.pallas_call(body, out_shape=tuple(outs) if many else outs[0], in_specs...  42.9 us
    ppermute x10, waiting for transfers between devices, toward(): lax.ppermute(values, 'graph', [(i, i ^ reach) for i in range(shards)])  31.5 us
    ppermute x10, starting transfers between devices, toward(): lax.ppermute(values, 'graph', [(i, i ^ reach) for i in range(shards)])  24.8 us
    all_to_all x1, blocking collectives, spread(): lax.all_to_all(values, 'graph', split_axis=0, concat_axis=0, tiled=True,...  10.1 us
    all_to_all x2, starting transfers between devices, spread(): lax.all_to_all(values, 'graph', split_axis=0, concat_axis=0, tiled=True,...  10.1 us
    ppermute x6, waiting for transfers between devices, swap(): lax.ppermute(values, 'mp', [(i, cores - 1 - i) for i in range(cores)])  6.35 us
  transfers between devices with their start and end apart: 18, of which 11 were waited for; matrix products, arithmetic and copies ran while one was open for 1% of the time, Pallas kernels for 23%

profile of v8, /device:TPU:0, one launch (start us, length us, event | category | flops | bytes accessed | tf_op | source)
XLA Modules:
  0.0 129.9 jit_solution(4378256665422105354)
XLA Ops:
  0.6 4.1 %collective-permute-start.1 = (bf16[4,128,384]{2,1,0:T(8,128)(2,1)}, bf16[4,128,384]{2,1,0:T(8,128)(2,1)S(1)}, u32[]{:S(2)}, u32[]{:S(2)}) collective-permute-start(bf16[4,128,384]{2,1,0:T(8,128)(2,1)} %bitcast.21), channel_id=1, source_target_pairs={{0,16},{2,18},{4,20},{6,22},{8,24},{10,26},{12,28},{14,30},{16,0},... | collective-permute-start | bytes 1179656 | tf_op jit(solution)/shard_map/ppermute | solution.py:619
  5.7 10.1 %all_to_all.15.got_ref = s32[8,1,384]{2,1,0:T(1,128)S(1)} all-to-all(s32[8,1,384]{2,1,0:T(1,128)S(1)} %shard_map.156), channel_id=1, replica_groups={{0,2,4,6,8,10,12,14},{16,18,20,22,24,26,28,30},{1,3,5,7,9,11,13,15},{17..., dimensions={0} | all-to-all | bytes 24576 | tf_op jit(solution)/shard_map/all_to_all | solution.py:624
  16.0 2.6 %shard_map.158.near_hbm = bf16[8,256,384]{2,1,0:T(8,128)(2,1)} custom-call(s32[8,2]{1,0:T(8,128)S(1)} %copy.20.asked_ref, bf16[4,128,384]{2,1,0:T(8,128)(2,1)} %bitcast.22), custom_call_target="tpu_custom_call" | custom-call | flops 1000 | bytes 1966144 | tf_op jit(solution)/shard_map/pallas_call | solution.py:56
  18.6 3.9 %collective-permute-done.1.mate_ref = bf16[4,128,384]{2,1,0:T(8,128)(2,1)S(1)} collective-permute-done((bf16[4,128,384]{2,1,0:T(8,128)(2,1)}, bf16[4,128,384]{2,1,0:T(8,128)(2,1)S(1)}, u32[]{:S(2)}, u32[]{:S(2)}) %collective-permute-start.1) | collective-permute-done | bytes 393248 | tf_op jit(solution)/shard_map/ppermute | solution.py:619
  24.1 4.0 %all-to-all-start.1 = ((bf16[8,256,384]{2,1,0:T(8,128)(2,1)}), bf16[8,256,384]{2,1,0:T(8,128)(2,1)S(1)}, u32[]{:S(2)}, u32[]{:S(2)}) async-start(bf16[8,256,384]{2,1,0:T(8,128)(2,1)} %shard_map.159), calls=%async_computation.1 | async-start | bytes 3145728 | tf_op jit(solution)/shard_map/all_to_all | solution.py:624
  28.2 7.1 %shard_map.162.mine_hbm = bf16[512,768]{1,0:T(8,128)(2,1)} custom-call(s32[1,2]{1,0:T(1,128)S(1)} %copy-done.12, bf16[512,768]{1,0:T(8,128)(2,1)} %bitcast.36, bf16[3,768,384]{2,1,0:T(8,128)(2,1)} %bitcast.45, bf16[384,768]{1,0:T(8,128)(2,1)} %w_out_hbm.1), custom_call_target="tpu_custom_call" | custom-call | flops 1610612736 | bytes 3932168 | tf_op jit(solution)/shard_map/pallas_call | solution.py:56
  35.3 2.5 %collective-permute-done.5.other_ref = bf16[512,768]{1,0:T(8,128)(2,1)S(1)} collective-permute-done((bf16[512,768]{1,0:T(8,128)(2,1)}, bf16[512,768]{1,0:T(8,128)(2,1)S(1)}, u32[]{:S(2)}, u32[]{:S(2)}) %collective-permute-start.5) | collective-permute-done | bytes 786464 | tf_op jit(solution)/shard_map/ppermute | solution.py:616
  37.8 5.9 %shard_map.163 = (bf16[512,768]{1,0:T(8,128)(2,1)S(1)}, bf16[512,768]{1,0:T(8,128)(2,1)S(1)}) custom-call(bf16[512,768]{1,0:T(8,128)(2,1)S(1)} %bitcast.37, bf16[512,768]{1,0:T(8,128)(2,1)} %shard_map.162.mine_hbm, bf16[512,768]{1,0:T(8,128)(2,1)S(1)} %collective-permute-done.5.other_ref, bf16[768,1536]{1,0:T(8,128)(2,1)} %up_hbm.1, ...), custom_call_target="tpu_custom_call" | custom-call | flops 2415919104 | bytes 8656896 | tf_op jit(solution)/shard_map/pallas_call | solution.py:56
  44.0 2.2 %collective-permute-done.6.other_ref = bf16[512,768]{1,0:T(8,128)(2,1)S(1)} collective-permute-done((bf16[512,768]{1,0:T(8,128)(2,1)S(1)}, bf16[512,768]{1,0:T(8,128)(2,1)S(1)}, u32[]{:S(2)}, u32[]{:S(2)}) %collective-permute-start.6) | collective-permute-done | bytes 786464 | tf_op jit(solution)/shard_map/ppermute | solution.py:616
  47.5 3.3 %collective-permute-start.7 = (f32[1,1,1536]{2,1,0:T(1,128)S(1)}, f32[1,1,1536]{2,1,0:T(1,128)S(1)}, u32[]{:S(2)}, u32[]{:S(2)}) collective-permute-start(f32[1,1,1536]{2,1,0:T(1,128)S(1)} %shard_map.164), channel_id=1, source_target_pairs={{0,16},{2,18},{4,20},{6,22},{8,24},{10,26},{12,28},{14,30},{16,0},... | collective-permute-start | bytes 18440 | tf_op jit(solution)/shard_map/ppermute | solution.py:619
  54.5 2.9 %collective-permute-start = (s32[8,1,384]{2,1,0:T(1,128)S(1)}, s32[8,1,384]{2,1,0:T(1,128)S(1)}, u32[]{:S(2)}, u32[]{:S(2)}) collective-permute-start(s32[8,1,384]{2,1,0:T(1,128)S(1)} %all_to_all.15.got_ref), channel_id=1, source_target_pairs={{0,16},{2,18},{4,20},{6,22},{8,24},{10,26},{12,28},{14,30},{16,0},... | collective-permute-start | bytes 36872 | tf_op jit(solution)/shard_map/ppermute | solution.py:619
  63.3 2.2 %shard_map.161 = bf16[2,128,384]{2,1,0:T(8,128)(2,1)S(1)} custom-call(s32[4,5]{1,0:T(4,128)} %ids_ref.5, s32[1]{0:T(128)} %bitcast.self_ref.refs_0_, bf16[4,5,128,128]{3,2,1,0:T(8,128)(2,1)} %get-tuple-element.26.kept_hbm, bf16[4,128,384]{2,1,0:T(8,128)(2,1)} %bitcast.24, bf16[8,256,384]{2,1,0:T(8,128)(2,1)S(1)} %all-to-all-done.1.remote_ref), custom_call_target="tpu_custom_call" | custom-call | flops 125829120 | bytes 2818132 | tf_op jit(solution)/shard_map/pallas_call | solution.py:56
  68.4 2.6 %collective-permute-done.10.far_ref = f32[8,1,1536]{2,1,0:T(1,128)S(1)} collective-permute-done((f32[8,1,1536]{2,1,0:T(1,128)S(1)}, f32[8,1,1536]{2,1,0:T(1,128)S(1)}, u32[]{:S(2)}, u32[]{:S(2)}) %collective-permute-start.10) | collective-permute-done | bytes 49184 | tf_op jit(solution)/shard_map/ppermute | solution.py:619
  71.0 4.2 %shard_map.165 = (bf16[512,384]{1,0:T(8,128)(2,1)}, bf16[512,384]{1,0:T(8,128)(2,1)S(1)}, bf16[512,384]{1,0:T(8,128)(2,1)}, bf16[512,384]{1,0:T(8,128)(2,1)}) custom-call(s32[1]{0:T(128)} %bitcast.self_ref.refs_0_, s32[1]{0:T(128)} %bitcast.1.core_ref.refs_1_, bf16[256,384]{1,0:T(8,128)(2,1)S(1)} %bitcast.29, bf16[256,384]{1,0:T(8,128)(2,1)S(1)} %bitcast.31, ...), custom_call_target="tpu_custom_call" | custom-call | flops 301989888 | bytes 4685832 | tf_op jit(solution)/shard_map/pallas_call | solution.py:56
  77.0 4.2 %shard_map.166 = (bf16[16,128,384]{2,1,0:T(8,128)(2,1)}, bf16[512,384]{1,0:T(8,128)(2,1)}) custom-call(s32[4,5]{1,0:T(4,128)S(1)} %copy-done.10, s32[1]{0:T(128)} %bitcast.self_ref.refs_0_, s32[1]{0:T(128)} %bitcast.1.core_ref.refs_1_, bf16[512,384]{1,0:T(8,128)(2,1)S(1)} %get-tuple-element.34.mine_ref, ...), custom_call_target="tpu_custom_call" | custom-call | flops 553648128 | bytes 3997784 | tf_op jit(solution)/shard_map/pallas_call | solution.py:56
  81.2 6.1 %all-to-all-start.2 = ((bf16[16,128,384]{2,1,0:T(8,128)(2,1)}), bf16[16,128,384]{2,1,0:T(8,128)(2,1)S(1)}, u32[]{:S(2)}, u32[]{:S(2)}) async-start(bf16[16,128,384]{2,1,0:T(8,128)(2,1)} %get-tuple-element.47), calls=%async_computation.2 | async-start | bytes 3145728 | tf_op jit(solution)/shard_map/all_to_all | solution.py:624
  87.4 2.9 %shard_map.167 = (bf16[8,56,384]{2,1,0:T(8,128)(2,1)S(1)}, bf16[8,56,384]{2,1,0:T(8,128)(2,1)S(1)}) custom-call(s32[1]{0:T(128)} %bitcast.self_ref.refs_0_, s32[1]{0:T(128)} %bitcast.1.core_ref.refs_1_, bf16[512,384]{1,0:T(8,128)(2,1)} %get-tuple-element.33.refs_2_, bf16[512,384]{1,0:T(8,128)(2,1)} %copy-done.8, bf16[512,384]{1,0:T(8,128)(2,1)} %get-tuple-element.35.refs_4_, ...), custom_call_target="tpu_custom_call" | custom-call | flops 402653184 | bytes 2916360 | tf_op jit(solution)/shard_map/pallas_call | solution.py:56
  92.2 10.4 %collective-permute-done.12.theirs_ref = bf16[8,56,384]{2,1,0:T(8,128)(2,1)S(1)} collective-permute-done((bf16[8,56,384]{2,1,0:T(8,128)(2,1)S(1)}, bf16[8,56,384]{2,1,0:T(8,128)(2,1)S(1)}, u32[]{:S(2)}, u32[]{:S(2)}) %collective-permute-start.12) | collective-permute-done | bytes 344096 | tf_op jit(solution)/shard_map/ppermute | solution.py:619
  102.7 3.6 %collective-permute-start.13 = (bf16[4,56,384]{2,1,0:T(8,128)(2,1)S(1)}, bf16[4,56,384]{2,1,0:T(8,128)(2,1)S(1)}, u32[]{:S(2)}, u32[]{:S(2)}) collective-permute-start(bf16[4,56,384]{2,1,0:T(8,128)(2,1)S(1)} %get-tuple-element.40), channel_id=1, source_target_pairs={{0,4},{2,6},{4,0},{6,2},{8,12},{10,14},{12,8},{14,10},{16,20},{18,... | collective-permute-start | bytes 516104 | tf_op jit(solution)/shard_map/ppermute | solution.py:619
  106.4 5.7 %collective-permute-done.13.theirs_ref = bf16[4,56,384]{2,1,0:T(8,128)(2,1)S(1)} collective-permute-done((bf16[4,56,384]{2,1,0:T(8,128)(2,1)S(1)}, bf16[4,56,384]{2,1,0:T(8,128)(2,1)S(1)}, u32[]{:S(2)}, u32[]{:S(2)}) %collective-permute-start.13) | collective-permute-done | bytes 172064 | tf_op jit(solution)/shard_map/ppermute | solution.py:619
  112.2 3.5 %collective-permute-start.14 = (bf16[2,56,384]{2,1,0:T(8,128)(2,1)S(1)}, bf16[2,56,384]{2,1,0:T(8,128)(2,1)S(1)}, u32[]{:S(2)}, u32[]{:S(2)}) collective-permute-start(bf16[2,56,384]{2,1,0:T(8,128)(2,1)S(1)} %get-tuple-element.42), channel_id=1, source_target_pairs={{0,8},{2,10},{4,12},{6,14},{8,0},{10,2},{12,4},{14,6},{16,24},{18,... | collective-permute-start | bytes 258056 | tf_op jit(solution)/shard_map/ppermute | solution.py:619
  115.6 5.1 %collective-permute-done.14.theirs_ref = bf16[2,56,384]{2,1,0:T(8,128)(2,1)S(1)} collective-permute-done((bf16[2,56,384]{2,1,0:T(8,128)(2,1)S(1)}, bf16[2,56,384]{2,1,0:T(8,128)(2,1)S(1)}, u32[]{:S(2)}, u32[]{:S(2)}) %collective-permute-start.14) | collective-permute-done | bytes 86048 | tf_op jit(solution)/shard_map/ppermute | solution.py:619
  121.0 2.4 %shard_map.172.local_hbm = f32[4,128,384]{2,1,0:T(8,128)S(1)} custom-call(s32[4,5]{1,0:T(4,128)S(1)} %copy-done.10, s32[1]{0:T(128)} %bitcast.self_ref.refs_0_, bf16[4,128,384]{2,1,0:T(8,128)(2,1)S(1)} %bitcast.27, bf16[4,5,128,128]{3,2,1,0:T(8,128)(2,1)S(1)} %copy-done.4, bf16[4,128,384]{2,1,0:T(8,128)(2,1)S(1)} %bitcast.26), custom_call_target="tpu_custom_call" | custom-call | flops 251658240 | bytes 2228308 | tf_op jit(solution)/shard_map/pallas_call | solution.py:56
  127.2 2.6 %shard_map.173 = bf16[4,128,384]{2,1,0:T(8,128)(2,1)} custom-call(s32[1]{0:T(128)} %bitcast.self_ref.refs_0_, s32[8,2]{1,0:T(8,128)S(1)} %copy.20.asked_ref, s32[8,2]{1,0:T(8,128)S(1)} %copy.23.mate_ref, f32[4,128,384]{2,1,0:T(8,128)} %copy-done.3, bf16[16,128,384]{2,1,0:T(8,128)(2,1)S(1)} %all-to-all-done.2.got_ref), custom_call_target="tpu_custom_call" | custom-call | flops 1000 | bytes 2752644 | tf_op jit(solution)/shard_map/pallas_call | solution.py:56
  (68 shorter events, 24.6 us)
Async XLA Ops:
  0.6 21.9 %collective-permute-start.1 = (bf16[4,128,384]{2,1,0:T(8,128)(2,1)}, bf16[4,128,384]{2,1,0:T(8,128)(2,1)S(1)}, u32[]{:S(2)}, u32[]{:S(2)}) collective-permute-start(bf16[4,128,384]{2,1,0:T(8,128)(2,1)} %bitcast.21), channel_id=1, source_target_pairs={{0,16},{2,18},{4,20},{6,22},{8,24},{10,26},{12,28},{14,30},{16,0},... | collective-permute-start | bytes 1179656 | tf_op jit(solution)/shard_map/ppermute | solution.py:619
  24.1 37.1 %all-to-all-start.1 = ((bf16[8,256,384]{2,1,0:T(8,128)(2,1)}), bf16[8,256,384]{2,1,0:T(8,128)(2,1)S(1)}, u32[]{:S(2)}, u32[]{:S(2)}) async-start(bf16[8,256,384]{2,1,0:T(8,128)(2,1)} %shard_map.159), calls=%async_computation.1 | async-start | bytes 3145728 | tf_op jit(solution)/shard_map/all_to_all | solution.py:624
  35.2 2.6 %collective-permute-start.5 = (bf16[512,768]{1,0:T(8,128)(2,1)}, bf16[512,768]{1,0:T(8,128)(2,1)S(1)}, u32[]{:S(2)}, u32[]{:S(2)}) collective-permute-start(bf16[512,768]{1,0:T(8,128)(2,1)} %shard_map.162.mine_hbm), channel_id=1, source_target_pairs={{0,1},{1,0},{2,3},{3,2},{4,5},{5,4},{6,7},{7,6},{8,9},{9,8},{10,11... | collective-permute-start | bytes 2359304 | tf_op jit(solution)/shard_map/ppermute | solution.py:616
  43.7 15.4 %copy-start = (bf16[512,384]{1,0:T(8,128)(2,1)S(1)}, bf16[512,384]{1,0:T(8,128)(2,1)}, u32[]{:S(2)}) copy-start(bf16[512,384]{1,0:T(8,128)(2,1)} %param.20) | copy-start | bytes 1179652
  43.8 15.4 %copy-start.4 = (bf16[4,5,128,128]{3,2,1,0:T(8,128)(2,1)S(1)}, bf16[4,5,128,128]{3,2,1,0:T(8,128)(2,1)}, u32[]{:S(2)}) copy-start(bf16[4,5,128,128]{3,2,1,0:T(8,128)(2,1)} %adj_ref.5) | copy-start | bytes 1966084
  43.8 15.4 %copy-start.9 = (s32[4,5]{1,0:T(4,128)S(1)}, s32[4,5]{1,0:T(4,128)}, u32[]{:S(2)}) copy-start(s32[4,5]{1,0:T(4,128)} %ids_ref.5) | copy-start | bytes 244
  43.8 2.4 %collective-permute-start.6 = (bf16[512,768]{1,0:T(8,128)(2,1)S(1)}, bf16[512,768]{1,0:T(8,128)(2,1)S(1)}, u32[]{:S(2)}, u32[]{:S(2)}) collective-permute-start(bf16[512,768]{1,0:T(8,128)(2,1)S(1)} %get-tuple-element.31.mine_ref), channel_id=1, source_target_pairs={{0,1},{1,0},{2,3},{3,2},{4,5},{5,4},{6,7},{7,6},{8,9},{9,8},{10,11... | collective-permute-start | bytes 2359304 | tf_op jit(solution)/shard_map/ppermute | solution.py:616
  47.5 4.9 %collective-permute-start.7 = (f32[1,1,1536]{2,1,0:T(1,128)S(1)}, f32[1,1,1536]{2,1,0:T(1,128)S(1)}, u32[]{:S(2)}, u32[]{:S(2)}) collective-permute-start(f32[1,1,1536]{2,1,0:T(1,128)S(1)} %shard_map.164), channel_id=1, source_target_pairs={{0,16},{2,18},{4,20},{6,22},{8,24},{10,26},{12,28},{14,30},{16,0},... | collective-permute-start | bytes 18440 | tf_op jit(solution)/shard_map/ppermute | solution.py:619
  50.8 17.5 %collective-permute-start.4 = (bf16[384,768]{1,0:T(8,128)(2,1)}, bf16[384,768]{1,0:T(8,128)(2,1)}, u32[]{:S(2)}, u32[]{:S(2)}) collective-permute-start(bf16[384,768]{1,0:T(8,128)(2,1)} %w_own_ref.3), channel_id=1, source_target_pairs={{0,1},{1,0},{2,3},{3,2},{4,5},{5,4},{6,7},{7,6},{8,9},{9,8},{10,11... | collective-permute-start | bytes 1769480 | tf_op jit(solution)/shard_map/ppermute | solution.py:616
  52.5 5.0 %collective-permute-start.8 = (f32[2,1,1536]{2,1,0:T(1,128)S(1)}, f32[2,1,1536]{2,1,0:T(1,128)S(1)}, u32[]{:S(2)}, u32[]{:S(2)}) collective-permute-start(f32[2,1,1536]{2,1,0:T(1,128)S(1)} %pad_maximum_fusion.2), channel_id=1, source_target_pairs={{0,8},{2,10},{4,12},{6,14},{8,0},{10,2},{12,4},{14,6},{16,24},{18,... | collective-permute-start | bytes 36872 | tf_op jit(solution)/shard_map/ppermute | solution.py:619
  54.5 4.6 %collective-permute-start = (s32[8,1,384]{2,1,0:T(1,128)S(1)}, s32[8,1,384]{2,1,0:T(1,128)S(1)}, u32[]{:S(2)}, u32[]{:S(2)}) collective-permute-start(s32[8,1,384]{2,1,0:T(1,128)S(1)} %all_to_all.15.got_ref), channel_id=1, source_target_pairs={{0,16},{2,18},{4,20},{6,22},{8,24},{10,26},{12,28},{14,30},{16,0},... | collective-permute-start | bytes 36872 | tf_op jit(solution)/shard_map/ppermute | solution.py:619
  57.5 8.5 %collective-permute-start.9 = (f32[4,1,1536]{2,1,0:T(1,128)S(1)}, f32[4,1,1536]{2,1,0:T(1,128)}, u32[]{:S(2)}, u32[]{:S(2)}) collective-permute-start(f32[4,1,1536]{2,1,0:T(1,128)S(1)} %pad_maximum_fusion.1), channel_id=1, source_target_pairs={{0,4},{2,6},{4,0},{6,2},{8,12},{10,14},{12,8},{14,10},{16,20},{18,... | collective-permute-start | bytes 73736 | tf_op jit(solution)/shard_map/ppermute | solution.py:619
  63.2 7.7 %collective-permute-start.2 = (bf16[256,384]{1,0:T(8,128)(2,1)S(1)}, bf16[256,384]{1,0:T(8,128)(2,1)S(1)}, u32[]{:S(2)}, u32[]{:S(2)}) collective-permute-start(bf16[256,384]{1,0:T(8,128)(2,1)S(1)} %bitcast.28), channel_id=1, source_target_pairs={{0,1},{1,0},{2,3},{3,2},{4,5},{5,4},{6,7},{7,6},{8,9},{9,8},{10,11... | collective-permute-start | bytes 589832 | tf_op jit(solution)/shard_map/ppermute | solution.py:616
  65.5 5.4 %collective-permute-start.3 = (bf16[256,384]{1,0:T(8,128)(2,1)S(1)}, bf16[256,384]{1,0:T(8,128)(2,1)S(1)}, u32[]{:S(2)}, u32[]{:S(2)}) collective-permute-start(bf16[256,384]{1,0:T(8,128)(2,1)S(1)} %bitcast.30), channel_id=1, source_target_pairs={{0,1},{1,0},{2,3},{3,2},{4,5},{5,4},{6,7},{7,6},{8,9},{9,8},{10,11... | collective-permute-start | bytes 589832 | tf_op jit(solution)/shard_map/ppermute | solution.py:616
  66.8 10.2 %copy-start.10 = (s32[4,5]{1,0:T(4,128)S(1)}, s32[4,5]{1,0:T(4,128)}, u32[]{:S(2)}) copy-start(s32[4,5]{1,0:T(4,128)} %ids_ref.5) | copy-start | bytes 244
  66.8 4.2 %collective-permute-start.10 = (f32[8,1,1536]{2,1,0:T(1,128)S(1)}, f32[8,1,1536]{2,1,0:T(1,128)S(1)}, u32[]{:S(2)}, u32[]{:S(2)}) collective-permute-start(f32[8,1,1536]{2,1,0:T(1,128)S(1)} %pad_maximum_fusion.near_ref), channel_id=1, source_target_pairs={{0,2},{2,0},{4,6},{6,4},{8,10},{10,8},{12,14},{14,12},{16,18},{18,... | collective-permute-start | bytes 147464 | tf_op jit(solution)/shard_map/ppermute | solution.py:619
  75.2 1.8 %collective-permute-start.11 = (bf16[512,384]{1,0:T(8,128)(2,1)S(1)}, bf16[512,384]{1,0:T(8,128)(2,1)S(1)}, u32[]{:S(2)}, u32[]{:S(2)}) collective-permute-start(bf16[512,384]{1,0:T(8,128)(2,1)S(1)} %get-tuple-element.34.mine_ref), channel_id=1, source_target_pairs={{0,1},{1,0},{2,3},{3,2},{4,5},{5,4},{6,7},{7,6},{8,9},{9,8},{10,11... | collective-permute-start | bytes 1179656 | tf_op jit(solution)/shard_map/ppermute | solution.py:616
  81.2 45.9 %all-to-all-start.2 = ((bf16[16,128,384]{2,1,0:T(8,128)(2,1)}), bf16[16,128,384]{2,1,0:T(8,128)(2,1)S(1)}, u32[]{:S(2)}, u32[]{:S(2)}) async-start(bf16[16,128,384]{2,1,0:T(8,128)(2,1)} %get-tuple-element.47), calls=%async_computation.2 | async-start | bytes 3145728 | tf_op jit(solution)/shard_map/all_to_all | solution.py:624
  87.4 33.7 %copy-start.2 = (bf16[512,384]{1,0:T(8,128)(2,1)S(1)}, bf16[512,384]{1,0:T(8,128)(2,1)}, u32[]{:S(2)}) copy-start(bf16[512,384]{1,0:T(8,128)(2,1)} %refs_8_.1) | copy-start | bytes 1179652
  87.4 33.7 %copy-start.5 = (bf16[512,384]{1,0:T(8,128)(2,1)S(1)}, bf16[512,384]{1,0:T(8,128)(2,1)}, u32[]{:S(2)}) copy-start(bf16[512,384]{1,0:T(8,128)(2,1)} %get-tuple-element.36.refs_5_) | copy-start | bytes 1179652
  90.3 12.3 %collective-permute-start.12 = (bf16[8,56,384]{2,1,0:T(8,128)(2,1)S(1)}, bf16[8,56,384]{2,1,0:T(8,128)(2,1)S(1)}, u32[]{:S(2)}, u32[]{:S(2)}) collective-permute-start(bf16[8,56,384]{2,1,0:T(8,128)(2,1)S(1)} %get-tuple-element.38), channel_id=1, source_target_pairs={{0,2},{2,0},{4,6},{6,4},{8,10},{10,8},{12,14},{14,12},{16,18},{18,... | collective-permute-start | bytes 1032200 | tf_op jit(solution)/shard_map/ppermute | solution.py:619
  102.7 9.4 %collective-permute-start.13 = (bf16[4,56,384]{2,1,0:T(8,128)(2,1)S(1)}, bf16[4,56,384]{2,1,0:T(8,128)(2,1)S(1)}, u32[]{:S(2)}, u32[]{:S(2)}) collective-permute-start(bf16[4,56,384]{2,1,0:T(8,128)(2,1)S(1)} %get-tuple-element.40), channel_id=1, source_target_pairs={{0,4},{2,6},{4,0},{6,2},{8,12},{10,14},{12,8},{14,10},{16,20},{18,... | collective-permute-start | bytes 516104 | tf_op jit(solution)/shard_map/ppermute | solution.py:619
  112.2 8.6 %collective-permute-start.14 = (bf16[2,56,384]{2,1,0:T(8,128)(2,1)S(1)}, bf16[2,56,384]{2,1,0:T(8,128)(2,1)S(1)}, u32[]{:S(2)}, u32[]{:S(2)}) collective-permute-start(bf16[2,56,384]{2,1,0:T(8,128)(2,1)S(1)} %get-tuple-element.42), channel_id=1, source_target_pairs={{0,8},{2,10},{4,12},{6,14},{8,0},{10,2},{12,4},{14,6},{16,24},{18,... | collective-permute-start | bytes 258056 | tf_op jit(solution)/shard_map/ppermute | solution.py:619
  120.8 5.7 %collective-permute-start.15 = (bf16[1,56,384]{2,1,0:T(8,128)(2,1)S(1)}, bf16[1,56,384]{2,1,0:T(8,128)(2,1)S(1)}, u32[]{:S(2)}, u32[]{:S(2)}) collective-permute-start(bf16[1,56,384]{2,1,0:T(8,128)(2,1)S(1)} %get-tuple-element.44), channel_id=1, source_target_pairs={{0,16},{2,18},{4,20},{6,22},{8,24},{10,26},{12,28},{14,30},{16,0},... | collective-permute-start | bytes 129032 | tf_op jit(solution)/shard_map/ppermute | solution.py:619
  (8 other events, 51.7 us)

commit v9 on v8

--- a/solution.py
+++ b/solution.py
@@ -18,6 +18,7 @@
 NO_NODE = -(1 << 20)
 ROOT = 0.7978845608028654
 CUBE = 0.044715
+
 
 VMEM = pl.BlockSpec(memory_space=pltpu.VMEM)
 HBM = pl.BlockSpec(memory_space=pltpu.HBM)
@@ -312,12 +313,21 @@
         out_ref[:, :, t * width : (t + 1) * width] = pooled.reshape(1, 1, width)
 
 
-def pooled_rows(me, near_ref, far_ref, width):
-    shards = 2 * near_ref.shape[0]
+def digits(shards):
+    high, found = shards.bit_length() - 1, []
+    while high > 0:
+        low = max(high - 2, 0)
+        found.append((low, high - low))
+        high = low
+    return found
+
+
+def pooled_rows(me, pieces, width):
+    shards = sum(piece.shape[0] for piece in pieces)
     parts = []
-    for first in range(0, near_ref.shape[2], width):
-        for ref in (near_ref, far_ref):
-            part = ref[:, :, first : first + width].reshape(shards // 2, width)
+    for first in range(0, pieces[0].shape[2], width):
+        for ref in pieces:
+            part = ref[:, :, first : first + width].reshape(ref.shape[0], width)
             parts.append(part.astype(jnp.bfloat16))
     stacked = jnp.concatenate(parts, axis=0)
     texts = stacked.shape[0]
@@ -325,11 +335,9 @@
     column = lax.broadcasted_iota(jnp.int32, (texts, texts), 1)
     place = column & (shards - 1)
     offset = jnp.zeros_like(place)
-    reach = 1
-    while reach < shards:
-        offset = 2 * offset + (place & 1)
-        place = lax.shift_right_logical(place, 1)
-        reach *= 2
+    for low, count in digits(shards):
+        offset = offset + ((place & ((1 << count) - 1)) << low)
+        place = lax.shift_right_logical(place, count)
     source = column - (column & (shards - 1)) + (offset ^ me)
     order = jnp.where(row == source, 1.0, 0.0).astype(jnp.bfloat16)
     return mm(order, stacked).astype(jnp.bfloat16)
@@ -378,14 +386,17 @@
 
 def forward_body(
     self_ref, core_ref, top_ref, bottom_ref, far_top_ref, far_bottom_ref, w_own_ref, w_other_ref,
-    grad_ref, own_ref, base_hbm, pick_ref, near_ref, far_ref, node_hbm, slope_ref, agg_hbm, slope_hbm,
-    rows_ref, node_ref, agg_ref, base_ref, node_sems, agg_sems, slope_sems, base_sems
+    grad_ref, own_ref, base_hbm, pick_ref, *refs
 ):
+    (
+        *pieces, node_hbm, slope_ref, agg_hbm, slope_hbm,
+        rows_ref, node_ref, agg_ref, base_ref, node_sems, agg_sems, slope_sems, base_sems
+    ) = refs
     based = copies([(base_hbm, base_ref)], base_sems)
     half = top_ref.shape[1]
     start = pl.multiple_of(core_ref[0] * half, LANES)
     far = pl.multiple_of((1 - core_ref[0]) * half, LANES)
-    rows_ref[...] = pooled_rows(self_ref[0], near_ref, far_ref, rows_ref.shape[1])
+    rows_ref[...] = pooled_rows(self_ref[0], pieces, rows_ref.shape[1])
     texts = rows_ref.shape[0]
     here = rows_ref[:, pl.ds(start, half)]
     w_own = w_own_ref[:, pl.ds(start, half)]
@@ -486,28 +497,6 @@
     down_ref[...] = down.astype(jnp.bfloat16)
     down_copy = pltpu.make_async_copy(down_ref, down_hbm, sems.at[0])
     down_copy.start()
-
-    def slot_of(r, k):
-        tile_id = ids_ref[r, k]
-        _, owner, _ = tile_of(tile_id, tiles_here)
-        away = (tile_id >= 0) & (owner != me)
-        return away, jnp.where(away, owner, shards)
-
-    def slot_copy(slot):
-        return pltpu.make_async_copy(send_ref.at[slot], send_hbm.at[slot], slot_sems.at[slot])
-
-    def each_away(r, act):
-        def one(k, carry):
-            away, slot = slot_of(r, k)
-
-            @pl.when(away)
-            def _():
-                act(slot_copy(slot))
-
-            return carry
-
-        lax.fori_loop(0, entries, one, 0)
-
     for r in range(tiles_here):
         rows = slice(r * tile_rows, (r + 1) * tile_rows)
         for first in range(0, entries, 6):
@@ -515,11 +504,12 @@
             side_by_side = jnp.concatenate([adj_ref[r, k] for k in group], axis=1)
             product = mm(side_by_side, down_ref[rows, :], (0, 0)).astype(jnp.bfloat16)
             for k in group:
-                _, slot = slot_of(r, k)
+                tile_id = ids_ref[r, k]
+                _, owner, _ = tile_of(tile_id, tiles_here)
+                slot = jnp.where((tile_id >= 0) & (owner != me), owner, shards)
                 send_ref[slot] = product[(k - first) * tile_rows : (k - first + 1) * tile_rows]
-        each_away(r, lambda copy: copy.start())
-    for r in range(tiles_here):
-        each_away(r, lambda copy: copy.wait())
+    for copy in copies([(send_ref.at[q], send_hbm.at[q]) for q in range(shards)], slot_sems):
+        copy.wait()
     down_copy.wait()
 
 
@@ -715,13 +705,12 @@
         [SMEM, VMEM, VMEM, VMEM, VMEM],
         flops=20 * count * width,
     )
-    near = pooled
-    reach = peers
-    far = toward(near, reach)
-    while reach > 1:
-        reach = reach // 2
-        near = jnp.concatenate([near, far], axis=0)
-        far = toward(near, reach)
+    pieces = [pooled]
+    for low, bits in digits(shards):
+        state = pieces[0] if len(pieces) == 1 else jnp.concatenate(pieces, axis=0)
+        pieces = [state]
+        for c in range(1, 1 << bits):
+            pieces.append(toward(state, c << low))
 
     kept, pick, own, base = call(
         mask_body,
@@ -770,9 +759,9 @@
         [
             me, core, top, bottom, swap(top), swap(bottom), w_gnn, w_other,
             out_grad,
-            own.reshape(nodes_here, slots), base.reshape(nodes_here, half), picked, near, far,
-        ],
-        [SMEM, SMEM] + [HELD] * 4 + [VMEM] * 4 + [HBM] + [VMEM] * 3,
+            own.reshape(nodes_here, slots), base.reshape(nodes_here, half), picked, *pieces,
+        ],
+        [SMEM, SMEM] + [HELD] * 4 + [VMEM] * 4 + [HBM] + [VMEM] * (1 + len(pieces)),
         flops=4 * nodes_here * half * half,
         scratch=[
             pltpu.VMEM((texts, width), jnp.bfloat16),

time: 131 us -> 129 us (0.985)
    ppermute x6, waiting for transfers between devices: 6.35 us -> 4.2 us  [swap(): lax.ppermute(values, 'mp', [(i, cores - 1 - i) for i in range(cores)])]
    ppermute x10 -> x12, waiting for transfers between devices: 31.5 us -> 33.1 us  [toward(): lax.ppermute(values, 'graph', [(i, i ^ reach) for i in range(shards)])]
    ppermute x10 -> x12, starting transfers between devices: 24.8 us -> 25.2 us  [toward(): lax.ppermute(values, 'graph', [(i, i ^ reach) for i in range(shards)])]
  transfers between devices with their start and end apart: 18 -> 20, of which waited for: 11 -> 11; matrix products, arithmetic and copies ran while one was open for 1% -> 0% of each run, Pallas kernels for 23% -> 24%
where the time goes in v9:
time: 129 us; the launch traced here: 128 us
  Pallas kernels  42.6 us (33%)
  waiting for transfers between devices  37.3 us (29%)
  starting transfers between devices  35.6 us (28%)
  blocking collectives  10.1 us (8%)
  local copies, waits for them, and re-layouts  1.32 us (1%)
    pallas_call x18, Pallas kernels, call(): pl.pallas_call(body, out_shape=tuple(outs) if many else outs[0], in_specs...  42.6 us
    ppermute x12, waiting for transfers between devices, toward(): lax.ppermute(values, 'graph', [(i, i ^ reach) for i in range(shards)])  33.1 us
    ppermute x12, starting transfers between devices, toward(): lax.ppermute(values, 'graph', [(i, i ^ reach) for i in range(shards)])  25.2 us
    all_to_all x1, blocking collectives, spread(): lax.all_to_all(values, 'graph', split_axis=0, concat_axis=0, tiled=True,...  10.1 us
    all_to_all x2, starting transfers between devices, spread(): lax.all_to_all(values, 'graph', split_axis=0, concat_axis=0, tiled=True,...  9.18 us
    ppermute x6, waiting for transfers between devices, swap(): lax.ppermute(values, 'mp', [(i, cores - 1 - i) for i in range(cores)])  4.2 us
  transfers between devices with their start and end apart: 20, of which 11 were waited for; matrix products, arithmetic and copies ran while one was open for 0% of the time, Pallas kernels for 24%

profile of v9, /device:TPU:0, one launch (start us, length us, event | category | flops | bytes accessed | tf_op | source)
XLA Modules:
  0.0 128.2 jit_solution(14488992332306301557)
XLA Ops:
  0.6 4.1 %collective-permute-start.1 = (bf16[4,128,384]{2,1,0:T(8,128)(2,1)}, bf16[4,128,384]{2,1,0:T(8,128)(2,1)S(1)}, u32[]{:S(2)}, u32[]{:S(2)}) collective-permute-start(bf16[4,128,384]{2,1,0:T(8,128)(2,1)} %bitcast.21), channel_id=1, source_target_pairs={{0,16},{2,18},{4,20},{6,22},{8,24},{10,26},{12,28},{14,30},{16,0},... | collective-permute-start | bytes 1179656 | tf_op jit(solution)/shard_map/ppermute | solution.py:609
  5.7 10.1 %all_to_all.15.got_ref = s32[8,1,384]{2,1,0:T(1,128)S(1)} all-to-all(s32[8,1,384]{2,1,0:T(1,128)S(1)} %shard_map.156), channel_id=1, replica_groups={{0,2,4,6,8,10,12,14},{16,18,20,22,24,26,28,30},{1,3,5,7,9,11,13,15},{17..., dimensions={0} | all-to-all | bytes 24576 | tf_op jit(solution)/shard_map/all_to_all | solution.py:614
  16.0 2.6 %shard_map.158.near_hbm = bf16[8,256,384]{2,1,0:T(8,128)(2,1)} custom-call(s32[8,2]{1,0:T(8,128)S(1)} %copy.20.asked_ref, bf16[4,128,384]{2,1,0:T(8,128)(2,1)} %bitcast.22), custom_call_target="tpu_custom_call" | custom-call | flops 1000 | bytes 1966144 | tf_op jit(solution)/shard_map/pallas_call | solution.py:57
  18.6 3.9 %collective-permute-done.1.mate_ref = bf16[4,128,384]{2,1,0:T(8,128)(2,1)S(1)} collective-permute-done((bf16[4,128,384]{2,1,0:T(8,128)(2,1)}, bf16[4,128,384]{2,1,0:T(8,128)(2,1)S(1)}, u32[]{:S(2)}, u32[]{:S(2)}) %collective-permute-start.1) | collective-permute-done | bytes 393248 | tf_op jit(solution)/shard_map/ppermute | solution.py:609
  24.1 4.0 %all-to-all-start.1 = ((bf16[8,256,384]{2,1,0:T(8,128)(2,1)}), bf16[8,256,384]{2,1,0:T(8,128)(2,1)S(1)}, u32[]{:S(2)}, u32[]{:S(2)}) async-start(bf16[8,256,384]{2,1,0:T(8,128)(2,1)} %shard_map.159), calls=%async_computation.1 | async-start | bytes 3145728 | tf_op jit(solution)/shard_map/all_to_all | solution.py:614
  28.1 7.1 %shard_map.162.mine_hbm = bf16[512,768]{1,0:T(8,128)(2,1)} custom-call(s32[1,2]{1,0:T(1,128)S(1)} %copy-done.12, bf16[512,768]{1,0:T(8,128)(2,1)} %bitcast.36, bf16[3,768,384]{2,1,0:T(8,128)(2,1)} %bitcast.45, bf16[384,768]{1,0:T(8,128)(2,1)} %w_out_hbm.1), custom_call_target="tpu_custom_call" | custom-call | flops 1610612736 | bytes 3932168 | tf_op jit(solution)/shard_map/pallas_call | solution.py:57
  35.3 2.5 %collective-permute-done.5.other_ref = bf16[512,768]{1,0:T(8,128)(2,1)S(1)} collective-permute-done((bf16[512,768]{1,0:T(8,128)(2,1)}, bf16[512,768]{1,0:T(8,128)(2,1)S(1)}, u32[]{:S(2)}, u32[]{:S(2)}) %collective-permute-start.5) | collective-permute-done | bytes 786464 | tf_op jit(solution)/shard_map/ppermute | solution.py:606
  37.8 5.9 %shard_map.163 = (bf16[512,768]{1,0:T(8,128)(2,1)S(1)}, bf16[512,768]{1,0:T(8,128)(2,1)S(1)}) custom-call(bf16[512,768]{1,0:T(8,128)(2,1)S(1)} %bitcast.37, bf16[512,768]{1,0:T(8,128)(2,1)} %shard_map.162.mine_hbm, bf16[512,768]{1,0:T(8,128)(2,1)S(1)} %collective-permute-done.5.other_ref, bf16[768,1536]{1,0:T(8,128)(2,1)} %up_hbm.1, ...), custom_call_target="tpu_custom_call" | custom-call | flops 2415919104 | bytes 8656896 | tf_op jit(solution)/shard_map/pallas_call | solution.py:57
  44.3 3.3 %collective-permute-start = (s32[8,1,384]{2,1,0:T(1,128)S(1)}, s32[8,1,384]{2,1,0:T(1,128)S(1)}, u32[]{:S(2)}, u32[]{:S(2)}) collective-permute-start(s32[8,1,384]{2,1,0:T(1,128)S(1)} %all_to_all.15.got_ref), channel_id=1, source_target_pairs={{0,16},{2,18},{4,20},{6,22},{8,24},{10,26},{12,28},{14,30},{16,0},... | collective-permute-start | bytes 36872 | tf_op jit(solution)/shard_map/ppermute | solution.py:609
  52.7 4.4 %collective-permute-start.9 = (f32[1,1,1536]{2,1,0:T(1,128)S(1)}, f32[1,1,1536]{2,1,0:T(1,128)S(1)}, u32[]{:S(2)}, u32[]{:S(2)}) collective-permute-start(f32[1,1,1536]{2,1,0:T(1,128)S(1)} %shard_map.164), channel_id=1, source_target_pairs={{0,24},{2,26},{4,28},{6,30},{8,16},{10,18},{12,20},{14,22},{16,8},... | collective-permute-start | bytes 18440 | tf_op jit(solution)/shard_map/ppermute | solution.py:609
  59.8 2.2 %shard_map.161 = bf16[2,128,384]{2,1,0:T(8,128)(2,1)S(1)} custom-call(s32[4,5]{1,0:T(4,128)} %ids_ref.5, s32[1]{0:T(128)} %bitcast.self_ref.refs_0_, bf16[4,5,128,128]{3,2,1,0:T(8,128)(2,1)} %get-tuple-element.26.kept_hbm, bf16[4,128,384]{2,1,0:T(8,128)(2,1)} %bitcast.24, bf16[8,256,384]{2,1,0:T(8,128)(2,1)S(1)} %all-to-all-done.1.remote_ref), custom_call_target="tpu_custom_call" | custom-call | flops 125829120 | bytes 2818132 | tf_op jit(solution)/shard_map/pallas_call | solution.py:57
  68.0 2.3 %collective-permute-done.12.refs_3_ = f32[4,1,1536]{2,1,0:T(1,128)S(1)} collective-permute-done((f32[4,1,1536]{2,1,0:T(1,128)S(1)}, f32[4,1,1536]{2,1,0:T(1,128)S(1)}, u32[]{:S(2)}, u32[]{:S(2)}) %collective-permute-start.12) | collective-permute-done | bytes 24608 | tf_op jit(solution)/shard_map/ppermute | solution.py:609
  70.4 4.4 %shard_map.165 = (bf16[512,384]{1,0:T(8,128)(2,1)}, bf16[512,384]{1,0:T(8,128)(2,1)S(1)}, bf16[512,384]{1,0:T(8,128)(2,1)}, bf16[512,384]{1,0:T(8,128)(2,1)}) custom-call(s32[1]{0:T(128)} %bitcast.self_ref.refs_0_, s32[1]{0:T(128)} %bitcast.1.core_ref.refs_1_, bf16[256,384]{1,0:T(8,128)(2,1)S(1)} %bitcast.29, bf16[256,384]{1,0:T(8,128)(2,1)S(1)} %bitcast.31, ...), custom_call_target="tpu_custom_call" | custom-call | flops 301989888 | bytes 4685832 | tf_op jit(solution)/shard_map/pallas_call | solution.py:57
  76.6 3.9 %shard_map.166 = (bf16[16,128,384]{2,1,0:T(8,128)(2,1)}, bf16[512,384]{1,0:T(8,128)(2,1)}) custom-call(s32[4,5]{1,0:T(4,128)S(1)} %copy-done.10, s32[1]{0:T(128)} %bitcast.self_ref.refs_0_, s32[1]{0:T(128)} %bitcast.1.core_ref.refs_1_, bf16[512,384]{1,0:T(8,128)(2,1)S(1)} %get-tuple-element.34.mine_ref, ...), custom_call_target="tpu_custom_call" | custom-call | flops 553648128 | bytes 3997784 | tf_op jit(solution)/shard_map/pallas_call | solution.py:57
  80.5 5.2 %all-to-all-start.2 = ((bf16[16,128,384]{2,1,0:T(8,128)(2,1)}), bf16[16,128,384]{2,1,0:T(8,128)(2,1)S(1)}, u32[]{:S(2)}, u32[]{:S(2)}) async-start(bf16[16,128,384]{2,1,0:T(8,128)(2,1)} %get-tuple-element.47), calls=%async_computation.2 | async-start | bytes 3145728 | tf_op jit(solution)/shard_map/all_to_all | solution.py:614
  85.7 2.9 %shard_map.167 = (bf16[8,56,384]{2,1,0:T(8,128)(2,1)S(1)}, bf16[8,56,384]{2,1,0:T(8,128)(2,1)S(1)}) custom-call(s32[1]{0:T(128)} %bitcast.self_ref.refs_0_, s32[1]{0:T(128)} %bitcast.1.core_ref.refs_1_, bf16[512,384]{1,0:T(8,128)(2,1)} %get-tuple-element.33.refs_2_, bf16[512,384]{1,0:T(8,128)(2,1)} %copy-done.8, bf16[512,384]{1,0:T(8,128)(2,1)} %get-tuple-element.35.refs_4_, ...), custom_call_target="tpu_custom_call" | custom-call | flops 402653184 | bytes 2916360 | tf_op jit(solution)/shard_map/pallas_call | solution.py:57
  90.6 10.4 %collective-permute-done.14.theirs_ref = bf16[8,56,384]{2,1,0:T(8,128)(2,1)S(1)} collective-permute-done((bf16[8,56,384]{2,1,0:T(8,128)(2,1)S(1)}, bf16[8,56,384]{2,1,0:T(8,128)(2,1)S(1)}, u32[]{:S(2)}, u32[]{:S(2)}) %collective-permute-start.14) | collective-permute-done | bytes 344096 | tf_op jit(solution)/shard_map/ppermute | solution.py:609
  101.0 3.6 %collective-permute-start.15 = (bf16[4,56,384]{2,1,0:T(8,128)(2,1)S(1)}, bf16[4,56,384]{2,1,0:T(8,128)(2,1)S(1)}, u32[]{:S(2)}, u32[]{:S(2)}) collective-permute-start(bf16[4,56,384]{2,1,0:T(8,128)(2,1)S(1)} %get-tuple-element.40), channel_id=1, source_target_pairs={{0,4},{2,6},{4,0},{6,2},{8,12},{10,14},{12,8},{14,10},{16,20},{18,... | collective-permute-start | bytes 516104 | tf_op jit(solution)/shard_map/ppermute | solution.py:609
  104.7 5.7 %collective-permute-done.15.theirs_ref = bf16[4,56,384]{2,1,0:T(8,128)(2,1)S(1)} collective-permute-done((bf16[4,56,384]{2,1,0:T(8,128)(2,1)S(1)}, bf16[4,56,384]{2,1,0:T(8,128)(2,1)S(1)}, u32[]{:S(2)}, u32[]{:S(2)}) %collective-permute-start.15) | collective-permute-done | bytes 172064 | tf_op jit(solution)/shard_map/ppermute | solution.py:609
  110.5 3.5 %collective-permute-start.16 = (bf16[2,56,384]{2,1,0:T(8,128)(2,1)S(1)}, bf16[2,56,384]{2,1,0:T(8,128)(2,1)S(1)}, u32[]{:S(2)}, u32[]{:S(2)}) collective-permute-start(bf16[2,56,384]{2,1,0:T(8,128)(2,1)S(1)} %get-tuple-element.42), channel_id=1, source_target_pairs={{0,8},{2,10},{4,12},{6,14},{8,0},{10,2},{12,4},{14,6},{16,24},{18,... | collective-permute-start | bytes 258056 | tf_op jit(solution)/shard_map/ppermute | solution.py:609
  114.0 5.1 %collective-permute-done.16.theirs_ref = bf16[2,56,384]{2,1,0:T(8,128)(2,1)S(1)} collective-permute-done((bf16[2,56,384]{2,1,0:T(8,128)(2,1)S(1)}, bf16[2,56,384]{2,1,0:T(8,128)(2,1)S(1)}, u32[]{:S(2)}, u32[]{:S(2)}) %collective-permute-start.16) | collective-permute-done | bytes 86048 | tf_op jit(solution)/shard_map/ppermute | solution.py:609
  119.4 2.4 %shard_map.172.local_hbm = f32[4,128,384]{2,1,0:T(8,128)S(1)} custom-call(s32[4,5]{1,0:T(4,128)S(1)} %copy-done.10, s32[1]{0:T(128)} %bitcast.self_ref.refs_0_, bf16[4,128,384]{2,1,0:T(8,128)(2,1)S(1)} %bitcast.27, bf16[4,5,128,128]{3,2,1,0:T(8,128)(2,1)S(1)} %copy-done.4, bf16[4,128,384]{2,1,0:T(8,128)(2,1)S(1)} %bitcast.26), custom_call_target="tpu_custom_call" | custom-call | flops 251658240 | bytes 2228308 | tf_op jit(solution)/shard_map/pallas_call | solution.py:57
  122.7 2.1 %collective-permute-done.17.theirs_ref = bf16[1,56,384]{2,1,0:T(8,128)(2,1)S(1)} collective-permute-done((bf16[1,56,384]{2,1,0:T(8,128)(2,1)S(1)}, bf16[1,56,384]{2,1,0:T(8,128)(2,1)S(1)}, u32[]{:S(2)}, u32[]{:S(2)}) %collective-permute-start.17) | collective-permute-done | bytes 43040 | tf_op jit(solution)/shard_map/ppermute | solution.py:609
  125.5 2.6 %shard_map.173 = bf16[4,128,384]{2,1,0:T(8,128)(2,1)} custom-call(s32[1]{0:T(128)} %bitcast.self_ref.refs_0_, s32[8,2]{1,0:T(8,128)S(1)} %copy.20.asked_ref, s32[8,2]{1,0:T(8,128)S(1)} %copy.23.mate_ref, f32[4,128,384]{2,1,0:T(8,128)} %copy-done.3, bf16[16,128,384]{2,1,0:T(8,128)(2,1)S(1)} %all-to-all-done.2.got_ref), custom_call_target="tpu_custom_call" | custom-call | flops 1000 | bytes 2752644 | tf_op jit(solution)/shard_map/pallas_call | solution.py:57
  (70 shorter events, 22.9 us)
Async XLA Ops:
  0.6 21.9 %collective-permute-start.1 = (bf16[4,128,384]{2,1,0:T(8,128)(2,1)}, bf16[4,128,384]{2,1,0:T(8,128)(2,1)S(1)}, u32[]{:S(2)}, u32[]{:S(2)}) collective-permute-start(bf16[4,128,384]{2,1,0:T(8,128)(2,1)} %bitcast.21), channel_id=1, source_target_pairs={{0,16},{2,18},{4,20},{6,22},{8,24},{10,26},{12,28},{14,30},{16,0},... | collective-permute-start | bytes 1179656 | tf_op jit(solution)/shard_map/ppermute | solution.py:609
  24.1 33.7 %all-to-all-start.1 = ((bf16[8,256,384]{2,1,0:T(8,128)(2,1)}), bf16[8,256,384]{2,1,0:T(8,128)(2,1)S(1)}, u32[]{:S(2)}, u32[]{:S(2)}) async-start(bf16[8,256,384]{2,1,0:T(8,128)(2,1)} %shard_map.159), calls=%async_computation.1 | async-start | bytes 3145728 | tf_op jit(solution)/shard_map/all_to_all | solution.py:614
  35.2 14.1 %copy-start = (bf16[512,384]{1,0:T(8,128)(2,1)S(1)}, bf16[512,384]{1,0:T(8,128)(2,1)}, u32[]{:S(2)}) copy-start(bf16[512,384]{1,0:T(8,128)(2,1)} %param.20) | copy-start | bytes 1179652
  35.2 14.1 %copy-start.4 = (bf16[4,5,128,128]{3,2,1,0:T(8,128)(2,1)S(1)}, bf16[4,5,128,128]{3,2,1,0:T(8,128)(2,1)}, u32[]{:S(2)}) copy-start(bf16[4,5,128,128]{3,2,1,0:T(8,128)(2,1)} %adj_ref.5) | copy-start | bytes 1966084
  35.2 2.6 %collective-permute-start.5 = (bf16[512,768]{1,0:T(8,128)(2,1)}, bf16[512,768]{1,0:T(8,128)(2,1)S(1)}, u32[]{:S(2)}, u32[]{:S(2)}) collective-permute-start(bf16[512,768]{1,0:T(8,128)(2,1)} %shard_map.162.mine_hbm), channel_id=1, source_target_pairs={{0,1},{1,0},{2,3},{3,2},{4,5},{5,4},{6,7},{7,6},{8,9},{9,8},{10,11... | collective-permute-start | bytes 2359304 | tf_op jit(solution)/shard_map/ppermute | solution.py:606
  43.7 7.7 %collective-permute-start.6 = (bf16[512,768]{1,0:T(8,128)(2,1)S(1)}, bf16[512,768]{1,0:T(8,128)(2,1)S(1)}, u32[]{:S(2)}, u32[]{:S(2)}) collective-permute-start(bf16[512,768]{1,0:T(8,128)(2,1)S(1)} %get-tuple-element.31.mine_ref), channel_id=1, source_target_pairs={{0,1},{1,0},{2,3},{3,2},{4,5},{5,4},{6,7},{7,6},{8,9},{9,8},{10,11... | collective-permute-start | bytes 2359304 | tf_op jit(solution)/shard_map/ppermute | solution.py:606
  43.9 21.7 %collective-permute-start.4 = (bf16[384,768]{1,0:T(8,128)(2,1)}, bf16[384,768]{1,0:T(8,128)(2,1)}, u32[]{:S(2)}, u32[]{:S(2)}) collective-permute-start(bf16[384,768]{1,0:T(8,128)(2,1)} %w_own_ref.3), channel_id=1, source_target_pairs={{0,1},{1,0},{2,3},{3,2},{4,5},{5,4},{6,7},{7,6},{8,9},{9,8},{10,11... | collective-permute-start | bytes 1769480 | tf_op jit(solution)/shard_map/ppermute | solution.py:606
  44.3 5.0 %collective-permute-start = (s32[8,1,384]{2,1,0:T(1,128)S(1)}, s32[8,1,384]{2,1,0:T(1,128)S(1)}, u32[]{:S(2)}, u32[]{:S(2)}) collective-permute-start(s32[8,1,384]{2,1,0:T(1,128)S(1)} %all_to_all.15.got_ref), channel_id=1, source_target_pairs={{0,16},{2,18},{4,20},{6,22},{8,24},{10,26},{12,28},{14,30},{16,0},... | collective-permute-start | bytes 36872 | tf_op jit(solution)/shard_map/ppermute | solution.py:609
  52.7 9.3 %collective-permute-start.9 = (f32[1,1,1536]{2,1,0:T(1,128)S(1)}, f32[1,1,1536]{2,1,0:T(1,128)S(1)}, u32[]{:S(2)}, u32[]{:S(2)}) collective-permute-start(f32[1,1,1536]{2,1,0:T(1,128)S(1)} %shard_map.164), channel_id=1, source_target_pairs={{0,24},{2,26},{4,28},{6,30},{8,16},{10,18},{12,20},{14,22},{16,8},... | collective-permute-start | bytes 18440 | tf_op jit(solution)/shard_map/ppermute | solution.py:609
  57.2 5.4 %collective-permute-start.8 = (f32[1,1,1536]{2,1,0:T(1,128)S(1)}, f32[1,1,1536]{2,1,0:T(1,128)S(1)}, u32[]{:S(2)}, u32[]{:S(2)}) collective-permute-start(f32[1,1,1536]{2,1,0:T(1,128)S(1)} %shard_map.164), channel_id=1, source_target_pairs={{0,16},{2,18},{4,20},{6,22},{8,24},{10,26},{12,28},{14,30},{16,0},... | collective-permute-start | bytes 18440 | tf_op jit(solution)/shard_map/ppermute | solution.py:609
  57.2 5.4 %collective-permute-start.7 = (f32[1,1,1536]{2,1,0:T(1,128)S(1)}, f32[1,1,1536]{2,1,0:T(1,128)S(1)}, u32[]{:S(2)}, u32[]{:S(2)}) collective-permute-start(f32[1,1,1536]{2,1,0:T(1,128)S(1)} %shard_map.164), channel_id=1, source_target_pairs={{0,8},{2,10},{4,12},{6,14},{8,0},{10,2},{12,4},{14,6},{16,24},{18,... | collective-permute-start | bytes 18440 | tf_op jit(solution)/shard_map/ppermute | solution.py:609
  59.8 10.6 %collective-permute-start.2 = (bf16[256,384]{1,0:T(8,128)(2,1)S(1)}, bf16[256,384]{1,0:T(8,128)(2,1)S(1)}, u32[]{:S(2)}, u32[]{:S(2)}) collective-permute-start(bf16[256,384]{1,0:T(8,128)(2,1)S(1)} %bitcast.28), channel_id=1, source_target_pairs={{0,1},{1,0},{2,3},{3,2},{4,5},{5,4},{6,7},{7,6},{8,9},{9,8},{10,11... | collective-permute-start | bytes 589832 | tf_op jit(solution)/shard_map/ppermute | solution.py:606
  62.0 8.3 %collective-permute-start.3 = (bf16[256,384]{1,0:T(8,128)(2,1)S(1)}, bf16[256,384]{1,0:T(8,128)(2,1)S(1)}, u32[]{:S(2)}, u32[]{:S(2)}) collective-permute-start(bf16[256,384]{1,0:T(8,128)(2,1)S(1)} %bitcast.30), channel_id=1, source_target_pairs={{0,1},{1,0},{2,3},{3,2},{4,5},{5,4},{6,7},{7,6},{8,9},{9,8},{10,11... | collective-permute-start | bytes 589832 | tf_op jit(solution)/shard_map/ppermute | solution.py:606
  62.6 3.9 %collective-permute-start.10 = (f32[4,1,1536]{2,1,0:T(1,128)S(1)}, f32[4,1,1536]{2,1,0:T(1,128)S(1)}, u32[]{:S(2)}, u32[]{:S(2)}) collective-permute-start(f32[4,1,1536]{2,1,0:T(1,128)S(1)} %pad_maximum_fusion.refs_0_), channel_id=1, source_target_pairs={{0,2},{2,0},{4,6},{6,4},{8,10},{10,8},{12,14},{14,12},{16,18},{18,... | collective-permute-start | bytes 73736 | tf_op jit(solution)/shard_map/ppermute | solution.py:609
  64.2 3.8 %collective-permute-start.11 = (f32[4,1,1536]{2,1,0:T(1,128)S(1)}, f32[4,1,1536]{2,1,0:T(1,128)S(1)}, u32[]{:S(2)}, u32[]{:S(2)}) collective-permute-start(f32[4,1,1536]{2,1,0:T(1,128)S(1)} %pad_maximum_fusion.refs_0_), channel_id=1, source_target_pairs={{0,4},{2,6},{4,0},{6,2},{8,12},{10,14},{12,8},{14,10},{16,20},{18,... | collective-permute-start | bytes 73736 | tf_op jit(solution)/shard_map/ppermute | solution.py:609
  65.7 4.7 %collective-permute-start.12 = (f32[4,1,1536]{2,1,0:T(1,128)S(1)}, f32[4,1,1536]{2,1,0:T(1,128)S(1)}, u32[]{:S(2)}, u32[]{:S(2)}) collective-permute-start(f32[4,1,1536]{2,1,0:T(1,128)S(1)} %pad_maximum_fusion.refs_0_), channel_id=1, source_target_pairs={{0,6},{2,4},{4,2},{6,0},{8,14},{10,12},{12,10},{14,8},{16,22},{18,... | collective-permute-start | bytes 73736 | tf_op jit(solution)/shard_map/ppermute | solution.py:609
  74.8 1.8 %collective-permute-start.13 = (bf16[512,384]{1,0:T(8,128)(2,1)S(1)}, bf16[512,384]{1,0:T(8,128)(2,1)S(1)}, u32[]{:S(2)}, u32[]{:S(2)}) collective-permute-start(bf16[512,384]{1,0:T(8,128)(2,1)S(1)} %get-tuple-element.34.mine_ref), channel_id=1, source_target_pairs={{0,1},{1,0},{2,3},{3,2},{4,5},{5,4},{6,7},{7,6},{8,9},{9,8},{10,11... | collective-permute-start | bytes 1179656 | tf_op jit(solution)/shard_map/ppermute | solution.py:606
  80.5 45.0 %all-to-all-start.2 = ((bf16[16,128,384]{2,1,0:T(8,128)(2,1)}), bf16[16,128,384]{2,1,0:T(8,128)(2,1)S(1)}, u32[]{:S(2)}, u32[]{:S(2)}) async-start(bf16[16,128,384]{2,1,0:T(8,128)(2,1)} %get-tuple-element.47), calls=%async_computation.2 | async-start | bytes 3145728 | tf_op jit(solution)/shard_map/all_to_all | solution.py:614
  85.7 33.7 %copy-start.2 = (bf16[512,384]{1,0:T(8,128)(2,1)S(1)}, bf16[512,384]{1,0:T(8,128)(2,1)}, u32[]{:S(2)}) copy-start(bf16[512,384]{1,0:T(8,128)(2,1)} %refs_8_.1) | copy-start | bytes 1179652
  85.7 33.7 %copy-start.5 = (bf16[512,384]{1,0:T(8,128)(2,1)S(1)}, bf16[512,384]{1,0:T(8,128)(2,1)}, u32[]{:S(2)}) copy-start(bf16[512,384]{1,0:T(8,128)(2,1)} %get-tuple-element.36.refs_5_) | copy-start | bytes 1179652
  88.6 12.3 %collective-permute-start.14 = (bf16[8,56,384]{2,1,0:T(8,128)(2,1)S(1)}, bf16[8,56,384]{2,1,0:T(8,128)(2,1)S(1)}, u32[]{:S(2)}, u32[]{:S(2)}) collective-permute-start(bf16[8,56,384]{2,1,0:T(8,128)(2,1)S(1)} %get-tuple-element.38), channel_id=1, source_target_pairs={{0,2},{2,0},{4,6},{6,4},{8,10},{10,8},{12,14},{14,12},{16,18},{18,... | collective-permute-start | bytes 1032200 | tf_op jit(solution)/shard_map/ppermute | solution.py:609
  101.0 9.4 %collective-permute-start.15 = (bf16[4,56,384]{2,1,0:T(8,128)(2,1)S(1)}, bf16[4,56,384]{2,1,0:T(8,128)(2,1)S(1)}, u32[]{:S(2)}, u32[]{:S(2)}) collective-permute-start(bf16[4,56,384]{2,1,0:T(8,128)(2,1)S(1)} %get-tuple-element.40), channel_id=1, source_target_pairs={{0,4},{2,6},{4,0},{6,2},{8,12},{10,14},{12,8},{14,10},{16,20},{18,... | collective-permute-start | bytes 516104 | tf_op jit(solution)/shard_map/ppermute | solution.py:609
  110.5 8.6 %collective-permute-start.16 = (bf16[2,56,384]{2,1,0:T(8,128)(2,1)S(1)}, bf16[2,56,384]{2,1,0:T(8,128)(2,1)S(1)}, u32[]{:S(2)}, u32[]{:S(2)}) collective-permute-start(bf16[2,56,384]{2,1,0:T(8,128)(2,1)S(1)} %get-tuple-element.42), channel_id=1, source_target_pairs={{0,8},{2,10},{4,12},{6,14},{8,0},{10,2},{12,4},{14,6},{16,24},{18,... | collective-permute-start | bytes 258056 | tf_op jit(solution)/shard_map/ppermute | solution.py:609
  119.1 5.7 %collective-permute-start.17 = (bf16[1,56,384]{2,1,0:T(8,128)(2,1)S(1)}, bf16[1,56,384]{2,1,0:T(8,128)(2,1)S(1)}, u32[]{:S(2)}, u32[]{:S(2)}) collective-permute-start(bf16[1,56,384]{2,1,0:T(8,128)(2,1)S(1)} %get-tuple-element.44), channel_id=1, source_target_pairs={{0,16},{2,18},{4,20},{6,22},{8,24},{10,26},{12,28},{14,30},{16,0},... | collective-permute-start | bytes 129032 | tf_op jit(solution)/shard_map/ppermute | solution.py:609
  (10 other events, 88.2 us)

commit v10 on v9

--- a/solution.py
+++ b/solution.py
@@ -320,6 +320,11 @@
         found.append((low, high - low))
         high = low
     return found
+
+
+def rising(shards):
+    total = shards.bit_length() - 1
+    return [(low, min(2, total - low)) for low in range(0, total, 2)]
 
 
 def pooled_rows(me, pieces, width):
@@ -437,12 +442,13 @@
 
 def chunk_body(
     per, texts_here, self_ref, core_ref, mine_ref, other_ref, agg_ref, down_ref, pick_ref, own_ref,
-    grad_ref, keep_ref, give_ref, w_ref, text_ref
+    grad_ref, *refs
 ):
-    kept, _, half = keep_ref.shape
-    shards = 2 * kept
+    *part_refs, w_ref, text_ref, all_ref = refs
+    shards, rows_each, half = all_ref.shape
+    ways, kept = len(part_refs), shards // len(part_refs)
     deep = up_to(per, ROWS)
-    text_rows = keep_ref.shape[1] - deep
+    text_rows = rows_each - deep
     me = self_ref[0]
     own = pl.multiple_of(core_ref[0] * half, LANES)
     far = pl.multiple_of((1 - core_ref[0]) * half, LANES)
@@ -462,23 +468,12 @@
             high = line.astype(jnp.bfloat16).astype(jnp.float32)
             block = jnp.where(row == i, high, block)
             block = jnp.where(row == text_rows // 2 + i, line - high, block)
-        block = block.astype(jnp.bfloat16)
         step = q ^ me
-        turned = step * 0
-        reach = 1
-        while reach < shards:
-            turned = 2 * turned + ((step // reach) & 1)
-            reach *= 2
-
-        @pl.when(turned < kept)
-        def _():
-            keep_ref[turned, :deep, :] = piece
-            keep_ref[turned, deep:, :] = block
-
-        @pl.when(turned >= kept)
-        def _():
-            give_ref[turned - kept, :deep, :] = piece
-            give_ref[turned - kept, deep:, :] = block
+        spot = (step & (ways - 1)) * kept + lax.shift_right_logical(step, ways.bit_length() - 1)
+        all_ref[spot, :deep, :] = piece
+        all_ref[spot, deep:, :] = block.astype(jnp.bfloat16)
+    for c in range(ways):
+        part_refs[c][...] = all_ref[c * kept : (c + 1) * kept]
 
 
 def backward_body(
@@ -513,24 +508,26 @@
     down_copy.wait()
 
 
-def fold(mine, theirs, deep):
-    total = mine.astype(jnp.float32) + theirs.astype(jnp.float32)
+def fold(refs, s, deep):
+    total = sum(ref[s].astype(jnp.float32) for ref in refs)
     lines = (total.shape[0] - deep) // 2
     return total[:deep, :], total[deep : deep + lines, :] + total[deep + lines :, :]
 
 
-def fold_body(deep, mine_ref, theirs_ref, keep_ref, give_ref):
-    kept = keep_ref.shape[0]
-    for s in range(2 * kept):
-        w_sum, text = fold(mine_ref[s], theirs_ref[s], deep)
+def fold_body(deep, taken, *refs):
+    in_refs, out_refs = refs[:taken], refs[taken:]
+    ways = len(out_refs)
+    for s in range(in_refs[0].shape[0]):
+        w_sum, text = fold(in_refs, s, deep)
         high = text.astype(jnp.bfloat16).astype(jnp.float32)
-        out_ref = (keep_ref if s < kept else give_ref).at[s % kept]
+        out_ref = out_refs[s % ways].at[s // ways]
         out_ref[:deep, :] = w_sum.astype(jnp.bfloat16)
         out_ref[deep:, :] = jnp.concatenate([high, text - high], axis=0).astype(jnp.bfloat16)
 
 
-def close_body(deep, mine_ref, theirs_ref, w_ref, text_ref):
-    w_sum, text = fold(mine_ref[0], theirs_ref[0], deep)
+def close_body(deep, taken, *refs):
+    w_ref, text_ref = refs[taken:]
+    w_sum, text = fold(refs[:taken], 0, deep)
     w_ref[...] = w_sum
     text_ref[...] = text[: text_ref.shape[0], :]
 
@@ -778,7 +775,9 @@
     grad_tiles = out_grad.reshape(tiles_here, tile_rows, half)
     slope_other = swap(slope)
     text_rows = up_to(2 * texts_here, 8)
-    halves = (shards // 2, deep + text_rows, half)
+    bits = [(low, count) for low, count in rising(shards)]
+    ways = 1 << bits[0][1]
+    portion = (shards // ways, deep + text_rows, half)
     send, down = call(
         backward_body,
         [shape((shards, tile_rows, half)), shape((nodes_here, half))],
@@ -794,9 +793,9 @@
         out_specs=[HBM] * 2,
     )
     returned = spread(send)
-    keep, give = call(
+    parts = call(
         functools.partial(chunk_body, per, texts_here),
-        [shape(halves), shape(halves)],
+        [shape(portion)] * ways,
         [
             me, core, slope_kept, slope_other, aggregate, down, picked,
             own.reshape(nodes_here, slots), out_grad,
@@ -806,6 +805,7 @@
         scratch=[
             pltpu.VMEM((width + ROWS, half), jnp.float32),
             pltpu.VMEM((slots, half), jnp.float32),
+            pltpu.VMEM((shards, deep + text_rows, half), jnp.bfloat16),
         ],
     )
     local = call(
@@ -815,24 +815,25 @@
         [SMEM, SMEM] + [VMEM] * 3,
         flops=2 * adj_values.size * half,
     )
-    reach = 1
-    given = toward(give, reach)
-    while 2 * reach < shards:
-        part = (shards // (4 * reach), deep + text_rows, half)
-        keep, give = call(
-            functools.partial(fold_body, deep),
-            [shape(part), shape(part)],
-            [keep, given],
-            [VMEM] * 2,
-            flops=4 * math.prod(part),
-        )
-        reach = 2 * reach
-        given = toward(give, reach)
+    for turn, (low, _) in enumerate(bits):
+        arrived = [parts[0]]
+        for c in range(1, len(parts)):
+            arrived.append(toward(parts[c], c << low))
+        if turn + 1 < len(bits):
+            ways = 1 << bits[turn + 1][1]
+            portion = (portion[0] // ways,) + portion[1:]
+            parts = call(
+                functools.partial(fold_body, deep, len(arrived)),
+                [shape(portion)] * ways,
+                arrived,
+                [VMEM] * len(arrived),
+                flops=4 * math.prod(portion),
+            )
     w_part, text_grad = call(
-        functools.partial(close_body, deep),
+        functools.partial(close_body, deep, len(arrived)),
         [shape((deep, half), jnp.float32), shape((texts_here, half), jnp.float32)],
-        [keep, given],
-        [VMEM] * 2,
+        arrived,
+        [VMEM] * len(arrived),
         flops=1000,
     )
     node_grad = call(

time: 129 us -> 130 us (level)
  waiting for transfers between devices: 37.3 us -> 40.3 us
    ppermute x12 -> x14, waiting for transfers between devices: 33.1 us -> 36 us  [toward(): lax.ppermute(values, 'graph', [(i, i ^ reach) for i in range(shards)])]
    ppermute x12 -> x14, starting transfers between devices: 25.2 us -> 24 us  [toward(): lax.ppermute(values, 'graph', [(i, i ^ reach) for i in range(shards)])]
    pallas_call x18 -> x16, Pallas kernels: 42.6 us -> 42.3 us  [call(): pl.pallas_call(body, out_shape=tuple(outs) if many else outs[0], in_specs...]
  transfers between devices with their start and end apart: 20 -> 22, of which waited for: 11 -> 11; matrix products, arithmetic and copies ran while one was open for 0% -> 0% of each run, Pallas kernels for 24% -> 23%
where the time goes in v10:
time: 130 us
  Pallas kernels  42.3 us (33%)
  waiting for transfers between devices  40.3 us (31%)
  starting transfers between devices  34.5 us (27%)
  blocking collectives  10.1 us (8%)
  local copies, waits for them, and re-layouts  1.32 us (1%)
    pallas_call x16, Pallas kernels, call(): pl.pallas_call(body, out_shape=tuple(outs) if many else outs[0], in_specs...  42.3 us
    ppermute x14, waiting for transfers between devices, toward(): lax.ppermute(values, 'graph', [(i, i ^ reach) for i in range(shards)])  36 us
    ppermute x14, starting transfers between devices, toward(): lax.ppermute(values, 'graph', [(i, i ^ reach) for i in range(shards)])  24 us
    all_to_all x1, blocking collectives, spread(): lax.all_to_all(values, 'graph', split_axis=0, concat_axis=0, tiled=True,...  10.1 us
    all_to_all x2, starting transfers between devices, spread(): lax.all_to_all(values, 'graph', split_axis=0, concat_axis=0, tiled=True,...  9.18 us
    ppermute x6, waiting for transfers between devices, swap(): lax.ppermute(values, 'mp', [(i, cores - 1 - i) for i in range(cores)])  4.2 us
  transfers between devices with their start and end apart: 22, of which 11 were waited for; matrix products, arithmetic and copies ran while one was open for 0% of the time, Pallas kernels for 23%

profile of v10, /device:TPU:0, one launch (start us, length us, event | category | flops | bytes accessed | tf_op | source)
XLA Modules:
  0.0 129.6 jit_solution(527421990097544554)
XLA Ops:
  0.6 4.1 %collective-permute-start.1 = (bf16[4,128,384]{2,1,0:T(8,128)(2,1)}, bf16[4,128,384]{2,1,0:T(8,128)(2,1)S(1)}, u32[]{:S(2)}, u32[]{:S(2)}) collective-permute-start(bf16[4,128,384]{2,1,0:T(8,128)(2,1)} %bitcast.21), channel_id=1, source_target_pairs={{0,16},{2,18},{4,20},{6,22},{8,24},{10,26},{12,28},{14,30},{16,0},... | collective-permute-start | bytes 1179656 | tf_op jit(solution)/shard_map/ppermute | solution.py:606
  5.7 10.1 %all_to_all.15.got_ref = s32[8,1,384]{2,1,0:T(1,128)S(1)} all-to-all(s32[8,1,384]{2,1,0:T(1,128)S(1)} %shard_map.156), channel_id=1, replica_groups={{0,2,4,6,8,10,12,14},{16,18,20,22,24,26,28,30},{1,3,5,7,9,11,13,15},{17..., dimensions={0} | all-to-all | bytes 24576 | tf_op jit(solution)/shard_map/all_to_all | solution.py:611
  16.0 2.6 %shard_map.158.near_hbm = bf16[8,256,384]{2,1,0:T(8,128)(2,1)} custom-call(s32[8,2]{1,0:T(8,128)S(1)} %copy.20.asked_ref, bf16[4,128,384]{2,1,0:T(8,128)(2,1)} %bitcast.22), custom_call_target="tpu_custom_call" | custom-call | flops 1000 | bytes 1966144 | tf_op jit(solution)/shard_map/pallas_call | solution.py:57
  18.6 3.9 %collective-permute-done.1.mate_ref = bf16[4,128,384]{2,1,0:T(8,128)(2,1)S(1)} collective-permute-done((bf16[4,128,384]{2,1,0:T(8,128)(2,1)}, bf16[4,128,384]{2,1,0:T(8,128)(2,1)S(1)}, u32[]{:S(2)}, u32[]{:S(2)}) %collective-permute-start.1) | collective-permute-done | bytes 393248 | tf_op jit(solution)/shard_map/ppermute | solution.py:606
  24.1 4.0 %all-to-all-start.1 = ((bf16[8,256,384]{2,1,0:T(8,128)(2,1)}), bf16[8,256,384]{2,1,0:T(8,128)(2,1)S(1)}, u32[]{:S(2)}, u32[]{:S(2)}) async-start(bf16[8,256,384]{2,1,0:T(8,128)(2,1)} %shard_map.159), calls=%async_computation.1 | async-start | bytes 3145728 | tf_op jit(solution)/shard_map/all_to_all | solution.py:611
  28.1 7.1 %shard_map.162.mine_hbm = bf16[512,768]{1,0:T(8,128)(2,1)} custom-call(s32[1,2]{1,0:T(1,128)S(1)} %copy-done.12, bf16[512,768]{1,0:T(8,128)(2,1)} %bitcast.36, bf16[3,768,384]{2,1,0:T(8,128)(2,1)} %bitcast.45, bf16[384,768]{1,0:T(8,128)(2,1)} %w_out_hbm.1), custom_call_target="tpu_custom_call" | custom-call | flops 1610612736 | bytes 3932168 | tf_op jit(solution)/shard_map/pallas_call | solution.py:57
  35.3 2.5 %collective-permute-done.5.other_ref = bf16[512,768]{1,0:T(8,128)(2,1)S(1)} collective-permute-done((bf16[512,768]{1,0:T(8,128)(2,1)}, bf16[512,768]{1,0:T(8,128)(2,1)S(1)}, u32[]{:S(2)}, u32[]{:S(2)}) %collective-permute-start.5) | collective-permute-done | bytes 786464 | tf_op jit(solution)/shard_map/ppermute | solution.py:603
  37.8 5.9 %shard_map.163 = (bf16[512,768]{1,0:T(8,128)(2,1)S(1)}, bf16[512,768]{1,0:T(8,128)(2,1)S(1)}) custom-call(bf16[512,768]{1,0:T(8,128)(2,1)S(1)} %bitcast.37, bf16[512,768]{1,0:T(8,128)(2,1)} %shard_map.162.mine_hbm, bf16[512,768]{1,0:T(8,128)(2,1)S(1)} %collective-permute-done.5.other_ref, bf16[768,1536]{1,0:T(8,128)(2,1)} %up_hbm.1, ...), custom_call_target="tpu_custom_call" | custom-call | flops 2415919104 | bytes 8656896 | tf_op jit(solution)/shard_map/pallas_call | solution.py:57
  44.3 3.3 %collective-permute-start = (s32[8,1,384]{2,1,0:T(1,128)S(1)}, s32[8,1,384]{2,1,0:T(1,128)S(1)}, u32[]{:S(2)}, u32[]{:S(2)}) collective-permute-start(s32[8,1,384]{2,1,0:T(1,128)S(1)} %all_to_all.15.got_ref), channel_id=1, source_target_pairs={{0,16},{2,18},{4,20},{6,22},{8,24},{10,26},{12,28},{14,30},{16,0},... | collective-permute-start | bytes 36872 | tf_op jit(solution)/shard_map/ppermute | solution.py:606
  49.3 2.1 %shard_map.157 = (bf16[4,5,128,128]{3,2,1,0:T(8,128)(2,1)}, bf16[4,128,128]{2,1,0:T(8,128)(2,1)}, bf16[4,128,128]{2,1,0:T(8,128)(2,1)}, bf16[4,128,384]{2,1,0:T(8,128)(2,1)}) custom-call(s32[4,5]{1,0:T(4,128)S(1)} %copy-done.9, s32[1]{0:T(128)} %bitcast.self_ref.refs_0_, s32[8,1,384]{2,1,0:T(1,128)S(1)} %all_to_all.15.got_ref, ...), custom_call_target="tpu_custom_call" | custom-call | flops 83886080 | bytes 2383956 | tf_op jit(solution)/shard_map/pallas_call | solution.py:57
  52.7 4.4 %collective-permute-start.9 = (f32[1,1,1536]{2,1,0:T(1,128)S(1)}, f32[1,1,1536]{2,1,0:T(1,128)S(1)}, u32[]{:S(2)}, u32[]{:S(2)}) collective-permute-start(f32[1,1,1536]{2,1,0:T(1,128)S(1)} %shard_map.164), channel_id=1, source_target_pairs={{0,24},{2,26},{4,28},{6,30},{8,16},{10,18},{12,20},{14,22},{16,8},... | collective-permute-start | bytes 18440 | tf_op jit(solution)/shard_map/ppermute | solution.py:606
  59.8 2.2 %shard_map.161 = bf16[2,128,384]{2,1,0:T(8,128)(2,1)S(1)} custom-call(s32[4,5]{1,0:T(4,128)} %ids_ref.5, s32[1]{0:T(128)} %bitcast.self_ref.refs_0_, bf16[4,5,128,128]{3,2,1,0:T(8,128)(2,1)} %get-tuple-element.26.kept_hbm, bf16[4,128,384]{2,1,0:T(8,128)(2,1)} %bitcast.24, bf16[8,256,384]{2,1,0:T(8,128)(2,1)S(1)} %all-to-all-done.1.remote_ref), custom_call_target="tpu_custom_call" | custom-call | flops 125829120 | bytes 2818132 | tf_op jit(solution)/shard_map/pallas_call | solution.py:57
  68.0 2.3 %collective-permute-done.12.refs_3_ = f32[4,1,1536]{2,1,0:T(1,128)S(1)} collective-permute-done((f32[4,1,1536]{2,1,0:T(1,128)S(1)}, f32[4,1,1536]{2,1,0:T(1,128)S(1)}, u32[]{:S(2)}, u32[]{:S(2)}) %collective-permute-start.12) | collective-permute-done | bytes 24608 | tf_op jit(solution)/shard_map/ppermute | solution.py:606
  70.4 4.4 %shard_map.165 = (bf16[512,384]{1,0:T(8,128)(2,1)}, bf16[512,384]{1,0:T(8,128)(2,1)S(1)}, bf16[512,384]{1,0:T(8,128)(2,1)}, bf16[512,384]{1,0:T(8,128)(2,1)}) custom-call(s32[1]{0:T(128)} %bitcast.self_ref.refs_0_, s32[1]{0:T(128)} %bitcast.1.core_ref.refs_1_, bf16[256,384]{1,0:T(8,128)(2,1)S(1)} %bitcast.29, bf16[256,384]{1,0:T(8,128)(2,1)S(1)} %bitcast.31, ...), custom_call_target="tpu_custom_call" | custom-call | flops 301989888 | bytes 4685832 | tf_op jit(solution)/shard_map/pallas_call | solution.py:57
  76.6 3.9 %shard_map.166 = (bf16[16,128,384]{2,1,0:T(8,128)(2,1)}, bf16[512,384]{1,0:T(8,128)(2,1)}) custom-call(s32[4,5]{1,0:T(4,128)S(1)} %copy-done.10, s32[1]{0:T(128)} %bitcast.self_ref.refs_0_, s32[1]{0:T(128)} %bitcast.1.core_ref.refs_1_, bf16[512,384]{1,0:T(8,128)(2,1)S(1)} %get-tuple-element.34.mine_ref, ...), custom_call_target="tpu_custom_call" | custom-call | flops 553648128 | bytes 3997784 | tf_op jit(solution)/shard_map/pallas_call | solution.py:57
  80.5 5.2 %all-to-all-start.2 = ((bf16[16,128,384]{2,1,0:T(8,128)(2,1)}), bf16[16,128,384]{2,1,0:T(8,128)(2,1)S(1)}, u32[]{:S(2)}, u32[]{:S(2)}) async-start(bf16[16,128,384]{2,1,0:T(8,128)(2,1)} %get-tuple-element.47), calls=%async_computation.2 | async-start | bytes 3145728 | tf_op jit(solution)/shard_map/all_to_all | solution.py:611
  85.7 2.6 %shard_map.167 = (bf16[4,56,384]{2,1,0:T(8,128)(2,1)S(1)}, bf16[4,56,384]{2,1,0:T(8,128)(2,1)S(1)}, bf16[4,56,384]{2,1,0:T(8,128)(2,1)S(1)}, bf16[4,56,384]{2,1,0:T(8,128)(2,1)S(1)}) custom-call(s32[1]{0:T(128)} %bitcast.self_ref.refs_0_, s32[1]{0:T(128)} %bitcast.1.core_ref.refs_1_, bf16[512,384]{1,0:T(8,128)(2,1)} %get-tuple-element.33.refs_2_, ...), custom_call_target="tpu_custom_call" | custom-call | flops 402653184 | bytes 2916360 | tf_op jit(solution)/shard_map/pallas_call | solution.py:57
  91.8 5.4 %collective-permute-done.14.refs_1_ = bf16[4,56,384]{2,1,0:T(8,128)(2,1)S(1)} collective-permute-done((bf16[4,56,384]{2,1,0:T(8,128)(2,1)S(1)}, bf16[4,56,384]{2,1,0:T(8,128)(2,1)S(1)}, u32[]{:S(2)}, u32[]{:S(2)}) %collective-permute-start.14) | collective-permute-done | bytes 172064 | tf_op jit(solution)/shard_map/ppermute | solution.py:606
  97.3 10.5 %collective-permute-done.15.refs_2_ = bf16[4,56,384]{2,1,0:T(8,128)(2,1)S(1)} collective-permute-done((bf16[4,56,384]{2,1,0:T(8,128)(2,1)S(1)}, bf16[4,56,384]{2,1,0:T(8,128)(2,1)S(1)}, u32[]{:S(2)}, u32[]{:S(2)}) %collective-permute-start.15) | collective-permute-done | bytes 172064 | tf_op jit(solution)/shard_map/ppermute | solution.py:606
  107.7 2.1 %collective-permute-done.16.refs_3_ = bf16[4,56,384]{2,1,0:T(8,128)(2,1)S(1)} collective-permute-done((bf16[4,56,384]{2,1,0:T(8,128)(2,1)S(1)}, bf16[4,56,384]{2,1,0:T(8,128)(2,1)S(1)}, u32[]{:S(2)}, u32[]{:S(2)}) %collective-permute-start.16) | collective-permute-done | bytes 172064 | tf_op jit(solution)/shard_map/ppermute | solution.py:606
  110.0 3.3 %collective-permute-start.18 = (bf16[1,56,384]{2,1,0:T(8,128)(2,1)S(1)}, bf16[1,56,384]{2,1,0:T(8,128)(2,1)S(1)}, u32[]{:S(2)}, u32[]{:S(2)}) collective-permute-start(bf16[1,56,384]{2,1,0:T(8,128)(2,1)S(1)} %get-tuple-element.43), channel_id=1, source_target_pairs={{0,16},{2,18},{4,20},{6,22},{8,24},{10,26},{12,28},{14,30},{16,0},... | collective-permute-start | bytes 129032 | tf_op jit(solution)/shard_map/ppermute | solution.py:606
  114.6 2.4 %shard_map.170.local_hbm = f32[4,128,384]{2,1,0:T(8,128)S(1)} custom-call(s32[4,5]{1,0:T(4,128)S(1)} %copy-done.10, s32[1]{0:T(128)} %bitcast.self_ref.refs_0_, bf16[4,128,384]{2,1,0:T(8,128)(2,1)S(1)} %bitcast.27, bf16[4,5,128,128]{3,2,1,0:T(8,128)(2,1)S(1)} %copy-done.4, bf16[4,128,384]{2,1,0:T(8,128)(2,1)S(1)} %bitcast.26), custom_call_target="tpu_custom_call" | custom-call | flops 251658240 | bytes 2228308 | tf_op jit(solution)/shard_map/pallas_call | solution.py:57
  117.9 8.2 %collective-permute-done.18.refs_2_ = bf16[1,56,384]{2,1,0:T(8,128)(2,1)S(1)} collective-permute-done((bf16[1,56,384]{2,1,0:T(8,128)(2,1)S(1)}, bf16[1,56,384]{2,1,0:T(8,128)(2,1)S(1)}, u32[]{:S(2)}, u32[]{:S(2)}) %collective-permute-start.18) | collective-permute-done | bytes 43040 | tf_op jit(solution)/shard_map/ppermute | solution.py:606
  126.8 2.6 %shard_map.171 = bf16[4,128,384]{2,1,0:T(8,128)(2,1)} custom-call(s32[1]{0:T(128)} %bitcast.self_ref.refs_0_, s32[8,2]{1,0:T(8,128)S(1)} %copy.20.asked_ref, s32[8,2]{1,0:T(8,128)S(1)} %copy.23.mate_ref, f32[4,128,384]{2,1,0:T(8,128)} %copy-done.3, bf16[16,128,384]{2,1,0:T(8,128)(2,1)S(1)} %all-to-all-done.2.got_ref), custom_call_target="tpu_custom_call" | custom-call | flops 1000 | bytes 2752644 | tf_op jit(solution)/shard_map/pallas_call | solution.py:57
  (72 shorter events, 23.3 us)
Async XLA Ops:
  0.6 21.9 %collective-permute-start.1 = (bf16[4,128,384]{2,1,0:T(8,128)(2,1)}, bf16[4,128,384]{2,1,0:T(8,128)(2,1)S(1)}, u32[]{:S(2)}, u32[]{:S(2)}) collective-permute-start(bf16[4,128,384]{2,1,0:T(8,128)(2,1)} %bitcast.21), channel_id=1, source_target_pairs={{0,16},{2,18},{4,20},{6,22},{8,24},{10,26},{12,28},{14,30},{16,0},... | collective-permute-start | bytes 1179656 | tf_op jit(solution)/shard_map/ppermute | solution.py:606
  24.1 33.7 %all-to-all-start.1 = ((bf16[8,256,384]{2,1,0:T(8,128)(2,1)}), bf16[8,256,384]{2,1,0:T(8,128)(2,1)S(1)}, u32[]{:S(2)}, u32[]{:S(2)}) async-start(bf16[8,256,384]{2,1,0:T(8,128)(2,1)} %shard_map.159), calls=%async_computation.1 | async-start | bytes 3145728 | tf_op jit(solution)/shard_map/all_to_all | solution.py:611
  35.2 2.6 %collective-permute-start.5 = (bf16[512,768]{1,0:T(8,128)(2,1)}, bf16[512,768]{1,0:T(8,128)(2,1)S(1)}, u32[]{:S(2)}, u32[]{:S(2)}) collective-permute-start(bf16[512,768]{1,0:T(8,128)(2,1)} %shard_map.162.mine_hbm), channel_id=1, source_target_pairs={{0,1},{1,0},{2,3},{3,2},{4,5},{5,4},{6,7},{7,6},{8,9},{9,8},{10,11... | collective-permute-start | bytes 2359304 | tf_op jit(solution)/shard_map/ppermute | solution.py:603
  43.7 7.7 %collective-permute-start.6 = (bf16[512,768]{1,0:T(8,128)(2,1)S(1)}, bf16[512,768]{1,0:T(8,128)(2,1)S(1)}, u32[]{:S(2)}, u32[]{:S(2)}) collective-permute-start(bf16[512,768]{1,0:T(8,128)(2,1)S(1)} %get-tuple-element.31.mine_ref), channel_id=1, source_target_pairs={{0,1},{1,0},{2,3},{3,2},{4,5},{5,4},{6,7},{7,6},{8,9},{9,8},{10,11... | collective-permute-start | bytes 2359304 | tf_op jit(solution)/shard_map/ppermute | solution.py:603
  43.9 21.7 %collective-permute-start.4 = (bf16[384,768]{1,0:T(8,128)(2,1)}, bf16[384,768]{1,0:T(8,128)(2,1)}, u32[]{:S(2)}, u32[]{:S(2)}) collective-permute-start(bf16[384,768]{1,0:T(8,128)(2,1)} %w_own_ref.3), channel_id=1, source_target_pairs={{0,1},{1,0},{2,3},{3,2},{4,5},{5,4},{6,7},{7,6},{8,9},{9,8},{10,11... | collective-permute-start | bytes 1769480 | tf_op jit(solution)/shard_map/ppermute | solution.py:603
  44.3 5.0 %collective-permute-start = (s32[8,1,384]{2,1,0:T(1,128)S(1)}, s32[8,1,384]{2,1,0:T(1,128)S(1)}, u32[]{:S(2)}, u32[]{:S(2)}) collective-permute-start(s32[8,1,384]{2,1,0:T(1,128)S(1)} %all_to_all.15.got_ref), channel_id=1, source_target_pairs={{0,16},{2,18},{4,20},{6,22},{8,24},{10,26},{12,28},{14,30},{16,0},... | collective-permute-start | bytes 36872 | tf_op jit(solution)/shard_map/ppermute | solution.py:606
  52.7 9.3 %collective-permute-start.9 = (f32[1,1,1536]{2,1,0:T(1,128)S(1)}, f32[1,1,1536]{2,1,0:T(1,128)S(1)}, u32[]{:S(2)}, u32[]{:S(2)}) collective-permute-start(f32[1,1,1536]{2,1,0:T(1,128)S(1)} %shard_map.164), channel_id=1, source_target_pairs={{0,24},{2,26},{4,28},{6,30},{8,16},{10,18},{12,20},{14,22},{16,8},... | collective-permute-start | bytes 18440 | tf_op jit(solution)/shard_map/ppermute | solution.py:606
  57.2 5.4 %collective-permute-start.8 = (f32[1,1,1536]{2,1,0:T(1,128)S(1)}, f32[1,1,1536]{2,1,0:T(1,128)S(1)}, u32[]{:S(2)}, u32[]{:S(2)}) collective-permute-start(f32[1,1,1536]{2,1,0:T(1,128)S(1)} %shard_map.164), channel_id=1, source_target_pairs={{0,16},{2,18},{4,20},{6,22},{8,24},{10,26},{12,28},{14,30},{16,0},... | collective-permute-start | bytes 18440 | tf_op jit(solution)/shard_map/ppermute | solution.py:606
  57.2 5.4 %collective-permute-start.7 = (f32[1,1,1536]{2,1,0:T(1,128)S(1)}, f32[1,1,1536]{2,1,0:T(1,128)S(1)}, u32[]{:S(2)}, u32[]{:S(2)}) collective-permute-start(f32[1,1,1536]{2,1,0:T(1,128)S(1)} %shard_map.164), channel_id=1, source_target_pairs={{0,8},{2,10},{4,12},{6,14},{8,0},{10,2},{12,4},{14,6},{16,24},{18,... | collective-permute-start | bytes 18440 | tf_op jit(solution)/shard_map/ppermute | solution.py:606
  59.8 10.6 %collective-permute-start.2 = (bf16[256,384]{1,0:T(8,128)(2,1)S(1)}, bf16[256,384]{1,0:T(8,128)(2,1)S(1)}, u32[]{:S(2)}, u32[]{:S(2)}) collective-permute-start(bf16[256,384]{1,0:T(8,128)(2,1)S(1)} %bitcast.28), channel_id=1, source_target_pairs={{0,1},{1,0},{2,3},{3,2},{4,5},{5,4},{6,7},{7,6},{8,9},{9,8},{10,11... | collective-permute-start | bytes 589832 | tf_op jit(solution)/shard_map/ppermute | solution.py:603
  62.0 8.3 %collective-permute-start.3 = (bf16[256,384]{1,0:T(8,128)(2,1)S(1)}, bf16[256,384]{1,0:T(8,128)(2,1)S(1)}, u32[]{:S(2)}, u32[]{:S(2)}) collective-permute-start(bf16[256,384]{1,0:T(8,128)(2,1)S(1)} %bitcast.30), channel_id=1, source_target_pairs={{0,1},{1,0},{2,3},{3,2},{4,5},{5,4},{6,7},{7,6},{8,9},{9,8},{10,11... | collective-permute-start | bytes 589832 | tf_op jit(solution)/shard_map/ppermute | solution.py:603
  62.6 3.9 %collective-permute-start.10 = (f32[4,1,1536]{2,1,0:T(1,128)S(1)}, f32[4,1,1536]{2,1,0:T(1,128)S(1)}, u32[]{:S(2)}, u32[]{:S(2)}) collective-permute-start(f32[4,1,1536]{2,1,0:T(1,128)S(1)} %pad_maximum_fusion.refs_0_), channel_id=1, source_target_pairs={{0,2},{2,0},{4,6},{6,4},{8,10},{10,8},{12,14},{14,12},{16,18},{18,... | collective-permute-start | bytes 73736 | tf_op jit(solution)/shard_map/ppermute | solution.py:606
  64.2 3.8 %collective-permute-start.11 = (f32[4,1,1536]{2,1,0:T(1,128)S(1)}, f32[4,1,1536]{2,1,0:T(1,128)S(1)}, u32[]{:S(2)}, u32[]{:S(2)}) collective-permute-start(f32[4,1,1536]{2,1,0:T(1,128)S(1)} %pad_maximum_fusion.refs_0_), channel_id=1, source_target_pairs={{0,4},{2,6},{4,0},{6,2},{8,12},{10,14},{12,8},{14,10},{16,20},{18,... | collective-permute-start | bytes 73736 | tf_op jit(solution)/shard_map/ppermute | solution.py:606
  65.7 4.7 %collective-permute-start.12 = (f32[4,1,1536]{2,1,0:T(1,128)S(1)}, f32[4,1,1536]{2,1,0:T(1,128)S(1)}, u32[]{:S(2)}, u32[]{:S(2)}) collective-permute-start(f32[4,1,1536]{2,1,0:T(1,128)S(1)} %pad_maximum_fusion.refs_0_), channel_id=1, source_target_pairs={{0,6},{2,4},{4,2},{6,0},{8,14},{10,12},{12,10},{14,8},{16,22},{18,... | collective-permute-start | bytes 73736 | tf_op jit(solution)/shard_map/ppermute | solution.py:606
  74.8 1.8 %collective-permute-start.13 = (bf16[512,384]{1,0:T(8,128)(2,1)S(1)}, bf16[512,384]{1,0:T(8,128)(2,1)S(1)}, u32[]{:S(2)}, u32[]{:S(2)}) collective-permute-start(bf16[512,384]{1,0:T(8,128)(2,1)S(1)} %get-tuple-element.34.mine_ref), channel_id=1, source_target_pairs={{0,1},{1,0},{2,3},{3,2},{4,5},{5,4},{6,7},{7,6},{8,9},{9,8},{10,11... | collective-permute-start | bytes 1179656 | tf_op jit(solution)/shard_map/ppermute | solution.py:603
  80.5 46.3 %all-to-all-start.2 = ((bf16[16,128,384]{2,1,0:T(8,128)(2,1)}), bf16[16,128,384]{2,1,0:T(8,128)(2,1)S(1)}, u32[]{:S(2)}, u32[]{:S(2)}) async-start(bf16[16,128,384]{2,1,0:T(8,128)(2,1)} %get-tuple-element.47), calls=%async_computation.2 | async-start | bytes 3145728 | tf_op jit(solution)/shard_map/all_to_all | solution.py:611
  85.7 28.9 %copy-start.2 = (bf16[512,384]{1,0:T(8,128)(2,1)S(1)}, bf16[512,384]{1,0:T(8,128)(2,1)}, u32[]{:S(2)}) copy-start(bf16[512,384]{1,0:T(8,128)(2,1)} %refs_8_.1) | copy-start | bytes 1179652
  85.7 28.9 %copy-start.5 = (bf16[512,384]{1,0:T(8,128)(2,1)S(1)}, bf16[512,384]{1,0:T(8,128)(2,1)}, u32[]{:S(2)}) copy-start(bf16[512,384]{1,0:T(8,128)(2,1)} %get-tuple-element.36.refs_5_) | copy-start | bytes 1179652
  88.3 9.0 %collective-permute-start.14 = (bf16[4,56,384]{2,1,0:T(8,128)(2,1)S(1)}, bf16[4,56,384]{2,1,0:T(8,128)(2,1)S(1)}, u32[]{:S(2)}, u32[]{:S(2)}) collective-permute-start(bf16[4,56,384]{2,1,0:T(8,128)(2,1)S(1)} %get-tuple-element.38), channel_id=1, source_target_pairs={{0,2},{2,0},{4,6},{6,4},{8,10},{10,8},{12,14},{14,12},{16,18},{18,... | collective-permute-start | bytes 516104 | tf_op jit(solution)/shard_map/ppermute | solution.py:606
  90.3 17.4 %collective-permute-start.15 = (bf16[4,56,384]{2,1,0:T(8,128)(2,1)S(1)}, bf16[4,56,384]{2,1,0:T(8,128)(2,1)S(1)}, u32[]{:S(2)}, u32[]{:S(2)}) collective-permute-start(bf16[4,56,384]{2,1,0:T(8,128)(2,1)S(1)} %get-tuple-element.39), channel_id=1, source_target_pairs={{0,4},{2,6},{4,0},{6,2},{8,12},{10,14},{12,8},{14,10},{16,20},{18,... | collective-permute-start | bytes 516104 | tf_op jit(solution)/shard_map/ppermute | solution.py:606
  91.7 18.1 %collective-permute-start.16 = (bf16[4,56,384]{2,1,0:T(8,128)(2,1)S(1)}, bf16[4,56,384]{2,1,0:T(8,128)(2,1)S(1)}, u32[]{:S(2)}, u32[]{:S(2)}) collective-permute-start(bf16[4,56,384]{2,1,0:T(8,128)(2,1)S(1)} %get-tuple-element.40), channel_id=1, source_target_pairs={{0,6},{2,4},{4,2},{6,0},{8,14},{10,12},{12,10},{14,8},{16,22},{18,... | collective-permute-start | bytes 516104 | tf_op jit(solution)/shard_map/ppermute | solution.py:606
  110.0 8.0 %collective-permute-start.17 = (bf16[1,56,384]{2,1,0:T(8,128)(2,1)S(1)}, bf16[1,56,384]{2,1,0:T(8,128)(2,1)S(1)}, u32[]{:S(2)}, u32[]{:S(2)}) collective-permute-start(bf16[1,56,384]{2,1,0:T(8,128)(2,1)S(1)} %get-tuple-element.42), channel_id=1, source_target_pairs={{0,8},{2,10},{4,12},{6,14},{8,0},{10,2},{12,4},{14,6},{16,24},{18,... | collective-permute-start | bytes 129032 | tf_op jit(solution)/shard_map/ppermute | solution.py:606
  110.0 16.1 %collective-permute-start.18 = (bf16[1,56,384]{2,1,0:T(8,128)(2,1)S(1)}, bf16[1,56,384]{2,1,0:T(8,128)(2,1)S(1)}, u32[]{:S(2)}, u32[]{:S(2)}) collective-permute-start(bf16[1,56,384]{2,1,0:T(8,128)(2,1)S(1)} %get-tuple-element.43), channel_id=1, source_target_pairs={{0,16},{2,18},{4,20},{6,22},{8,24},{10,26},{12,28},{14,30},{16,0},... | collective-permute-start | bytes 129032 | tf_op jit(solution)/shard_map/ppermute | solution.py:606
  113.3 12.8 %collective-permute-start.19 = (bf16[1,56,384]{2,1,0:T(8,128)(2,1)S(1)}, bf16[1,56,384]{2,1,0:T(8,128)(2,1)S(1)}, u32[]{:S(2)}, u32[]{:S(2)}) collective-permute-start(bf16[1,56,384]{2,1,0:T(8,128)(2,1)S(1)} %get-tuple-element.44), channel_id=1, source_target_pairs={{0,24},{2,26},{4,28},{6,30},{8,16},{10,18},{12,20},{14,22},{16,8},... | collective-permute-start | bytes 129032 | tf_op jit(solution)/shard_map/ppermute | solution.py:606
  (12 other events, 116.4 us)
